TPU v7x, 32 devices: a 4x4x1 block of a 4x4x8 slice. The times are simulated.
32 devices in a mesh: data: 1 (over z), tp: 32 (over y, x, core).
Axes of the slice: x: 4, y: 4, z: 1, core: 2. Of those that a mesh axis runs over, the one named last changes fastest.
The devices are a block of a 4x4x8 slice.
Arguments:
- hidden: bfloat16 [2, 768, 4096], P('data')
- seg_ids: int32 [2, 768], P('data')
- grad_out: bfloat16 [2, 768, 4096], P('data')
- gain_attn: float32 [4096], replicated
- gain_mlp: float32 [4096], replicated
- w_q: bfloat16 [4096, 4096], P(None, 'tp')
- w_k: bfloat16 [4096, 1024], replicated
- w_v: bfloat16 [4096, 1024], replicated
- w_o: bfloat16 [4096, 4096], P('tp')
- w_gate: bfloat16 [4096, 14336], P(None, 'tp')
- w_up: bfloat16 [4096, 14336], P(None, 'tp')
- w_down: bfloat16 [14336, 4096], P('tp')
Outputs:
- output 1: bfloat16 [2, 768, 4096], P('data')
- output 2: bfloat16 [2, 768, 4096], P('data')
- output 3: float32 [4096], P('data')
- output 4: float32 [4096], P('data')
- output 5: float32 [4096, 4096], P('data', 'tp')
- output 6: float32 [4096, 1024], P('data')
- output 7: float32 [4096, 1024], P('data')
- output 8: float32 [4096, 4096], P(('data', 'tp'))
- output 9: float32 [4096, 14336], P('data', 'tp')
- output 10: float32 [4096, 14336], P('data', 'tp')
- output 11: float32 [14336, 4096], P(('data', 'tp'))
All inputs are finite; a program needn't handle non-finite values.
Results may differ from a plain program's by a relative error of at most 0.02.
Values are sent between devices in bfloat16 or wider.
A program may use at most 768 MiB of HBM per device.

v0:
```python
import functools
import jax
import jax.numpy as jnp
from jax import lax
from jax.sharding import PartitionSpec as P

HEAD_DIM = 128
EPS = 1e-5


def rms_forward(x_in, gain):
    x_float = x_in.astype(jnp.float32)
    inv_rms = lax.rsqrt(jnp.mean(x_float * x_float, axis=-1, keepdims=True) + EPS)
    normed = x_float * inv_rms
    return (normed * gain).astype(jnp.bfloat16), normed, inv_rms


def rms_backward(grad_norm, normed, inv_rms, gain):
    grad_float = grad_norm.astype(jnp.float32)
    lead_axes = tuple(range(grad_float.ndim - 1))
    gain_grad = jnp.sum(grad_float * normed, axis=lead_axes)
    scaled = grad_float * gain
    grad_x = inv_rms * (scaled - normed * jnp.mean(scaled * normed, axis=-1, keepdims=True))
    return grad_x, gain_grad


def local_attention(q_loc, k_loc, v_loc, allowed):
    scores = jnp.einsum('bqkgd,bskd->bkgqs', q_loc, k_loc, preferred_element_type=jnp.float32) * HEAD_DIM ** -0.5
    scores = jnp.where(allowed[:, None, None], scores, -1e30)
    probs = jax.nn.softmax(scores, axis=-1).astype(jnp.bfloat16)
    return jnp.einsum('bkgqs,bskd->bqkgd', probs, v_loc, preferred_element_type=jnp.float32)


def project(acts, weight):
    return jnp.einsum('bsd,de->bse', acts, weight, preferred_element_type=jnp.float32)


def solution(mesh):
    tp_size = mesh.shape['tp']

    def device_step(hidden, seg_ids, grad_out, gain_attn, gain_mlp, w_q, w_k, w_v, w_o, w_gate, w_up, w_down):
        seq_len = hidden.shape[1]
        width = hidden.shape[2]
        loc_heads = w_q.shape[1] // HEAD_DIM
        kv_heads = w_k.shape[1] // HEAD_DIM
        group = loc_heads * tp_size // kv_heads
        kv_loc = max(1, loc_heads // group)
        grp_loc = loc_heads // kv_loc
        kv_start = lax.axis_index('tp') * loc_heads // group
        w_k_loc = lax.dynamic_slice_in_dim(w_k, kv_start * HEAD_DIM, kv_loc * HEAD_DIM, axis=1)
        w_v_loc = lax.dynamic_slice_in_dim(w_v, kv_start * HEAD_DIM, kv_loc * HEAD_DIM, axis=1)
        positions = jnp.arange(seq_len)
        allowed = (positions[:, None] >= positions[None, :])[None] & (seg_ids[:, :, None] == seg_ids[:, None, :])
        attn_fn = functools.partial(local_attention, allowed=allowed)

        def forward(x_in):
            normed_a, xn_attn, inv_attn = rms_forward(x_in, gain_attn)
            q_loc = project(normed_a, w_q).astype(jnp.bfloat16).reshape(2, seq_len, kv_loc, grp_loc, HEAD_DIM)
            k_loc = project(normed_a, w_k_loc).astype(jnp.bfloat16).reshape(2, seq_len, kv_loc, HEAD_DIM)
            v_loc = project(normed_a, w_v_loc).astype(jnp.bfloat16).reshape(2, seq_len, kv_loc, HEAD_DIM)
            ctx, attn_pull = jax.vjp(attn_fn, q_loc, k_loc, v_loc)
            ctx_b = ctx.astype(jnp.bfloat16).reshape(2, seq_len, loc_heads * HEAD_DIM)
            attn_part = jnp.einsum('bse,ed->bsd', ctx_b, w_o, preferred_element_type=jnp.float32).astype(jnp.bfloat16)
            attn_out = lax.psum(attn_part, 'tp')
            resid = (x_in.astype(jnp.float32) + attn_out.astype(jnp.float32)).astype(jnp.bfloat16)
            mixed, xn_mlp, inv_mlp = rms_forward(resid, gain_mlp)
            gate = project(mixed, w_gate)
            upper = project(mixed, w_up)
            act = (jax.nn.silu(gate) * upper).astype(jnp.bfloat16)
            mlp_part = jnp.einsum('bsf,fd->bsd', act, w_down, preferred_element_type=jnp.float32).astype(jnp.bfloat16)
            mlp_out = lax.psum(mlp_part, 'tp')
            y_out = (resid.astype(jnp.float32) + mlp_out.astype(jnp.float32)).astype(jnp.bfloat16)
            return y_out, (normed_a, xn_attn, inv_attn, ctx_b, attn_pull, xn_mlp, inv_mlp, mixed, gate, upper, act)

        def spread_kv(kv_part):
            base = jnp.zeros((width, kv_heads * HEAD_DIM), jnp.float32)
            return lax.dynamic_update_slice(base, kv_part, (0, kv_start * HEAD_DIM))

        y_out, _ = forward(hidden)
        x_again, _ = lax.optimization_barrier((hidden, y_out))
        _, kept = forward(x_again)
        normed_a, xn_attn, inv_attn, ctx_b, attn_pull, xn_mlp, inv_mlp, mixed, gate, upper, act = kept
        grad_act = jnp.einsum('bsd,fd->bsf', grad_out, w_down, preferred_element_type=jnp.float32)
        grad_w_down = jnp.einsum('bsf,bsd->fd', act, grad_out, preferred_element_type=jnp.float32)
        sigmoid_g = jax.nn.sigmoid(gate)
        grad_gate = (grad_act * upper * sigmoid_g * (1.0 + gate * (1.0 - sigmoid_g))).astype(jnp.bfloat16)
        grad_up = (grad_act * gate * sigmoid_g).astype(jnp.bfloat16)
        grad_w_gate = jnp.einsum('bsd,bsf->df', mixed, grad_gate, preferred_element_type=jnp.float32)
        grad_w_up = jnp.einsum('bsd,bsf->df', mixed, grad_up, preferred_element_type=jnp.float32)
        mixed_part = (jnp.einsum('bsf,df->bsd', grad_gate, w_gate, preferred_element_type=jnp.float32) + jnp.einsum('bsf,df->bsd', grad_up, w_up, preferred_element_type=jnp.float32)).astype(jnp.bfloat16)
        grad_mixed = lax.psum(mixed_part, 'tp')
        resid_back, grad_gain_mlp = rms_backward(grad_mixed, xn_mlp, inv_mlp, gain_mlp)
        grad_resid = grad_out.astype(jnp.float32) + resid_back
        resid_b = grad_resid.astype(jnp.bfloat16)
        grad_w_o = jnp.einsum('bse,bsd->ed', ctx_b, resid_b, preferred_element_type=jnp.float32)
        grad_ctx = jnp.einsum('bsd,ed->bse', resid_b, w_o, preferred_element_type=jnp.float32)
        grad_q, grad_k, grad_v = attn_pull(grad_ctx.reshape(2, seq_len, kv_loc, grp_loc, HEAD_DIM))
        grad_q = grad_q.reshape(2, seq_len, loc_heads * HEAD_DIM)
        grad_k = grad_k.reshape(2, seq_len, kv_loc * HEAD_DIM)
        grad_v = grad_v.reshape(2, seq_len, kv_loc * HEAD_DIM)
        grad_w_q = jnp.einsum('bsd,bse->de', normed_a, grad_q, preferred_element_type=jnp.float32)
        part_w_k = jnp.einsum('bsd,bse->de', normed_a, grad_k, preferred_element_type=jnp.float32)
        part_w_v = jnp.einsum('bsd,bse->de', normed_a, grad_v, preferred_element_type=jnp.float32)
        normed_part = (jnp.einsum('bse,de->bsd', grad_q, w_q, preferred_element_type=jnp.float32) + jnp.einsum('bse,de->bsd', grad_k, w_k_loc, preferred_element_type=jnp.float32) + jnp.einsum('bse,de->bsd', grad_v, w_v_loc, preferred_element_type=jnp.float32)).astype(jnp.bfloat16)
        grad_normed = lax.psum(normed_part, 'tp')
        input_back, grad_gain_attn = rms_backward(grad_normed, xn_attn, inv_attn, gain_attn)
        grad_in = (grad_resid + input_back).astype(jnp.bfloat16)
        grad_w_k = lax.psum(spread_kv(part_w_k), 'tp')
        grad_w_v = lax.psum(spread_kv(part_w_v), 'tp')
        return (y_out, grad_in, grad_gain_attn, grad_gain_mlp, grad_w_q, grad_w_k, grad_w_v, grad_w_o, grad_w_gate, grad_w_up, grad_w_down)

    spec_act = P('data', None, None)
    spec_rows = P('data', None)
    spec_gain = P(None)
    spec_cols = P(None, 'tp')
    spec_tprows = P('tp', None)
    spec_whole = P(None, None)
    spec_stack = P(('data', 'tp'), None)
    in_specs = (spec_act, spec_rows, spec_act, spec_gain, spec_gain, spec_cols, spec_whole, spec_whole, spec_tprows, spec_cols, spec_cols, spec_tprows)
    out_specs = (spec_act, spec_act, P('data'), P('data'), P('data', 'tp'), spec_rows, spec_rows, spec_stack, P('data', 'tp'), P('data', 'tp'), spec_stack)
    return jax.shard_map(device_step, mesh=mesh, in_specs=in_specs, out_specs=out_specs, check_vma=False)
```

profile of v0, /device:TPU:97, one launch (start us, length us, event | category | flops | bytes accessed | tf_op | source)
XLA Modules:
  0.0 1202.9 jit_solution(16403989850479212639)
XLA Ops:
  7.3 0.2 iota_compare_fusion
  7.5 7.2 fusion.18
  14.8 8.9 fusion.101
  23.6 9.0 fusion.92
  32.7 10.6 fusion.71
  43.3 3.5 fusion.53
  46.8 10.3 convolution_convert_fusion.2
  57.2 0.1 all-reduce.10.cloned.1.call-start
  57.2 125.5 %all-reduce.8.cloned.1.call-done = bf16[2,768,4096]{2,1,0:T(8,128)(2,1)} async-done(((bf16[2,768,4096]{2,1,0:T(8,128)(2,1)}), bf16[2,768,4096]{2,1,0:T(8,128)(2,1)}) %all-reduce.8.cloned.1.call-update) | async-done | bytes 12582928 | tf_op jit(solution)/shard_map/psum | solution.py:64
  182.7 11.8 fusion.22
  194.6 7.5 fusion.34
  202.1 7.9 multiply_convert_fusion.3
  210.0 9.7 convolution_convert_fusion.1
  219.7 0.1 all-reduce.12.cloned.1.call-start
  219.8 121.1 %all-reduce.10.cloned.1.call-done = bf16[2,768,4096]{2,1,0:T(8,128)(2,1)} async-done(((bf16[2,768,4096]{2,1,0:T(8,128)(2,1)}), bf16[2,768,4096]{2,1,0:T(8,128)(2,1)}) %all-reduce.10.cloned.1.call-update) | async-done | bytes 12582928 | tf_op jit(solution)/shard_map/psum | solution.py:71
  340.9 14.9 %fusion.25 = bf16[2,768,4096]{2,1,0:T(8,128)(2,1)} fusion(bf16[2,768,4096]{2,1,0:T(8,128)(2,1)} %copy-done.6, bf16[2,768,4096]{2,1,0:T(8,128)(2,1)} %all-reduce.10.cloned.1.call-done), kind=kLoop, calls=%fused_computation.39 | loop fusion | flops 25165824 | bytes 37748736 | tf_op jit(solution)/shard_map/convert_element_type | solution.py:72
  355.7 7.1 fusion.29
  362.9 8.5 convolution_convert_fusion.5
  371.4 8.3 convolution_convert_fusion.4
  379.7 5.0 convolution_convert_fusion.6
  384.8 1.5 fusion.70
  386.3 1.8 fusion.155
  388.1 0.4 copy-done.8
  388.5 2.2 fusion.109
  390.7 0.7 copy-done.9
  391.4 6.6 convolution_convert_fusion
  398.1 0.1 all-reduce.14.cloned.1.call-start
  398.1 121.1 %all-reduce.12.cloned.1.call-done = bf16[2,768,4096]{2,1,0:T(8,128)(2,1)} async-done(((bf16[2,768,4096]{2,1,0:T(8,128)(2,1)}), bf16[2,768,4096]{2,1,0:T(8,128)(2,1)}) %all-reduce.12.cloned.1.call-update) | async-done | bytes 12582928 | tf_op jit(solution)/shard_map/psum | solution.py:64
  519.2 11.8 fusion.16
  531.1 7.7 fusion.63
  538.8 10.0 fusion.58
  548.8 10.9 multiply_convert_fusion.1
  559.7 11.7 fusion.61
  571.4 15.8 %add_convert_fusion.1 = bf16[2,768,4096]{2,1,0:T(8,128)(2,1)} fusion(f32[2,768,4096]{2,1,0:T(8,128)} %fusion.61, bf16[2,768,448]{1,2,0:T(8,128)(2,1)} %get-tuple-element.23, bf16[4096,448]{0,1:T(8,128)(2,1)} %param.22), kind=kOutput, calls=%fused_computation.46 | convolution fusion | flops 5649727488 | bytes 42795008 | tf_op jit(solution)/shard_map/bsf,df->bsd/dot_general | solution.py:90
  587.3 0.1 all-reduce.16.cloned.1.call-start
  587.4 121.1 %all-reduce.14.cloned.1.call-done = bf16[2,768,4096]{2,1,0:T(8,128)(2,1)} async-done(((bf16[2,768,4096]{2,1,0:T(8,128)(2,1)}), bf16[2,768,4096]{2,1,0:T(8,128)(2,1)}) %all-reduce.14.cloned.1.call-update) | async-done | bytes 12582928 | tf_op jit(solution)/shard_map/psum | solution.py:91
  708.5 16.0 %fusion.17 = (f32[4096]{0:T(1024)}, f32[2,768]{1,0:T(2,128)S(1)}) fusion(bf16[2,768,4096]{2,1,0:T(8,128)(2,1)} %copy-done.2, bf16[2,768,4096]{2,1,0:T(8,128)(2,1)} %all-reduce.14.cloned.1.call-done, f32[2,768]{1,0:T(2,128)S(1)} %add_rsqrt_fusion, f32[4096]{0:T(1024)S(1)} %copy-done.13), kind=kLoop, calls=%fused_computation.31 | loop fusion | flops 50326016 | bytes 25210880 | tf_op jit(solution)/shard_map/reduce_sum | solution.py:21
  724.4 13.6 %fusion.31 = bf16[2,768,4096]{2,1,0:T(8,128)(2,1)S(1)} fusion(f32[2,768]{1,0:T(2,128)S(1)} %broadcast_multiply_fusion.1, bf16[2,768,4096]{2,1,0:T(8,128)(2,1)} %copy-done.2, f32[4096]{0:T(1024)S(1)} %copy-done.13, bf16[2,768,4096]{2,1,0:T(8,128)(2,1)S(1)} %copy-done.3, f32[2,768]{1,0:T(2,128)S(1)} %add_rsqrt_fusion, bf16[2,768,4096]{2,1,0:T(8,128)(2,1)} %param.14), kind=kLoop, calls=%fused_computation.47 | loop fusion | flops 62914560 | bytes 50360320 | tf_op jit(solution)/shard_map/convert_element_type | solution.py:94
  738.0 3.5 convolution_bitcast_fusion.7
  741.6 1.0 copy-done.4
  742.6 2.5 fusion.52
  745.1 3.2 convolution_convert_fusion.8
  748.3 3.7 convolution_convert_fusion.7
  752.0 2.8 fusion.112
  754.8 10.1 fusion.118
  764.9 11.3 fusion.122
  776.2 22.3 %add_convert_fusion = bf16[2,768,4096]{2,1,0:T(8,128)(2,1)} fusion(f32[2,768,4096]{2,1,0:T(8,128)} %fusion.118, f32[2,768,4096]{2,1,0:T(8,128)} %fusion.122, bf16[2,768,128]{1,2,0:T(8,128)(2,1)S(1)} %fusion.112, bf16[4096,1024]{1,0:T(8,128)(2,1)} %param.19, s32[]{:T(128)S(6)} %select_n.23), kind=kOutput, calls=%fused_computation.45 | convolution fusion | flops 1629487104 | bytes 64356356 | tf_op jit(solution)/shard_map/bse,de->bsd/dot_general | solution.py:104
  798.6 0.2 all-reduce.18.cloned.1.call-start
  798.8 8.3 broadcast.135.clone
  807.1 10.2 fusion.43
  817.4 8.3 broadcast.135.clone.1
  825.7 6.3 fusion.42
  832.0 11.7 convolution_bitcast_fusion.1
  843.7 11.1 convolution_bitcast_fusion
  854.9 13.8 %convolution_bitcast_fusion.2 = f32[448,4096]{1,0:T(8,128)} fusion(bf16[2,768,4096]{2,1,0:T(8,128)(2,1)} %param.14, f32[2,768,448]{1,2,0:T(8,128)} %fusion.58, f32[2,768,448]{1,2,0:T(8,128)} %fusion.63), kind=kOutput, calls=%fused_computation.58 | convolution fusion | flops 5641273344 | bytes 25427968 | tf_op jit(solution)/shard_map/bsf,bsd->fd/dot_general | solution.py:84
  868.7 3.1 convolution_bitcast_fusion.3
  871.8 5.5 convolution_bitcast_fusion.6
  877.4 42.4 %all-reduce.16.cloned.1.call-done = bf16[2,768,4096]{2,1,0:T(8,128)(2,1)} async-done(((bf16[2,768,4096]{2,1,0:T(8,128)(2,1)}), bf16[2,768,4096]{2,1,0:T(8,128)(2,1)}) %all-reduce.16.cloned.1.call-update) | async-done | bytes 12582928 | tf_op jit(solution)/shard_map/psum | solution.py:105
  919.7 14.7 %fusion.28 = (f32[4096]{0:T(1024)}, f32[2,768]{1,0:T(2,128)S(1)}) fusion(bf16[2,768,4096]{2,1,0:T(8,128)(2,1)} %param.12, bf16[2,768,4096]{2,1,0:T(8,128)(2,1)} %all-reduce.16.cloned.1.call-done, f32[2,768]{1,0:T(2,128)S(1)} %copy-done.18, f32[4096]{0:T(1024)S(1)} %copy-done.16), kind=kLoop, calls=%fused_computation.42 | loop fusion | flops 50326016 | bytes 25210880 | tf_op jit(solution)/shard_map/reduce_sum | solution.py:21
  934.5 26.0 %fusion.11 = bf16[2,768,4096]{2,1,0:T(8,128)(2,1)} fusion(bf16[2,768,4096]{2,1,0:T(8,128)(2,1)S(1)} %copy-done.5, bf16[2,768,4096]{2,1,0:T(8,128)(2,1)} %param.12, f32[2,768]{1,0:T(2,128)S(1)} %broadcast_multiply_fusion, f32[2,768]{1,0:T(2,128)S(1)} %copy-done.18, f32[4096]{0:T(1024)S(1)} %copy-done.16, f32[2,768]{1,0:T(2,128)S(1)} %copy-done.20, ...), kind=kLoop, calls=%fused_computation.25 | loop fusion | flops 113246208 | bytes 75554816 | tf_op jit(solution)/shard_map/convert_element_type | solution.py:107
  960.5 212.6 %all-reduce.18.cloned.1.call-done = (f32[4096,1024]{1,0:T(8,128)}, f32[4096,1024]{1,0:T(8,128)}) async-done(((f32[4096,1024]{1,0:T(8,128)}, f32[4096,1024]{1,0:T(8,128)}), (f32[4096,1024]{1,0:T(8,128)}, f32[4096,1024]{1,0:T(8,128)})) %all-reduce.18.cloned.1.call-update) | async-done | bytes 33554448 | tf_op jit(solution)/shard_map/psum | solution.py:108
  1173.0 12.8 %copy.60 = f32[4096,1024]{1,0:T(8,128)} copy(f32[4096,1024]{1,0:T(8,128)} %get-tuple-element.36) | data formatting | bytes 33554432
  1185.9 3.6 copy-done.7
  1189.5 6.2 copy.61
  (111 shorter events, 0.7 us)
Async XLA Ops:
  7.2 39.6 %copy-start = (bf16[128,4096]{1,0:T(8,128)(2,1)S(1)}, bf16[128,4096]{1,0:T(8,128)(2,1)}, u32[]{:S(2)}) copy-start(bf16[128,4096]{1,0:T(8,128)(2,1)} %param.20) | copy-start | bytes 3145732
  7.2 7.5 copy-start.15
  7.2 7.5 copy-start.11
  7.2 175.5 %all-reduce.8.cloned.1.call-start = ((), (), s32[]{:S(2)}) async-start(), calls=%async_computation | async-start | bytes 25165824 | tf_op jit(solution)/shard_map/psum | solution.py:64
  23.6 9.0 copy-start.14
  57.2 137.4 %copy-start.13 = (f32[4096]{0:T(1024)S(1)}, f32[4096]{0:T(1024)}, u32[]{:S(2)}) copy-start(f32[4096]{0:T(1024)} %param.16) | copy-start | bytes 49156
  57.2 283.7 %all-reduce.10.cloned.1.call-start = ((), (), s32[]{:S(2)}) async-start(), calls=%async_computation.1 | async-start | bytes 25165824 | tf_op jit(solution)/shard_map/psum | solution.py:71
  182.7 11.8 copy-start.22
  194.5 7.5 copy-start.6
  194.5 7.5 copy-start.25
  202.1 8.0 copy-start.21
  219.7 299.5 %all-reduce.12.cloned.1.call-start = ((), (), s32[]{:S(2)}) async-start(), calls=%async_computation.2 | async-start | bytes 25165824 | tf_op jit(solution)/shard_map/psum | solution.py:64
  362.8 16.9 %copy-start.17 = (f32[2,768]{1,0:T(2,128)}, f32[2,768]{1,0:T(2,128)S(1)}, u32[]{:S(2)}) copy-start(f32[2,768]{1,0:T(2,128)S(1)} %add_rsqrt_fusion.1) | copy-start | bytes 18436
  362.8 16.9 %slice-start = ((s8[12582912]{0:T(1024)(128)(4,1)}), s8[4194304]{0:T(1024)(128)(4,1)S(1)}, s32[]{:S(2)}) async-start(s8[12582912]{0:T(1024)(128)(4,1)} %bitcast.216), calls=%async_computation.6 | async-start | bytes 8388608
  362.9 16.9 %slice-start.1 = ((s8[12582912]{0:T(1024)(128)(4,1)}), s8[4194304]{0:T(1024)(128)(4,1)S(1)}, s32[]{:S(2)}) async-start(s8[12582912]{0:T(1024)(128)(4,1)} %bitcast.216), calls=%async_computation.7 | async-start | bytes 8388608
  371.4 13.4 %copy-start.26 = (bf16[2,768,128]{2,1,0:T(8,128)(2,1)}, bf16[2,768,128]{2,1,0:T(8,128)(2,1)S(1)}, u32[]{:S(2)}) copy-start(bf16[2,768,128]{2,1,0:T(8,128)(2,1)S(1)} %convolution_convert_fusion.5) | copy-start | bytes 1179652
  371.4 8.3 slice-start.2
  386.3 2.2 copy-start.8
  390.7 0.8 copy-start.9
  398.1 310.4 %all-reduce.14.cloned.1.call-start = ((), (), s32[]{:S(2)}) async-start(), calls=%async_computation.3 | async-start | bytes 25165824 | tf_op jit(solution)/shard_map/psum | solution.py:91
  519.2 11.8 copy-start.23
  531.0 7.8 copy-start.2
  531.0 17.7 %slice-start.12 = ((s8[12582912]{0:T(1024)(128)(4,1)}), s8[4194304]{0:T(1024)(128)(4,1)S(1)}, s32[]{:S(2)}) async-start(s8[12582912]{0:T(1024)(128)(4,1)} %bitcast.224), calls=%async_computation.18 | async-start | bytes 8388608
  531.1 17.7 %slice-start.13 = ((s8[12582912]{0:T(1024)(128)(4,1)}), s8[4194304]{0:T(1024)(128)(4,1)S(1)}, s32[]{:S(2)}) async-start(s8[12582912]{0:T(1024)(128)(4,1)} %bitcast.224), calls=%async_computation.19 | async-start | bytes 8388608
  538.8 10.0 slice-start.14
  548.8 10.9 copy-start.24
  559.7 11.7 copy-start.29
  587.3 332.4 %all-reduce.16.cloned.1.call-start = ((), (), s32[]{:S(2)}) async-start(), calls=%async_computation.4 | async-start | bytes 25165824 | tf_op jit(solution)/shard_map/psum | solution.py:105
  708.5 16.0 %copy-start.3 = (bf16[2,768,4096]{2,1,0:T(8,128)(2,1)S(1)}, bf16[2,768,4096]{2,1,0:T(8,128)(2,1)}, u32[]{:S(2)}) copy-start(bf16[2,768,4096]{2,1,0:T(8,128)(2,1)} %all-reduce.14.cloned.1.call-done) | copy-start | bytes 37748740
  708.5 34.1 %slice-start.15 = ((s8[4718592]{0:T(1024)(128)(4,1)}), s8[4194304]{0:T(1024)(128)(4,1)S(1)}, s32[]{:S(2)}) async-start(s8[4718592]{0:T(1024)(128)(4,1)} %bitcast.226), calls=%async_computation.21 | async-start | bytes 8388608
  724.4 13.6 %copy-start.19 = (f32[2,768]{1,0:T(2,128)}, f32[2,768]{1,0:T(2,128)S(1)}, u32[]{:S(2)}) copy-start(f32[2,768]{1,0:T(2,128)S(1)} %broadcast_multiply_fusion.1) | copy-start | bytes 18436
  724.4 18.1 %slice-start.16 = ((s8[4718592]{0:T(1024)(128)(4,1)}), s8[524288]{0:T(1024)(128)(4,1)S(1)}, s32[]{:S(2)}) async-start(s8[4718592]{0:T(1024)(128)(4,1)} %bitcast.226), calls=%async_computation.22 | async-start | bytes 1048576
  738.0 4.5 copy-start.4
  742.6 2.5 copy-start.27
  752.0 2.9 copy-start.12
  798.5 8.6 copy-start.16
  798.5 8.6 copy-start.18
  798.6 374.5 %all-reduce.18.cloned.1.call-start = ((), (), s32[]{:S(2)}) async-start(), calls=%async_computation.5 | async-start | bytes 67108864 | tf_op jit(solution)/shard_map/psum | solution.py:108
  807.1 18.6 %slice-start.3 = ((s8[12582912]{0:T(1024)(128)(4,1)}), s8[4194304]{0:T(1024)(128)(4,1)S(1)}, s32[]{:S(2)}) async-start(s8[12582912]{0:T(1024)(128)(4,1)} %bitcast.218), calls=%async_computation.9 | async-start | bytes 8388608
  807.1 18.6 %slice-start.4 = ((s8[12582912]{0:T(1024)(128)(4,1)}), s8[4194304]{0:T(1024)(128)(4,1)S(1)}, s32[]{:S(2)}) async-start(s8[12582912]{0:T(1024)(128)(4,1)} %bitcast.218), calls=%async_computation.10 | async-start | bytes 8388608
  817.4 8.3 slice-start.5
  832.0 11.7 copy-start.28
  843.7 24.9 %slice-start.9 = ((s8[12582912]{0:T(1024)(128)(4,1)}), s8[4194304]{0:T(1024)(128)(4,1)S(1)}, s32[]{:S(2)}) async-start(s8[12582912]{0:T(1024)(128)(4,1)} %bitcast.222), calls=%async_computation.15 | async-start | bytes 8388608
  843.7 25.0 %slice-start.10 = ((s8[12582912]{0:T(1024)(128)(4,1)}), s8[4194304]{0:T(1024)(128)(4,1)S(1)}, s32[]{:S(2)}) async-start(s8[12582912]{0:T(1024)(128)(4,1)} %bitcast.222), calls=%async_computation.16 | async-start | bytes 8388608
  843.7 28.1 %slice-start.6 = ((s8[12582912]{0:T(1024)(128)(4,1)}), s8[4194304]{0:T(1024)(128)(4,1)S(1)}, s32[]{:S(2)}) async-start(s8[12582912]{0:T(1024)(128)(4,1)} %bitcast.220), calls=%async_computation.12 | async-start | bytes 8388608
  843.7 28.1 %slice-start.7 = ((s8[12582912]{0:T(1024)(128)(4,1)}), s8[4194304]{0:T(1024)(128)(4,1)S(1)}, s32[]{:S(2)}) async-start(s8[12582912]{0:T(1024)(128)(4,1)} %bitcast.220), calls=%async_computation.13 | async-start | bytes 8388608
  854.8 13.8 %slice-start.11 = ((s8[12582912]{0:T(1024)(128)(4,1)}), s8[4194304]{0:T(1024)(128)(4,1)S(1)}, s32[]{:S(2)}) async-start(s8[12582912]{0:T(1024)(128)(4,1)} %bitcast.222), calls=%async_computation.17 | async-start | bytes 8388608
  854.9 13.8 %copy-start.10 = (bf16[2,768,128]{1,2,0:T(8,128)(2,1)S(1)}, bf16[2,768,128]{1,2,0:T(8,128)(2,1)}, u32[]{:S(2)}) copy-start(bf16[2,768,128]{1,2,0:T(8,128)(2,1)} %copy-done.9) | copy-start | bytes 1179652
  854.9 17.0 %slice-start.8 = ((s8[12582912]{0:T(1024)(128)(4,1)}), s8[4194304]{0:T(1024)(128)(4,1)S(1)}, s32[]{:S(2)}) async-start(s8[12582912]{0:T(1024)(128)(4,1)} %bitcast.220), calls=%async_computation.14 | async-start | bytes 8388608
  877.4 57.1 %copy-start.20 = (f32[2,768]{1,0:T(2,128)S(1)}, f32[2,768]{1,0:T(2,128)}, u32[]{:S(2)}) copy-start(f32[2,768]{1,0:T(2,128)} %copy-done.19) | copy-start | bytes 18436
  919.7 14.7 %copy-start.5 = (bf16[2,768,4096]{2,1,0:T(8,128)(2,1)S(1)}, bf16[2,768,4096]{2,1,0:T(8,128)(2,1)}, u32[]{:S(2)}) copy-start(bf16[2,768,4096]{2,1,0:T(8,128)(2,1)} %all-reduce.16.cloned.1.call-done) | copy-start | bytes 37748740
  1173.0 16.4 %copy-start.7 = (f32[4096,1024]{1,0:T(8,128)S(1)}, f32[4096,1024]{1,0:T(8,128)}, u32[]{:S(2)}) copy-start(f32[4096,1024]{1,0:T(8,128)} %get-tuple-element.37) | copy-start | bytes 50331652
  1189.5 6.2 copy-start.1
Sparse Core Ops, SparseCore 0:
  57.3 125.3 all-reduce.7
  219.9 120.9 all-reduce.9
  398.2 120.9 all-reduce.11
  587.4 120.9 all-reduce.13
  798.6 121.0 all-reduce.15
  924.2 248.7 all-reduce.17
where the time goes:
time: 1210 us; the launch traced here: 1200 us
  waiting for transfers between devices  744 us (61%)
  matrix products  273 us (23%)
  other arithmetic  129 us (11%)
  local copies, waits for them, and re-layouts  41.6 us (3%)
  between operations  15.2 us (1%)
    psum x2, waiting for transfers between devices, forward(): attn_out = lax.psum(attn_part, 'tp')  247 us
    psum x1, waiting for transfers between devices, device_step(): grad_w_k = lax.psum(spread_kv(part_w_k), 'tp')  213 us
    psum x1, waiting for transfers between devices, device_step(): grad_mixed = lax.psum(mixed_part, 'tp')  121 us
    psum x1, waiting for transfers between devices, forward(): mlp_out = lax.psum(mlp_part, 'tp')  121 us
    dot_general x9, matrix products, project(): jnp.einsum('bsd,de->bse', acts, weight, preferred_element_type=jnp.float32)  72.8 us
    psum x1, waiting for transfers between devices, device_step(): grad_normed = lax.psum(normed_part, 'tp')  42.4 us
    reduce_sum x4, other arithmetic, rms_forward(): jnp.mean(x_float * x_float, axis=-1, keepdims=True) + EPS  37.9 us
    reduce_sum x2, other arithmetic, rms_backward(): gain_grad = jnp.sum(grad_float * normed, axis=lead_axes)  30.7 us
  transfers between devices with their start and end apart: 6, of which 6 were waited for; matrix products, arithmetic and copies ran while one was open for 10% of the time, Pallas kernels for 0%

commit v1 on v0

v1 whole, which is shorter than its diff:
```python
import functools
import math
import jax
import jax.numpy as jnp
from jax import lax
from jax.experimental import pallas as pl
from jax.experimental.pallas import tpu as pltpu
from jax.sharding import PartitionSpec as P

HEAD_DIM = 128
EPS = 1e-5
MESH = pl.DeviceIdType.MESH
F32 = jnp.float32
BF16 = jnp.bfloat16


def dot(lhs, rhs, dims):
    return lax.dot_general(lhs, rhs, (dims, ((), ())), preferred_element_type=F32)


def sum_rows_gather(mode, side, part_ref, refs, outs, scr):
    tp_idx = lax.axis_index('tp')
    core = lax.rem(tp_idx, 2)
    chip = lax.div(tp_idx, 2)
    x_pos = lax.rem(chip, side)
    y_pos = lax.div(chip, side)

    def wrap(pos):
        return lax.rem(pos + 2 * side, side)

    def at_chip(y_at, x_at):
        return {'tp': (y_at * side + x_at) * 2 + core}

    partner = {'tp': chip * 2 + (1 - core)}

    class Colour:
        pass

    colours = []
    for index in range(2):
        col = Colour()
        col.index = index
        col.first = x_pos if index == 0 else y_pos
        col.second = y_pos if index == 0 else x_pos
        colours.append(col)

    def block(col, second, first):
        return (second, first) if col.index == 0 else (first, second)

    def peer1(col, shift):
        return at_chip(*block(col, col.second, wrap(col.first + shift)))

    def peer2(col, shift):
        return at_chip(*block(col, wrap(col.second + shift), col.first))

    part, gat = scr['part'], scr['gat']
    rows, width = part.shape[2], part.shape[3]
    quarter = width // 4

    def cols(col, half):
        return pl.ds((col.index * 2 + half) * quarter, quarter)

    def both_cols(col):
        return pl.ds(col.index * 2 * quarter, 2 * quarter)

    pending = []

    def send(src, dst, sems, index, device):
        copy = pltpu.make_async_remote_copy(src, dst, scr[sems + '_s'].at[index], scr[sems + '_r'].at[index], device_id=device, device_id_type=MESH)
        copy.start()
        pending.append(copy)

    def arrive(dst, sems, index):
        pltpu.make_async_remote_copy(dst, dst, scr[sems + '_s'].at[index], scr[sems + '_r'].at[index], device_id=partner, device_id_type=MESH).wait_recv()

    barrier = pltpu.get_barrier_semaphore()
    peers = [partner]
    if mode == 'da':
        peers += [at_chip(y_pos, wrap(x_pos + shift)) for shift in range(1, side)]
        peers += [at_chip(wrap(y_pos + shift), x_pos) for shift in range(1, side)]
    else:
        peers += [at_chip(y_pos, wrap(x_pos + shift)) for shift in (1, side - 1)]
        peers += [at_chip(wrap(y_pos + shift), x_pos) for shift in (1, side - 1)]

    order = (2, 1, 3, 0)
    loads = {}
    for shift_a in order:
        for shift_b in order:
            y_at, x_at = wrap(y_pos + shift_a), wrap(x_pos + shift_b)
            load = pltpu.make_async_copy(part_ref.at[y_at, x_at], part.at[y_at, x_at], scr['load'].at[shift_a * 4 + shift_b])
            load.start()
            loads[shift_a, shift_b] = load
    for peer in peers:
        pl.semaphore_signal(barrier, inc=1, device_id=peer, device_id_type=MESH)
    pl.semaphore_wait(barrier, len(peers))
    for load in loads.values():
        load.wait()

    signs = (1, -1)

    def add_into(where, at_cols, *terms):
        total = part[(*where, slice(None), at_cols)].astype(F32)
        for term in terms:
            total = total + term[...].astype(F32)
        part[(*where, slice(None), at_cols)] = total.astype(BF16)

    def piece(where, at_cols):
        return part.at[(*where, slice(None), at_cols)]

    shifts = (2, 1, 3, 0)

    def first_far(step):
        for col in colours:
            second = wrap(col.second + shifts[step])
            for way, sign in enumerate(signs):
                src = piece(block(col, second, wrap(col.first + 2)), cols(col, way))
                index = (col.index * 2 + way) * 4 + step
                send(src, scr['r1'].at[index], 'r1', index, peer1(col, sign))

    def first_near(step):
        for col in colours:
            second = wrap(col.second + shifts[step])
            for way, sign in enumerate(signs):
                src = piece(block(col, second, wrap(col.first + sign)), cols(col, 1 - way))
                index = (col.index * 2 + way) * 4 + step
                send(src, scr['r2'].at[index], 'r2', index, peer1(col, sign))

    def first_relay(step):
        for col in colours:
            second = wrap(col.second + shifts[step])
            for way, sign in enumerate(signs):
                where = block(col, second, wrap(col.first + sign))
                index = (col.index * 2 + way) * 4 + step
                arrive(scr['r1'].at[index], 'r1', index)
                add_into(where, cols(col, way), scr['r1'].at[index])
                send(piece(where, cols(col, way)), scr['r3'].at[index], 'r3', index, peer1(col, sign))

    def first_end(step):
        for col in colours:
            where = block(col, wrap(col.second + shifts[step]), col.first)
            for way in range(2):
                index_3 = (col.index * 2 + way) * 4 + step
                index_2 = (col.index * 2 + 1 - way) * 4 + step
                arrive(scr['r2'].at[index_2], 'r2', index_2)
                arrive(scr['r3'].at[index_3], 'r3', index_3)
                add_into(where, cols(col, way), scr['r2'].at[index_2], scr['r3'].at[index_3])

    def second_far():
        for col in colours:
            for way, sign in enumerate(signs):
                index = col.index * 2 + way
                src = piece(block(col, wrap(col.second + 2), col.first), cols(col, way))
                send(src, scr['s1'].at[index], 's1', index, peer2(col, sign))

    def second_near(way):
        sign = signs[way]
        for col in colours:
            index = col.index * 2 + way
            where = block(col, wrap(col.second + sign), col.first)
            send(piece(where, cols(col, 1 - way)), scr['s2'].at[index], 's2', index, peer2(col, sign))

    def second_relay(way):
        sign = signs[way]
        for col in colours:
            index = col.index * 2 + way
            where = block(col, wrap(col.second + sign), col.first)
            arrive(scr['s1'].at[index], 's1', index)
            add_into(where, cols(col, way), scr['s1'].at[index])
            send(piece(where, cols(col, way)), scr['s3'].at[index], 's3', index, peer2(col, sign))

    def second_end():
        for col in colours:
            where = block(col, col.second, col.first)
            for way in range(2):
                index_3 = col.index * 2 + way
                index_2 = col.index * 2 + 1 - way
                arrive(scr['s2'].at[index_2], 's2', index_2)
                arrive(scr['s3'].at[index_3], 's3', index_3)
                add_into(where, cols(col, way), scr['s2'].at[index_2], scr['s3'].at[index_3])

    first_far(0)
    first_near(0)
    first_far(1)
    first_relay(0)
    first_near(1)
    first_far(2)
    first_relay(1)
    first_near(2)
    first_far(3)
    first_end(0)
    second_far()
    first_relay(2)
    first_near(3)
    first_end(1)
    second_near(0)
    second_relay(0)
    first_relay(3)
    first_end(2)
    second_near(1)
    second_relay(1)
    first_end(3)
    second_end()

    own = (y_pos, x_pos)
    row_step(mode, part, gat, own, refs, outs, scr)

    def spread(ref, where, at_cols):
        return ref.at[(*where, slice(None), at_cols)]

    def ring2_own(half_of_way):
        for col in colours:
            where = block(col, col.second, col.first)
            for way, sign in enumerate(signs):
                half = way if half_of_way == 0 else 1 - way
                at = spread(gat, where, cols(col, half))
                send(at, at, 'h1', (col.index * 2 + way) * 2 + half_of_way, peer2(col, sign))

    def ring1_block(step, half_of_way):
        for col in colours:
            where = block(col, wrap(col.second + back[step]), col.first)
            for way, sign in enumerate(signs):
                half = way if half_of_way == 0 else 1 - way
                at = spread(gat, where, cols(col, half))
                send(at, at, 'h2', ((col.index * 2 + way) * 4 + step) * 2 + half_of_way, peer1(col, sign))

    back = (0, side - 1, 1, 2)

    def ring2_arrive(way, half_of_way):
        sign = signs[way]
        half = way if half_of_way == 0 else 1 - way
        for col in colours:
            where = block(col, wrap(col.second - sign), col.first)
            at = spread(gat, where, cols(col, half))
            arrive(at, 'h1', (col.index * 2 + way) * 2 + half_of_way)
            if half_of_way == 0:
                send(at, at, 'f1', col.index * 2 + way, peer2(col, sign))

    def ring2_relayed():
        for col in colours:
            where = block(col, wrap(col.second + 2), col.first)
            for way in range(2):
                arrive(spread(gat, where, cols(col, way)), 'f1', col.index * 2 + way)

    def ring1_arrive(step, half_of_way):
        for col in colours:
            second = wrap(col.second + back[step])
            for way, sign in enumerate(signs):
                half = way if half_of_way == 0 else 1 - way
                at = spread(gat, block(col, second, wrap(col.first - sign)), cols(col, half))
                arrive(at, 'h2', ((col.index * 2 + way) * 4 + step) * 2 + half_of_way)
                if half_of_way == 0:
                    send(at, at, 'f2', (col.index * 2 + way) * 4 + step, peer1(col, sign))

    def ring1_relayed(step):
        for col in colours:
            second = wrap(col.second + back[step])
            for way in range(2):
                at = spread(gat, block(col, second, wrap(col.first + 2)), cols(col, way))
                arrive(at, 'f2', (col.index * 2 + way) * 4 + step)

    stores = []

    def keep(col, where):
        slot = (col.index * side + where[0]) * side + where[1]
        at = spread(gat, where, both_cols(col))
        if 'own' in outs:
            store = pltpu.make_async_copy(at, spread(outs['own'], where, both_cols(col)), scr['own_s'].at[slot])
            store.start()
            stores.append(store)
        target = spread(outs['full'].at[core], where, both_cols(col))
        store = pltpu.make_async_copy(at, target, scr['full_s'].at[slot])
        store.start()
        stores.append(store)
        copy = pltpu.make_async_remote_copy(at, target, scr['d2d_s'].at[slot], scr['d2d_r'].at[slot], device_id=partner, device_id_type=MESH)
        copy.start()
        pending.append(copy)

    def keep_step(step, firsts):
        for col in colours:
            for shift in firsts:
                keep(col, block(col, wrap(col.second + back[step]), wrap(col.first + shift)))

    ring2_own(0)
    ring1_block(0, 0)
    ring2_own(1)
    ring1_block(0, 1)
    keep_step(0, (0,))
    if mode == 'da':
        gain_sum_core(outs, scr, send, arrive, partner)
    ring2_arrive(0, 0)
    ring2_arrive(1, 0)
    ring2_arrive(0, 1)
    ring1_block(1, 0)
    ring1_block(1, 1)
    ring2_arrive(1, 1)
    ring1_block(2, 0)
    ring1_block(2, 1)
    keep_step(1, (0,))
    keep_step(2, (0,))
    ring1_arrive(0, 0)
    if mode == 'da':
        gain_sum_ring(1, scr, send, arrive, [at_chip(wrap(y_pos + shift), x_pos) for shift in range(1, side)])
    ring2_relayed()
    ring1_block(3, 0)
    ring1_block(3, 1)
    keep_step(3, (0,))
    ring1_arrive(0, 1)
    keep_step(0, (1, side - 1))
    ring1_arrive(1, 0)
    if mode == 'da':
        gain_sum_ring(2, scr, send, arrive, [at_chip(y_pos, wrap(x_pos + shift)) for shift in range(1, side)])
        outs['gain'][...] = scr['gain_tot'][...]
    ring1_arrive(2, 0)
    ring1_relayed(0)
    keep_step(0, (2,))
    ring1_arrive(1, 1)
    keep_step(1, (1, side - 1))
    ring1_arrive(2, 1)
    keep_step(2, (1, side - 1))
    ring1_arrive(3, 0)
    ring1_relayed(1)
    keep_step(1, (2,))
    ring1_relayed(2)
    keep_step(2, (2,))
    ring1_arrive(3, 1)
    keep_step(3, (1, side - 1))
    ring1_relayed(3)
    keep_step(3, (2,))

    for store in stores:
        store.wait()
    for copy in pending:
        copy.wait_send()
    for col_index in range(2):
        for y_at in range(side):
            for x_at in range(side):
                slot = (col_index * side + y_at) * side + x_at
                target = spread(outs['full'].at[1 - core], (y_at, x_at), pl.ds(col_index * 2 * quarter, 2 * quarter))
                pltpu.make_async_remote_copy(target, target, scr['d2d_s'].at[slot], scr['d2d_r'].at[slot], device_id=partner, device_id_type=MESH).wait_recv()


def gain_sum_core(outs, scr, send, arrive, partner):
    send(scr['gain_own'], scr['gain_in'].at[0], 'gain', 0, partner)
    arrive(scr['gain_in'].at[0], 'gain', 0)
    scr['gain_tot'][...] = scr['gain_own'][...] + scr['gain_in'][0]


def gain_sum_ring(stage, scr, send, arrive, peers):
    hold = scr['gain_hold'].at[stage - 1]
    hold[...] = scr['gain_tot'][...]
    base = 1 + (stage - 1) * len(peers)
    for index, peer in enumerate(peers):
        send(hold, scr['gain_in'].at[base + index], 'gain', base + index, peer)
    total = hold[...]
    for index in range(len(peers)):
        arrive(scr['gain_in'].at[base + index], 'gain', base + index)
        total = total + scr['gain_in'][base + index]
    scr['gain_tot'][...] = total


def row_step(mode, part, gat, own, refs, outs, scr):
    rows, width = part.shape[2], part.shape[3]
    tile = 16
    if mode != 'o':
        gain_slot = 0 if mode == 'dm' else 1
        gain_out = outs['gain'] if mode == 'dm' else scr['gain_own']
        gain_total = jnp.zeros((1, width), F32)
    for start in range(0, rows, tile):
        at = pl.ds(start, tile)
        summed = part[(*own, at, slice(None))].astype(F32)
        gain = refs['gain'][...]
        if mode == 'o':
            resid = (refs['x_rows'][at, :].astype(F32) + summed).astype(BF16)
            outs['h_rows'][at, :] = resid
            z_in = resid.astype(F32)
            inv = lax.rsqrt(jnp.mean(z_in * z_in, axis=-1, keepdims=True) + EPS)
            gat[(*own, at, slice(None))] = (z_in * inv * gain).astype(BF16)
            continue
        z_in = refs['z_rows'][at, :].astype(F32)
        inv = lax.rsqrt(jnp.mean(z_in * z_in, axis=-1, keepdims=True) + EPS)
        normed = z_in * inv
        gain_total = gain_total + jnp.sum(summed * normed, axis=0, keepdims=True)
        scaled = summed * gain
        back = inv * (scaled - normed * jnp.mean(scaled * normed, axis=-1, keepdims=True))
        total = refs['up_rows'][at, :].astype(F32) + back
        if mode == 'dm':
            outs['d_rows'][at, :] = total
        gat[(*own, at, slice(None))] = total.astype(BF16)
    if mode == 'dm':
        outs['gain'][...] = gain_total
    if mode == 'da':
        scr['gain_own'][0:1, :] = refs['gain_mlp'][...]
        scr['gain_own'][1:2, :] = gain_total


def reduce_gather(mode, side, collective_id, part, *row_args):
    chips = side * side
    seq, width = part.shape
    rows = seq // chips
    part = part.reshape(side, side, rows, width)
    names_in = {'o': ('x_rows', 'gain'), 'dm': ('z_rows', 'up_rows', 'gain'), 'da': ('z_rows', 'up_rows', 'gain', 'gain_mlp')}[mode]
    full = jax.ShapeDtypeStruct((2, side, side, rows, width), BF16)
    own = jax.ShapeDtypeStruct((side, side, rows, width), BF16)
    any_spec = pl.BlockSpec(memory_space=pl.ANY)
    vmem_spec = pl.BlockSpec(memory_space=pltpu.VMEM)
    outs = {'full': (full, any_spec)}
    if mode != 'da':
        outs['own'] = (own, any_spec)
    if mode == 'o':
        outs['h_rows'] = (jax.ShapeDtypeStruct((rows, width), BF16), vmem_spec)
    if mode == 'dm':
        outs['d_rows'] = (jax.ShapeDtypeStruct((rows, width), F32), vmem_spec)
        outs['gain'] = (jax.ShapeDtypeStruct((1, width), F32), vmem_spec)
    if mode == 'da':
        outs['gain'] = (jax.ShapeDtypeStruct((2, width), F32), vmem_spec)
    names_out = tuple(outs)
    quarter = width // 4
    dma = pltpu.SemaphoreType.DMA
    scratch = {
        'part': pltpu.VMEM((side, side, rows, width), BF16),
        'gat': pltpu.VMEM((side, side, rows, width), BF16),
        'load': dma((chips,)),
        'full_s': dma((2 * chips,)),
        'd2d_s': dma((2 * chips,)),
        'd2d_r': dma((2 * chips,)),
    }
    if mode != 'da':
        scratch['own_s'] = dma((2 * chips,))
    for name, count in (('r1', 16), ('r2', 16), ('r3', 16), ('s1', 4), ('s2', 4), ('s3', 4)):
        scratch[name] = pltpu.VMEM((count, rows, quarter), BF16)
    for name, count in (('r1', 16), ('r2', 16), ('r3', 16), ('s1', 4), ('s2', 4), ('s3', 4), ('h1', 8), ('h2', 32), ('f1', 4), ('f2', 16)):
        scratch[name + '_s'] = dma((count,))
        scratch[name + '_r'] = dma((count,))
    if mode == 'da':
        terms = 1 + 2 * (side - 1)
        scratch['gain_own'] = pltpu.VMEM((2, width), F32)
        scratch['gain_tot'] = pltpu.VMEM((2, width), F32)
        scratch['gain_hold'] = pltpu.VMEM((2, 2, width), F32)
        scratch['gain_in'] = pltpu.VMEM((terms, 2, width), F32)
        scratch['gain_s'] = dma((terms,))
        scratch['gain_r'] = dma((terms,))
    names_scr = tuple(scratch)

    def kernel(part_ref, *rest):
        refs = dict(zip(names_in, rest))
        rest = rest[len(names_in):]
        out_refs = dict(zip(names_out, rest))
        scr = dict(zip(names_scr, rest[len(names_out):]))
        sum_rows_gather(mode, side, part_ref, refs, out_refs, scr)

    results = pl.pallas_call(
        kernel,
        name='sum_rows_gather_' + mode,
        out_shape=[outs[name][0] for name in names_out],
        in_specs=[any_spec] + [vmem_spec] * len(names_in),
        out_specs=[outs[name][1] for name in names_out],
        scratch_shapes=[scratch[name] for name in names_scr],
        compiler_params=pltpu.CompilerParams(collective_id=collective_id, has_side_effects=True, vmem_limit_bytes=40 * 2 ** 20),
        cost_estimate=pl.CostEstimate(flops=400_000_000, bytes_accessed=40_000_000, transcendentals=0),
    )(part, *row_args)
    results = dict(zip(names_out, results))
    results['full'] = results['full'].reshape(2, seq, width)
    if 'own' in results:
        results['own'] = results['own'].reshape(seq, width)
    return results


def solution(mesh):
    tp_size = mesh.shape['tp']
    chips = tp_size // 2
    side = math.isqrt(chips)
    swap_pairs = [(index, index ^ 1) for index in range(tp_size)]

    def device_step(hidden, seg_ids, grad_out, gain_attn, gain_mlp, w_q, w_k, w_v, w_o, w_gate, w_up, w_down):
        seq_len, width = hidden.shape[1:]
        hidden_loc = w_gate.shape[1]
        kv_heads = w_k.shape[1] // HEAD_DIM
        per_kv = tp_size // kv_heads
        rows = seq_len // chips
        tp_idx = lax.axis_index('tp')
        core = tp_idx % 2
        chip = tp_idx // 2
        kv_col = (tp_idx // per_kv) * HEAD_DIM
        scale = HEAD_DIM ** -0.5

        def swap(value):
            return lax.ppermute(value, 'tp', swap_pairs)

        def in_order(mine, other):
            return lax.optimization_barrier(jnp.where(core == 0, jnp.stack([mine, other]), jnp.stack([other, mine])))

        def own_rows(value):
            return lax.dynamic_slice_in_dim(value, chip * rows, rows, axis=0)

        gain_attn_row = gain_attn[None, :]
        gain_mlp_row = gain_mlp[None, :]
        x_own = lax.dynamic_index_in_dim(hidden, core, 0, keepdims=False)
        dy_own = lax.dynamic_index_in_dim(grad_out, core, 0, keepdims=False)
        seg_own = lax.dynamic_index_in_dim(seg_ids, core, 0, keepdims=False)

        w_q_2 = swap(w_q)
        w_o_2 = swap(w_o)
        w_gate_2 = swap(w_gate)
        w_up_2 = swap(w_up)
        w_down_2 = swap(w_down)
        w_k_loc = lax.dynamic_slice_in_dim(w_k, kv_col, HEAD_DIM, axis=1)
        w_v_loc = lax.dynamic_slice_in_dim(w_v, kv_col, HEAD_DIM, axis=1)
        w_in = jnp.concatenate([w_q, w_q_2, w_k_loc, w_v_loc], axis=1)
        w_out = jnp.concatenate([w_o, w_o_2], axis=0)

        def rms_forward(x_in):
            x_float = x_in.astype(F32)
            inv_rms = lax.rsqrt(jnp.mean(x_float * x_float, axis=-1, keepdims=True) + EPS)
            return (x_float * inv_rms * gain_attn).astype(BF16)

        normed_own = rms_forward(x_own)
        qkv = dot(normed_own, w_in, ((1,), (0,))).astype(BF16)
        queries = qkv[:, :2 * HEAD_DIM].reshape(seq_len, 2, HEAD_DIM)
        keys = qkv[:, 2 * HEAD_DIM:3 * HEAD_DIM]
        values = qkv[:, 3 * HEAD_DIM:]
        positions = jnp.arange(seq_len)
        allowed = (positions[:, None] >= positions[None, :]) & (seg_own[:, None] == seg_own[None, :])
        scores = jnp.einsum('qhd,kd->hqk', queries, keys, preferred_element_type=F32) * scale
        probs = jax.nn.softmax(jnp.where(allowed[None], scores, -1e30), axis=-1)
        probs_b = probs.astype(BF16)
        ctx = jnp.einsum('hqk,kd->qhd', probs_b, values, preferred_element_type=F32).astype(BF16).reshape(seq_len, 2 * HEAD_DIM)
        ctx_full = in_order(ctx[:, :HEAD_DIM], swap(ctx[:, HEAD_DIM:]))
        attn_part = dot(ctx, w_out, ((1,), (0,))).astype(BF16)
        x_rows = own_rows(x_own)
        dy_rows = own_rows(dy_own)
        first = reduce_gather('o', side, 1, attn_part, x_rows, gain_mlp_row)
        mixed_own, mixed_full, h_rows = first['own'], first['full'], first['h_rows']

        acts, grads_gate, grads_up = [], [], []
        for gate_w, up_w, down_w in ((w_gate, w_up, w_down), (w_gate_2, w_up_2, w_down_2)):
            gate = dot(mixed_own, gate_w, ((1,), (0,)))
            upper = dot(mixed_own, up_w, ((1,), (0,)))
            grad_act = dot(dy_own, down_w, ((1,), (1,)))
            sigmoid_g = jax.nn.sigmoid(gate)
            silu_g = gate * sigmoid_g
            acts.append((silu_g * upper).astype(BF16))
            grads_gate.append((grad_act * upper * sigmoid_g * (1.0 + gate * (1.0 - sigmoid_g))).astype(BF16))
            grads_up.append((grad_act * silu_g).astype(BF16))
        mixed_part = (dot(grads_gate[0], w_gate, ((1,), (1,))) + dot(grads_up[0], w_up, ((1,), (1,)))
                      + dot(grads_gate[1], w_gate_2, ((1,), (1,))) + dot(grads_up[1], w_up_2, ((1,), (1,)))).astype(BF16)
        act_full = in_order(acts[0], swap(acts[1]))
        gate_full = in_order(grads_gate[0], swap(grads_gate[1]))
        up_full = in_order(grads_up[0], swap(grads_up[1]))

        mlp_part = jnp.einsum('bsf,fd->bsd', act_full, w_down, preferred_element_type=F32).astype(BF16).reshape(2 * seq_len, width)
        mlp_rows = lax.psum_scatter(mlp_part, 'tp', scatter_dimension=0, tiled=True)
        h_there = lax.ppermute(h_rows, 'tp', [(index, (index % 2) * chips + index // 2) for index in range(tp_size)])
        y_rows = (h_there.astype(F32) + mlp_rows.astype(F32)).astype(BF16)
        y_out = lax.all_gather(y_rows, 'tp', axis=0, tiled=True).reshape(2, seq_len, width)

        second = reduce_gather('dm', side, 2, mixed_part, h_rows, dy_rows, gain_mlp_row)
        resid_own, resid_full, resid_rows, gain_mlp_part = second['own'], second['full'], second['d_rows'], second['gain']

        grad_ctx = dot(resid_own, w_out, ((1,), (1,))).astype(BF16).reshape(seq_len, 2, HEAD_DIM)
        grad_probs = jnp.einsum('qhd,kd->hqk', grad_ctx, values, preferred_element_type=F32)
        grad_v = jnp.einsum('hqk,qhd->kd', probs_b, grad_ctx, preferred_element_type=F32).astype(BF16)
        grad_scores = (probs * (grad_probs - jnp.sum(grad_probs * probs, axis=-1, keepdims=True)) * scale).astype(BF16)
        grad_q = jnp.einsum('hqk,kd->qhd', grad_scores, keys, preferred_element_type=F32).astype(BF16).reshape(seq_len, 2 * HEAD_DIM)
        grad_k = jnp.einsum('hqk,qhd->kd', grad_scores, queries, preferred_element_type=F32).astype(BF16)
        grad_q_full = in_order(grad_q[:, :HEAD_DIM], swap(grad_q[:, HEAD_DIM:]))

        share = per_kv // 2
        grad_kv = jnp.concatenate([grad_k, grad_v], axis=1).reshape(share, seq_len // share, 2 * HEAD_DIM)
        place = chip % share
        kv_sum = lax.dynamic_index_in_dim(grad_kv, place, 0, keepdims=False).astype(F32)
        for step in range(1, share):
            to_send = lax.dynamic_index_in_dim(grad_kv, (place + step) % share, 0, keepdims=False)
            moves = [(index, (index // per_kv) * per_kv + (index % per_kv + 2 * step) % per_kv) for index in range(tp_size)]
            kv_sum = kv_sum + lax.ppermute(to_send, 'tp', moves).astype(F32)
        kv_all = lax.all_gather(kv_sum.astype(BF16), 'tp', axis=0, tiled=False)
        kv_all = kv_all.reshape(kv_heads, share, 2, seq_len // share, 2 * HEAD_DIM).transpose(2, 1, 3, 0, 4).reshape(2, seq_len, kv_heads, 2 * HEAD_DIM)
        grad_k_all = kv_all[..., :HEAD_DIM].reshape(2, seq_len, kv_heads * HEAD_DIM)
        grad_v_all = kv_all[..., HEAD_DIM:].reshape(2, seq_len, kv_heads * HEAD_DIM)

        normed_part = dot(jnp.concatenate([grad_q, grad_k, grad_v], axis=1), w_in, ((1,), (1,))).astype(BF16)
        third = reduce_gather('da', side, 3, normed_part, x_rows, resid_rows, gain_attn_row, gain_mlp_part)
        grad_in, gain_grads = third['full'], third['gain']

        def weight_grad(lhs, rhs):
            return jnp.einsum('bsd,bse->de', lhs, rhs, preferred_element_type=F32)

        normed_full = rms_forward(hidden)
        grad_w_down = weight_grad(act_full, grad_out)
        grad_w_gate = weight_grad(mixed_full, gate_full)
        grad_w_up = weight_grad(mixed_full, up_full)
        grad_w_o = weight_grad(ctx_full, resid_full)
        grad_w_q = weight_grad(normed_full, grad_q_full)
        grad_w_k = weight_grad(normed_full, grad_k_all)
        grad_w_v = weight_grad(normed_full, grad_v_all)
        return (y_out, grad_in, gain_grads[1], gain_grads[0], grad_w_q, grad_w_k, grad_w_v, grad_w_o, grad_w_gate, grad_w_up, grad_w_down)

    spec_act = P('data', None, None)
    spec_rows = P('data', None)
    spec_gain = P(None)
    spec_cols = P(None, 'tp')
    spec_tprows = P('tp', None)
    spec_whole = P(None, None)
    spec_stack = P(('data', 'tp'), None)
    in_specs = (spec_act, spec_rows, spec_act, spec_gain, spec_gain, spec_cols, spec_whole, spec_whole, spec_tprows, spec_cols, spec_cols, spec_tprows)
    out_specs = (spec_act, spec_act, P('data'), P('data'), P('data', 'tp'), spec_rows, spec_rows, spec_stack, P('data', 'tp'), P('data', 'tp'), spec_stack)
    return jax.shard_map(device_step, mesh=mesh, in_specs=in_specs, out_specs=out_specs, check_vma=False)
```

time: 1210 us -> 664 us (0.55)
  waiting for transfers between devices: 744 us -> 18.5 us
  Pallas kernels: 0 us -> 320 us
  other arithmetic: 129 us -> 20.1 us
  matrix products: 273 us -> 221 us
  local copies, waits for them, and re-layouts: 41.6 us -> 57.9 us
    psum x6 -> x0, waiting for transfers between devices: 744 us -> none  [the longest x2 247 us: forward(): attn_out = lax.psum(attn_part, 'tp')]
    pallas_call x0 -> x3, Pallas kernels: none -> 320 us  [reduce_gather(): pl.pallas_call(kernel, name='sum_rows_gather_' + mode, out_shape=[outs[na...]
    dot_general x33 -> x27, matrix products: 273 us -> 216 us  [the longest x14 95.6 us: dot(): lax.dot_general(lhs, rhs, (dims, ((), ())), preferred_element_type=F32)]
    convert_element_type x3 -> x2, other arithmetic: 54.4 us -> 3.53 us  [the longest x1 1.87 us: device_step(): y_rows = (h_there.astype(F32) + mlp_rows.astype(F32)).astype(BF16)]
    reduce_sum x4 -> x0, other arithmetic: 36 us -> none  [the longest x2 30.7 us: rms_backward(): gain_grad = jnp.sum(grad_float * normed, axis=lead_axes)]
    reduce_sum x4 -> x2, other arithmetic: 37.9 us -> 11.2 us  [rms_forward(): jnp.mean(x_float * x_float, axis=-1, keepdims=True) + EPS]
    ppermute x0 -> x12, waiting for transfers between devices: none -> 18.3 us  [the longest x1 10.6 us: device_step(): lax.ppermute(h_rows, 'tp', [(index, index % 2 * chips + index // 2) for i...]
    another operation x2, local copies, waits for them, and re-layouts: 16.6 us -> 0.06 us  [in_order(): jnp.stack([mine, other])]
  transfers between devices with their start and end apart: 6 -> 15, of which waited for: 6 -> 3; matrix products, arithmetic and copies ran while one was open for 10% -> 39% of each run, Pallas kernels for 0% -> 48%
where the time goes in v1:
time: 664 us; the launch traced here: 661 us
  Pallas kernels  320 us (48%)
  matrix products  221 us (33%)
  local copies, waits for them, and re-layouts  57.9 us (9%)
  other arithmetic  20.1 us (3%)
  waiting for transfers between devices  18.5 us (3%)
  between operations  14.9 us (2%)
  starting transfers between devices  8.97 us (1%)
    pallas_call x3, Pallas kernels, reduce_gather(): pl.pallas_call(kernel, name='sum_rows_gather_' + mode, out_shape=[outs[na...  320 us
    dot_general x14, matrix products, dot(): lax.dot_general(lhs, rhs, (dims, ((), ())), preferred_element_type=F32)  95.6 us
    dot_general x7, matrix products, weight_grad(): return jnp.einsum('bsd,bse->de', lhs, rhs, preferred_element_type=F32)  82.4 us
    unnamed x71, local copies, waits for them, and re-layouts  27.7 us
  transfers between devices with their start and end apart: 15, of which 3 were waited for; matrix products, arithmetic and copies ran while one was open for 39% of the time, Pallas kernels for 48%

profile of v1, /device:TPU:97, one launch (start us, length us, event | category | flops | bytes accessed | tf_op | source)
XLA Modules:
  0.0 661.2 jit_solution(7567066366660332642)
XLA Ops:
  7.3 2.1 collective-permute-start
  9.5 0.4 collective-permute-start.4
  10.0 0.4 collective-permute-start.3
  10.4 4.1 fusion.5
  14.5 0.4 fusion.34
  14.9 1.1 dynamic-slice_bitcast_fusion.1.rest_0_
  16.1 1.3 constant_dynamic-update-slice_fusion.1
  17.4 1.7 constant_dynamic-slice_fusion
  19.2 7.8 %fusion.39 = bf16[768,512]{0,1:T(8,128)(2,1)S(1)} fusion(f32[4096]{0:T(1024)S(1)} %copy-done.4, f32[768]{0:T(1024)S(1)} %add_rsqrt_fusion.1, bf16[2,768,4096]{2,1,0:T(8,128)(2,1)} %param.12, s32[]{:T(128)S(6)} %select_n.81, bf16[4096,128]{1,0:T(8,128)(2,1)S(1)} %get-tuple-element.45, bf16[4096,128]{1,0:T(8,128)(2,1)S(1)} %get-tuple-element.46, ...), kind=kOutput, calls=%fused_computation.54 | convolution fusion | flops 3250978816 | bytes 11291652 | tf_op jit(solution)/shard_map/dot_general | solution.py:18
  27.1 1.7 constant_dynamic-update-slice_fusion
  28.8 5.2 fusion.76
  34.0 2.9 convolution_convert_fusion.3
  37.0 0.7 copy-done.11
  37.7 1.8 convolution_convert_fusion.2
  39.5 93.4 %sum_rows_gather_o.1 = (bf16[2,4,4,48,4096]{4,3,2,1,0:T(8,128)(2,1)}, bf16[4,4,48,4096]{3,2,1,0:T(8,128)(2,1)S(1)}, bf16[48,4096]{1,0:T(8,128)(2,1)S(1)}) custom-call(bf16[4,4,48,4096]{3,2,1,0:T(8,128)(2,1)S(1)} %bitcast.196, bf16[48,4096]{1,0:T(8,128)(2,1)S(1)} %dynamic-slice_bitcast_fusion.1.rest_0_, f32[1,4096]{1,0:T(1,128)S(1)} %bitcast.198), custom_call_target="tpu_custom_call" | custom-call | flops 400000000 | bytes 40000000 | tf_op jit(solution)/shard_map/sum_rows_gather_o/pallas_call | solution.py:451
  133.0 3.1 fusion.79
  136.1 4.2 fusion.80
  140.2 6.9 %fusion.14 = f32[768,448]{0,1:T(8,128)S(1)} fusion(bf16[448,4096]{1,0:T(8,128)(2,1)} %collective-permute-done.6, bf16[2,768,4096]{2,1,0:T(8,128)(2,1)} %param.14, s32[]{:T(128)S(6)} %select_n.81), kind=kOutput, calls=%fused_computation.20 | convolution fusion | flops 2818572288 | bytes 11337732 | tf_op jit(solution)/shard_map/dot_general | solution.py:18
  147.1 5.3 fusion.81
  152.5 7.4 %multiply_convert_fusion.1 = (bf16[768,448]{0,1:T(8,128)(2,1)}, bf16[768,448]{0,1:T(8,128)(2,1)}, bf16[768,448]{0,1:T(8,128)(2,1)S(1)}) fusion(f32[768,448]{0,1:T(8,128)S(1)} %fusion.14, f32[768,448]{0,1:T(8,128)S(1)} %fusion.81, bf16[768,4096]{1,0:T(8,128)(2,1)S(1)} %bitcast.204, bf16[4096,448]{0,1:T(8,128)(2,1)} %collective-permute-done.3), kind=kOutput, calls=%fused_computation.59 | convolution fusion | flops 2823733248 | bytes 14778368 | tf_op jit(solution)/shard_map/dot_general | solution.py:18
  160.1 5.0 multiply_convert_fusion.2
  165.4 9.7 %convolution_convert_fusion = bf16[2,768,4096]{2,1,0:T(8,128)(2,1)} fusion(bf16[2,768,448]{1,2,0:T(8,128)(2,1)S(1)} %maximum_select_fusion, bf16[448,4096]{1,0:T(8,128)(2,1)S(1)} %copy-done.24), kind=kOutput, calls=%fused_computation.13 | convolution fusion | flops 5643436032 | bytes 17629184 | tf_op jit(solution)/shard_map/bsf,fd->bsd/dot_general | solution.py:550
  175.3 1.1 dynamic-slice_bitcast_fusion.rest_1_
  176.4 9.0 %fusion.82 = f32[768,4096]{1,0:T(8,128)} fusion(bf16[768,448]{0,1:T(8,128)(2,1)S(1)} %get-tuple-element.32, bf16[4096,448]{0,1:T(8,128)(2,1)} %param.21), kind=kOutput, calls=%fused_computation.123 | convolution fusion | flops 2818572288 | bytes 16941056 | tf_op jit(solution)/shard_map/dot_general | solution.py:18
  185.4 6.6 %fusion.83 = f32[768,4096]{1,0:T(8,128)} fusion(bf16[768,448]{0,1:T(8,128)(2,1)S(1)} %get-tuple-element.31, bf16[4096,448]{0,1:T(8,128)(2,1)S(1)} %copy-done.9), kind=kOutput, calls=%fused_computation.124 | convolution fusion | flops 2818572288 | bytes 16941056 | tf_op jit(solution)/shard_map/dot_general | solution.py:18
  192.0 10.5 %fusion.84 = f32[768,4096]{1,0:T(8,128)} fusion(bf16[768,448]{0,1:T(8,128)(2,1)} %get-tuple-element.34, bf16[4096,448]{0,1:T(8,128)(2,1)} %collective-permute-done.3), kind=kOutput, calls=%fused_computation.125 | convolution fusion | flops 2818572288 | bytes 16941056 | tf_op jit(solution)/shard_map/dot_general | solution.py:18
  202.5 20.3 %add_convert_fusion = bf16[768,4096]{1,0:T(8,128)(2,1)} fusion(f32[768,4096]{1,0:T(8,128)} %fusion.84, f32[768,4096]{1,0:T(8,128)} %fusion.82, f32[768,4096]{1,0:T(8,128)} %fusion.83, bf16[768,448]{0,1:T(8,128)(2,1)} %get-tuple-element.35, bf16[4096,448]{0,1:T(8,128)(2,1)} %collective-permute-done.4), kind=kOutput, calls=%fused_computation.12 | convolution fusion | flops 2831155200 | bytes 48398336 | tf_op jit(solution)/shard_map/dot_general | solution.py:18
  222.9 2.8 copy-done.2
  225.6 100.9 %sum_rows_gather_dm.1 = (bf16[2,4,4,48,4096]{4,3,2,1,0:T(8,128)(2,1)}, bf16[4,4,48,4096]{3,2,1,0:T(8,128)(2,1)S(1)}, f32[48,4096]{1,0:T(8,128)S(1)}, f32[1,4096]{1,0:T(1,128)S(1)}) custom-call(bf16[4,4,48,4096]{3,2,1,0:T(8,128)(2,1)S(1)} %bitcast.195, bf16[48,4096]{1,0:T(8,128)(2,1)S(1)} %get-tuple-element.20.rest_0_, ...), custom_call_target="tpu_custom_call" | custom-call | flops 400000000 | bytes 40000000 | tf_op jit(solution)/shard_map/sum_rows_gather_dm/pallas_call | solution.py:451
  326.6 1.8 convolution_convert_fusion.4
  328.4 0.7 copy-done.20
  329.2 3.9 fusion.61
  333.1 9.2 %fusion.48 = bf16[768,128]{0,1:T(8,128)(2,1)} fusion(bf16[768,2,128]{0,2,1:T(8,128)(2,1)S(1)} %bitcast.222, f32[768,768,2]{1,0,2:T(8,128)} %fusion.61, f32[2,768,768]{1,2,0:T(8,128)} %get-tuple-element.44, f32[2,768]{1,0:T(2,128)S(1)} %get-tuple-element.43), kind=kOutput, calls=%fused_computation.75 | convolution fusion | flops 310348032 | bytes 10033152 | tf_op jit(solution)/shard_map/hqk,qhd->kd/dot_general | solution.py:564
  342.3 3.4 fusion.49
  345.7 0.7 copy-done.22
  346.4 0.8 pad_maximum_fusion.3
  347.2 1.2 copy.65
  348.3 0.7 dynamic-slice_bitcast_fusion.2
  349.0 6.3 collective-permute-done.8
  355.4 1.7 fusion.60
  357.1 4.4 collective-permute-start.2
  361.6 10.6 %collective-permute-done.2 = bf16[48,4096]{1,0:T(8,128)(2,1)S(1)} collective-permute-done((bf16[48,4096]{1,0:T(8,128)(2,1)S(1)}, bf16[48,4096]{1,0:T(8,128)(2,1)S(1)}, u32[]{:S(2)}, u32[]{:S(2)}) %collective-permute-start.2) | collective-permute-done | bytes 393248 | tf_op jit(solution)/shard_map/ppermute | solution.py:552
  372.2 1.9 add_convert_fusion.1
  374.1 7.1 %fusion.2 = f32[2,768]{1,0:T(2,128)S(1)} fusion(bf16[2,768,4096]{2,1,0:T(8,128)(2,1)} %param.12), kind=kLoop, calls=%fused_computation.4 | loop fusion | flops 18872832 | bytes 12589056 | tf_op jit(solution)/shard_map/reduce_sum | solution.py:513
  381.4 1.4 collective-permute-done.9
  383.5 8.7 %fusion.44 = bf16[128,2,768]{2,0,1:T(8,128)(2,1)S(1)} fusion(f32[768,768,2]{1,0,2:T(8,128)} %fusion.61, bf16[768,512]{0,1:T(8,128)(2,1)} %copy-done.17, f32[2,768,768]{1,2,0:T(8,128)} %get-tuple-element.44, f32[2,768]{1,0:T(2,128)S(1)} %get-tuple-element.43), kind=kOutput, calls=%fused_computation.68 | convolution fusion | flops 310446336 | bytes 19476480 | tf_op jit(solution)/shard_map/hqk,kd->qhd/dot_general | solution.py:563
  392.5 5.9 convolution_convert_fusion.1
  398.4 125.5 %sum_rows_gather_da.1 = (bf16[2,4,4,48,4096]{4,3,2,1,0:T(8,128)(2,1)}, f32[2,4096]{1,0:T(2,128)S(1)}) custom-call(bf16[4,4,48,4096]{3,2,1,0:T(8,128)(2,1)S(1)} %bitcast.197, bf16[48,4096]{1,0:T(8,128)(2,1)S(1)} %dynamic-slice_bitcast_fusion.1.rest_0_, f32[48,4096]{1,0:T(8,128)S(1)} %get-tuple-element.23.rest_1_, f32[1,4096]{1,0:T(1,128)S(1)} %bitcast.200, ...), custom_call_target="tpu_custom_call" | custom-call | flops 400000000 | bytes 40000000 | tf_op jit(solution)/shard_map/sum_rows_gather_da/pallas_call | solution.py:451
  523.9 0.6 fusion.75
  524.6 8.0 %convolution_bitcast_fusion.5 = f32[128,4096]{1,0:T(8,128)} fusion(bf16[2,768,128]{1,2,0:T(8,128)(2,1)S(1)} %maximum_select_fusion.4, bf16[2,768,4096]{2,1,0:T(8,128)(2,1)} %bitcast.209), kind=kOutput, calls=%fused_computation.33 | convolution fusion | flops 1610612736 | bytes 15073280 | tf_op jit(solution)/shard_map/bsd,bse->de/dot_general | solution.py:585
  532.7 6.3 fusion.24
  539.0 1.8 maximum_select_fusion.2
  540.8 2.1 maximum_select_fusion.1
  542.9 12.6 %convolution_bitcast_fusion.4 = f32[448,4096]{1,0:T(8,128)} fusion(bf16[2,768,448]{1,2,0:T(8,128)(2,1)S(1)} %copy-done.14, bf16[2,768,4096]{2,1,0:T(8,128)(2,1)} %param.14), kind=kOutput, calls=%fused_computation.29 | convolution fusion | flops 5637144576 | bytes 21299200 | tf_op jit(solution)/shard_map/bsd,bse->de/dot_general | solution.py:585
  555.5 7.9 %convolution_bitcast_fusion.2 = f32[4096,448]{0,1:T(8,128)} fusion(bf16[2,768,448]{1,2,0:T(8,128)(2,1)S(1)} %maximum_select_fusion.2, bf16[2,768,4096]{2,1,0:T(8,128)(2,1)S(1)} %bitcast.235), kind=kOutput, calls=%fused_computation.27 | convolution fusion | flops 5637144576 | bytes 21299200 | tf_op jit(solution)/shard_map/bsd,bse->de/dot_general | solution.py:585
  563.4 7.9 %convolution_bitcast_fusion.3 = f32[4096,448]{0,1:T(8,128)} fusion(bf16[2,768,448]{1,2,0:T(8,128)(2,1)S(1)} %maximum_select_fusion.1, bf16[2,768,4096]{2,1,0:T(8,128)(2,1)S(1)} %bitcast.236), kind=kOutput, calls=%fused_computation.28 | convolution fusion | flops 5637144576 | bytes 21299200 | tf_op jit(solution)/shard_map/bsd,bse->de/dot_general | solution.py:585
  571.3 6.4 copy.48
  577.7 3.8 fusion.74
  581.5 5.8 reshape.166
  587.3 6.0 reshape.165
  593.3 20.3 %convolution_bitcast_fusion = f32[4096,1024]{1,0:T(8,128)} fusion(bf16[2,768,1024]{2,1,0:T(8,128)(2,1)} %reshape.166, bf16[2,768,4096]{2,1,0:T(8,128)(2,1)} %param.12, f32[4096]{0:T(1024)S(1)} %copy-done.4, f32[2,768]{1,0:T(2,128)S(1)} %add_rsqrt_fusion), kind=kOutput, calls=%fused_computation.14 | convolution fusion | flops 12910067712 | bytes 32528384 | tf_op jit(solution)/shard_map/bsd,bse->de/dot_general | solution.py:585
  613.6 19.4 %convolution_bitcast_fusion.1 = f32[4096,1024]{1,0:T(8,128)} fusion(bf16[2,768,1024]{2,1,0:T(8,128)(2,1)S(1)} %copy-done.10, bf16[2,768,4096]{2,1,0:T(8,128)(2,1)} %param.12, f32[4096]{0:T(1024)S(1)} %copy-done.4, f32[2,768]{1,0:T(2,128)S(1)} %add_rsqrt_fusion), kind=kOutput, calls=%fused_computation.15 | convolution fusion | flops 12910067712 | bytes 32528384 | tf_op jit(solution)/shard_map/bsd,bse->de/dot_general | solution.py:585
  632.9 10.6 %copy.69 = bf16[2,768,4096]{2,1,0:T(8,128)(2,1)} copy(bf16[2,768,4096]{2,1,0:T(8,128)(2,1)} %bitcast.211) | data formatting | bytes 25165824
  643.6 10.7 %copy.70 = bf16[2,768,4096]{2,1,0:T(8,128)(2,1)} copy(bf16[2,768,4096]{2,1,0:T(8,128)(2,1)} %bitcast.212) | data formatting | bytes 25165824
  (102 shorter events, 2.5 us)
Async XLA Ops:
  7.2 7.3 %copy-start = (s32[2,768]{1,0:T(2,128)S(1)}, s32[2,768]{1,0:T(2,128)}, u32[]{:S(2)}) copy-start(s32[2,768]{1,0:T(2,128)} %param.13) | copy-start | bytes 18436
  7.2 365.0 %reduce-scatter.2.cloned.1.call-start = ((), (), s32[]{:S(2)}) async-start(), calls=%async_computation.1 | async-start | bytes 12976128 | tf_op jit(solution)/shard_map/reduce_scatter | solution.py:551
  7.3 11.9 %collective-permute-start = (bf16[4096,128]{1,0:T(8,128)(2,1)}, bf16[4096,128]{1,0:T(8,128)(2,1)}, u32[]{:S(2)}, u32[]{:S(2)}) collective-permute-start(bf16[4096,128]{1,0:T(8,128)(2,1)} %param.17), channel_id=1, source_target_pairs={{0,1},{1,0},{2,3},{3,2},{4,5},{5,4},{6,7},{7,6},{8,9},{9,8},{10,11... | collective-permute-start | bytes 3145736 | tf_op jit(solution)/shard_map/ppermute | solution.py:487
  9.4 17.7 %collective-permute-start.1 = (bf16[128,4096]{1,0:T(8,128)(2,1)}, bf16[128,4096]{1,0:T(8,128)(2,1)}, u32[]{:S(2)}, u32[]{:S(2)}) collective-permute-start(bf16[128,4096]{1,0:T(8,128)(2,1)} %param.20), channel_id=1, source_target_pairs={{0,1},{1,0},{2,3},{3,2},{4,5},{5,4},{6,7},{7,6},{8,9},{9,8},{10,11... | collective-permute-start | bytes 3145736 | tf_op jit(solution)/shard_map/ppermute | solution.py:487
  9.5 137.6 %collective-permute-start.4 = (bf16[4096,448]{0,1:T(8,128)(2,1)}, bf16[4096,448]{0,1:T(8,128)(2,1)}, u32[]{:S(2)}, u32[]{:S(2)}) collective-permute-start(bf16[4096,448]{0,1:T(8,128)(2,1)} %param.22), channel_id=1, source_target_pairs={{0,1},{1,0},{2,3},{3,2},{4,5},{5,4},{6,7},{7,6},{8,9},{9,8},{10,11... | collective-permute-start | bytes 11010056 | tf_op jit(solution)/shard_map/ppermute | solution.py:487
  9.9 130.3 %collective-permute-start.6 = (bf16[448,4096]{1,0:T(8,128)(2,1)}, bf16[448,4096]{1,0:T(8,128)(2,1)}, u32[]{:S(2)}, u32[]{:S(2)}) collective-permute-start(bf16[448,4096]{1,0:T(8,128)(2,1)} %param.23), channel_id=1, source_target_pairs={{0,1},{1,0},{2,3},{3,2},{4,5},{5,4},{6,7},{7,6},{8,9},{9,8},{10,11... | collective-permute-start | bytes 11010056 | tf_op jit(solution)/shard_map/ppermute | solution.py:487
  10.0 142.4 %collective-permute-start.3 = (bf16[4096,448]{0,1:T(8,128)(2,1)}, bf16[4096,448]{0,1:T(8,128)(2,1)}, u32[]{:S(2)}, u32[]{:S(2)}) collective-permute-start(bf16[4096,448]{0,1:T(8,128)(2,1)} %param.21), channel_id=1, source_target_pairs={{0,1},{1,0},{2,3},{3,2},{4,5},{5,4},{6,7},{7,6},{8,9},{9,8},{10,11... | collective-permute-start | bytes 11010056 | tf_op jit(solution)/shard_map/ppermute | solution.py:487
  14.5 4.7 copy-start.4
  19.1 7.8 %copy-start.15 = (bf16[4096,128]{1,0:T(8,128)(2,1)}, bf16[4096,128]{1,0:T(8,128)(2,1)S(1)}, u32[]{:S(2)}) copy-start(bf16[4096,128]{1,0:T(8,128)(2,1)S(1)} %get-tuple-element.45) | copy-start | bytes 3145732
  19.2 7.8 %copy-start.16 = (bf16[4096,128]{1,0:T(8,128)(2,1)}, bf16[4096,128]{1,0:T(8,128)(2,1)S(1)}, u32[]{:S(2)}) copy-start(bf16[4096,128]{1,0:T(8,128)(2,1)S(1)} %get-tuple-element.46) | copy-start | bytes 3145732
  27.0 1.8 copy-start.17
  27.1 6.9 %copy-start.18 = (bf16[768,256]{0,1:T(8,128)(2,1)}, bf16[768,256]{0,1:T(8,128)(2,1)S(1)}, u32[]{:S(2)}) copy-start(bf16[768,256]{0,1:T(8,128)(2,1)S(1)} %slice.46) | copy-start | bytes 1179652
  28.8 8.2 %copy-start.5 = (bf16[256,4096]{1,0:T(8,128)(2,1)}, bf16[256,4096]{1,0:T(8,128)(2,1)S(1)}, u32[]{:S(2)}) copy-start(bf16[256,4096]{1,0:T(8,128)(2,1)S(1)} %constant_dynamic-update-slice_fusion) | copy-start | bytes 6291460
  36.9 0.8 copy-start.11
  36.9 2.6 copy-start.3
  39.5 93.4 %copy-start.7 = (bf16[4096,448]{0,1:T(8,128)(2,1)S(1)}, bf16[4096,448]{0,1:T(8,128)(2,1)}, u32[]{:S(2)}) copy-start(bf16[4096,448]{0,1:T(8,128)(2,1)} %param.21) | copy-start | bytes 11010052
  132.9 3.1 copy-start.8
  147.1 13.0 %slice-start.3 = ((s8[12582912]{0:T(1024)(128)(4,1)}), s8[4194304]{0:T(1024)(128)(4,1)S(1)}, s32[]{:S(2)}) async-start(s8[12582912]{0:T(1024)(128)(4,1)} %bitcast.231), calls=%async_computation.7 | async-start | bytes 8388608
  147.1 12.9 %slice-start.4 = ((s8[12582912]{0:T(1024)(128)(4,1)}), s8[4194304]{0:T(1024)(128)(4,1)S(1)}, s32[]{:S(2)}) async-start(s8[12582912]{0:T(1024)(128)(4,1)} %bitcast.231), calls=%async_computation.8 | async-start | bytes 8388608
  152.4 7.6 %slice-start.5 = ((s8[12582912]{0:T(1024)(128)(4,1)}), s8[4194304]{0:T(1024)(128)(4,1)S(1)}, s32[]{:S(2)}) async-start(s8[12582912]{0:T(1024)(128)(4,1)} %bitcast.231), calls=%async_computation.9 | async-start | bytes 8388608
  152.5 7.6 %copy-start.23 = (bf16[448,4096]{1,0:T(8,128)(2,1)S(1)}, bf16[448,4096]{1,0:T(8,128)(2,1)}, u32[]{:S(2)}) copy-start(bf16[448,4096]{1,0:T(8,128)(2,1)} %param.23) | copy-start | bytes 11010052
  159.8 5.5 copy-start.24
  159.8 5.3 collective-permute-start.5
  165.4 9.7 %copy-start.13 = (bf16[2,768,448]{1,2,0:T(8,128)(2,1)}, bf16[2,768,448]{1,2,0:T(8,128)(2,1)S(1)}, u32[]{:S(2)}) copy-start(bf16[2,768,448]{1,2,0:T(8,128)(2,1)S(1)} %maximum_select_fusion) | copy-start | bytes 4128772
  175.2 396.1 %all-gather.6.cloned.1.call-start = ((), (), s32[]{:S(2)}) async-start(), calls=%async_computation.3 | async-start | bytes 6488064 | tf_op jit(solution)/shard_map/all_gather | solution.py:575
  176.4 9.0 %copy-start.9 = (bf16[4096,448]{0,1:T(8,128)(2,1)S(1)}, bf16[4096,448]{0,1:T(8,128)(2,1)}, u32[]{:S(2)}) copy-start(bf16[4096,448]{0,1:T(8,128)(2,1)} %param.22) | copy-start | bytes 11010052
  222.9 2.8 copy-start.2
  225.6 100.9 %copy-start.6 = (bf16[256,4096]{1,0:T(8,128)(2,1)S(1)}, bf16[256,4096]{1,0:T(8,128)(2,1)}, u32[]{:S(2)}) copy-start(bf16[256,4096]{1,0:T(8,128)(2,1)} %copy-done.5) | copy-start | bytes 6291460
  328.4 0.7 copy-start.20
  328.4 4.6 copy-start.19
  342.3 4.1 copy-start.21
  345.7 0.7 copy-start.22
  349.0 6.3 collective-permute-start.8
  357.1 275.9 %all-gather.4.cloned.1.call-start = ((), (), s32[]{:S(2)}) async-start(), calls=%async_computation.2 | async-start | bytes 12976128 | tf_op jit(solution)/shard_map/all_gather | solution.py:554
  357.1 15.0 %collective-permute-start.2 = (bf16[48,4096]{1,0:T(8,128)(2,1)S(1)}, bf16[48,4096]{1,0:T(8,128)(2,1)S(1)}, u32[]{:S(2)}, u32[]{:S(2)}) collective-permute-start(bf16[48,4096]{1,0:T(8,128)(2,1)S(1)} %get-tuple-element.20.rest_0_), channel_id=1, source_target_pairs={{0,0},{1,16},{2,1},{3,17},{4,2},{5,18},{6,3},{7,19},{8,4},{9,20},{... | collective-permute-start | bytes 1179656 | tf_op jit(solution)/shard_map/ppermute | solution.py:552
  374.1 7.1 %copy-start.12 = (bf16[128,2,768]{2,0,1:T(8,128)(2,1)S(1)}, bf16[128,2,768]{2,0,1:T(8,128)(2,1)}, u32[]{:S(2)}) copy-start(bf16[128,2,768]{2,0,1:T(8,128)(2,1)} %copy-done.11) | copy-start | bytes 1179652
  381.3 1.5 collective-permute-start.9
  382.9 156.1 %collective-permute-start.11 = (bf16[768,448]{0,1:T(8,128)(2,1)}, bf16[768,448]{0,1:T(8,128)(2,1)}, u32[]{:S(2)}, u32[]{:S(2)}) collective-permute-start(bf16[768,448]{0,1:T(8,128)(2,1)} %get-tuple-element.35), channel_id=1, source_target_pairs={{0,1},{1,0},{2,3},{3,2},{4,5},{5,4},{6,7},{7,6},{8,9},{9,8},{10,11... | collective-permute-start | bytes 2064392 | tf_op jit(solution)/shard_map/ppermute | solution.py:487
  383.1 157.7 %collective-permute-start.10 = (bf16[768,448]{0,1:T(8,128)(2,1)}, bf16[768,448]{0,1:T(8,128)(2,1)}, u32[]{:S(2)}, u32[]{:S(2)}) collective-permute-start(bf16[768,448]{0,1:T(8,128)(2,1)} %get-tuple-element.34), channel_id=1, source_target_pairs={{0,1},{1,0},{2,3},{3,2},{4,5},{5,4},{6,7},{7,6},{8,9},{9,8},{10,11... | collective-permute-start | bytes 2064392 | tf_op jit(solution)/shard_map/ppermute | solution.py:487
  392.2 140.4 %collective-permute-start.7 = (bf16[768,128]{0,1:T(8,128)(2,1)S(1)}, bf16[768,128]{0,1:T(8,128)(2,1)S(1)}, u32[]{:S(2)}, u32[]{:S(2)}) collective-permute-start(bf16[768,128]{0,1:T(8,128)(2,1)S(1)} %get-tuple-element.40), channel_id=1, source_target_pairs={{0,1},{1,0},{2,3},{3,2},{4,5},{5,4},{6,7},{7,6},{8,9},{9,8},{10,11... | collective-permute-start | bytes 589832 | tf_op jit(solution)/shard_map/ppermute | solution.py:487
  398.3 134.3 %slice-start = ((s8[12582912]{0:T(1024)(128)(4,1)}), s8[4194304]{0:T(1024)(128)(4,1)S(1)}, s32[]{:S(2)}) async-start(s8[12582912]{0:T(1024)(128)(4,1)} %bitcast.206), calls=%async_computation.4 | async-start | bytes 8388608
  524.5 8.1 %slice-start.1 = ((s8[12582912]{0:T(1024)(128)(4,1)}), s8[4194304]{0:T(1024)(128)(4,1)S(1)}, s32[]{:S(2)}) async-start(s8[12582912]{0:T(1024)(128)(4,1)} %bitcast.206), calls=%async_computation.5 | async-start | bytes 8388608
  524.5 8.1 %slice-start.2 = ((s8[12582912]{0:T(1024)(128)(4,1)}), s8[4194304]{0:T(1024)(128)(4,1)S(1)}, s32[]{:S(2)}) async-start(s8[12582912]{0:T(1024)(128)(4,1)} %bitcast.206), calls=%async_computation.6 | async-start | bytes 8388608
  539.0 3.9 copy-start.14
  539.0 16.5 %slice-start.6 = ((s8[12582912]{0:T(1024)(128)(4,1)}), s8[4194304]{0:T(1024)(128)(4,1)S(1)}, s32[]{:S(2)}) async-start(s8[12582912]{0:T(1024)(128)(4,1)} %bitcast.233), calls=%async_computation.10 | async-start | bytes 8388608
  542.9 12.7 %slice-start.7 = ((s8[12582912]{0:T(1024)(128)(4,1)}), s8[4194304]{0:T(1024)(128)(4,1)S(1)}, s32[]{:S(2)}) async-start(s8[12582912]{0:T(1024)(128)(4,1)} %bitcast.233), calls=%async_computation.11 | async-start | bytes 8388608
  542.9 12.6 %slice-start.8 = ((s8[12582912]{0:T(1024)(128)(4,1)}), s8[4194304]{0:T(1024)(128)(4,1)S(1)}, s32[]{:S(2)}) async-start(s8[12582912]{0:T(1024)(128)(4,1)} %bitcast.233), calls=%async_computation.12 | async-start | bytes 8388608
  593.3 20.3 %copy-start.10 = (bf16[2,768,1024]{2,1,0:T(8,128)(2,1)S(1)}, bf16[2,768,1024]{2,1,0:T(8,128)(2,1)}, u32[]{:S(2)}) copy-start(bf16[2,768,1024]{2,1,0:T(8,128)(2,1)} %reshape.165) | copy-start | bytes 9437188
  643.6 10.7 %copy-start.1 = (s32[2,768]{1,0:T(2,128)S(1)}, s32[2,768]{1,0:T(2,128)}, u32[]{:S(2)}) copy-start(s32[2,768]{1,0:T(2,128)} %param.13) | copy-start | bytes 18436
Sparse Core Ops, SparseCore 0:
  175.3 115.3 reduce-scatter.1
  357.2 48.3 all-gather.5
  407.7 82.0 all-gather.3

commit v2 on v0

v2 whole, which is shorter than its diff:
```python
import functools
import math
import jax
import jax.numpy as jnp
from jax import lax
from jax.experimental import pallas as pl
from jax.experimental.pallas import tpu as pltpu
from jax.sharding import PartitionSpec as P

HEAD_DIM = 128
EPS = 1e-5
MESH = pl.DeviceIdType.MESH
F32 = jnp.float32
BF16 = jnp.bfloat16
MIB = 2 ** 20
ANY = pl.BlockSpec(memory_space=pl.ANY)
VMEM = pl.BlockSpec(memory_space=pltpu.VMEM)


def dot(lhs, rhs, dims):
    return lax.dot_general(lhs, rhs, (dims, ((), ())), preferred_element_type=F32)


NN = ((1,), (0,))
NT = ((1,), (1,))


SIGNS = (1, -1)


class Colour:
    def __init__(self, index, first, second):
        self.index, self.first, self.second = index, first, second


class Torus:
    def __init__(self, side):
        self.side = side
        tp_idx = lax.axis_index('tp')
        self.core = lax.rem(tp_idx, 2)
        self.chip = lax.div(tp_idx, 2)
        self.x = lax.rem(self.chip, side)
        self.y = lax.div(self.chip, side)
        self.partner = {'tp': self.chip * 2 + (1 - self.core)}
        self.colours = (Colour(0, self.x, self.y), Colour(1, self.y, self.x))
        self.pending = []

    def wrap(self, pos):
        return lax.rem(pos + 2 * self.side, self.side)

    def at_chip(self, y_at, x_at):
        return {'tp': (y_at * self.side + x_at) * 2 + self.core}

    def block(self, col, second, first):
        return (second, first) if col.index == 0 else (first, second)

    def peer1(self, col, shift):
        return self.at_chip(*self.block(col, col.second, self.wrap(col.first + shift)))

    def peer2(self, col, shift):
        return self.at_chip(*self.block(col, self.wrap(col.second + shift), col.first))

    def signal_all(self):
        barrier = pltpu.get_barrier_semaphore()
        peers = [self.partner]
        peers += [self.at_chip(self.y, self.wrap(self.x + shift)) for shift in SIGNS]
        peers += [self.at_chip(self.wrap(self.y + shift), self.x) for shift in SIGNS]
        for peer in peers:
            pl.semaphore_signal(barrier, inc=1, device_id=peer, device_id_type=MESH)
        return lambda: pl.semaphore_wait(barrier, len(peers))

    def send(self, src, dst, sems, index, device):
        copy = pltpu.make_async_remote_copy(src, dst, sems[0].at[index], sems[1].at[index], device_id=device, device_id_type=MESH)
        copy.start()
        self.pending.append(copy)

    def arrive(self, dst, sems, index):
        pltpu.make_async_remote_copy(dst, dst, sems[0].at[index], sems[1].at[index], device_id=self.partner, device_id_type=MESH).wait_recv()

    def drain(self):
        for copy in self.pending:
            copy.wait_send()


RS_BUFFERS = (('r1', 16), ('r2', 16), ('r3', 16), ('s1', 4), ('s2', 4), ('s3', 4))
AG_SEMS = (('h1', 8), ('h2', 32), ('f1', 4), ('f2', 16))


class ReduceScatter:
    SHIFTS = (2, 1, 3, 0)

    def __init__(self, torus, part, scr, name):
        self.torus, self.part, self.scr, self.name = torus, part, scr, name
        self.quarter = part.shape[3] // 4

    def buf(self, kind, index):
        return self.scr[self.name + kind].at[index]

    def sems(self, kind):
        return self.scr[self.name + kind + '_s'], self.scr[self.name + kind + '_r']

    def cols(self, col, half):
        return pl.ds((col.index * 2 + half) * self.quarter, self.quarter)

    def piece(self, where, at_cols):
        return self.part.at[(*where, slice(None), at_cols)]

    def send(self, where, at_cols, kind, index, peer):
        self.torus.send(self.piece(where, at_cols), self.buf(kind, index), self.sems(kind), index, peer)

    def add(self, where, at_cols, *kinds):
        total = self.part[(*where, slice(None), at_cols)].astype(F32)
        for kind, index in kinds:
            self.torus.arrive(self.buf(kind, index), self.sems(kind), index)
            total = total + self.buf(kind, index)[...].astype(F32)
        self.part[(*where, slice(None), at_cols)] = total.astype(BF16)

    def each(self, step):
        wrap = self.torus.wrap
        for col in self.torus.colours:
            second = wrap(col.second + self.SHIFTS[step])
            for way, sign in enumerate(SIGNS):
                yield col, second, way, sign, (col.index * 2 + way) * 4 + step

    def far(self, step):
        for col, second, way, sign, index in self.each(step):
            where = self.torus.block(col, second, self.torus.wrap(col.first + 2))
            self.send(where, self.cols(col, way), 'r1', index, self.torus.peer1(col, sign))

    def near(self, step):
        for col, second, way, sign, index in self.each(step):
            where = self.torus.block(col, second, self.torus.wrap(col.first + sign))
            self.send(where, self.cols(col, 1 - way), 'r2', index, self.torus.peer1(col, sign))

    def relay(self, step):
        for col, second, way, sign, index in self.each(step):
            where = self.torus.block(col, second, self.torus.wrap(col.first + sign))
            self.add(where, self.cols(col, way), ('r1', index))
            self.send(where, self.cols(col, way), 'r3', index, self.torus.peer1(col, sign))

    def end(self, step):
        for col, second, way, sign, index in self.each(step):
            where = self.torus.block(col, second, col.first)
            other = (col.index * 2 + 1 - way) * 4 + step
            self.add(where, self.cols(col, way), ('r2', other), ('r3', index))

    def far2(self):
        for col in self.torus.colours:
            for way, sign in enumerate(SIGNS):
                where = self.torus.block(col, self.torus.wrap(col.second + 2), col.first)
                self.send(where, self.cols(col, way), 's1', col.index * 2 + way, self.torus.peer2(col, sign))

    def near2(self, way):
        for col in self.torus.colours:
            where = self.torus.block(col, self.torus.wrap(col.second + SIGNS[way]), col.first)
            self.send(where, self.cols(col, 1 - way), 's2', col.index * 2 + way, self.torus.peer2(col, SIGNS[way]))

    def relay2(self, way):
        for col in self.torus.colours:
            index = col.index * 2 + way
            where = self.torus.block(col, self.torus.wrap(col.second + SIGNS[way]), col.first)
            self.add(where, self.cols(col, way), ('s1', index))
            self.send(where, self.cols(col, way), 's3', index, self.torus.peer2(col, SIGNS[way]))

    def end2(self):
        for col in self.torus.colours:
            where = self.torus.block(col, col.second, col.first)
            for way in range(2):
                self.add(where, self.cols(col, way), ('s2', col.index * 2 + 1 - way), ('s3', col.index * 2 + way))

    def steps(self, fill):
        call = functools.partial
        return [call(fill, 2), call(self.far, 0), call(self.far, 1), call(fill, 1), call(fill, 3),
                call(self.near, 0), call(self.relay, 0), call(self.near, 1), call(self.far, 2), call(self.relay, 1),
                call(fill, 0), call(self.near, 2), call(self.far, 3), call(self.end, 0), call(self.far2),
                call(self.relay, 2), call(self.near, 3), call(self.end, 1), call(self.near2, 0), call(self.relay2, 0),
                call(self.relay, 3), call(self.end, 2), call(self.near2, 1), call(self.relay2, 1), call(self.end, 3),
                call(self.end2)]


class AllGather:
    def __init__(self, torus, gat, scr, name, by_rows, keep):
        self.torus, self.gat, self.scr, self.name, self.by_rows, self.keep_piece = torus, gat, scr, name, by_rows, keep
        self.quarter = gat.shape[2 if by_rows else 3] // 4
        self.back = (0, torus.side - 1, 1, 2)

    def sems(self, kind):
        return self.scr[self.name + kind + '_s'], self.scr[self.name + kind + '_r']

    def piece(self, ref, where, first, count):
        at = pl.ds(first * self.quarter, count * self.quarter)
        return ref.at[(*where, at, slice(None))] if self.by_rows else ref.at[(*where, slice(None), at)]

    def half(self, col, where, half):
        return self.piece(self.gat, where, col.index * 2 + half, 1)

    def own2(self, turn):
        for col in self.torus.colours:
            where = self.torus.block(col, col.second, col.first)
            for way, sign in enumerate(SIGNS):
                at = self.half(col, where, way if turn == 0 else 1 - way)
                self.torus.send(at, at, self.sems('h1'), (col.index * 2 + way) * 2 + turn, self.torus.peer2(col, sign))

    def send1(self, step, turn):
        for col in self.torus.colours:
            where = self.torus.block(col, self.torus.wrap(col.second + self.back[step]), col.first)
            for way, sign in enumerate(SIGNS):
                at = self.half(col, where, way if turn == 0 else 1 - way)
                self.torus.send(at, at, self.sems('h2'), ((col.index * 2 + way) * 4 + step) * 2 + turn, self.torus.peer1(col, sign))

    def arrive2(self, way, turn):
        sign = SIGNS[way]
        for col in self.torus.colours:
            where = self.torus.block(col, self.torus.wrap(col.second - sign), col.first)
            at = self.half(col, where, way if turn == 0 else 1 - way)
            self.torus.arrive(at, self.sems('h1'), (col.index * 2 + way) * 2 + turn)
            if turn == 0:
                self.torus.send(at, at, self.sems('f1'), col.index * 2 + way, self.torus.peer2(col, sign))

    def relayed2(self):
        for col in self.torus.colours:
            where = self.torus.block(col, self.torus.wrap(col.second + 2), col.first)
            for way in range(2):
                self.torus.arrive(self.half(col, where, way), self.sems('f1'), col.index * 2 + way)

    def arrive1(self, step, turn):
        for col in self.torus.colours:
            second = self.torus.wrap(col.second + self.back[step])
            for way, sign in enumerate(SIGNS):
                where = self.torus.block(col, second, self.torus.wrap(col.first - sign))
                at = self.half(col, where, way if turn == 0 else 1 - way)
                self.torus.arrive(at, self.sems('h2'), ((col.index * 2 + way) * 4 + step) * 2 + turn)
                if turn == 0:
                    self.torus.send(at, at, self.sems('f2'), (col.index * 2 + way) * 4 + step, self.torus.peer1(col, sign))

    def relayed1(self, step):
        for col in self.torus.colours:
            second = self.torus.wrap(col.second + self.back[step])
            for way in range(2):
                where = self.torus.block(col, second, self.torus.wrap(col.first + 2))
                self.torus.arrive(self.half(col, where, way), self.sems('f2'), (col.index * 2 + way) * 4 + step)

    def keep(self, step, firsts):
        for col in self.torus.colours:
            for shift in firsts:
                where = self.torus.block(col, self.torus.wrap(col.second + self.back[step]), self.torus.wrap(col.first + shift))
                slot = (col.index * self.torus.side + where[0]) * self.torus.side + where[1]
                self.keep_piece(slot, lambda ref, where=where, col=col: self.piece(ref, where, col.index * 2, 2))

    def steps(self):
        call = functools.partial
        beside = (1, self.torus.side - 1)
        return [call(self.own2, 0), call(self.send1, 0, 0), call(self.own2, 1), call(self.send1, 0, 1), call(self.keep, 0, (0,)),
                call(self.arrive2, 0, 0), call(self.arrive2, 1, 0), call(self.arrive2, 0, 1), call(self.send1, 1, 0), call(self.send1, 1, 1),
                call(self.arrive2, 1, 1), call(self.send1, 2, 0), call(self.send1, 2, 1), call(self.keep, 1, (0,)), call(self.keep, 2, (0,)),
                call(self.arrive1, 0, 0), call(self.relayed2), call(self.send1, 3, 0), call(self.send1, 3, 1), call(self.keep, 3, (0,)),
                call(self.arrive1, 0, 1), call(self.keep, 0, beside), call(self.arrive1, 1, 0), call(self.arrive1, 2, 0),
                call(self.relayed1, 0), call(self.keep, 0, (2,)), call(self.arrive1, 1, 1), call(self.keep, 1, beside),
                call(self.arrive1, 2, 1), call(self.keep, 2, beside), call(self.arrive1, 3, 0), call(self.relayed1, 1), call(self.keep, 1, (2,)),
                call(self.relayed1, 2), call(self.keep, 2, (2,)), call(self.arrive1, 3, 1), call(self.keep, 3, beside),
                call(self.relayed1, 3), call(self.keep, 3, (2,))]


class Store:
    def __init__(self, torus, full, scr, name, own=None):
        self.torus, self.full, self.scr, self.name, self.own = torus, full, scr, name, own
        self.stores = []

    def sem(self, kind, slot):
        return self.scr[self.name + kind].at[slot]

    def keep(self, gat):
        def put(slot, piece):
            pairs = [('full_s', self.full.at[self.torus.core])]
            if self.own is not None:
                pairs.append(('own_s', self.own))
            for kind, ref in pairs:
                store = pltpu.make_async_copy(piece(gat), piece(ref), self.sem(kind, slot))
                store.start()
                self.stores.append(store)
            sems = self.scr[self.name + 'd2d_s'], self.scr[self.name + 'd2d_r']
            self.torus.send(piece(gat), piece(self.full.at[self.torus.core]), sems, slot, self.torus.partner)
        return put

    def drain(self, gather):
        for store in self.stores:
            store.wait()
        side = self.torus.side
        for colour in range(2):
            for y_at in range(side):
                for x_at in range(side):
                    target = gather.piece(self.full.at[1 - self.torus.core], (y_at, x_at), colour * 2, 2)
                    sems = self.scr[self.name + 'd2d_s'], self.scr[self.name + 'd2d_r']
                    self.torus.arrive(target, sems, (colour * side + y_at) * side + x_at)


def rs_scratch(name, side, rows, width):
    dma = pltpu.SemaphoreType.DMA
    scratch = {name + 'part': pltpu.VMEM((side, side, rows, width), BF16)}
    for kind, count in RS_BUFFERS:
        scratch[name + kind] = pltpu.VMEM((count, rows, width // 4), BF16)
        scratch[name + kind + '_s'] = dma((count,))
        scratch[name + kind + '_r'] = dma((count,))
    return scratch


def ag_scratch(name, side, rows, width, own):
    dma = pltpu.SemaphoreType.DMA
    scratch = {name + 'gat': pltpu.VMEM((side, side, rows, width), BF16)}
    for kind, count in AG_SEMS:
        scratch[name + kind + '_s'] = dma((count,))
        scratch[name + kind + '_r'] = dma((count,))
    for kind in ('full_s', 'd2d_s', 'd2d_r') + (('own_s',) if own else ()):
        scratch[name + kind] = dma((2 * side * side,))
    return scratch


class Weights:
    def __init__(self, refs, buf, sem, by_rows):
        self.refs, self.buf, self.sem, self.by_rows = refs, buf, sem, by_rows
        self.copies = [[], []]

    def start(self):
        for colour in range(2):
            for index, ref in enumerate(self.refs):
                if self.by_rows:
                    half, depth = ref.shape[0] // 2, ref.shape[1]
                    rows, cols = pl.ds(colour * half, half), pl.ds(index * depth, depth)
                    copy = pltpu.make_async_copy(ref.at[rows, :], self.buf.at[rows, cols], self.sem.at[colour, index])
                else:
                    half, depth = ref.shape[1] // 2, ref.shape[0]
                    rows, cols = pl.ds(index * depth, depth), pl.ds(colour * half, half)
                    copy = pltpu.make_async_copy(ref.at[:, cols], self.buf.at[rows, cols], self.sem.at[colour, index])
                copy.start()
                self.copies[colour].append(copy)

    def wait(self, colour):
        for copy in self.copies[colour]:
            copy.wait()
        self.copies[colour] = []


def fill_partial(torus, part, lhs, weights):
    rows, width = part.shape[2:]
    tile = min(512, width // 2)

    def fill(shift):
        for col in torus.colours:
            weights.wait(col.index)
            first = torus.wrap(col.first + shift)
            left = []
            for ref in lhs:
                depth = ref.shape[3]
                value = ref[:, first] if col.index == 0 else ref[first]
                left.append((value.reshape(torus.side * rows, depth), depth))

            def body(step, carry, col=col, first=first, left=left):
                at = pl.ds(pl.multiple_of(col.index * (width // 2) + step * tile, tile), tile)
                total = None
                base = 0
                for value, depth in left:
                    if weights.by_rows:
                        term = dot(value, weights.buf[at, base:base + depth], NT)
                    else:
                        term = dot(value, weights.buf[base:base + depth, at], NN)
                    total = term if total is None else total + term
                    base += depth
                total = total.astype(BF16).reshape(torus.side, rows, tile)
                if col.index == 0:
                    part[:, first, :, at] = total
                else:
                    part[first, :, :, at] = total
                return carry

            lax.fori_loop(0, (width // 2) // tile, body, 0)

    return fill


def run(*lists):
    keyed = []
    for order, steps in enumerate(lists):
        keyed += [((index + 0.5) / len(steps), order, step) for index, step in enumerate(steps)]
    for _, _, step in sorted(keyed, key=lambda item: item[:2]):
        step()


def swap_scratch(count):
    return {'swap_s': pltpu.SemaphoreType.DMA((count,)), 'swap_r': pltpu.SemaphoreType.DMA((count,))}


def swap_start(torus, scr, pairs):
    for index, (src, dst) in enumerate(pairs):
        torus.send(src, dst, (scr['swap_s'], scr['swap_r']), index, torus.partner)


def swap_end(torus, scr, pairs):
    for index, (_, dst) in enumerate(pairs):
        torus.arrive(dst, (scr['swap_s'], scr['swap_r']), index)


def row_tiles(rows):
    return [pl.ds(start, 16) for start in range(0, rows, 16)]


def rms_back(z_in, gain, grad):
    inv = lax.rsqrt(jnp.mean(z_in * z_in, axis=-1, keepdims=True) + EPS)
    normed = z_in * inv
    scaled = grad * gain
    back = inv * (scaled - normed * jnp.mean(scaled * normed, axis=-1, keepdims=True))
    return back, jnp.sum(grad * normed, axis=0, keepdims=True)


def call_kernel(name, body, ins, outs, scratch, vmem_mib, flops, collective_id=None):
    names_in, names_out, names_scr = tuple(ins), tuple(outs), tuple(scratch)

    def kernel(*refs):
        refs = list(refs)
        take = lambda names: {key: refs.pop(0) for key in names}
        body(take(names_in), take(names_out), take(names_scr))

    results = pl.pallas_call(
        kernel,
        name=name,
        out_shape=[outs[key][0] for key in names_out],
        in_specs=[ins[key][1] for key in names_in],
        out_specs=[outs[key][1] for key in names_out],
        scratch_shapes=[scratch[key] for key in names_scr],
        compiler_params=pltpu.CompilerParams(collective_id=collective_id, has_side_effects=collective_id is not None, vmem_limit_bytes=int(vmem_mib * MIB)),
        cost_estimate=pl.CostEstimate(flops=int(flops), bytes_accessed=40_000_000, transcendentals=0),
    )(*[ins[key][0] for key in names_in])
    return dict(zip(names_out, results))


def shape(dims, dtype=BF16):
    return jax.ShapeDtypeStruct(dims, dtype)


def sum_attention(side, ctx, normed, w_out, x_rows, gain):
    seq, depth = ctx.shape
    width = gain.shape[1]
    rows = seq // (side * side)
    block = (side, side, rows, width)

    def body(ins, outs, scr):
        torus = Torus(side)
        weights = Weights([ins['w_a'], ins['w_b']], scr['w'], scr['w_s'], False)
        weights.start()
        wait = torus.signal_all()
        part = scr['part']
        fill = fill_partial(torus, part, [ins['ctx']], weights)
        scatter = ReduceScatter(torus, part, scr, '')
        steps = scatter.steps(fill)
        steps[0]()
        wait()
        swaps = [(ins['ctx'].at[:, :, :, pl.ds(depth // 2, depth // 2)], outs['ctx_other']), (ins['normed'], outs['normed_other'])]
        swap_start(torus, scr, swaps)
        run(steps[1:])
        gat = scr['gat']
        own = (torus.y, torus.x)
        for at in row_tiles(rows):
            resid = (ins['x_rows'][at, :].astype(F32) + part[(*own, at, slice(None))].astype(F32)).astype(BF16)
            outs['h_rows'][at, :] = resid
            z_in = resid.astype(F32)
            inv = lax.rsqrt(jnp.mean(z_in * z_in, axis=-1, keepdims=True) + EPS)
            gat[(*own, at, slice(None))] = (z_in * inv * ins['gain'][...]).astype(BF16)
        store = Store(torus, outs['full'], scr, '')
        gather = AllGather(torus, gat, scr, '', False, store.keep(gat))
        run(gather.steps())
        store.drain(gather)
        swap_end(torus, scr, swaps)
        torus.drain()

    ins = {'ctx': (ctx.reshape(side, side, rows, depth), VMEM), 'w_a': (w_out[0], ANY), 'w_b': (w_out[1], ANY), 'x_rows': (x_rows, VMEM), 'gain': (gain, VMEM), 'normed': (normed, ANY)}
    outs = {'full': (shape((2, *block)), ANY), 'h_rows': (shape((rows, width)), VMEM), 'ctx_other': (shape((side, side, rows, depth // 2)), ANY), 'normed_other': (shape((seq, width)), ANY)}
    scratch = {**rs_scratch('', side, rows, width), **ag_scratch('', side, rows, width, False), 'w': pltpu.VMEM((depth, width), BF16), 'w_s': pltpu.SemaphoreType.DMA((2, 2)), **swap_scratch(2)}
    return call_kernel('sum_attention', body, ins, outs, scratch, 36, 4e8, 1)


def sum_mlp(side, grads, acts, w_gates, w_ups, w_downs, h_rows, dy_rows, gain):
    seq, depth = grads[0].shape
    width = gain.shape[1]
    rows = seq // (side * side)
    block = (side, side, rows, width)

    def body(ins, outs, scr):
        torus = Torus(side)
        weights = Weights([ins[f'w_{index}'] for index in range(4)], scr['w'], scr['w_s'], False)
        weights.start()
        weights_p = Weights([ins[f'wd_{index}'] for index in range(2)], scr['wd'], scr['wd_s'], False)
        weights_p.start()
        wait = torus.signal_all()
        scatter = ReduceScatter(torus, scr['part'], scr, '')
        steps = scatter.steps(fill_partial(torus, scr['part'], [ins[f'g_{index}'] for index in range(4)], weights))
        scatter_p = ReduceScatter(torus, scr['p_part'], scr, 'p_')
        fill_p = fill_partial(torus, scr['p_part'], [ins[f'a_{index}'] for index in range(2)], weights_p)
        steps_p = scatter_p.steps(fill_p)
        steps[0]()
        wait()
        swaps = [(ins['g_2'], outs['gate_other']), (ins['g_3'], outs['up_other']), (ins['a_1'], outs['act_other'])]
        swap_start(torus, scr, swaps)
        early = [steps_p[0], steps_p[3], steps_p[4], steps_p[10]]
        rest_p = [step for index, step in enumerate(steps_p) if index not in (0, 3, 4, 10)]
        run(steps[1:22], early)
        for step in rest_p[:3]:
            step()
        run(steps[22:])
        own = (torus.y, torus.x)
        gain_total = jnp.zeros((1, width), F32)
        gat = scr['gat']
        for at in row_tiles(rows):
            back, gain_part = rms_back(ins['h_rows'][at, :].astype(F32), ins['gain'][...], scr['part'][(*own, at, slice(None))].astype(F32))
            gain_total = gain_total + gain_part
            total = ins['dy_rows'][at, :].astype(F32) + back
            outs['d_rows'][at, :] = total
            gat[(*own, at, slice(None))] = total.astype(BF16)
        outs['gain'][...] = gain_total
        store = Store(torus, outs['full'], scr, '', outs['own'])
        gather = AllGather(torus, gat, scr, '', False, store.keep(gat))
        run(gather.steps(), rest_p[3:])
        for at in row_tiles(rows):
            outs['y_rows'][at, :] = (ins['h_rows'][at, :].astype(F32) + scr['p_part'][(*own, at, slice(None))].astype(F32)).astype(BF16)
        store.drain(gather)
        swap_end(torus, scr, swaps)
        torus.drain()

    ins = {}
    for index, grad in enumerate(grads):
        ins[f'g_{index}'] = (grad.reshape(side, side, rows, depth), VMEM)
    for index, act in enumerate(acts):
        ins[f'a_{index}'] = (act.reshape(side, side, rows, depth), VMEM)
    for index, weight in enumerate((w_gates[0], w_ups[0], w_gates[1], w_ups[1])):
        ins[f'w_{index}'] = (weight, ANY)
    for index, weight in enumerate(w_downs):
        ins[f'wd_{index}'] = (weight, ANY)
    ins.update(h_rows=(h_rows, VMEM), dy_rows=(dy_rows, VMEM), gain=(gain, VMEM))
    outs = {'full': (shape((2, *block)), ANY), 'own': (shape(block), ANY), 'd_rows': (shape((rows, width), F32), VMEM), 'gain': (shape((1, width), F32), VMEM), 'y_rows': (shape((rows, width)), VMEM)}
    outs.update({key: (shape((side, side, rows, depth)), ANY) for key in ('gate_other', 'up_other', 'act_other')})
    scratch = {**rs_scratch('', side, rows, width), **rs_scratch('p_', side, rows, width), **ag_scratch('', side, rows, width, True),
               'w': pltpu.VMEM((4 * depth, width), BF16), 'w_s': pltpu.SemaphoreType.DMA((2, 4)), 'wd': pltpu.VMEM((2 * depth, width), BF16), 'wd_s': pltpu.SemaphoreType.DMA((2, 2)), **swap_scratch(3)}
    return call_kernel('sum_mlp', body, ins, outs, scratch, 60, 6e8, 2)


def sum_input(side, dqkv, w_in, dkv, x_rows, d_rows, gain, gain_mlp_part):
    seq, depth = dqkv.shape
    width = gain.shape[1]
    rows = seq // (side * side)
    tokens, pair = dkv.shape[1:]

    def body(ins, outs, scr):
        torus = Torus(side)
        weights = Weights([ins['w_in']], scr['w'], scr['w_s'], True)
        weights.start()
        wait = torus.signal_all()
        part = scr['part']
        scatter = ReduceScatter(torus, part, scr, '')
        steps = scatter.steps(fill_partial(torus, part, [ins['dqkv']], weights))
        own = (torus.y, torus.x)
        gat = scr['k_gat']
        store = Store(torus, outs['kv'], scr, 'k_')
        gather = AllGather(torus, gat, scr, 'k_', True, store.keep(gat))
        place = lax.rem(torus.x, 2)
        mate = torus.at_chip(torus.y, torus.x + 1 - 2 * place)
        mate_sems = scr['mate_s'], scr['mate_r']

        def mate_send():
            torus.send(ins['dkv'].at[1 - place], scr['mate'].at[0], mate_sems, 0, mate)

        def mate_add():
            torus.arrive(scr['mate'].at[0], mate_sems, 0)
            gat[own] = (ins['dkv'][place].astype(F32) + scr['mate'][0].astype(F32)).astype(BF16)

        steps[0]()
        wait()
        swaps = [(ins['dqkv'].at[:, :, :, pl.ds(pair // 2, pair // 2)], outs['q_other'])]
        swap_start(torus, scr, swaps)
        mate_send()
        for step in steps[1:5]:
            step()
        mate_add()
        run(steps[5:], gather.steps())
        gain_total = jnp.zeros((1, width), F32)
        for at in row_tiles(rows):
            back, gain_part = rms_back(ins['x_rows'][at, :].astype(F32), ins['gain'][...], part[(*own, at, slice(None))].astype(F32))
            gain_total = gain_total + gain_part
            outs['rows'][at, :] = (ins['d_rows'][at, :] + back).astype(BF16)
        row = lax.broadcasted_iota(jnp.int32, (16, width), 0)
        extra = jnp.zeros((16, width), F32)
        for index, value in enumerate((gain_total, ins['gain_mlp'][...])):
            for level in range(3):
                rounded = value.astype(BF16).astype(F32)
                extra = jnp.where(row == index * 3 + level, rounded, extra)
                value = value - rounded
        outs['rows'][rows:rows + 16, :] = extra.astype(BF16)
        store.drain(gather)
        swap_end(torus, scr, swaps)
        torus.drain()

    ins = {'dqkv': (dqkv.reshape(side, side, rows, depth), VMEM), 'w_in': (w_in, ANY), 'dkv': (dkv, VMEM), 'x_rows': (x_rows, VMEM), 'd_rows': (d_rows, VMEM), 'gain': (gain, VMEM), 'gain_mlp': (gain_mlp_part, VMEM)}
    outs = {'rows': (shape((rows + 16, width)), VMEM), 'kv': (shape((2, side, side, tokens, pair)), ANY), 'q_other': (shape((side, side, rows, pair // 2)), ANY)}
    dma = pltpu.SemaphoreType.DMA
    scratch = {**rs_scratch('', side, rows, width), **ag_scratch('k_', side, tokens, pair, False), 'w': pltpu.VMEM((width, depth), BF16), 'w_s': dma((2, 1)),
               'mate': pltpu.VMEM((1, tokens, pair), BF16), 'mate_s': dma((1,)), 'mate_r': dma((1,)), **swap_scratch(1)}
    return call_kernel('sum_input', body, ins, outs, scratch, 36, 3e8, 3)


def mlp_grads(mixed_full, grad_out, w_gates, w_ups, w_downs):
    seq, width = grad_out.shape[1:]
    depth = w_gates[0].shape[0]

    def body(ins, outs, scr):
        core = lax.rem(lax.axis_index('tp'), 2)
        copies = {}

        def load(key, src, dst):
            copies[key] = pltpu.make_async_copy(src, dst, scr['sem'].at[len(copies)])
            copies[key].start()

        load('m', ins['m'].at[core], scr['m'])
        load('g0', ins['g0'], scr['w'].at[0])
        load('u0', ins['u0'], scr['w'].at[1])
        load('dy', ins['dy'].at[core], scr['dy'])
        load('d0', ins['d0'], scr['w'].at[2])
        load('g1', ins['g1'], scr['w'].at[3])
        load('u1', ins['u1'], scr['w'].at[4])
        load('d1', ins['d1'], scr['w'].at[5])
        tile = min(256, seq)
        for index in range(2):
            for key in (('m', 'g0', 'u0', 'dy', 'd0') if index == 0 else ('g1', 'u1', 'd1')):
                copies[key].wait()

            def step(tile_index, carry, index=index):
                at = pl.ds(pl.multiple_of(tile_index * tile, tile), tile)
                mixed = scr['m'][at, :]
                gate = dot(mixed, scr['w'][3 * index], NT)
                upper = dot(mixed, scr['w'][3 * index + 1], NT)
                grad_act = dot(scr['dy'][at, :], scr['w'][3 * index + 2], NT)
                sigmoid_g = 1.0 / (1.0 + jnp.exp(-gate))
                silu_g = gate * sigmoid_g
                outs[f'a{index}'][at, :] = (silu_g * upper).astype(BF16)
                outs[f'dg{index}'][at, :] = (grad_act * upper * sigmoid_g * (1.0 + gate * (1.0 - sigmoid_g))).astype(BF16)
                outs[f'du{index}'][at, :] = (grad_act * silu_g).astype(BF16)
                return carry

            lax.fori_loop(0, seq // tile, step, 0)

    ins = {'m': (mixed_full, ANY), 'dy': (grad_out, ANY)}
    for index in range(2):
        ins[f'g{index}'] = (w_gates[index], ANY)
        ins[f'u{index}'] = (w_ups[index], ANY)
        ins[f'd{index}'] = (w_downs[index], ANY)
    outs = {f'{name}{index}': (shape((seq, depth)), VMEM) for index in range(2) for name in ('a', 'dg', 'du')}
    scratch = {'m': pltpu.VMEM((seq, width), BF16), 'dy': pltpu.VMEM((seq, width), BF16), 'w': pltpu.VMEM((6, depth, width), BF16), 'sem': pltpu.SemaphoreType.DMA((8,))}
    return call_kernel('mlp_grads', body, ins, outs, scratch, 58, 17e9)


def weight_grads_mlp(mixed_full, grad_out, resid_full, grads_gate, grads_up, acts, ctxs):
    seq, width = grad_out.shape[1:]
    depth, head = acts[0].shape[1], ctxs[0].shape[1]
    tile = min(512, width)

    def kernel(m_ref, dy_ref, dh_ref, *refs):
        sides = (refs[0:2], refs[2:4], refs[4:6], refs[6:8])
        out_gate, out_up, out_down, out_o, left = refs[8:]
        core = lax.rem(lax.axis_index('tp'), 2)

        @pl.when(pl.program_id(0) == 0)
        def _():
            base = 0
            for pair in sides:
                for half in range(2):
                    left[half, base:base + pair[half].shape[1], :] = pair[half][...].T
                base += pair[0].shape[1]

        def product(base, size, ref):
            return dot(left[0, base:base + size, :], ref[core], NN) + dot(left[1, base:base + size, :], ref[1 - core], NN)

        both = product(0, 2 * depth, m_ref)
        out_gate[...] = both[:depth]
        out_up[...] = both[depth:]
        out_down[...] = product(2 * depth, depth, dy_ref)
        out_o[...] = product(3 * depth, head, dh_ref)

    slab = pl.BlockSpec((2, seq, tile), lambda step: (0, 0, step))
    whole = pl.BlockSpec(memory_space=pltpu.VMEM)
    out = lambda size: pl.BlockSpec((size, tile), lambda step: (0, step))
    return pl.pallas_call(
        kernel,
        name='weight_grads_mlp',
        grid=(width // tile,),
        out_shape=[shape((depth, width), F32)] * 3 + [shape((head, width), F32)],
        in_specs=[slab] * 3 + [whole] * 8,
        out_specs=[out(depth)] * 3 + [out(head)],
        scratch_shapes=[pltpu.VMEM((2, 3 * depth + head, seq), BF16)],
        compiler_params=pltpu.CompilerParams(vmem_limit_bytes=56 * MIB),
        cost_estimate=pl.CostEstimate(flops=18_500_000_000, bytes_accessed=60_000_000, transcendentals=0),
    )(mixed_full, grad_out, resid_full, *grads_gate, *grads_up, *acts, *ctxs)


def weight_grads_qkv(normeds, kv_full, grads_q, kv_heads):
    seq, width = normeds[0].shape
    chips, tokens, pair = kv_full.shape[1:]
    head = pair // 2
    share = seq // tokens
    tile = min(256, width)
    kv_width = kv_heads * head

    def kernel(a_own, a_other, kv_ref, q_own, q_other, out_q, out_k, out_v, right, left):
        core = lax.rem(lax.axis_index('tp'), 2)

        @pl.when(pl.program_id(0) == 0)
        def _():
            for half, q_ref in enumerate((q_own, q_other)):
                right[half, :, 2 * kv_width:] = q_ref[...]
                batch = core if half == 0 else 1 - core
                for chip in range(chips):
                    at = pl.ds((chip % share) * tokens, tokens)
                    base = (chip // share) * head
                    right[half, at, base:base + head] = kv_ref[batch, chip, :, :head]
                    right[half, at, kv_width + base:kv_width + base + head] = kv_ref[batch, chip, :, head:]

        left[0] = a_own[...].T
        left[1] = a_other[...].T

        def product(base, size):
            return dot(left[0], right[0, :, base:base + size], NN) + dot(left[1], right[1, :, base:base + size], NN)

        out_k[...] = product(0, kv_width)
        out_v[...] = product(kv_width, kv_width)
        out_q[...] = product(2 * kv_width, head)

    whole = pl.BlockSpec(memory_space=pltpu.VMEM)
    slab = pl.BlockSpec((seq, tile), lambda step: (0, step))
    out = lambda size: pl.BlockSpec((tile, size), lambda step: (step, 0))
    return pl.pallas_call(
        kernel,
        name='weight_grads_qkv',
        grid=(width // tile,),
        out_shape=[shape((width, head), F32), shape((width, kv_width), F32), shape((width, kv_width), F32)],
        in_specs=[slab, slab, whole, whole, whole],
        out_specs=[out(head), out(kv_width), out(kv_width)],
        scratch_shapes=[pltpu.VMEM((2, seq, 2 * kv_width + head), BF16), pltpu.VMEM((2, tile, seq), BF16)],
        compiler_params=pltpu.CompilerParams(vmem_limit_bytes=56 * MIB),
        cost_estimate=pl.CostEstimate(flops=27_500_000_000, bytes_accessed=60_000_000, transcendentals=0),
    )(*normeds, kv_full, *grads_q)


def in_place(gathered, rows):
    blocks, _, width = gathered.shape
    slots = 8

    def kernel(src, dst, buf, in_sem, out_sem):
        def load(index):
            return pltpu.make_async_copy(src.at[index, pl.ds(0, rows), :], buf.at[index % slots], in_sem.at[index % slots])

        def store(index):
            return pltpu.make_async_copy(buf.at[index % slots], dst.at[index % 2, index // 2], out_sem.at[index % slots])

        ahead = slots // 2
        for index in range(blocks + ahead):
            if index < blocks:
                if index >= slots:
                    store(index - slots).wait()
                load(index).start()
            if index >= ahead:
                load(index - ahead).wait()
                store(index - ahead).start()
        for index in range(blocks - slots, blocks):
            store(index).wait()

    return pl.pallas_call(
        kernel,
        name='in_place',
        out_shape=shape((2, blocks // 2, rows, width)),
        in_specs=[ANY],
        out_specs=ANY,
        scratch_shapes=[pltpu.VMEM((slots, rows, width), BF16), pltpu.SemaphoreType.DMA((slots,)), pltpu.SemaphoreType.DMA((slots,))],
        compiler_params=pltpu.CompilerParams(vmem_limit_bytes=16 * MIB),
        cost_estimate=pl.CostEstimate(flops=20_000_000, bytes_accessed=25_000_000, transcendentals=0),
    )(gathered)


def solution(mesh):
    tp_size = mesh.shape['tp']
    chips = tp_size // 2
    side = math.isqrt(chips)
    swap_pairs = [(index, index ^ 1) for index in range(tp_size)]

    def device_step(hidden, seg_ids, grad_out, gain_attn, gain_mlp, w_q, w_k, w_v, w_o, w_gate, w_up, w_down):
        seq_len, width = hidden.shape[1:]
        kv_heads = w_k.shape[1] // HEAD_DIM
        per_kv = tp_size // kv_heads
        share = per_kv // 2
        rows = seq_len // chips
        tp_idx = lax.axis_index('tp')
        core = tp_idx % 2
        chip = tp_idx // 2
        kv_col = (tp_idx // per_kv) * HEAD_DIM
        scale = HEAD_DIM ** -0.5

        def swap(value):
            return lax.ppermute(value, 'tp', swap_pairs)

        def own_rows(value):
            return lax.dynamic_slice_in_dim(value, chip * rows, rows, axis=0)

        gain_attn_row = gain_attn[None, :]
        gain_mlp_row = gain_mlp[None, :]
        x_own = lax.dynamic_index_in_dim(hidden, core, 0, keepdims=False)
        dy_own = lax.dynamic_index_in_dim(grad_out, core, 0, keepdims=False)
        seg_own = lax.dynamic_index_in_dim(seg_ids, core, 0, keepdims=False)

        w_q_2 = swap(w_q)
        w_outs = (w_o, swap(w_o))
        w_gates = (w_gate.T, swap(w_gate.T))
        w_ups = (w_up.T, swap(w_up.T))
        w_downs = (w_down, swap(w_down))
        w_k_loc = lax.dynamic_slice_in_dim(w_k, kv_col, HEAD_DIM, axis=1)
        w_v_loc = lax.dynamic_slice_in_dim(w_v, kv_col, HEAD_DIM, axis=1)
        w_in = jnp.concatenate([w_q, w_q_2, w_k_loc, w_v_loc], axis=1)

        x_float = x_own.astype(F32)
        inv_own = lax.rsqrt(jnp.mean(x_float * x_float, axis=-1, keepdims=True) + EPS)
        normed_own = lax.optimization_barrier((x_float * inv_own * gain_attn).astype(BF16))
        qkv = dot(normed_own, w_in, NN).astype(BF16)
        queries = qkv[:, :2 * HEAD_DIM].reshape(seq_len, 2, HEAD_DIM)
        keys = qkv[:, 2 * HEAD_DIM:3 * HEAD_DIM]
        values = qkv[:, 3 * HEAD_DIM:]
        positions = jnp.arange(seq_len)
        allowed = (positions[:, None] >= positions[None, :]) & (seg_own[:, None] == seg_own[None, :])
        scores = jnp.einsum('qhd,kd->hqk', queries, keys, preferred_element_type=F32) * scale
        probs = jax.nn.softmax(jnp.where(allowed[None], scores, -1e30), axis=-1)
        probs_b = probs.astype(BF16)
        ctx = jnp.einsum('hqk,kd->qhd', probs_b, values, preferred_element_type=F32).astype(BF16).reshape(seq_len, 2 * HEAD_DIM)
        x_rows = own_rows(x_own)
        dy_rows = own_rows(dy_own)
        first = sum_attention(side, ctx, normed_own, w_outs, x_rows, gain_mlp_row)
        mixed_full = first['full'].reshape(2, seq_len, width)

        mlp = mlp_grads(mixed_full, grad_out, w_gates, w_ups, w_downs)
        second = sum_mlp(side, [mlp['dg0'], mlp['du0'], mlp['dg1'], mlp['du1']], [mlp['a0'], mlp['a1']], w_gates, w_ups, w_downs, first['h_rows'], dy_rows, gain_mlp_row)
        resid_own, resid_full = second['own'].reshape(seq_len, width), second['full'].reshape(2, seq_len, width)

        y_out = in_place(lax.all_gather(second['y_rows'], 'tp'), rows).reshape(2, seq_len, width)

        w_out = jnp.concatenate(w_outs, axis=0)
        grad_ctx = dot(resid_own, w_out, NT).astype(BF16).reshape(seq_len, 2, HEAD_DIM)
        grad_probs = jnp.einsum('qhd,kd->hqk', grad_ctx, values, preferred_element_type=F32)
        grad_v = jnp.einsum('hqk,qhd->kd', probs_b, grad_ctx, preferred_element_type=F32).astype(BF16)
        grad_scores = (probs * (grad_probs - jnp.sum(grad_probs * probs, axis=-1, keepdims=True)) * scale).astype(BF16)
        grad_q = jnp.einsum('hqk,kd->qhd', grad_scores, keys, preferred_element_type=F32).astype(BF16).reshape(seq_len, 2 * HEAD_DIM)
        grad_k = jnp.einsum('hqk,qhd->kd', grad_scores, queries, preferred_element_type=F32).astype(BF16)
        grad_kv = jnp.concatenate([grad_k, grad_v], axis=1)
        third = sum_input(side, jnp.concatenate([grad_q, grad_kv], axis=1), w_in, grad_kv.reshape(share, seq_len // share, 2 * HEAD_DIM), x_rows, second['d_rows'], gain_attn_row, second['gain'])

        gathered = lax.all_gather(third['rows'], 'tp')
        grad_in = in_place(gathered, rows).reshape(2, seq_len, width)
        gain_grads = jnp.sum(gathered[:, rows:].astype(F32), axis=0)
        grad_gain_attn = gain_grads[0] + gain_grads[1] + gain_grads[2]
        grad_gain_mlp = gain_grads[3] + gain_grads[4] + gain_grads[5]

        def flat(value):
            return value.reshape(seq_len, value.shape[-1])

        grad_gate_t, grad_up_t, grad_w_down, grad_w_o = weight_grads_mlp(
            mixed_full, grad_out, resid_full, (mlp['dg0'], flat(second['gate_other'])), (mlp['du0'], flat(second['up_other'])), (mlp['a0'], flat(second['act_other'])),
            (ctx[:, :HEAD_DIM], flat(first['ctx_other'])))
        kv_full = third['kv'].reshape(2, chips, seq_len // share, 2 * HEAD_DIM)
        grad_w_q, grad_w_k, grad_w_v = weight_grads_qkv((normed_own, first['normed_other']), kv_full, (grad_q[:, :HEAD_DIM], flat(third['q_other'])), kv_heads)
        return (y_out, grad_in, grad_gain_attn, grad_gain_mlp, grad_w_q, grad_w_k, grad_w_v, grad_w_o, grad_gate_t.T, grad_up_t.T, grad_w_down)

    spec_act = P('data', None, None)
    spec_rows = P('data', None)
    spec_gain = P(None)
    spec_cols = P(None, 'tp')
    spec_tprows = P('tp', None)
    spec_whole = P(None, None)
    spec_stack = P(('data', 'tp'), None)
    in_specs = (spec_act, spec_rows, spec_act, spec_gain, spec_gain, spec_cols, spec_whole, spec_whole, spec_tprows, spec_cols, spec_cols, spec_tprows)
    out_specs = (spec_act, spec_act, P('data'), P('data'), P('data', 'tp'), spec_rows, spec_rows, spec_stack, P('data', 'tp'), P('data', 'tp'), spec_stack)
    return jax.shard_map(device_step, mesh=mesh, in_specs=in_specs, out_specs=out_specs, check_vma=False)
```

time: 1210 us -> 520 us (0.43)
  waiting for transfers between devices: 744 us -> 0.16 us
  Pallas kernels: 0 us -> 400 us
  matrix products: 273 us -> 40.6 us
  other arithmetic: 129 us -> 20.6 us
    psum x6 -> x0, waiting for transfers between devices: 744 us -> none  [the longest x2 247 us: forward(): attn_out = lax.psum(attn_part, 'tp')]
    pallas_call x0 -> x8, Pallas kernels: none -> 400 us  [the longest x4 316 us: call_kernel(): pl.pallas_call(kernel, name=name, out_shape=[outs[key][0] for key in name...]
    dot_general x33 -> x7, matrix products: 273 us -> 35.5 us  [the longest x2 9.15 us: dot(): lax.dot_general(lhs, rhs, (dims, ((), ())), preferred_element_type=F32)]
    reduce_sum x8 -> x2, other arithmetic: 73.9 us -> 6.94 us  [the longest x1 4.07 us: device_step(): jnp.mean(x_float * x_float, axis=-1, keepdims=True) + EPS]
    convert_element_type x3 -> x1, other arithmetic: 54.4 us -> 8.22 us  [device_step(): (x_float * inv_own * gain_attn).astype(BF16)]
    another operation x2 -> x1, local copies, waits for them, and re-layouts: 16.6 us -> 0.25 us  [sum_attention(): ctx.reshape(side, side, rows, depth)]
    unnamed x96 -> x58, local copies, waits for them, and re-layouts: 24.9 us -> 25.5 us
  transfers between devices with their start and end apart: 6 -> 7, of which waited for: 6 -> 0; matrix products, arithmetic and copies ran while one was open for 10% -> 13% of each run, Pallas kernels for 0% -> 45%
where the time goes in v2:
time: 520 us; the launch traced here: 512 us
  Pallas kernels  400 us (77%)
  matrix products  40.6 us (8%)
  local copies, waits for them, and re-layouts  31.9 us (6%)
  other arithmetic  20.6 us (4%)
  between operations  15 us (3%)
    pallas_call x4, Pallas kernels, call_kernel(): pl.pallas_call(kernel, name=name, out_shape=[outs[key][0] for key in name...  316 us
    pallas_call x1, Pallas kernels, weight_grads_qkv(): pl.pallas_call(kernel, name='weight_grads_qkv', grid=(width // tile,), ou...  38.3 us
    pallas_call x1, Pallas kernels, weight_grads_mlp(): pl.pallas_call(kernel, name='weight_grads_mlp', grid=(width // tile,), ou...  28.9 us
    unnamed x58, local copies, waits for them, and re-layouts  25.5 us
    pallas_call x2, Pallas kernels, in_place(): pl.pallas_call(kernel, name='in_place', out_shape=shape((2, blocks // 2,...  16.8 us
  transfers between devices with their start and end apart: 7, of which 0 were waited for; matrix products, arithmetic and copies ran while one was open for 13% of the time, Pallas kernels for 45%

profile of v2, /device:TPU:97, one launch (start us, length us, event | category | flops | bytes accessed | tf_op | source)
XLA Modules:
  0.0 511.9 jit_solution(12475257703670486607)
XLA Ops:
  7.2 0.0 copy-start
  7.2 0.1 all-gather.5.cloned.1.call-start
  7.3 2.1 collective-permute-start
  9.4 0.1 collective-permute-start.1
  9.5 0.4 collective-permute-start.2
  9.9 0.1 collective-permute-start.3
  10.1 0.4 collective-permute-start.4
  10.4 4.1 fusion.2
  14.6 8.2 %fusion.4.refs_5_.a_own = bf16[768,4096]{1,0:T(8,128)(2,1)} fusion(f32[4096]{0:T(1024)S(1)} %copy-done.10, f32[768]{0:T(1024)S(1)} %add_rsqrt_fusion, bf16[2,768,4096]{2,1,0:T(8,128)(2,1)} %param.12, s32[]{:T(128)S(6)} %select_n.38), kind=kLoop, calls=%fused_computation.6 | loop fusion | flops 12582912 | bytes 12602372 | tf_op jit(solution)/shard_map/convert_element_type | solution.py:824
  22.8 1.2 dynamic-slice_bitcast_fusion.1.refs_3_
  24.0 1.9 dynamic-slice_bitcast_fusion.refs_13_
  25.9 0.4 fusion.11
  26.3 1.7 constant_dynamic-slice_fusion
  28.0 0.0 copy-start.16
  28.0 0.0 copy-start.17
  28.0 7.3 %convolution_convert_fusion = bf16[768,512]{0,1:T(8,128)(2,1)S(1)} fusion(bf16[768,4096]{1,0:T(8,128)(2,1)} %fusion.4.refs_5_.a_own, bf16[4096,128]{1,0:T(8,128)(2,1)S(1)} %get-tuple-element.71, bf16[4096,128]{1,0:T(8,128)(2,1)S(1)} %get-tuple-element.72, bf16[4096,128]{1,0:T(8,128)(2,1)} %collective-permute-done, bf16[4096,128]{1,0:T(8,128)(2,1)S(1)} %copy-done.18), kind=kOutput, calls=%fused_computation.30 | convolution fusion | flops 3238395904 | bytes 11272192 | tf_op jit(solution)/shard_map/dot_general | solution.py:21
  35.4 0.0 copy-start.21
  35.4 0.8 copy-done.21
  36.2 5.1 fusion.42
  41.3 3.0 convolution_convert_fusion.1
  44.4 0.7 copy-done.19
  45.1 0.6 copy.26
  45.7 0.3 reshape_reshape.3.refs_0_
  46.0 0.0 copy-start.3
  46.0 2.8 copy-done.3
  48.8 80.0 %sum_attention.1 = (bf16[2,4,4,48,4096]{4,3,2,1,0:T(8,128)(2,1)}, bf16[48,4096]{1,0:T(8,128)(2,1)S(1)}, bf16[4,4,48,128]{3,2,1,0:T(8,128)(2,1)S(1)}, bf16[768,4096]{1,0:T(8,128)(2,1)S(1)}) custom-call(bf16[4,4,48,256]{3,2,1,0:T(8,128)(2,1)S(1)} %reshape_reshape.3.refs_0_, bf16[128,4096]{1,0:T(8,128)(2,1)S(1)} %copy-done.6, ...), custom_call_target="tpu_custom_call" | custom-call | flops 400000000 | bytes 40000000 | tf_op jit(solution)/shard_map/sum_attention/pallas_call | solution.py:422
  128.9 0.7 copy-done.8
  129.6 2.7 copy-done.12
  132.3 0.7 copy-done.14
  133.0 30.8 %mlp_grads.1 = (bf16[768,448]{1,0:T(8,128)(2,1)}, bf16[768,448]{1,0:T(8,128)(2,1)}, bf16[768,448]{1,0:T(8,128)(2,1)}, bf16[768,448]{1,0:T(8,128)(2,1)}, bf16[768...) custom-call(bf16[2,768,4096]{2,1,0:T(8,128)(2,1)} %bitcast.159, bf16[2,768,4096]{2,1,0:T(8,128)(2,1)} %dy_ref.1, ...), custom_call_target="tpu_custom_call" | custom-call | flops 16999999488 | bytes 40000000 | tf_op jit(solution)/shard_map/mlp_grads/pallas_call | solution.py:422
  163.8 128.7 %sum_mlp.1 = (bf16[2,4,4,48,4096]{4,3,2,1,0:T(8,128)(2,1)}, bf16[4,4,48,4096]{3,2,1,0:T(8,128)(2,1)}, f32[48,4096]{1,0:T(8,128)}, f32[1,4096]{1,0:T(1,128)}, bf1...) custom-call(bf16[4,4,48,448]{3,2,1,0:T(8,128)(2,1)} %bitcast.146, ...), custom_call_target="tpu_custom_call" | custom-call | flops 600000000 | bytes 40000000 | tf_op jit(solution)/shard_map/sum_mlp/pallas_call | solution.py:422
  292.5 0.1 all-gather.5.cloned.1.call-update
  292.6 0.1 all-gather.7.cloned.1.call-start
  292.7 4.2 pad_maximum_fusion.refs_1_
  296.9 1.3 copy-done.27
  298.2 1.8 fusion.20
  300.1 0.0 copy-start.25
  300.1 0.7 copy-done.25
  300.8 3.0 fusion.33
  303.8 8.6 %fusion.23 = bf16[128,2,768]{2,0,1:T(8,128)(2,1)S(1)} fusion(f32[768,768,2]{1,0,2:T(8,128)} %fusion.33, bf16[768,512]{0,1:T(8,128)(2,1)S(1)} %copy-done.22, f32[2,768,768]{1,2,0:T(8,128)} %get-tuple-element.70, f32[2,768]{1,0:T(2,128)S(1)} %get-tuple-element.69), kind=kOutput, calls=%fused_computation.32 | convolution fusion | flops 310446336 | bytes 19476480 | tf_op jit(solution)/shard_map/hqk,kd->qhd/dot_general | solution.py:851
  312.4 0.4 copy.30
  312.9 0.3 concatenate.22
  313.1 0.0 copy-start.26
  313.2 8.4 %fusion.27 = bf16[768,128]{1,0:T(8,128)(2,1)S(1)} fusion(bf16[768,2,128]{0,2,1:T(8,128)(2,1)S(1)} %bitcast.154, f32[768,768,2]{1,0,2:T(8,128)} %fusion.33, f32[2,768,768]{1,2,0:T(8,128)} %get-tuple-element.70, f32[2,768]{1,0:T(2,128)S(1)} %get-tuple-element.69), kind=kOutput, calls=%fused_computation.38 | convolution fusion | flops 310348032 | bytes 10033152 | tf_op jit(solution)/shard_map/hqk,qhd->kd/dot_general | solution.py:852
  321.6 0.0 copy-start.4
  321.6 3.3 fusion.28
  325.0 0.1 pad_maximum_fusion.1.refs_0_
  325.1 0.1 copy-done.4
  325.2 0.2 copy-done.7
  325.4 76.9 %sum_input.1 = (bf16[64,4096]{1,0:T(8,128)(2,1)}, bf16[2,4,4,384,256]{4,3,2,1,0:T(8,128)(2,1)S(1)}, bf16[4,4,48,128]{3,2,1,0:T(8,128)(2,1)S(1)}) custom-call(bf16[4,4,48,512]{3,2,1,0:T(8,128)(2,1)S(1)} %pad_maximum_fusion.1.refs_0_, bf16[4096,512]{1,0:T(8,128)(2,1)S(1)} %copy-done.4, bf16[2,384,256]{2,1,0:T(8,128)(2,1)S(1)} %bitcast.126, ...), custom_call_target="tpu_custom_call" | custom-call | flops 300000000 | bytes 40000000 | tf_op jit(solution)/shard_map/sum_input/pallas_call | solution.py:422
  402.3 2.6 copy-done.13
  404.9 0.1 all-gather.7.cloned.1.call-update
  405.0 0.8 copy.48.refs_6_
  405.9 0.8 copy.47.q_own
  406.7 28.9 %weight_grads_mlp.1 = (f32[448,4096]{1,0:T(8,128)}, f32[448,4096]{1,0:T(8,128)}, f32[448,4096]{1,0:T(8,128)}, f32[128,4096]{1,0:T(8,128)}) custom-call(bf16[2,768,4096]{2,1,0:T(8,128)(2,1)} %bitcast.160, bf16[2,768,4096]{2,1,0:T(8,128)(2,1)} %dy_ref.1, bf16[2,768,4096]{2,1,0:T(8,128)(2,1)} %bitcast.161, bf16[768,448]{1,0:T(8,128)(2,1)} %get-tuple-element.40.refs_0_, ...), custom_call_target="tpu_custom_call" | custom-call | flops 18499999744 | bytes 60000000 | tf_op jit(solution)/shard_map/weight_grads_mlp/pallas_call | solution.py:687
  435.6 38.3 %weight_grads_qkv.1 = (f32[4096,128]{1,0:T(8,128)}, f32[4096,1024]{1,0:T(8,128)}, f32[4096,1024]{1,0:T(8,128)}) custom-call(bf16[768,4096]{1,0:T(8,128)(2,1)} %fusion.4.refs_5_.a_own, bf16[768,4096]{1,0:T(8,128)(2,1)} %copy-done.12, bf16[2,16,384,256]{3,2,1,0:T(8,128)(2,1)} %bitcast.130, bf16[768,128]{1,0:T(8,128)(2,1)} %copy.47.q_own, ...), custom_call_target="tpu_custom_call" | custom-call | flops 27499999232 | bytes 60000000 | tf_op jit(solution)/shard_map/weight_grads_qkv/pallas_call | solution.py:735
  473.8 0.0 all-gather.5.cloned.1.call-done
  473.9 4.6 copy-done.5
  478.4 8.4 %in_place.2 = bf16[2,16,48,4096]{3,2,1,0:T(8,128)(2,1)} custom-call(bf16[32,48,4096]{2,1,0:T(8,128)(2,1)S(1)} %bitcast.125), custom_call_target="tpu_custom_call" | custom-call | flops 20000000 | bytes 25000000 | tf_op jit(solution)/shard_map/in_place/pallas_call | solution.py:771
  486.9 0.0 all-gather.7.cloned.1.call-done
  486.9 5.8 %copy-done.2 = bf16[2048,4096]{1,0:T(8,128)(2,1)S(1)} copy-done((bf16[2048,4096]{1,0:T(8,128)(2,1)S(1)}, bf16[2048,4096]{1,0:T(8,128)(2,1)}, u32[]{:S(2)}) %copy-start.2) | copy-done | bytes 16777240
  492.7 8.4 %in_place.3 = bf16[2,16,48,4096]{3,2,1,0:T(8,128)(2,1)} custom-call(bf16[32,64,4096]{2,1,0:T(8,128)(2,1)S(1)} %bitcast.124), custom_call_target="tpu_custom_call" | custom-call | flops 20000000 | bytes 25000000 | tf_op jit(solution)/shard_map/in_place/pallas_call | solution.py:771
  501.1 2.9 convert_reduce_fusion
  504.0 0.7 slice_add_fusion
  (46 shorter events, 0.2 us)
Async XLA Ops:
  7.2 18.7 %copy-start = (s32[2,768]{1,0:T(2,128)S(1)}, s32[2,768]{1,0:T(2,128)}, u32[]{:S(2)}) copy-start(s32[2,768]{1,0:T(2,128)} %param.13) | copy-start | bytes 18436
  7.2 7.3 %copy-start.10 = (f32[4096]{0:T(1024)S(1)}, f32[4096]{0:T(1024)}, u32[]{:S(2)}) copy-start(f32[4096]{0:T(1024)} %param.15) | copy-start | bytes 49156
  7.2 466.6 %all-gather.5.cloned.1.call-start = ((), (), s32[]{:S(2)}) async-start(), calls=%async_computation | async-start | bytes 12976128 | tf_op jit(solution)/shard_map/all_gather | solution.py:844
  7.3 20.7 %collective-permute-start = (bf16[4096,128]{1,0:T(8,128)(2,1)}, bf16[4096,128]{1,0:T(8,128)(2,1)}, u32[]{:S(2)}, u32[]{:S(2)}) collective-permute-start(bf16[4096,128]{1,0:T(8,128)(2,1)} %param.17), channel_id=1, source_target_pairs={{0,1},{1,0},{2,3},{3,2},{4,5},{5,4},{6,7},{7,6},{8,9},{9,8},{10,11... | collective-permute-start | bytes 3145736 | tf_op jit(solution)/shard_map/ppermute | solution.py:802
  9.4 36.6 %collective-permute-start.1 = (bf16[128,4096]{1,0:T(8,128)(2,1)}, bf16[128,4096]{1,0:T(8,128)(2,1)S(1)}, u32[]{:S(2)}, u32[]{:S(2)}) collective-permute-start(bf16[128,4096]{1,0:T(8,128)(2,1)} %refs_1_.2), channel_id=1, source_target_pairs={{0,1},{1,0},{2,3},{3,2},{4,5},{5,4},{6,7},{7,6},{8,9},{9,8},{10,11... | collective-permute-start | bytes 3145736 | tf_op jit(solution)/shard_map/ppermute | solution.py:802
  9.5 123.4 %collective-permute-start.2 = (bf16[448,4096]{1,0:T(8,128)(2,1)}, bf16[448,4096]{1,0:T(8,128)(2,1)}, u32[]{:S(2)}, u32[]{:S(2)}) collective-permute-start(bf16[448,4096]{1,0:T(8,128)(2,1)} %bitcast.135), channel_id=1, source_target_pairs={{0,1},{1,0},{2,3},{3,2},{4,5},{5,4},{6,7},{7,6},{8,9},{9,8},{10,11... | collective-permute-start | bytes 11010056 | tf_op jit(solution)/shard_map/ppermute | solution.py:802
  9.9 123.1 %collective-permute-start.3 = (bf16[448,4096]{1,0:T(8,128)(2,1)}, bf16[448,4096]{1,0:T(8,128)(2,1)}, u32[]{:S(2)}, u32[]{:S(2)}) collective-permute-start(bf16[448,4096]{1,0:T(8,128)(2,1)} %bitcast.138), channel_id=1, source_target_pairs={{0,1},{1,0},{2,3},{3,2},{4,5},{5,4},{6,7},{7,6},{8,9},{9,8},{10,11... | collective-permute-start | bytes 11010056 | tf_op jit(solution)/shard_map/ppermute | solution.py:802
  10.1 122.9 %collective-permute-start.4 = (bf16[448,4096]{1,0:T(8,128)(2,1)}, bf16[448,4096]{1,0:T(8,128)(2,1)}, u32[]{:S(2)}, u32[]{:S(2)}) collective-permute-start(bf16[448,4096]{1,0:T(8,128)(2,1)} %refs_10_.1), channel_id=1, source_target_pairs={{0,1},{1,0},{2,3},{3,2},{4,5},{5,4},{6,7},{7,6},{8,9},{9,8},{10,11... | collective-permute-start | bytes 11010056 | tf_op jit(solution)/shard_map/ppermute | solution.py:802
  22.8 5.2 %copy-start.18 = (bf16[4096,128]{1,0:T(8,128)(2,1)S(1)}, bf16[4096,128]{1,0:T(8,128)(2,1)}, u32[]{:S(2)}) copy-start(bf16[4096,128]{1,0:T(8,128)(2,1)} %param.17) | copy-start | bytes 3145732
  28.0 7.4 %copy-start.16 = (bf16[4096,128]{1,0:T(8,128)(2,1)}, bf16[4096,128]{1,0:T(8,128)(2,1)S(1)}, u32[]{:S(2)}) copy-start(bf16[4096,128]{1,0:T(8,128)(2,1)S(1)} %get-tuple-element.71) | copy-start | bytes 3145732
  28.0 7.4 %copy-start.17 = (bf16[4096,128]{1,0:T(8,128)(2,1)}, bf16[4096,128]{1,0:T(8,128)(2,1)S(1)}, u32[]{:S(2)}) copy-start(bf16[4096,128]{1,0:T(8,128)(2,1)S(1)} %get-tuple-element.72) | copy-start | bytes 3145732
  35.4 0.9 copy-start.21
  36.2 5.1 copy-start.23
  41.3 4.7 copy-start.6
  41.3 4.7 copy-start.9
  44.4 0.8 copy-start.19
  46.0 2.8 copy-start.3
  128.9 0.7 copy-start.8
  129.6 2.7 copy-start.12
  132.3 0.7 copy-start.14
  292.6 194.3 %all-gather.7.cloned.1.call-start = ((), (), s32[]{:S(2)}) async-start(), calls=%async_computation.1 | async-start | bytes 17301504 | tf_op jit(solution)/shard_map/all_gather | solution.py:856
  292.6 5.6 %copy-start.27 = (bf16[4,4,48,4096]{3,2,1,0:T(8,128)(2,1)S(1)}, bf16[4,4,48,4096]{3,2,1,0:T(8,128)(2,1)}, u32[]{:S(2)}) copy-start(bf16[4,4,48,4096]{3,2,1,0:T(8,128)(2,1)} %get-tuple-element.48) | copy-start | bytes 18874372
  298.2 2.6 copy-start.22
  300.1 0.7 copy-start.25
  303.8 9.3 %copy-start.24 = (bf16[768,256]{0,1:T(8,128)(2,1)S(1)}, bf16[768,256]{0,1:T(8,128)(2,1)}, u32[]{:S(2)}) copy-start(bf16[768,256]{0,1:T(8,128)(2,1)} %copy-done.23) | copy-start | bytes 1179652
  313.1 8.4 %copy-start.26 = (bf16[768,256]{0,1:T(8,128)(2,1)S(1)}, bf16[768,256]{0,1:T(8,128)(2,1)}, u32[]{:S(2)}) copy-start(bf16[768,256]{0,1:T(8,128)(2,1)} %copy-done.25) | copy-start | bytes 1179652
  321.6 3.6 copy-start.4
  321.6 3.8 copy-start.7
  321.6 3.8 copy-start.11
  324.9 80.1 %copy-start.20 = (bf16[128,2,768]{2,0,1:T(8,128)(2,1)S(1)}, bf16[128,2,768]{2,0,1:T(8,128)(2,1)}, u32[]{:S(2)}) copy-start(bf16[128,2,768]{2,0,1:T(8,128)(2,1)} %copy-done.19) | copy-start | bytes 1179652
  402.3 2.6 copy-start.13
  404.9 30.6 %copy-start.15 = (bf16[4,4,48,128]{3,2,1,0:T(8,128)(2,1)}, bf16[4,4,48,128]{3,2,1,0:T(8,128)(2,1)S(1)}, u32[]{:S(2)}) copy-start(bf16[4,4,48,128]{3,2,1,0:T(8,128)(2,1)S(1)} %get-tuple-element.54) | copy-start | bytes 589828
  473.9 4.6 copy-start.5
  486.9 5.8 %copy-start.2 = (bf16[2048,4096]{1,0:T(8,128)(2,1)S(1)}, bf16[2048,4096]{1,0:T(8,128)(2,1)}, u32[]{:S(2)}) copy-start(bf16[2048,4096]{1,0:T(8,128)(2,1)} %all-gather.7.cloned.1.call-done) | copy-start | bytes 50331652
  492.7 12.0 %copy-start.1 = (s32[2,768]{1,0:T(2,128)S(1)}, s32[2,768]{1,0:T(2,128)}, u32[]{:S(2)}) copy-start(s32[2,768]{1,0:T(2,128)} %param.13) | copy-start | bytes 18436
Sparse Core Ops, SparseCore 0:
  292.7 70.0 all-gather.4
  405.1 68.0 all-gather.6

commit v3 on v2

v3 whole, which is shorter than its diff:
```python
import functools
import math
import types
import jax
import jax.numpy as jnp
from jax import lax
from jax.experimental import pallas as pl
from jax.experimental.pallas import tpu as pltpu
from jax.sharding import PartitionSpec as P

HEAD_DIM = 128
EPS = 1e-5
MESH = pl.DeviceIdType.MESH
F32 = jnp.float32
BF16 = jnp.bfloat16
MIB = 2 ** 20
ANY = pl.BlockSpec(memory_space=pl.ANY)
VMEM = pl.BlockSpec(memory_space=pltpu.VMEM)


def dot(lhs, rhs, dims):
    return lax.dot_general(lhs, rhs, (dims, ((), ())), preferred_element_type=F32)


NN = ((1,), (0,))
NT = ((1,), (1,))


SIGNS = (1, -1)


class Colour:
    def __init__(self, index, first, second):
        self.index, self.first, self.second = index, first, second


class Torus:
    def __init__(self, side):
        self.side = side
        tp_idx = lax.axis_index('tp')
        self.core = lax.rem(tp_idx, 2)
        self.chip = lax.div(tp_idx, 2)
        self.x = lax.rem(self.chip, side)
        self.y = lax.div(self.chip, side)
        self.partner = {'tp': self.chip * 2 + (1 - self.core)}
        self.colours = (Colour(0, self.x, self.y), Colour(1, self.y, self.x))
        self.pending = []

    def wrap(self, pos):
        return lax.rem(pos + 2 * self.side, self.side)

    def at_chip(self, y_at, x_at):
        return {'tp': (y_at * self.side + x_at) * 2 + self.core}

    def block(self, col, second, first):
        return (second, first) if col.index == 0 else (first, second)

    def peer1(self, col, shift):
        return self.at_chip(*self.block(col, col.second, self.wrap(col.first + shift)))

    def peer2(self, col, shift):
        return self.at_chip(*self.block(col, self.wrap(col.second + shift), col.first))

    def signal_all(self):
        barrier = pltpu.get_barrier_semaphore()
        peers = [self.partner]
        peers += [self.at_chip(self.y, self.wrap(self.x + shift)) for shift in SIGNS]
        peers += [self.at_chip(self.wrap(self.y + shift), self.x) for shift in SIGNS]
        for peer in peers:
            pl.semaphore_signal(barrier, inc=1, device_id=peer, device_id_type=MESH)
        return lambda: pl.semaphore_wait(barrier, len(peers))

    def send(self, src, dst, sems, index, device):
        copy = pltpu.make_async_remote_copy(src, dst, sems[0].at[index], sems[1].at[index], device_id=device, device_id_type=MESH)
        copy.start()
        self.pending.append(copy)

    def arrive(self, dst, sems, index):
        pltpu.make_async_remote_copy(dst, dst, sems[0].at[index], sems[1].at[index], device_id=self.partner, device_id_type=MESH).wait_recv()

    def drain(self):
        for copy in self.pending:
            copy.wait_send()


R1, R2, R3, S1, S2, S3 = range(6)
RS_COUNTS = (16, 16, 16, 4, 4, 4)
H1, H2, F1, F2 = range(4)
AG_COUNTS = (8, 32, 4, 16)


class ReduceScatter:
    SHIFTS = (2, 1, 3, 0)

    def __init__(self, torus, scr):
        self.torus, self.part, self.scr = torus, scr.part, scr
        self.quarter = scr.part.shape[3] // 4

    def buf(self, kind, index):
        return self.scr.bufs[kind].at[index]

    def sems(self, kind):
        return self.scr.out_sems[kind], self.scr.in_sems[kind]

    def cols(self, col, half):
        return pl.ds((col.index * 2 + half) * self.quarter, self.quarter)

    def piece(self, where, at_cols):
        return self.part.at[(*where, slice(None), at_cols)]

    def send(self, where, at_cols, kind, index, peer):
        self.torus.send(self.piece(where, at_cols), self.buf(kind, index), self.sems(kind), index, peer)

    def add(self, where, at_cols, *kinds):
        total = self.part[(*where, slice(None), at_cols)].astype(F32)
        for kind, index in kinds:
            self.torus.arrive(self.buf(kind, index), self.sems(kind), index)
            total = total + self.buf(kind, index)[...].astype(F32)
        self.part[(*where, slice(None), at_cols)] = total.astype(BF16)

    def each(self, step):
        wrap = self.torus.wrap
        for col in self.torus.colours:
            second = wrap(col.second + self.SHIFTS[step])
            for way, sign in enumerate(SIGNS):
                yield col, second, way, sign, (col.index * 2 + way) * 4 + step

    def far(self, step):
        for col, second, way, sign, index in self.each(step):
            where = self.torus.block(col, second, self.torus.wrap(col.first + 2))
            self.send(where, self.cols(col, way), R1, index, self.torus.peer1(col, sign))

    def near(self, step):
        for col, second, way, sign, index in self.each(step):
            where = self.torus.block(col, second, self.torus.wrap(col.first + sign))
            self.send(where, self.cols(col, 1 - way), R2, index, self.torus.peer1(col, sign))

    def relay(self, step):
        for col, second, way, sign, index in self.each(step):
            where = self.torus.block(col, second, self.torus.wrap(col.first + sign))
            self.add(where, self.cols(col, way), (R1, index))
            self.send(where, self.cols(col, way), R3, index, self.torus.peer1(col, sign))

    def end(self, step):
        for col, second, way, sign, index in self.each(step):
            where = self.torus.block(col, second, col.first)
            other = (col.index * 2 + 1 - way) * 4 + step
            self.add(where, self.cols(col, way), (R2, other), (R3, index))

    def far2(self):
        for col in self.torus.colours:
            for way, sign in enumerate(SIGNS):
                where = self.torus.block(col, self.torus.wrap(col.second + 2), col.first)
                self.send(where, self.cols(col, way), S1, col.index * 2 + way, self.torus.peer2(col, sign))

    def near2(self, way):
        for col in self.torus.colours:
            where = self.torus.block(col, self.torus.wrap(col.second + SIGNS[way]), col.first)
            self.send(where, self.cols(col, 1 - way), S2, col.index * 2 + way, self.torus.peer2(col, SIGNS[way]))

    def relay2(self, way):
        for col in self.torus.colours:
            index = col.index * 2 + way
            where = self.torus.block(col, self.torus.wrap(col.second + SIGNS[way]), col.first)
            self.add(where, self.cols(col, way), (S1, index))
            self.send(where, self.cols(col, way), S3, index, self.torus.peer2(col, SIGNS[way]))

    def end2(self):
        for col in self.torus.colours:
            where = self.torus.block(col, col.second, col.first)
            for way in range(2):
                self.add(where, self.cols(col, way), (S2, col.index * 2 + 1 - way), (S3, col.index * 2 + way))

    def steps(self, fill):
        call = functools.partial
        return [call(fill, 2), call(self.far, 0), call(self.far, 1), call(fill, 1), call(fill, 3),
                call(self.near, 0), call(self.relay, 0), call(self.near, 1), call(self.far, 2), call(self.relay, 1),
                call(fill, 0), call(self.near, 2), call(self.far, 3), call(self.end, 0), call(self.far2),
                call(self.relay, 2), call(self.near, 3), call(self.end, 1), call(self.near2, 0), call(self.relay2, 0),
                call(self.relay, 3), call(self.end, 2), call(self.near2, 1), call(self.relay2, 1), call(self.end, 3),
                call(self.end2)]


class AllGather:
    def __init__(self, torus, scr, by_rows, keep):
        self.torus, self.gat, self.scr, self.by_rows, self.keep_piece = torus, scr.gat, scr, by_rows, keep
        self.quarter = scr.gat.shape[2 if by_rows else 3] // 4
        self.back = (0, torus.side - 1, 1, 2)

    def sems(self, kind):
        return self.scr.out_sems[kind], self.scr.in_sems[kind]

    def piece(self, ref, where, first, count):
        at = pl.ds(first * self.quarter, count * self.quarter)
        return ref.at[(*where, at, slice(None))] if self.by_rows else ref.at[(*where, slice(None), at)]

    def half(self, col, where, half):
        return self.piece(self.gat, where, col.index * 2 + half, 1)

    def own2(self, turn):
        for col in self.torus.colours:
            where = self.torus.block(col, col.second, col.first)
            for way, sign in enumerate(SIGNS):
                at = self.half(col, where, way if turn == 0 else 1 - way)
                self.torus.send(at, at, self.sems(H1), (col.index * 2 + way) * 2 + turn, self.torus.peer2(col, sign))

    def send1(self, step, turn):
        for col in self.torus.colours:
            where = self.torus.block(col, self.torus.wrap(col.second + self.back[step]), col.first)
            for way, sign in enumerate(SIGNS):
                at = self.half(col, where, way if turn == 0 else 1 - way)
                self.torus.send(at, at, self.sems(H2), ((col.index * 2 + way) * 4 + step) * 2 + turn, self.torus.peer1(col, sign))

    def arrive2(self, way, turn):
        sign = SIGNS[way]
        for col in self.torus.colours:
            where = self.torus.block(col, self.torus.wrap(col.second - sign), col.first)
            at = self.half(col, where, way if turn == 0 else 1 - way)
            self.torus.arrive(at, self.sems(H1), (col.index * 2 + way) * 2 + turn)
            if turn == 0:
                self.torus.send(at, at, self.sems(F1), col.index * 2 + way, self.torus.peer2(col, sign))

    def relayed2(self):
        for col in self.torus.colours:
            where = self.torus.block(col, self.torus.wrap(col.second + 2), col.first)
            for way in range(2):
                self.torus.arrive(self.half(col, where, way), self.sems(F1), col.index * 2 + way)

    def arrive1(self, step, turn):
        for col in self.torus.colours:
            second = self.torus.wrap(col.second + self.back[step])
            for way, sign in enumerate(SIGNS):
                where = self.torus.block(col, second, self.torus.wrap(col.first - sign))
                at = self.half(col, where, way if turn == 0 else 1 - way)
                self.torus.arrive(at, self.sems(H2), ((col.index * 2 + way) * 4 + step) * 2 + turn)
                if turn == 0:
                    self.torus.send(at, at, self.sems(F2), (col.index * 2 + way) * 4 + step, self.torus.peer1(col, sign))

    def relayed1(self, step):
        for col in self.torus.colours:
            second = self.torus.wrap(col.second + self.back[step])
            for way in range(2):
                where = self.torus.block(col, second, self.torus.wrap(col.first + 2))
                self.torus.arrive(self.half(col, where, way), self.sems(F2), (col.index * 2 + way) * 4 + step)

    def keep(self, step, firsts):
        for col in self.torus.colours:
            for shift in firsts:
                where = self.torus.block(col, self.torus.wrap(col.second + self.back[step]), self.torus.wrap(col.first + shift))
                slot = (col.index * self.torus.side + where[0]) * self.torus.side + where[1]
                self.keep_piece(slot, lambda ref, where=where, col=col: self.piece(ref, where, col.index * 2, 2))

    def steps(self):
        call = functools.partial
        beside = (1, self.torus.side - 1)
        return [call(self.own2, 0), call(self.send1, 0, 0), call(self.own2, 1), call(self.send1, 0, 1), call(self.keep, 0, (0,)),
                call(self.arrive2, 0, 0), call(self.arrive2, 1, 0), call(self.arrive2, 0, 1), call(self.send1, 1, 0), call(self.send1, 1, 1),
                call(self.arrive2, 1, 1), call(self.send1, 2, 0), call(self.send1, 2, 1), call(self.keep, 1, (0,)), call(self.keep, 2, (0,)),
                call(self.arrive1, 0, 0), call(self.relayed2), call(self.send1, 3, 0), call(self.send1, 3, 1), call(self.keep, 3, (0,)),
                call(self.arrive1, 0, 1), call(self.keep, 0, beside), call(self.arrive1, 1, 0), call(self.arrive1, 2, 0),
                call(self.relayed1, 0), call(self.keep, 0, (2,)), call(self.arrive1, 1, 1), call(self.keep, 1, beside),
                call(self.arrive1, 2, 1), call(self.keep, 2, beside), call(self.arrive1, 3, 0), call(self.relayed1, 1), call(self.keep, 1, (2,)),
                call(self.relayed1, 2), call(self.keep, 2, (2,)), call(self.arrive1, 3, 1), call(self.keep, 3, beside),
                call(self.relayed1, 3), call(self.keep, 3, (2,))]


class Store:
    def __init__(self, torus, full, scr, own=None):
        self.torus, self.full, self.scr, self.own = torus, full, scr, own
        self.stores = []

    def keep(self, slot, piece):
        pairs = [(self.scr.full_sem, self.full.at[self.torus.core])]
        if self.own is not None:
            pairs.append((self.scr.own_sem, self.own))
        for sem, ref in pairs:
            store = pltpu.make_async_copy(piece(self.scr.gat), piece(ref), sem.at[slot])
            store.start()
            self.stores.append(store)
        self.torus.send(piece(self.scr.gat), piece(self.full.at[self.torus.core]), self.scr.cross_sems, slot, self.torus.partner)

    def drain(self, gather):
        for store in self.stores:
            store.wait()
        side = self.torus.side
        for colour in range(2):
            for y_at in range(side):
                for x_at in range(side):
                    target = gather.piece(self.full.at[1 - self.torus.core], (y_at, x_at), colour * 2, 2)
                    self.torus.arrive(target, self.scr.cross_sems, (colour * side + y_at) * side + x_at)


def rs_scratch(side, rows, width):
    dma = pltpu.SemaphoreType.DMA
    return dict(
        part=pltpu.VMEM((side, side, rows, width), BF16),
        bufs=[pltpu.VMEM((count, rows, width // 4), BF16) for count in RS_COUNTS],
        out_sems=[dma((count,)) for count in RS_COUNTS],
        in_sems=[dma((count,)) for count in RS_COUNTS],
    )


def ag_scratch(side, rows, width):
    dma = pltpu.SemaphoreType.DMA
    blocks = 2 * side * side
    return dict(
        gat=pltpu.VMEM((side, side, rows, width), BF16),
        out_sems=[dma((count,)) for count in AG_COUNTS],
        in_sems=[dma((count,)) for count in AG_COUNTS],
        full_sem=dma((blocks,)),
        own_sem=dma((blocks,)),
        cross_sems=[dma((blocks,)), dma((blocks,))],
    )


class Weights:
    def __init__(self, refs, buf, sem, by_rows):
        self.refs, self.buf, self.sem, self.by_rows = refs, buf, sem, by_rows
        self.copies = [[], []]

    def start(self):
        for colour in range(2):
            for index, ref in enumerate(self.refs):
                if self.by_rows:
                    half, depth = ref.shape[0] // 2, ref.shape[1]
                    rows, cols = pl.ds(colour * half, half), pl.ds(index * depth, depth)
                    copy = pltpu.make_async_copy(ref.at[rows, :], self.buf.at[rows, cols], self.sem.at[colour, index])
                else:
                    half, depth = ref.shape[1] // 2, ref.shape[0]
                    rows, cols = pl.ds(index * depth, depth), pl.ds(colour * half, half)
                    copy = pltpu.make_async_copy(ref.at[:, cols], self.buf.at[rows, cols], self.sem.at[colour, index])
                copy.start()
                self.copies[colour].append(copy)

    def wait(self, colour):
        for copy in self.copies[colour]:
            copy.wait()
        self.copies[colour] = []


def fill_partial(torus, part, lhs, weights):
    rows, width = part.shape[2:]
    tile = min(512, width // 2)

    def fill(shift):
        for col in torus.colours:
            weights.wait(col.index)
            first = torus.wrap(col.first + shift)
            left = []
            for ref in lhs:
                depth = ref.shape[3]
                value = ref[:, first] if col.index == 0 else ref[first]
                left.append((value.reshape(torus.side * rows, depth), depth))

            def body(step, carry, col=col, first=first, left=left):
                at = pl.ds(pl.multiple_of(col.index * (width // 2) + step * tile, tile), tile)
                total = None
                base = 0
                for value, depth in left:
                    if weights.by_rows:
                        term = dot(value, weights.buf[at, base:base + depth], NT)
                    else:
                        term = dot(value, weights.buf[base:base + depth, at], NN)
                    total = term if total is None else total + term
                    base += depth
                total = total.astype(BF16).reshape(torus.side, rows, tile)
                if col.index == 0:
                    part[:, first, :, at] = total
                else:
                    part[first, :, :, at] = total
                return carry

            lax.fori_loop(0, (width // 2) // tile, body, 0)

    return fill


def run(*lists):
    keyed = []
    for order, steps in enumerate(lists):
        keyed += [((index + 0.5) / len(steps), order, step) for index, step in enumerate(steps)]
    for _, _, step in sorted(keyed, key=lambda item: item[:2]):
        step()


def swap_start(torus, sems, pairs):
    for index, (src, dst) in enumerate(pairs):
        torus.send(src, dst, sems, index, torus.partner)


def swap_end(torus, sems, pairs):
    for index, (_, dst) in enumerate(pairs):
        torus.arrive(dst, sems, index)


def row_tiles(rows):
    return [pl.ds(start, 16) for start in range(0, rows, 16)]


def rms_back(z_in, gain, grad):
    inv = lax.rsqrt(jnp.mean(z_in * z_in, axis=-1, keepdims=True) + EPS)
    normed = z_in * inv
    scaled = grad * gain
    back = inv * (scaled - normed * jnp.mean(scaled * normed, axis=-1, keepdims=True))
    return back, jnp.sum(grad * normed, axis=0, keepdims=True)


def bag(tree):
    if isinstance(tree, dict):
        return types.SimpleNamespace(**{key: bag(value) for key, value in tree.items()})
    return [bag(value) for value in tree] if isinstance(tree, list) else tree


def call_kernel(name, body, ins, outs, scratch, flops, collective_id=None):
    is_leaf = lambda value: isinstance(value, tuple)
    in_leaves, in_tree = jax.tree.flatten(ins, is_leaf=is_leaf)
    out_leaves, out_tree = jax.tree.flatten(outs, is_leaf=is_leaf)
    scr_leaves, scr_tree = jax.tree.flatten(scratch)
    first_scr = len(in_leaves) + len(out_leaves)

    def kernel(*refs):
        body(bag(in_tree.unflatten(refs[:len(in_leaves)])), bag(out_tree.unflatten(refs[len(in_leaves):first_scr])), bag(scr_tree.unflatten(refs[first_scr:])))

    results = pl.pallas_call(
        kernel,
        name=name,
        out_shape=[leaf[0] for leaf in out_leaves],
        in_specs=[leaf[1] for leaf in in_leaves],
        out_specs=[leaf[1] for leaf in out_leaves],
        scratch_shapes=scr_leaves,
        compiler_params=pltpu.CompilerParams(collective_id=collective_id, has_side_effects=collective_id is not None, vmem_limit_bytes=60 * MIB),
        cost_estimate=pl.CostEstimate(flops=int(flops), bytes_accessed=40_000_000, transcendentals=0),
    )(*[leaf[0] for leaf in in_leaves])
    return bag(out_tree.unflatten(results))


def shape(dims, dtype=BF16):
    return jax.ShapeDtypeStruct(dims, dtype)


def sum_attention(side, ctx, normed, w_out, x_rows, gain):
    seq, depth = ctx.shape
    width = gain.shape[1]
    rows = seq // (side * side)

    def body(ins, outs, scr):
        torus = Torus(side)
        weights = Weights(ins.w_out, scr.w, scr.w_sem, False)
        weights.start()
        wait = torus.signal_all()
        part = scr.sum.part
        steps = ReduceScatter(torus, scr.sum).steps(fill_partial(torus, part, [ins.ctx], weights))
        steps[0]()
        wait()
        swaps = [(ins.ctx.at[:, :, :, pl.ds(depth // 2, depth // 2)], outs.ctx_other), (ins.normed, outs.normed_other)]
        swap_start(torus, scr.swap_sems, swaps)
        run(steps[1:])
        gat = scr.all.gat
        own = (torus.y, torus.x)
        for at in row_tiles(rows):
            resid = (ins.x_rows[at, :].astype(F32) + part[(*own, at, slice(None))].astype(F32)).astype(BF16)
            outs.h_rows[at, :] = resid
            z_in = resid.astype(F32)
            inv = lax.rsqrt(jnp.mean(z_in * z_in, axis=-1, keepdims=True) + EPS)
            gat[(*own, at, slice(None))] = (z_in * inv * ins.gain[...]).astype(BF16)
        store = Store(torus, outs.full, scr.all)
        gather = AllGather(torus, scr.all, False, store.keep)
        run(gather.steps())
        store.drain(gather)
        swap_end(torus, scr.swap_sems, swaps)
        torus.drain()

    dma = pltpu.SemaphoreType.DMA
    ins = dict(ctx=(ctx.reshape(side, side, rows, depth), VMEM), w_out=[(weight, ANY) for weight in w_out], x_rows=(x_rows, VMEM), gain=(gain, VMEM), normed=(normed, ANY))
    outs = dict(full=(shape((2, side, side, rows, width)), ANY), h_rows=(shape((rows, width)), VMEM), ctx_other=(shape((side, side, rows, depth // 2)), ANY), normed_other=(shape((seq, width)), ANY))
    scratch = dict(sum=rs_scratch(side, rows, width), all=ag_scratch(side, rows, width), w=pltpu.VMEM((depth, width), BF16), w_sem=dma((2, 2)), swap_sems=[dma((2,)), dma((2,))])
    return call_kernel('sum_attention', body, ins, outs, scratch, 4e8, 1)


def sum_mlp(side, grads, acts, w_gates, w_ups, w_downs, h_rows, dy_rows, gain):
    seq, depth = grads[0].shape
    width = gain.shape[1]
    rows = seq // (side * side)
    block = (side, side, rows, width)

    def body(ins, outs, scr):
        torus = Torus(side)
        weights = Weights(ins.w_in, scr.w, scr.w_sem, False)
        weights.start()
        weights_p = Weights(ins.w_downs, scr.wd, scr.wd_sem, False)
        weights_p.start()
        wait = torus.signal_all()
        steps = ReduceScatter(torus, scr.sum).steps(fill_partial(torus, scr.sum.part, ins.grads, weights))
        steps_p = ReduceScatter(torus, scr.sum_p).steps(fill_partial(torus, scr.sum_p.part, ins.acts, weights_p))
        steps[0]()
        wait()
        swaps = [(ins.grads[2], outs.gate_other), (ins.grads[3], outs.up_other), (ins.acts[1], outs.act_other)]
        swap_start(torus, scr.swap_sems, swaps)
        early = [steps_p[0], steps_p[3], steps_p[4], steps_p[10]]
        rest_p = [step for index, step in enumerate(steps_p) if index not in (0, 3, 4, 10)]
        run(steps[1:22], early)
        for step in rest_p[:3]:
            step()
        run(steps[22:])
        own = (torus.y, torus.x)
        gain_total = jnp.zeros((1, width), F32)
        gat = scr.all.gat
        for at in row_tiles(rows):
            back, gain_part = rms_back(ins.h_rows[at, :].astype(F32), ins.gain[...], scr.sum.part[(*own, at, slice(None))].astype(F32))
            gain_total = gain_total + gain_part
            total = ins.dy_rows[at, :].astype(F32) + back
            outs.d_rows[at, :] = total
            gat[(*own, at, slice(None))] = total.astype(BF16)
        outs.gain[...] = gain_total
        store = Store(torus, outs.full, scr.all, outs.own)
        gather = AllGather(torus, scr.all, False, store.keep)
        run(gather.steps(), rest_p[3:])
        for at in row_tiles(rows):
            outs.y_rows[at, :] = (ins.h_rows[at, :].astype(F32) + scr.sum_p.part[(*own, at, slice(None))].astype(F32)).astype(BF16)
        store.drain(gather)
        swap_end(torus, scr.swap_sems, swaps)
        torus.drain()

    blocked = lambda value: (value.reshape(side, side, rows, depth), VMEM)
    dma = pltpu.SemaphoreType.DMA
    ins = dict(grads=[blocked(grad) for grad in grads], acts=[blocked(act) for act in acts], w_in=[(weight, ANY) for weight in (w_gates[0], w_ups[0], w_gates[1], w_ups[1])],
               w_downs=[(weight, ANY) for weight in w_downs], h_rows=(h_rows, VMEM), dy_rows=(dy_rows, VMEM), gain=(gain, VMEM))
    other = (shape((side, side, rows, depth)), ANY)
    outs = dict(full=(shape((2, *block)), ANY), own=(shape(block), ANY), d_rows=(shape((rows, width), F32), VMEM), gain=(shape((1, width), F32), VMEM), y_rows=(shape((rows, width)), VMEM),
                gate_other=other, up_other=other, act_other=other)
    scratch = dict(sum=rs_scratch(side, rows, width), sum_p=rs_scratch(side, rows, width), all=ag_scratch(side, rows, width),
                   w=pltpu.VMEM((4 * depth, width), BF16), w_sem=dma((2, 4)), wd=pltpu.VMEM((2 * depth, width), BF16), wd_sem=dma((2, 2)), swap_sems=[dma((3,)), dma((3,))])
    return call_kernel('sum_mlp', body, ins, outs, scratch, 6e8, 2)


def sum_input(side, dqkv, w_qs, w_k, w_v, x_rows, d_rows, gain, gain_mlp_part):
    seq, depth = dqkv.shape
    width = gain.shape[1]
    rows = seq // (side * side)
    head = depth // 4
    half_side = side // 2
    tokens = seq // 2
    per_kv = 2 * side * side // (w_k.shape[1] // head)

    def body(ins, outs, scr):
        torus = Torus(side)
        kv_col = pl.multiple_of(lax.div(torus.chip * 2, per_kv) * head, head)
        weights = Weights([*ins.w_qs, ins.w_k.at[:, pl.ds(kv_col, head)], ins.w_v.at[:, pl.ds(kv_col, head)]], scr.w, scr.w_sem, True)
        weights.start()
        wait = torus.signal_all()
        part = scr.sum.part
        steps = ReduceScatter(torus, scr.sum).steps(fill_partial(torus, part, [ins.dqkv], weights))
        own = (torus.y, torus.x)
        gat = scr.all.gat
        store = Store(torus, outs.kv, scr.all)
        gather = AllGather(torus, scr.all, True, store.keep)
        place = lax.rem(torus.x, 2)
        mate = torus.at_chip(torus.y, torus.x + 1 - 2 * place)
        kv_cols = pl.ds(2 * head, 2 * head)

        def mate_add():
            torus.arrive(scr.mate, scr.mate_sems, 0)
            mine = ins.dqkv[pl.ds(place * half_side, half_side), :, :, kv_cols]
            gat[own] = (mine.astype(F32) + scr.mate[...].astype(F32)).astype(BF16).reshape(tokens, 2 * head)

        steps[0]()
        wait()
        swaps = [(ins.dqkv.at[:, :, :, pl.ds(head, head)], outs.q_other)]
        swap_start(torus, scr.swap_sems, swaps)
        torus.send(ins.dqkv.at[pl.ds((1 - place) * half_side, half_side), :, :, kv_cols], scr.mate, scr.mate_sems, 0, mate)
        for step in steps[1:5]:
            step()
        mate_add()
        run(steps[5:], gather.steps())
        gain_total = jnp.zeros((1, width), F32)
        for at in row_tiles(rows):
            back, gain_part = rms_back(ins.x_rows[at, :].astype(F32), ins.gain[...], part[(*own, at, slice(None))].astype(F32))
            gain_total = gain_total + gain_part
            outs.rows[at, :] = (ins.d_rows[at, :] + back).astype(BF16)
        row = lax.broadcasted_iota(jnp.int32, (8, width), 0)
        extra = jnp.zeros((8, width), F32)
        for index, value in enumerate((gain_total, ins.gain_mlp[...])):
            for level in range(3):
                rounded = value.astype(BF16).astype(F32)
                extra = jnp.where(row == index * 3 + level, rounded, extra)
                value = value - rounded
        outs.rows[rows:rows + 8, :] = extra.astype(BF16)
        store.drain(gather)
        swap_end(torus, scr.swap_sems, swaps)
        torus.drain()

    dma = pltpu.SemaphoreType.DMA
    ins = dict(dqkv=(dqkv.reshape(side, side, rows, depth), VMEM), w_qs=[(weight, ANY) for weight in w_qs], w_k=(w_k, ANY), w_v=(w_v, ANY), x_rows=(x_rows, VMEM), d_rows=(d_rows, VMEM),
               gain=(gain, VMEM), gain_mlp=(gain_mlp_part, VMEM))
    outs = dict(rows=(shape((rows + 8, width)), VMEM), kv=(shape((2, side, side, tokens, 2 * head)), ANY), q_other=(shape((side, side, rows, head)), ANY))
    scratch = dict(sum=rs_scratch(side, rows, width), all=ag_scratch(side, tokens, 2 * head), w=pltpu.VMEM((width, depth), BF16), w_sem=dma((2, 4)),
                   mate=pltpu.VMEM((half_side, side, rows, 2 * head), BF16), mate_sems=[dma((1,)), dma((1,))], swap_sems=[dma((1,)), dma((1,))])
    return call_kernel('sum_input', body, ins, outs, scratch, 3e8, 3)


def scores_softmax(qkv, seg_row, seg_col, head_index, tile_index, tile):
    reach = (tile_index + 1) * tile
    queries = qkv[tile_index * tile:reach, head_index * HEAD_DIM:(head_index + 1) * HEAD_DIM]
    scores = dot(qkv[:reach, 2 * HEAD_DIM:3 * HEAD_DIM], queries, NT) * HEAD_DIM ** -0.5
    key_at = lax.broadcasted_iota(jnp.int32, (reach, tile), 0)
    query_at = lax.broadcasted_iota(jnp.int32, (reach, tile), 1) + tile_index * tile
    allowed = (key_at <= query_at) & (seg_col[:reach, :] == seg_row[:, tile_index * tile:reach])
    scores = jnp.where(allowed, scores, -1e30)
    weights = jnp.exp(scores - jnp.max(scores, axis=0, keepdims=True))
    return weights * (1.0 / jnp.sum(weights, axis=0, keepdims=True)), queries


def segments(seg_ref):
    core = lax.rem(lax.axis_index('tp'), 2)
    seg_row = seg_ref[pl.ds(core, 1), :].astype(F32)
    return seg_row, jnp.broadcast_to(seg_row, (8, seg_row.shape[1])).T[:, :1]


def attention_forward(hidden, seg_ids, gain, w_qs, w_k, w_v, per_kv):
    seq, width = hidden.shape[1:]
    chunk = seq // 4
    tile = min(256, seq)
    depth = 4 * HEAD_DIM

    def body(ins, outs, scr):
        tp_idx = lax.axis_index('tp')
        kv_col = pl.multiple_of(lax.div(tp_idx, per_kv) * HEAD_DIM, HEAD_DIM)
        loads = []
        for index in range(4):
            at = pl.ds(index * chunk, chunk)
            loads.append(pltpu.make_async_copy(ins.hidden.at[lax.rem(tp_idx, 2), at, :], scr.x.at[at, :], scr.x_sem.at[index]))
        cols = [ins.w_qs[0], ins.w_qs[1], ins.w_k.at[:, pl.ds(kv_col, HEAD_DIM)], ins.w_v.at[:, pl.ds(kv_col, HEAD_DIM)]]
        for index, ref in enumerate(cols):
            loads.append(pltpu.make_async_copy(ref, scr.w.at[:, pl.ds(index * HEAD_DIM, HEAD_DIM)], scr.w_sem.at[index]))
        for load in loads:
            load.start()
        stores = []
        for index in range(4):
            loads[index].wait()

            def normalize(step, carry, index=index):
                at = pl.ds(pl.multiple_of(index * chunk + step * 16, 16), 16)
                x_float = scr.x[at, :].astype(F32)
                inv = lax.rsqrt(jnp.mean(x_float * x_float, axis=-1, keepdims=True) + EPS)
                scr.normed[at, :] = (x_float * inv * ins.gain[...]).astype(BF16)
                return carry

            lax.fori_loop(0, chunk // 16, normalize, 0)
            at = pl.ds(index * chunk, chunk)
            store = pltpu.make_async_copy(scr.normed.at[at, :], outs.normed.at[at, :], scr.out_sem.at[index])
            store.start()
            stores.append(store)
            if index == 0:
                for load in loads[4:]:
                    load.wait()
            outs.qkv[at, :] = dot(scr.normed[at, :], scr.w[...], NN).astype(BF16)
        seg_row, seg_col = segments(ins.seg)
        values_t = outs.qkv[:, 3 * HEAD_DIM:].T
        for head_index in range(2):
            for tile_index in range(seq // tile):
                probs, _ = scores_softmax(outs.qkv, seg_row, seg_col, head_index, tile_index, tile)
                ctx_t = dot(values_t[:, :(tile_index + 1) * tile], probs.astype(BF16), NN)
                outs.ctx[tile_index * tile:(tile_index + 1) * tile, head_index * HEAD_DIM:(head_index + 1) * HEAD_DIM] = ctx_t.T.astype(BF16)
        for store in stores:
            store.wait()

    dma = pltpu.SemaphoreType.DMA
    ins = dict(hidden=(hidden, ANY), seg=(seg_ids, VMEM), gain=(gain, VMEM), w_qs=[(weight, ANY) for weight in w_qs], w_k=(w_k, ANY), w_v=(w_v, ANY))
    outs = dict(normed=(shape((seq, width)), ANY), qkv=(shape((seq, depth)), VMEM), ctx=(shape((seq, 2 * HEAD_DIM)), VMEM))
    scratch = dict(x=pltpu.VMEM((seq, width), BF16), normed=pltpu.VMEM((seq, width), BF16), w=pltpu.VMEM((width, depth), BF16), x_sem=dma((4,)), w_sem=dma((4,)), out_sem=dma((4,)))
    return call_kernel('attention_forward', body, ins, outs, scratch, 5e9)


def attention_backward(resid, seg_ids, w_outs, qkv, token):
    seq, width = resid.shape
    chunk = seq // 4
    tile = min(256, seq)
    depth = 4 * HEAD_DIM

    def body(ins, outs, scr):
        loads = []
        for index in range(2):
            at = pl.ds(index * HEAD_DIM, HEAD_DIM)
            loads.append(pltpu.make_async_copy(ins.w_outs[index], scr.w.at[at, :], scr.w_sem.at[index]))
        for index in range(4):
            at = pl.ds(index * chunk, chunk)
            loads.append(pltpu.make_async_copy(ins.resid.at[at, :], scr.resid.at[at, :], scr.in_sem.at[index]))
        for load in loads:
            load.start()
        for load in loads[:2]:
            load.wait()
        for index in range(4):
            loads[2 + index].wait()
            at = pl.ds(index * chunk, chunk)
            scr.grad_ctx[at, :] = dot(scr.resid[at, :], scr.w[...], NT).astype(BF16)
        seg_row, seg_col = segments(ins.seg)
        keys_t = ins.qkv[:, 2 * HEAD_DIM:3 * HEAD_DIM].T
        scr.grad_k[...] = jnp.zeros_like(scr.grad_k)
        scr.grad_v[...] = jnp.zeros_like(scr.grad_v)
        for head_index in range(2):
            cols = slice(head_index * HEAD_DIM, (head_index + 1) * HEAD_DIM)
            for tile_index in range(seq // tile):
                reach = (tile_index + 1) * tile
                rows = slice(tile_index * tile, reach)
                probs, queries = scores_softmax(ins.qkv, seg_row, seg_col, head_index, tile_index, tile)
                grad_ctx = scr.grad_ctx[rows, cols]
                grad_probs = dot(ins.qkv[:reach, 3 * HEAD_DIM:], grad_ctx, NT)
                centre = jnp.sum(grad_probs * probs, axis=0, keepdims=True)
                grad_scores = (probs * (grad_probs - centre) * HEAD_DIM ** -0.5).astype(BF16)
                scr.grad_v[:reach, :] += dot(probs.astype(BF16), grad_ctx, NN)
                scr.grad_k[:reach, :] += dot(grad_scores, queries, NN)
                outs.dqkv[rows, cols] = dot(keys_t[:, :reach], grad_scores, NN).T.astype(BF16)
        outs.dqkv[:, 2 * HEAD_DIM:3 * HEAD_DIM] = scr.grad_k[...].astype(BF16)
        outs.dqkv[:, 3 * HEAD_DIM:] = scr.grad_v[...].astype(BF16)

    dma = pltpu.SemaphoreType.DMA
    ins = dict(resid=(resid, ANY), seg=(seg_ids, VMEM), w_outs=[(weight, ANY) for weight in w_outs], qkv=(qkv, VMEM), token=(token, ANY))
    outs = dict(dqkv=(shape((seq, depth)), VMEM))
    scratch = dict(resid=pltpu.VMEM((seq, width), BF16), w=pltpu.VMEM((2 * HEAD_DIM, width), BF16), grad_ctx=pltpu.VMEM((seq, 2 * HEAD_DIM), BF16),
                   grad_k=pltpu.VMEM((seq, HEAD_DIM), F32), grad_v=pltpu.VMEM((seq, HEAD_DIM), F32), w_sem=dma((2,)), in_sem=dma((4,)))
    return call_kernel('attention_backward', body, ins, outs, scratch, 4e9).dqkv


def mlp_grads(mixed_full, grad_out, w_gates, w_ups, w_downs):
    seq, width = grad_out.shape[1:]
    depth = w_gates[0].shape[0]
    tile = min(256, seq)

    def body(ins, outs, scr):
        core = lax.rem(lax.axis_index('tp'), 2)
        loads = []

        def load(src, dst):
            loads.append(pltpu.make_async_copy(src, dst, scr.sem.at[len(loads)]))
            loads[-1].start()

        load(ins.mixed.at[core], scr.mixed)
        load(ins.w_gates[0], scr.w.at[0])
        load(ins.w_ups[0], scr.w.at[1])
        load(ins.grad_out.at[core], scr.grad_out)
        load(ins.w_downs[0], scr.w.at[2])
        load(ins.w_gates[1], scr.w.at[3])
        load(ins.w_ups[1], scr.w.at[4])
        load(ins.w_downs[1], scr.w.at[5])
        for index in range(2):
            for copy in loads[:5] if index == 0 else loads[5:]:
                copy.wait()

            def step(tile_index, carry, index=index):
                at = pl.ds(pl.multiple_of(tile_index * tile, tile), tile)
                mixed = scr.mixed[at, :]
                gate = dot(mixed, scr.w[3 * index], NT)
                upper = dot(mixed, scr.w[3 * index + 1], NT)
                grad_act = dot(scr.grad_out[at, :], scr.w[3 * index + 2], NT)
                sigmoid_g = 1.0 / (1.0 + jnp.exp(-gate))
                silu_g = gate * sigmoid_g
                outs.acts[index][at, :] = (silu_g * upper).astype(BF16)
                outs.gates[index][at, :] = (grad_act * upper * sigmoid_g * (1.0 + gate * (1.0 - sigmoid_g))).astype(BF16)
                outs.ups[index][at, :] = (grad_act * silu_g).astype(BF16)
                return carry

            lax.fori_loop(0, seq // tile, step, 0)

    whole = lambda values: [(value, ANY) for value in values]
    ins = dict(mixed=(mixed_full, ANY), grad_out=(grad_out, ANY), w_gates=whole(w_gates), w_ups=whole(w_ups), w_downs=whole(w_downs))
    out = (shape((seq, depth)), VMEM)
    outs = dict(acts=[out, out], gates=[out, out], ups=[out, out])
    scratch = dict(mixed=pltpu.VMEM((seq, width), BF16), grad_out=pltpu.VMEM((seq, width), BF16), w=pltpu.VMEM((6, depth, width), BF16), sem=pltpu.SemaphoreType.DMA((8,)))
    return call_kernel('mlp_grads', body, ins, outs, scratch, 17e9)


def weight_grads_mlp(mixed_full, grad_out, resid_full, grads_gate, grads_up, acts, ctxs):
    seq, width = grad_out.shape[1:]
    depth, head = acts[0].shape[1], ctxs[1].shape[1]
    tile = min(512, width)

    def kernel(m_ref, dy_ref, dh_ref, *refs):
        sides = (refs[0:2], refs[2:4], refs[4:6], refs[6:8])
        out_gate, out_up, out_down, out_o, token, left = refs[8:]
        core = lax.rem(lax.axis_index('tp'), 2)

        @pl.when(pl.program_id(0) == 0)
        def _():
            base = 0
            for pair in sides:
                size = pair[1].shape[1]
                for half in range(2):
                    left[half, base:base + size, :] = pair[half][:, :size].T
                base += size

        def product(base, size, ref):
            return dot(left[0, base:base + size, :], ref[core], NN) + dot(left[1, base:base + size, :], ref[1 - core], NN)

        token[...] = jnp.zeros_like(token)
        both = product(0, 2 * depth, m_ref)
        out_gate[...] = both[:depth]
        out_up[...] = both[depth:]
        out_down[...] = product(2 * depth, depth, dy_ref)
        out_o[...] = product(3 * depth, head, dh_ref)

    slab = pl.BlockSpec((2, seq, tile), lambda step: (0, 0, step))
    whole = pl.BlockSpec(memory_space=pltpu.VMEM)
    out = lambda size: pl.BlockSpec((size, tile), lambda step: (0, step))
    return pl.pallas_call(
        kernel,
        name='weight_grads_mlp',
        grid=(width // tile,),
        out_shape=[shape((depth, width), F32)] * 3 + [shape((head, width), F32), shape((8, 128), F32)],
        in_specs=[slab] * 3 + [whole] * 8,
        out_specs=[out(depth)] * 3 + [out(head), pl.BlockSpec((8, 128), lambda step: (0, 0))],
        scratch_shapes=[pltpu.VMEM((2, 3 * depth + head, seq), BF16)],
        compiler_params=pltpu.CompilerParams(vmem_limit_bytes=60 * MIB),
        cost_estimate=pl.CostEstimate(flops=18_500_000_000, bytes_accessed=60_000_000, transcendentals=0),
    )(mixed_full, grad_out, resid_full, *grads_gate, *grads_up, *acts, *ctxs)


def weight_grads_qkv(normeds, kv_full, grads_q, kv_heads):
    seq, width = normeds[0].shape
    chips, tokens, pair = kv_full.shape[1:]
    head = pair // 2
    share = seq // tokens
    tile = min(256, width)
    kv_width = kv_heads * head

    def kernel(a_own, a_other, kv_ref, q_own, q_other, out_q, out_k, out_v, right, left):
        core = lax.rem(lax.axis_index('tp'), 2)

        @pl.when(pl.program_id(0) == 0)
        def _():
            for half, q_ref in enumerate((q_own, q_other)):
                right[half, :, 2 * kv_width:] = q_ref[:, :head]
                batch = core if half == 0 else 1 - core
                for chip in range(chips):
                    at = pl.ds((chip % share) * tokens, tokens)
                    base = (chip // share) * head
                    right[half, at, base:base + head] = kv_ref[batch, chip, :, :head]
                    right[half, at, kv_width + base:kv_width + base + head] = kv_ref[batch, chip, :, head:]

        left[0] = a_own[...].T
        left[1] = a_other[...].T

        def product(base, size):
            return dot(left[0], right[0, :, base:base + size], NN) + dot(left[1], right[1, :, base:base + size], NN)

        out_k[...] = product(0, kv_width)
        out_v[...] = product(kv_width, kv_width)
        out_q[...] = product(2 * kv_width, head)

    whole = pl.BlockSpec(memory_space=pltpu.VMEM)
    slab = pl.BlockSpec((seq, tile), lambda step: (0, step))
    out = lambda size: pl.BlockSpec((tile, size), lambda step: (step, 0))
    return pl.pallas_call(
        kernel,
        name='weight_grads_qkv',
        grid=(width // tile,),
        out_shape=[shape((width, head), F32), shape((width, kv_width), F32), shape((width, kv_width), F32)],
        in_specs=[slab, slab, whole, whole, whole],
        out_specs=[out(head), out(kv_width), out(kv_width)],
        scratch_shapes=[pltpu.VMEM((2, seq, 2 * kv_width + head), BF16), pltpu.VMEM((2, tile, seq), BF16)],
        compiler_params=pltpu.CompilerParams(vmem_limit_bytes=60 * MIB),
        cost_estimate=pl.CostEstimate(flops=27_500_000_000, bytes_accessed=60_000_000, transcendentals=0),
    )(*normeds, kv_full, *grads_q)


def in_place(gathered, rows):
    blocks, _, width = gathered.shape
    slots = 8

    def kernel(src, dst, buf, in_sem, out_sem):
        def load(index):
            return pltpu.make_async_copy(src.at[index, pl.ds(0, rows), :], buf.at[index % slots], in_sem.at[index % slots])

        def store(index):
            return pltpu.make_async_copy(buf.at[index % slots], dst.at[index % 2, index // 2], out_sem.at[index % slots])

        ahead = slots // 2
        for index in range(blocks + ahead):
            if index < blocks:
                if index >= slots:
                    store(index - slots).wait()
                load(index).start()
            if index >= ahead:
                load(index - ahead).wait()
                store(index - ahead).start()
        for index in range(blocks - slots, blocks):
            store(index).wait()

    return pl.pallas_call(
        kernel,
        name='in_place',
        out_shape=shape((2, blocks // 2, rows, width)),
        in_specs=[ANY],
        out_specs=ANY,
        scratch_shapes=[pltpu.VMEM((slots, rows, width), BF16), pltpu.SemaphoreType.DMA((slots,)), pltpu.SemaphoreType.DMA((slots,))],
        compiler_params=pltpu.CompilerParams(vmem_limit_bytes=60 * MIB),
        cost_estimate=pl.CostEstimate(flops=20_000_000, bytes_accessed=25_000_000, transcendentals=0),
    )(gathered)


def solution(mesh):
    tp_size = mesh.shape['tp']
    chips = tp_size // 2
    side = math.isqrt(chips)
    swap_pairs = [(index, index ^ 1) for index in range(tp_size)]

    def device_step(hidden, seg_ids, grad_out, gain_attn, gain_mlp, w_q, w_k, w_v, w_o, w_gate, w_up, w_down):
        seq_len, width = hidden.shape[1:]
        kv_heads = w_k.shape[1] // HEAD_DIM
        per_kv = tp_size // kv_heads
        share = per_kv // 2
        rows = seq_len // chips
        tp_idx = lax.axis_index('tp')

        def swap(value):
            return lax.ppermute(value, 'tp', swap_pairs)

        def own_rows(value):
            return lax.dynamic_slice(value, (tp_idx % 2, tp_idx // 2 * rows, 0), (1, rows, width))[0]

        def flat(value):
            return value.reshape(seq_len, value.shape[-1])

        gain_attn_row = gain_attn[None, :]
        gain_mlp_row = gain_mlp[None, :]
        x_rows = own_rows(hidden)

        w_qs = (w_q, swap(w_q))
        w_outs = (w_o, swap(w_o))
        w_gates = (w_gate.T, swap(w_gate.T))
        w_ups = (w_up.T, swap(w_up.T))
        w_downs = (w_down, swap(w_down))

        attn = attention_forward(hidden, seg_ids, gain_attn_row, w_qs, w_k, w_v, per_kv)
        first = sum_attention(side, attn.ctx, attn.normed, w_outs, x_rows, gain_mlp_row)
        mixed_full = first.full.reshape(2, seq_len, width)
        mlp = mlp_grads(mixed_full, grad_out, w_gates, w_ups, w_downs)
        second = sum_mlp(side, [mlp.gates[0], mlp.ups[0], mlp.gates[1], mlp.ups[1]], mlp.acts, w_gates, w_ups, w_downs, first.h_rows, own_rows(grad_out), gain_mlp_row)
        resid_full = second.full.reshape(2, seq_len, width)

        y_out = in_place(lax.all_gather(second.y_rows, 'tp'), rows).reshape(2, seq_len, width)
        grad_gate_t, grad_up_t, grad_w_down, grad_w_o, token = weight_grads_mlp(
            mixed_full, grad_out, resid_full, (mlp.gates[0], flat(second.gate_other)), (mlp.ups[0], flat(second.up_other)), (mlp.acts[0], flat(second.act_other)),
            (attn.ctx, flat(first.ctx_other)))
        dqkv = attention_backward(flat(second.own), seg_ids, w_outs, attn.qkv, token)
        third = sum_input(side, dqkv, w_qs, w_k, w_v, x_rows, second.d_rows, gain_attn_row, second.gain)

        gathered = lax.all_gather(third.rows, 'tp')
        grad_in = in_place(gathered, rows).reshape(2, seq_len, width)
        gain_grads = jnp.sum(gathered[:, rows:].astype(F32), axis=0)
        grad_gain_attn = gain_grads[0] + gain_grads[1] + gain_grads[2]
        grad_gain_mlp = gain_grads[3] + gain_grads[4] + gain_grads[5]
        kv_full = third.kv.reshape(2, chips, seq_len // share, 2 * HEAD_DIM)
        grad_w_q, grad_w_k, grad_w_v = weight_grads_qkv((attn.normed, first.normed_other), kv_full, (dqkv, flat(third.q_other)), kv_heads)
        return (y_out, grad_in, grad_gain_attn, grad_gain_mlp, grad_w_q, grad_w_k, grad_w_v, grad_w_o, grad_gate_t.T, grad_up_t.T, grad_w_down)

    spec_act = P('data', None, None)
    spec_rows = P('data', None)
    spec_gain = P(None)
    spec_cols = P(None, 'tp')
    spec_tprows = P('tp', None)
    spec_whole = P(None, None)
    spec_stack = P(('data', 'tp'), None)
    in_specs = (spec_act, spec_rows, spec_act, spec_gain, spec_gain, spec_cols, spec_whole, spec_whole, spec_tprows, spec_cols, spec_cols, spec_tprows)
    out_specs = (spec_act, spec_act, P('data'), P('data'), P('data', 'tp'), spec_rows, spec_rows, spec_stack, P('data', 'tp'), P('data', 'tp'), spec_stack)
    return jax.shard_map(device_step, mesh=mesh, in_specs=in_specs, out_specs=out_specs, check_vma=False)
```

time: 520 us -> 493 us (0.948)
  matrix products: 40.6 us -> 0 us
  Pallas kernels: 400 us -> 430 us
  waiting for transfers between devices: 0.16 us -> 27.8 us
  local copies, waits for them, and re-layouts: 31.9 us -> 5.47 us
  other arithmetic: 20.6 us -> 2.56 us
    dot_general x7 -> x0, matrix products: 35.5 us -> none  [the longest x2 9.15 us: dot(): lax.dot_general(lhs, rhs, (dims, ((), ())), preferred_element_type=F32)]
    pallas_call x4 -> x6, Pallas kernels: 316 us -> 341 us  [call_kernel(): pl.pallas_call(kernel, name=name, out_shape=[leaf[0] for leaf in out_leav...]
    unnamed x58 -> x4, local copies, waits for them, and re-layouts: 25.5 us -> 1.93 us
    all_gather x2, waiting for transfers between devices: 0.03 us -> 14.2 us  [the longest x1 14.2 us: device_step(): gathered = lax.all_gather(third.rows, 'tp')]
    ppermute x5, waiting for transfers between devices: 0.01 us -> 13.5 us  [swap(): return lax.ppermute(value, 'tp', swap_pairs)]
    convert_element_type x1 -> x0, other arithmetic: 8.22 us -> none  [device_step(): (x_float * inv_own * gain_attn).astype(BF16)]
  transfers between devices with their start and end apart: 7 -> 7, of which waited for: 0 -> 2; matrix products, arithmetic and copies ran while one was open for 13% -> 1% of each run, Pallas kernels for 45% -> 54%
where the time goes in v3:
time: 493 us; the launch traced here: 484 us
  Pallas kernels  430 us (87%)
  waiting for transfers between devices  27.8 us (6%)
  between operations  14.6 us (3%)
  local copies, waits for them, and re-layouts  5.47 us (1%)
    pallas_call x6, Pallas kernels, call_kernel(): pl.pallas_call(kernel, name=name, out_shape=[leaf[0] for leaf in out_leav...  341 us
    pallas_call x1, Pallas kernels, weight_grads_qkv(): pl.pallas_call(kernel, name='weight_grads_qkv', grid=(width // tile,), ou...  38.4 us
    pallas_call x1, Pallas kernels, weight_grads_mlp(): pl.pallas_call(kernel, name='weight_grads_mlp', grid=(width // tile,), ou...  29.4 us
    pallas_call x2, Pallas kernels, in_place(): pl.pallas_call(kernel, name='in_place', out_shape=shape((2, blocks // 2,...  21.3 us
    all_gather x1, waiting for transfers between devices, device_step(): gathered = lax.all_gather(third.rows, 'tp')  14.2 us
    ppermute x5, waiting for transfers between devices, swap(): return lax.ppermute(value, 'tp', swap_pairs)  13.5 us
  transfers between devices with their start and end apart: 7, of which 2 were waited for; matrix products, arithmetic and copies ran while one was open for 1% of the time, Pallas kernels for 54%

profile of v3, /device:TPU:97, one launch (start us, length us, event | category | flops | bytes accessed | tf_op | source)
XLA Modules:
  0.0 483.6 jit_solution(13091538585399591168)
XLA Ops:
  7.2 0.1 all-gather.5.cloned.1.call-start
  7.3 2.1 collective-permute-start.3
  9.4 0.1 collective-permute-start.4
  9.5 0.4 collective-permute-start.2
  9.9 0.1 collective-permute-start
  10.0 0.4 collective-permute-start.1
  10.4 1.8 dynamic-slice_bitcast_fusion.1.refs_5_.refs_8_
  12.2 1.8 dynamic-slice_bitcast_fusion.refs_2_
  13.9 13.5 %collective-permute-done.refs_5_.refs_6_ = bf16[4096,128]{1,0:T(8,128)(2,1)S(1)} collective-permute-done((bf16[4096,128]{1,0:T(8,128)(2,1)}, bf16[4096,128]{1,0:T(8,128)(2,1)S(1)}, u32[]{:S(2)}, u32[]{:S(2)}) %collective-permute-start) | collective-permute-done | bytes 1048608 | tf_op jit(solution)/shard_map/ppermute | solution.py:915
  27.4 0.0 copy-start
  27.4 1.0 copy-done
  28.4 17.8 %attention_forward.1 = (bf16[768,256]{1,0:T(8,128)(2,1)}, bf16[768,4096]{1,0:T(8,128)(2,1)}, bf16[768,512]{1,0:T(8,128)(2,1)}) custom-call(f32[1,4096]{1,0:T(1,128)} %bitcast.54, bf16[2,768,4096]{2,1,0:T(8,128)(2,1)} %refs_1_.1, s32[2,768]{1,0:T(2,128)} %refs_2_.5, bf16[4096,1024]{1,0:T(8,128)(2,1)} %refs_4_.5, bf16[4096,128]{1,0:T(8,128)(2,1)} %refs_5_.1, ...), custom_call_target="tpu_custom_call" | custom-call | flops 5000000000 | bytes 40000000 | tf_op jit(solution)/shard_map/attention_forward/pallas_call | solution.py:424
  46.2 0.0 collective-permute-done.1.refs_4_.refs_5_
  46.2 0.0 copy-start.1
  46.3 1.0 copy-done.1
  47.2 83.1 %sum_attention.1 = (bf16[4,4,48,128]{3,2,1,0:T(8,128)(2,1)}, bf16[2,4,4,48,4096]{4,3,2,1,0:T(8,128)(2,1)}, bf16[48,4096]{1,0:T(8,128)(2,1)}, bf16[768,4096]{1,0:T(8,128)(2,1)}) custom-call(bf16[4,4,48,256]{3,2,1,0:T(8,128)(2,1)} %bitcast.51, f32[1,4096]{1,0:T(1,128)} %bitcast.52, bf16[768,4096]{1,0:T(8,128)(2,1)} %get-tuple-element.44.refs_2_.a_own, ...), custom_call_target="tpu_custom_call" | custom-call | flops 400000000 | bytes 40000000 | tf_op jit(solution)/shard_map/sum_attention/pallas_call | solution.py:424
  130.3 0.0 collective-permute-done.3.refs_5_.refs_13_
  130.3 0.0 collective-permute-done.4.refs_7_.refs_14_
  130.4 0.0 collective-permute-done.2.refs_3_.refs_10_
  130.4 31.0 %mlp_grads.1 = (bf16[768,448]{1,0:T(8,128)(2,1)}, bf16[768,448]{1,0:T(8,128)(2,1)}, bf16[768,448]{1,0:T(8,128)(2,1)}, bf16[768,448]{1,0:T(8,128)(2,1)}, bf16[768...) custom-call(bf16[2,768,4096]{2,1,0:T(8,128)(2,1)} %dy_ref.1, bf16[2,768,4096]{2,1,0:T(8,128)(2,1)} %bitcast.58, ...), custom_call_target="tpu_custom_call" | custom-call | flops 16999999488 | bytes 40000000 | tf_op jit(solution)/shard_map/mlp_grads/pallas_call | solution.py:424
  161.4 128.6 %sum_mlp.1 = (bf16[4,4,48,448]{3,2,1,0:T(8,128)(2,1)}, f32[48,4096]{1,0:T(8,128)}, bf16[2,4,4,48,4096]{4,3,2,1,0:T(8,128)(2,1)}, f32[1,4096]{1,0:T(1,128)}, bf16...) custom-call(bf16[4,4,48,448]{3,2,1,0:T(8,128)(2,1)} %bitcast.44, ...), custom_call_target="tpu_custom_call" | custom-call | flops 600000000 | bytes 40000000 | tf_op jit(solution)/shard_map/sum_mlp/pallas_call | solution.py:424
  289.9 0.1 all-gather.5.cloned.1.call-update
  290.0 0.1 all-gather.7.cloned.1.call-start
  290.1 29.4 %weight_grads_mlp.1 = (f32[448,4096]{1,0:T(8,128)}, f32[448,4096]{1,0:T(8,128)}, f32[448,4096]{1,0:T(8,128)}, f32[128,4096]{1,0:T(8,128)}, f32[8,128]{1,0:T(8,128)}) custom-call(bf16[2,768,4096]{2,1,0:T(8,128)(2,1)} %bitcast.59, bf16[2,768,4096]{2,1,0:T(8,128)(2,1)} %dy_ref.1, bf16[2,768,4096]{2,1,0:T(8,128)(2,1)} %bitcast.60, ...), custom_call_target="tpu_custom_call" | custom-call | flops 18499999744 | bytes 60000000 | tf_op jit(solution)/shard_map/weight_grads_mlp/pallas_call | solution.py:804
  319.5 14.2 %attention_backward.1.q_own = bf16[768,512]{1,0:T(8,128)(2,1)} custom-call(bf16[768,512]{1,0:T(8,128)(2,1)} %get-tuple-element.55.refs_0_, bf16[768,4096]{1,0:T(8,128)(2,1)} %bitcast.61, s32[2,768]{1,0:T(2,128)} %refs_2_.5, f32[8,128]{1,0:T(8,128)} %get-tuple-element.62.refs_3_, bf16[128,4096]{1,0:T(8,128)(2,1)} %refs_4_.4, bf16[128,4096]{1,0:T(8,128)(2,1)} %copy-done.1), custom_call_target="tpu_custom_call" | custom-call | flops 4000000000 | bytes 40000000 | tf_op jit(solution)/shard_map/attention_backward/pallas_call | solution.py:424
  333.7 66.0 %sum_input.1 = (bf16[2,4,4,384,256]{4,3,2,1,0:T(8,128)(2,1)}, bf16[4,4,48,128]{3,2,1,0:T(8,128)(2,1)}, bf16[56,4096]{1,0:T(8,128)(2,1)}) custom-call(f32[48,4096]{1,0:T(8,128)} %get-tuple-element.54.refs_0_, bf16[4,4,48,512]{3,2,1,0:T(8,128)(2,1)} %bitcast.47, f32[1,4096]{1,0:T(1,128)} %bitcast.55, f32[1,4096]{1,0:T(1,128)} %get-tuple-element.63.refs_3_, ...), custom_call_target="tpu_custom_call" | custom-call | flops 300000000 | bytes 40000000 | tf_op jit(solution)/shard_map/sum_input/pallas_call | solution.py:424
  399.7 0.1 all-gather.7.cloned.1.call-update
  399.7 38.4 %weight_grads_qkv.1 = (f32[4096,128]{1,0:T(8,128)}, f32[4096,1024]{1,0:T(8,128)}, f32[4096,1024]{1,0:T(8,128)}) custom-call(bf16[768,4096]{1,0:T(8,128)(2,1)} %get-tuple-element.44.refs_2_.a_own, bf16[768,4096]{1,0:T(8,128)(2,1)} %get-tuple-element.65.a_other, bf16[2,16,384,256]{3,2,1,0:T(8,128)(2,1)} %bitcast.62, bf16[768,512]{1,0:T(8,128)(2,1)} %attention_backward.1.q_own, ...), custom_call_target="tpu_custom_call" | custom-call | flops 27499999232 | bytes 60000000 | tf_op jit(solution)/shard_map/weight_grads_qkv/pallas_call | solution.py:852
  438.1 0.0 all-gather.5.cloned.1.call-done
  438.2 10.7 %in_place.2 = bf16[2,16,48,4096]{3,2,1,0:T(8,128)(2,1)} custom-call(bf16[32,48,4096]{2,1,0:T(8,128)(2,1)} %bitcast.35), custom_call_target="tpu_custom_call" | custom-call | flops 20000000 | bytes 25000000 | tf_op jit(solution)/shard_map/in_place/pallas_call | solution.py:888
  448.8 14.2 %all-gather.7.cloned.1.call-done = bf16[1792,4096]{1,0:T(8,128)(2,1)} async-done(((bf16[56,4096]{1,0:T(8,128)(2,1)}), bf16[1792,4096]{1,0:T(8,128)(2,1)}) %all-gather.7.cloned.1.call-update) | async-done | bytes 14680080 | tf_op jit(solution)/shard_map/all_gather | solution.py:947
  463.0 10.7 %in_place.3 = bf16[2,16,48,4096]{3,2,1,0:T(8,128)(2,1)} custom-call(bf16[32,56,4096]{2,1,0:T(8,128)(2,1)} %bitcast.33), custom_call_target="tpu_custom_call" | custom-call | flops 20000000 | bytes 25000000 | tf_op jit(solution)/shard_map/in_place/pallas_call | solution.py:888
  473.7 1.9 convert_reduce_fusion
  475.6 0.7 slice_add_fusion
Async XLA Ops:
  7.2 431.0 %all-gather.5.cloned.1.call-start = ((), (), s32[]{:S(2)}) async-start(), calls=%async_computation | async-start | bytes 12976128 | tf_op jit(solution)/shard_map/all_gather | solution.py:940
  7.3 123.1 %collective-permute-start.3 = (bf16[448,4096]{1,0:T(8,128)(2,1)}, bf16[448,4096]{1,0:T(8,128)(2,1)}, u32[]{:S(2)}, u32[]{:S(2)}) collective-permute-start(bf16[448,4096]{1,0:T(8,128)(2,1)} %bitcast.38), channel_id=1, source_target_pairs={{0,1},{1,0},{2,3},{3,2},{4,5},{5,4},{6,7},{7,6},{8,9},{9,8},{10,11... | collective-permute-start | bytes 11010056 | tf_op jit(solution)/shard_map/ppermute | solution.py:915
  9.4 121.0 %collective-permute-start.4 = (bf16[448,4096]{1,0:T(8,128)(2,1)}, bf16[448,4096]{1,0:T(8,128)(2,1)}, u32[]{:S(2)}, u32[]{:S(2)}) collective-permute-start(bf16[448,4096]{1,0:T(8,128)(2,1)} %bitcast.41), channel_id=1, source_target_pairs={{0,1},{1,0},{2,3},{3,2},{4,5},{5,4},{6,7},{7,6},{8,9},{9,8},{10,11... | collective-permute-start | bytes 11010056 | tf_op jit(solution)/shard_map/ppermute | solution.py:915
  9.5 120.8 %collective-permute-start.2 = (bf16[448,4096]{1,0:T(8,128)(2,1)}, bf16[448,4096]{1,0:T(8,128)(2,1)}, u32[]{:S(2)}, u32[]{:S(2)}) collective-permute-start(bf16[448,4096]{1,0:T(8,128)(2,1)} %refs_9_.1), channel_id=1, source_target_pairs={{0,1},{1,0},{2,3},{3,2},{4,5},{5,4},{6,7},{7,6},{8,9},{9,8},{10,11... | collective-permute-start | bytes 11010056 | tf_op jit(solution)/shard_map/ppermute | solution.py:915
  9.9 17.5 %collective-permute-start = (bf16[4096,128]{1,0:T(8,128)(2,1)}, bf16[4096,128]{1,0:T(8,128)(2,1)S(1)}, u32[]{:S(2)}, u32[]{:S(2)}) collective-permute-start(bf16[4096,128]{1,0:T(8,128)(2,1)} %refs_5_.1), channel_id=1, source_target_pairs={{0,1},{1,0},{2,3},{3,2},{4,5},{5,4},{6,7},{7,6},{8,9},{9,8},{10,11... | collective-permute-start | bytes 3145736 | tf_op jit(solution)/shard_map/ppermute | solution.py:915
  10.0 36.2 %collective-permute-start.1 = (bf16[128,4096]{1,0:T(8,128)(2,1)}, bf16[128,4096]{1,0:T(8,128)(2,1)S(1)}, u32[]{:S(2)}, u32[]{:S(2)}) collective-permute-start(bf16[128,4096]{1,0:T(8,128)(2,1)} %refs_4_.4), channel_id=1, source_target_pairs={{0,1},{1,0},{2,3},{3,2},{4,5},{5,4},{6,7},{7,6},{8,9},{9,8},{10,11... | collective-permute-start | bytes 3145736 | tf_op jit(solution)/shard_map/ppermute | solution.py:915
  27.4 1.0 copy-start
  46.2 1.0 copy-start.1
  290.0 173.0 %all-gather.7.cloned.1.call-start = ((), (), s32[]{:S(2)}) async-start(), calls=%async_computation.1 | async-start | bytes 15138816 | tf_op jit(solution)/shard_map/all_gather | solution.py:947
Sparse Core Ops, SparseCore 0:
  290.1 58.5 all-gather.4
  399.9 63.1 all-gather.6

commit v4 on v3

v4 whole, which is shorter than its diff:
```python
import functools
import math
import types
import jax
import jax.numpy as jnp
from jax import lax
from jax.experimental import pallas as pl
from jax.experimental.pallas import tpu as pltpu
from jax.sharding import PartitionSpec as P

HEAD_DIM = 128
EPS = 1e-5
MESH = pl.DeviceIdType.MESH
F32 = jnp.float32
BF16 = jnp.bfloat16
LIMIT = 63 * 2 ** 20
K0, K1, K2, K3 = range(4)
PAIR = range(2)
ANY = pl.BlockSpec(memory_space=pl.ANY)
VMEM = pl.BlockSpec(memory_space=pltpu.VMEM)


def dot(lhs, rhs, dims):
    return lax.dot_general(lhs, rhs, (dims, ((), ())), preferred_element_type=F32)


NN = ((1,), (0,))
NT = ((1,), (1,))


SIGNS = (1, -1)


class Colour:
    def __init__(self, index, first, second):
        self.index, self.first, self.second = index, first, second


class Torus:
    def __init__(self, side):
        self.side = side
        tp_idx = lax.axis_index('tp')
        self.core = lax.rem(tp_idx, 2)
        self.chip = lax.div(tp_idx, 2)
        self.x = lax.rem(self.chip, side)
        self.y = lax.div(self.chip, side)
        self.partner = {'tp': self.chip * 2 + (1 - self.core)}
        self.colours = (Colour(0, self.x, self.y), Colour(1, self.y, self.x))
        self.pending = []

    def wrap(self, pos):
        return lax.rem(pos + 2 * self.side, self.side)

    def at_chip(self, y_at, x_at):
        return {'tp': (y_at * self.side + x_at) * 2 + self.core}

    def block(self, col, second, first):
        return (second, first) if col.index == 0 else (first, second)

    def peer1(self, col, shift):
        return self.at_chip(*self.block(col, col.second, self.wrap(col.first + shift)))

    def peer2(self, col, shift):
        return self.at_chip(*self.block(col, self.wrap(col.second + shift), col.first))

    def signal_all(self):
        barrier = pltpu.get_barrier_semaphore()
        peers = [self.partner]
        peers += [self.at_chip(self.y, self.wrap(self.x + shift)) for shift in SIGNS]
        peers += [self.at_chip(self.wrap(self.y + shift), self.x) for shift in SIGNS]
        for peer in peers:
            pl.semaphore_signal(barrier, inc=1, device_id=peer, device_id_type=MESH)
        return lambda: pl.semaphore_wait(barrier, len(peers))

    def send(self, src, dst, sems, index, device):
        copy = pltpu.make_async_remote_copy(src, dst, sems[K0].at[index], sems[K1].at[index], device_id=device, device_id_type=MESH)
        copy.start()
        self.pending.append(copy)

    def arrive(self, dst, sems, index):
        pltpu.make_async_remote_copy(dst, dst, sems[K0].at[index], sems[K1].at[index], device_id=self.partner, device_id_type=MESH).wait_recv()

    def drain(self):
        for copy in self.pending:
            copy.wait_send()


R1, R2, R3, S1, S2, S3 = range(6)
RS_COUNTS = (16, 16, 16, 4, 4, 4)
H1, H2, F1, F2 = range(4)
AG_COUNTS = (8, 32, 4, 16)


class ReduceScatter:
    SHIFTS = (2, 1, 3, 0)

    def __init__(self, torus, scr):
        self.torus, self.part, self.scr = torus, scr.part, scr
        self.quarter = scr.part.shape[K3] // 4

    def buf(self, kind, index):
        return self.scr.bufs[kind].at[index]

    def sems(self, kind):
        return self.scr.out_sems[kind], self.scr.in_sems[kind]

    def cols(self, col, half):
        return pl.ds((col.index * 2 + half) * self.quarter, self.quarter)

    def piece(self, where, at_cols):
        return self.part.at[(*where, slice(None), at_cols)]

    def send(self, where, at_cols, kind, index, peer):
        self.torus.send(self.piece(where, at_cols), self.buf(kind, index), self.sems(kind), index, peer)

    def add(self, where, at_cols, *kinds):
        total = self.part[(*where, slice(None), at_cols)].astype(F32)
        for kind, index in kinds:
            self.torus.arrive(self.buf(kind, index), self.sems(kind), index)
            total = total + self.buf(kind, index)[...].astype(F32)
        self.part[(*where, slice(None), at_cols)] = total.astype(BF16)

    def each(self, step):
        wrap = self.torus.wrap
        for col in self.torus.colours:
            second = wrap(col.second + self.SHIFTS[step])
            for way, sign in enumerate(SIGNS):
                yield col, second, way, sign, (col.index * 2 + way) * 4 + step

    def far(self, step):
        for col, second, way, sign, index in self.each(step):
            where = self.torus.block(col, second, self.torus.wrap(col.first + 2))
            self.send(where, self.cols(col, way), R1, index, self.torus.peer1(col, sign))

    def near(self, step):
        for col, second, way, sign, index in self.each(step):
            where = self.torus.block(col, second, self.torus.wrap(col.first + sign))
            self.send(where, self.cols(col, 1 - way), R2, index, self.torus.peer1(col, sign))

    def relay(self, step):
        for col, second, way, sign, index in self.each(step):
            where = self.torus.block(col, second, self.torus.wrap(col.first + sign))
            self.add(where, self.cols(col, way), (R1, index))
            self.send(where, self.cols(col, way), R3, index, self.torus.peer1(col, sign))

    def end(self, step):
        for col, second, way, sign, index in self.each(step):
            where = self.torus.block(col, second, col.first)
            other = (col.index * 2 + 1 - way) * 4 + step
            self.add(where, self.cols(col, way), (R2, other), (R3, index))

    def far2(self):
        for col in self.torus.colours:
            for way, sign in enumerate(SIGNS):
                where = self.torus.block(col, self.torus.wrap(col.second + 2), col.first)
                self.send(where, self.cols(col, way), S1, col.index * 2 + way, self.torus.peer2(col, sign))

    def near2(self, way):
        for col in self.torus.colours:
            where = self.torus.block(col, self.torus.wrap(col.second + SIGNS[way]), col.first)
            self.send(where, self.cols(col, 1 - way), S2, col.index * 2 + way, self.torus.peer2(col, SIGNS[way]))

    def relay2(self, way):
        for col in self.torus.colours:
            index = col.index * 2 + way
            where = self.torus.block(col, self.torus.wrap(col.second + SIGNS[way]), col.first)
            self.add(where, self.cols(col, way), (S1, index))
            self.send(where, self.cols(col, way), S3, index, self.torus.peer2(col, SIGNS[way]))

    def end2(self):
        for col in self.torus.colours:
            where = self.torus.block(col, col.second, col.first)
            for way in PAIR:
                self.add(where, self.cols(col, way), (S2, col.index * 2 + 1 - way), (S3, col.index * 2 + way))

    def steps(self, fill):
        call = functools.partial
        return [call(fill, K2), call(self.far, K0), call(self.far, K1), call(fill, K1), call(fill, K3),
                call(self.near, K0), call(self.relay, K0), call(self.near, K1), call(self.far, K2), call(self.relay, K1),
                call(fill, K0), call(self.near, K2), call(self.far, K3), call(self.end, K0), self.far2,
                call(self.relay, K2), call(self.near, K3), call(self.end, K1), call(self.near2, K0), call(self.relay2, K0),
                call(self.relay, K3), call(self.end, K2), call(self.near2, K1), call(self.relay2, K1), call(self.end, K3),
                self.end2]


class AllGather:
    def __init__(self, torus, scr, by_rows):
        self.torus, self.gat, self.scr, self.by_rows, self.store = torus, scr.gat, scr, by_rows, None
        self.quarter = scr.gat.shape[2 if by_rows else 3] // 4
        self.back = (0, torus.side - 1, 1, 2)

    def sems(self, kind):
        return self.scr.out_sems[kind], self.scr.in_sems[kind]

    def piece(self, ref, where, first, count):
        at = pl.ds(first * self.quarter, count * self.quarter)
        return ref.at[(*where, at, slice(None))] if self.by_rows else ref.at[(*where, slice(None), at)]

    def half(self, col, where, half):
        return self.piece(self.gat, where, col.index * 2 + half, 1)

    def own2(self, turn):
        for col in self.torus.colours:
            where = self.torus.block(col, col.second, col.first)
            for way, sign in enumerate(SIGNS):
                at = self.half(col, where, way if turn == 0 else 1 - way)
                self.torus.send(at, at, self.sems(H1), (col.index * 2 + way) * 2 + turn, self.torus.peer2(col, sign))

    def send1(self, step, turn):
        for col in self.torus.colours:
            where = self.torus.block(col, self.torus.wrap(col.second + self.back[step]), col.first)
            for way, sign in enumerate(SIGNS):
                at = self.half(col, where, way if turn == 0 else 1 - way)
                self.torus.send(at, at, self.sems(H2), ((col.index * 2 + way) * 4 + step) * 2 + turn, self.torus.peer1(col, sign))

    def arrive2(self, way, turn):
        sign = SIGNS[way]
        for col in self.torus.colours:
            where = self.torus.block(col, self.torus.wrap(col.second - sign), col.first)
            at = self.half(col, where, way if turn == 0 else 1 - way)
            self.torus.arrive(at, self.sems(H1), (col.index * 2 + way) * 2 + turn)
            if turn == 0:
                self.torus.send(at, at, self.sems(F1), col.index * 2 + way, self.torus.peer2(col, sign))

    def relayed2(self):
        for col in self.torus.colours:
            where = self.torus.block(col, self.torus.wrap(col.second + 2), col.first)
            for way in PAIR:
                self.torus.arrive(self.half(col, where, way), self.sems(F1), col.index * 2 + way)

    def arrive1(self, step, turn):
        for col in self.torus.colours:
            second = self.torus.wrap(col.second + self.back[step])
            for way, sign in enumerate(SIGNS):
                where = self.torus.block(col, second, self.torus.wrap(col.first - sign))
                at = self.half(col, where, way if turn == 0 else 1 - way)
                self.torus.arrive(at, self.sems(H2), ((col.index * 2 + way) * 4 + step) * 2 + turn)
                if turn == 0:
                    self.torus.send(at, at, self.sems(F2), (col.index * 2 + way) * 4 + step, self.torus.peer1(col, sign))

    def relayed1(self, step):
        for col in self.torus.colours:
            second = self.torus.wrap(col.second + self.back[step])
            for way in PAIR:
                where = self.torus.block(col, second, self.torus.wrap(col.first + 2))
                self.torus.arrive(self.half(col, where, way), self.sems(F2), (col.index * 2 + way) * 4 + step)

    def keep(self, step, firsts):
        for col in self.torus.colours:
            for shift in firsts:
                where = self.torus.block(col, self.torus.wrap(col.second + self.back[step]), self.torus.wrap(col.first + shift))
                self.store.keep(where, col.index, lambda ref, where=where, col=col: self.piece(ref, where, col.index * 2, 2))

    def steps(self, whole=None):
        call = functools.partial
        whole = whole or (lambda step: None)
        here, beside, across = (K0,), (K1, self.torus.side - 1), (K2,)
        result = []
        for turn in PAIR:
            result += [call(self.own2, turn), call(self.send1, K0, turn)]
        result += [call(self.keep, K0, here), call(self.arrive2, K0, K0), call(self.arrive2, K1, K0)]
        for way in PAIR:
            step = way + K1
            result += [call(self.arrive2, way, K1), call(self.send1, step, K0), call(self.send1, step, K1), call(self.keep, step, here)]
        result += [call(self.arrive1, K0, K0), self.relayed2, call(self.send1, K3, K0), call(self.send1, K3, K1), call(self.keep, K3, here),
                   call(self.arrive1, K0, K1), call(self.keep, K0, beside), call(self.arrive1, K1, K0), call(self.arrive1, K2, K0),
                   call(self.relayed1, K0), call(self.keep, K0, across), call(whole, K0)]
        for step in (K1, K2):
            result += [call(self.arrive1, step, K1), call(self.keep, step, beside)]
        result += [call(self.arrive1, K3, K0)]
        for step in (K1, K2):
            result += [call(self.relayed1, step), call(self.keep, step, across), call(whole, step)]
        return result + [call(self.arrive1, K3, K1), call(self.keep, K3, beside), call(self.relayed1, K3), call(self.keep, K3, across), call(whole, K3)]


class Store:
    def __init__(self, torus, scr, places, own=None):
        self.torus, self.scr, self.places, self.own = torus, scr, places, own
        self.stores = []

    def slot(self, where, colour, index):
        return ((index * 2 + colour) * self.torus.side + where[K0]) * self.torus.side + where[K1]

    def keep(self, where, colour, piece):
        for index, (src, dst) in enumerate(self.places(where, colour, self.torus.core)):
            slot = self.slot(where, colour, index)
            pairs = [(self.scr.full_sem, dst)]
            if self.own is not None:
                pairs.append((self.scr.own_sem, piece(self.own)))
            for sem, ref in pairs:
                store = pltpu.make_async_copy(src, ref, sem.at[slot])
                store.start()
                self.stores.append(store)
            self.torus.send(src, dst, self.scr.cross_sems, slot, self.torus.partner)

    def drain(self):
        for store in self.stores:
            store.wait()
        side = self.torus.side
        for colour in PAIR:
            for y_at in range(side):
                for x_at in range(side):
                    for index, (_, dst) in enumerate(self.places((y_at, x_at), colour, 1 - self.torus.core)):
                        self.torus.arrive(dst, self.scr.cross_sems, self.slot((y_at, x_at), colour, index))


def plain_places(gather, full):
    return lambda where, colour, half: [(gather.piece(gather.gat, where, colour * 2, 2), gather.piece(full.at[half], where, colour * 2, 2))]


def rs_scratch(side, rows, width):
    dma = pltpu.SemaphoreType.DMA
    return dict(
        part=pltpu.VMEM((side, side, rows, width), BF16),
        bufs=[pltpu.VMEM((count, rows, width // 4), BF16) for count in RS_COUNTS],
        out_sems=[dma((count,)) for count in RS_COUNTS],
        in_sems=[dma((count,)) for count in RS_COUNTS],
    )


def ag_scratch(side, rows, width, places=1):
    dma = pltpu.SemaphoreType.DMA
    blocks = 2 * side * side * places
    return dict(
        gat=pltpu.VMEM((side, side, rows, width), BF16),
        out_sems=[dma((count,)) for count in AG_COUNTS],
        in_sems=[dma((count,)) for count in AG_COUNTS],
        full_sem=dma((blocks,)),
        own_sem=dma((blocks,)),
        cross_sems=[dma((blocks,)), dma((blocks,))],
    )


class Weights:
    def __init__(self, refs, buf, sem, by_rows):
        self.refs, self.buf, self.sem, self.by_rows = refs, buf, sem, by_rows
        self.copies = [[], []]

    def start(self):
        for colour in PAIR:
            for index, ref in enumerate(self.refs):
                if self.by_rows:
                    half, depth = ref.shape[K0] // 2, ref.shape[K1]
                    rows, cols = pl.ds(colour * half, half), pl.ds(index * depth, depth)
                    copy = pltpu.make_async_copy(ref.at[rows, :], self.buf.at[rows, cols], self.sem.at[colour, index])
                else:
                    half, depth = ref.shape[K1] // 2, ref.shape[K0]
                    rows, cols = pl.ds(index * depth, depth), pl.ds(colour * half, half)
                    copy = pltpu.make_async_copy(ref.at[:, cols], self.buf.at[rows, cols], self.sem.at[colour, index])
                copy.start()
                self.copies[colour].append(copy)

    def wait(self, colour):
        for copy in self.copies[colour]:
            copy.wait()
        self.copies[colour] = []


def fill_partial(torus, part, lhs, weights):
    rows, width = part.shape[2:]
    tile = min(512, width // 2)

    def fill(shift):
        for col in torus.colours:
            weights.wait(col.index)
            first = torus.wrap(col.first + shift)
            left = []
            for ref in lhs:
                depth = ref.shape[K3]
                value = ref[:, first] if col.index == 0 else ref[first]
                left.append((value.reshape(torus.side * rows, depth), depth))

            def body(step, carry, col=col, first=first, left=left):
                at = pl.ds(pl.multiple_of(col.index * (width // 2) + step * tile, tile), tile)
                total = None
                base = 0
                for value, depth in left:
                    if weights.by_rows:
                        term = dot(value, weights.buf[at, base:base + depth], NT)
                    else:
                        term = dot(value, weights.buf[base:base + depth, at], NN)
                    total = term if total is None else total + term
                    base += depth
                total = total.astype(BF16).reshape(torus.side, rows, tile)
                if col.index == 0:
                    part[:, first, :, at] = total
                else:
                    part[first, :, :, at] = total
                return carry

            lax.fori_loop(0, (width // 2) // tile, body, 0)

    return fill


def run(*lists):
    keyed = []
    for order, steps in enumerate(lists):
        keyed += [((index + 0.5) / len(steps), order, step) for index, step in enumerate(steps)]
    for _, _, step in sorted(keyed, key=lambda item: item[:2]):
        step()


def swap_start(torus, sems, pairs):
    for index, (src, dst) in enumerate(pairs):
        torus.send(src, dst, sems, index, torus.partner)


def swap_end(torus, sems, pairs, first=0):
    for index, (_, dst) in enumerate(pairs):
        if index >= first:
            torus.arrive(dst, sems, index)


class Turner:
    def __init__(self, src, dst, scr):
        self.src, self.dst, self.scr = src, dst, scr
        self.unit = scr.turn_in.shape[K2]
        self.count = src.shape[K1] // self.unit

    def load(self, index):
        at = pl.ds(pl.multiple_of(index * self.unit, self.unit), self.unit)
        slot = lax.rem(index, 2)
        return pltpu.make_async_copy(self.src.at[:, at], self.scr.turn_in.at[slot], self.scr.turn_in_sem.at[slot])

    def save(self, index):
        at = pl.ds(pl.multiple_of(index * self.unit, self.unit), self.unit)
        slot = lax.rem(index, 2)
        return pltpu.make_async_copy(self.scr.turn_out.at[slot], self.dst.at[at, :], self.scr.turn_out_sem.at[slot])

    def steps(self, parts):
        each = self.count // parts

        def step(part):
            if part == 0:
                self.load(0).start()

            def body(index, carry):
                @pl.when(index + 1 < self.count)
                def _():
                    self.load(index + 1).start()

                self.load(index).wait()

                @pl.when(index >= 2)
                def _():
                    self.save(index - 2).wait()

                self.scr.turn_out[lax.rem(index, 2)] = self.scr.turn_in[lax.rem(index, 2)].T
                self.save(index).start()
                return carry

            lax.fori_loop(part * each, (part + 1) * each, body, 0)
            if part == parts - 1:
                self.save(self.count - 2).wait()
                self.save(self.count - 1).wait()

        return [functools.partial(step, part) for part in range(parts)]


def turner_scratch(rows, unit):
    dma = pltpu.SemaphoreType.DMA
    return dict(turn_in=pltpu.VMEM((2, rows, unit), BF16), turn_out=pltpu.VMEM((2, unit, rows), BF16), turn_in_sem=dma((K2,)), turn_out_sem=dma((K2,)))


def row_tiles(rows):
    return [pl.ds(start, 16) for start in range(0, rows, 16)]


def rms_back(z_in, gain, grad):
    inv = lax.rsqrt(jnp.mean(z_in * z_in, axis=-1, keepdims=True) + EPS)
    normed = z_in * inv
    scaled = grad * gain
    back = inv * (scaled - normed * jnp.mean(scaled * normed, axis=-1, keepdims=True))
    return back, jnp.sum(grad * normed, axis=0, keepdims=True)


def bag(tree):
    if isinstance(tree, dict):
        return types.SimpleNamespace(**{key: bag(value) for key, value in tree.items()})
    return [bag(value) for value in tree] if isinstance(tree, list) else tree


def call_kernel(name, body, ins, outs, scratch, flops, collective_id=None):
    is_leaf = lambda value: isinstance(value, tuple)
    in_leaves, in_tree = jax.tree.flatten(ins, is_leaf=is_leaf)
    out_leaves, out_tree = jax.tree.flatten(outs, is_leaf=is_leaf)
    scr_leaves, scr_tree = jax.tree.flatten(scratch)
    first_scr = len(in_leaves) + len(out_leaves)

    def kernel(*refs):
        body(bag(in_tree.unflatten(refs[:len(in_leaves)])), bag(out_tree.unflatten(refs[len(in_leaves):first_scr])), bag(scr_tree.unflatten(refs[first_scr:])))

    results = pl.pallas_call(
        kernel,
        name=name,
        out_shape=[leaf[K0] for leaf in out_leaves],
        in_specs=[leaf[K1] for leaf in in_leaves],
        out_specs=[leaf[K1] for leaf in out_leaves],
        scratch_shapes=scr_leaves,
        compiler_params=pltpu.CompilerParams(collective_id=collective_id, has_side_effects=collective_id is not None, vmem_limit_bytes=LIMIT),
        cost_estimate=pl.CostEstimate(flops=int(flops), bytes_accessed=int(4e7), transcendentals=0),
    )(*[leaf[K0] for leaf in in_leaves])
    return bag(out_tree.unflatten(results))


def shape(dims, dtype=BF16):
    return jax.ShapeDtypeStruct(dims, dtype)


def sum_attention(side, attn, w_outs, hidden, grad_out, gain, w_gate, w_up, w_down):
    seq, depth = attn.ctx.shape
    width = gain.shape[K1]
    hidden_loc = w_gate.shape[K0]
    rows = seq // (side * side)

    def body(ins, outs, scr):
        torus = Torus(side)
        weights = Weights(ins.w_outs, scr.w, scr.w_sem, False)
        weights.start()
        rows_at = pl.ds(pl.multiple_of(torus.chip * rows, rows), rows)
        x_load = pltpu.make_async_copy(ins.hidden.at[torus.core, rows_at, :], scr.x_rows, scr.x_sem.at[K0])
        x_load.start()

        def load_weight(src, slot):
            load = pltpu.make_async_copy(src, scr.w_mlp.at[slot], scr.w_mlp_sem.at[slot])
            load.start()
            return load

        loads = {slot: load_weight(src, slot) for slot, src in ((K0, ins.w_down), (K2, ins.w_gate), (K3, ins.w_up))}
        wait = torus.signal_all()
        part = scr.sum.part
        steps = ReduceScatter(torus, scr.sum).steps(fill_partial(torus, part, [ins.ctx], weights))
        steps[K0]()
        wait()
        other_ctx = ins.ctx.at[:, :, :, pl.ds(depth // 2, depth // 2)]
        swaps = [(ins.w_down, outs.w_down), (ins.w_gate, outs.w_gate), (ins.w_up, outs.w_up), (other_ctx, outs.ctx_other), (ins.normed, outs.normed_other)]
        swap_start(torus, scr.swap_sems, swaps)

        def dy_load(group):
            at = pl.ds(group * side * rows, side * rows)
            return pltpu.make_async_copy(ins.grad_out.at[torus.core, at, :], scr.dy.at[group % 2], scr.dy_sem.at[group % 2])

        def grad_act(group):
            if group == 0:
                torus.arrive(outs.w_down, scr.swap_sems, 0)
                loads[K1] = load_weight(outs.w_down, K1)
                for slot in PAIR:
                    loads[slot].wait()
            dy_load(group).wait()
            for slot in PAIR:
                product = dot(scr.dy[group % 2], scr.w_mlp[slot], NT)
                scr.grad_act[slot, group] = product.reshape(side, rows, hidden_loc)
            if group + 2 < side:
                dy_load(group + 2).start()

        dy_load(0).start()
        dy_load(1).start()
        half = len(steps) // 3
        run(steps[1:half])
        run(steps[half:], [functools.partial(grad_act, group) for group in range(side)])
        for index, (slot, out) in enumerate(((K0, outs.w_gate), (K1, outs.w_up))):
            torus.arrive(out, scr.swap_sems, index + 1)
            loads[slot] = load_weight(out, slot)
        scr.pre[...] = jnp.zeros_like(scr.pre)
        gat = scr.all.gat
        own = (torus.y, torus.x)
        x_load.wait()
        for at in row_tiles(rows):
            resid = (scr.x_rows[at, :].astype(F32) + part[(*own, at, slice(None))].astype(F32)).astype(BF16)
            outs.h_rows[at, :] = resid
            z_in = resid.astype(F32)
            inv = lax.rsqrt(jnp.mean(z_in * z_in, axis=-1, keepdims=True) + EPS)
            gat[(*own, at, slice(None))] = (z_in * inv * ins.gain[...]).astype(BF16)
        gather = AllGather(torus, scr.all, False)
        gather.store = Store(torus, scr.all, plain_places(gather, outs.full))

        def products(step):
            if step == 0:
                for load in (loads[slot] for slot in (K0, K1, K2, K3)):
                    load.wait()
            for col in torus.colours:
                second = torus.wrap(col.second + gather.back[step])
                at_cols = pl.ds(col.index * (width // 2), width // 2)
                mixed = gat[second, :, :, at_cols] if col.index == 0 else gat[:, second, :, at_cols]
                mixed = mixed.reshape(side * rows, width // 2)

                def body(slot, carry, col=col, second=second, at_cols=at_cols, mixed=mixed):
                    term = dot(mixed, scr.w_mlp[slot, :, at_cols], NT).reshape(side, rows, hidden_loc)
                    if col.index == 0:
                        scr.pre[slot, second] += term
                    else:
                        scr.pre[slot, :, second] += term
                    return carry

                lax.fori_loop(0, 4, body, 0)
            for inner, count in ((0, step + 1), (1, step)):

                def block(index, carry, inner=inner):
                    shift = lax.rem(3 * index + 3 * lax.div(index * (index - 1), 2), side)
                    pair = (gather.back[step], shift) if inner == 0 else (shift, gather.back[step])
                    y_at, x_at = torus.wrap(torus.y + pair[K0]), torus.wrap(torus.x + pair[K1])
                    for core in PAIR:
                        gate, upper = scr.pre[2 - 2 * core, y_at, x_at], scr.pre[3 - 2 * core, y_at, x_at]
                        grad = scr.grad_act[core, y_at, x_at]
                        sigmoid_g = 1.0 / (1.0 + jnp.exp(-gate))
                        silu_g = gate * sigmoid_g
                        outs.acts[core][y_at, x_at] = (silu_g * upper).astype(BF16)
                        outs.gates[core][y_at, x_at] = (grad * upper * sigmoid_g * (1.0 + gate * (1.0 - sigmoid_g))).astype(BF16)
                        outs.ups[core][y_at, x_at] = (grad * silu_g).astype(BF16)
                    return carry

                lax.fori_loop(0, count, block, 0)

        run(gather.steps(products))
        gather.store.drain()
        swap_end(torus, scr.swap_sems, swaps, 3)
        torus.drain()

    dma = pltpu.SemaphoreType.DMA
    block = (side, side, rows, hidden_loc)
    ins = dict(ctx=(attn.ctx.reshape(side, side, rows, depth), VMEM), w_outs=[(weight, ANY) for weight in w_outs], hidden=(hidden, ANY), grad_out=(grad_out, ANY), gain=(gain, VMEM),
               normed=(attn.normed, ANY), w_gate=(w_gate, ANY), w_up=(w_up, ANY), w_down=(w_down, ANY))
    out, weight = (shape(block), VMEM), (shape((hidden_loc, width)), ANY)
    outs = dict(full=(shape((2, side, side, rows, width)), ANY), h_rows=(shape((rows, width)), VMEM), ctx_other=(shape((side, side, rows, depth // 2)), ANY), normed_other=(shape((seq, width)), ANY),
                w_gate=weight, w_up=weight, w_down=weight, acts=[out, out], gates=[out, out], ups=[out, out])
    scratch = dict(sum=rs_scratch(side, rows, width), all=ag_scratch(side, rows, width), w=pltpu.VMEM((depth, width), BF16), w_sem=dma((K2, K2)), swap_sems=[dma((5,)), dma((5,))],
                   x_rows=pltpu.VMEM((rows, width), BF16), x_sem=dma((K1,)), w_mlp=pltpu.VMEM((4, hidden_loc, width), BF16), w_mlp_sem=dma((4,)),
                   dy=pltpu.VMEM((2, side * rows, width), BF16), dy_sem=dma((K2,)), pre=pltpu.VMEM((4, *block), F32), grad_act=pltpu.VMEM((2, *block), F32))
    return call_kernel('sum_attention', body, ins, outs, scratch, 4e8, 1)


def sum_mlp(side, mlp, w_gates, w_ups, w_downs, grad_out, gain):
    depth = w_gates[K0].shape[K0]
    width = gain.shape[K1]
    rows = mlp.h_rows.shape[K0]
    seq = rows * side * side
    block = (side, side, rows, width)

    def body(ins, outs, scr):
        torus = Torus(side)
        weights = Weights(ins.w_in, scr.w, scr.w_sem, False)
        weights.start()
        weights_p = Weights(ins.w_downs, scr.wd, scr.wd_sem, False)
        weights_p.start()
        rows_at = pl.ds(pl.multiple_of(torus.chip * rows, rows), rows)
        dy_load = pltpu.make_async_copy(ins.grad_out.at[torus.core, rows_at, :], scr.dy_rows, scr.dy_sem.at[K0])
        dy_load.start()
        wait = torus.signal_all()
        steps = ReduceScatter(torus, scr.sum).steps(fill_partial(torus, scr.sum.part, ins.grads, weights))
        steps_p = ReduceScatter(torus, scr.sum_p).steps(fill_partial(torus, scr.sum_p.part, ins.acts, weights_p))
        steps[K0]()
        wait()

        turned = []

        def turn(index):
            kind, core = index // 2, index % 2
            src = (ins.grads[2 * core], ins.grads[2 * core + 1], ins.acts[core])[kind]
            slot = index % 2
            if index >= 2:
                turned[index - 2]()
            scr.turn[slot] = src[...].reshape(seq, depth).T
            at = pl.ds(kind * depth, depth)
            if core == 0:
                save = pltpu.make_async_copy(scr.turn.at[slot], outs.left.at[at, :], scr.turn_sem.at[kind])
                save.start()
                turned.append(save.wait)
            else:
                torus.send(scr.turn.at[slot], outs.left_other.at[at, :], scr.swap_sems, kind, torus.partner)
                turned.append(torus.pending.pop().wait_send)

        turns = [functools.partial(turn, index) for index in range(6)]
        fills = (K0, K3, 4, 10)
        early = [steps_p[index] for index in fills]
        rest_p = [step for index, step in enumerate(steps_p) if index not in fills]
        late = 22
        run(steps[1:late], early)
        for step in rest_p[:3]:
            step()
        run(steps[late:])
        own = (torus.y, torus.x)
        gain_total = jnp.zeros((1, width), F32)
        gat = scr.all.gat
        dy_load.wait()
        for at in row_tiles(rows):
            back, gain_part = rms_back(ins.h_rows[at, :].astype(F32), ins.gain[...], scr.sum.part[(*own, at, slice(None))].astype(F32))
            gain_total = gain_total + gain_part
            total = scr.dy_rows[at, :].astype(F32) + back
            outs.d_rows[at, :] = total
            gat[(*own, at, slice(None))] = total.astype(BF16)
        outs.gain[...] = gain_total
        gather = AllGather(torus, scr.all, False)
        gather.store = Store(torus, scr.all, plain_places(gather, outs.full), outs.own)
        run(gather.steps(), rest_p[3:], turns)
        for at in row_tiles(rows):
            outs.y_rows[at, :] = (ins.h_rows[at, :].astype(F32) + scr.sum_p.part[(*own, at, slice(None))].astype(F32)).astype(BF16)
        turned[4]()
        turned[5]()
        for kind in range(3):
            torus.arrive(outs.left_other.at[pl.ds(kind * depth, depth), :], scr.swap_sems, kind)
        gather.store.drain()
        torus.drain()

    dma = pltpu.SemaphoreType.DMA
    ins = dict(grads=[(grad, VMEM) for grad in (mlp.gates[K0], mlp.ups[K0], mlp.gates[K1], mlp.ups[K1])], acts=[(act, VMEM) for act in mlp.acts],
               w_in=[(weight, ANY) for weight in (w_gates[K0], w_ups[K0], w_gates[K1], w_ups[K1])], w_downs=[(weight, ANY) for weight in w_downs],
               h_rows=(mlp.h_rows, VMEM), grad_out=(grad_out, ANY), gain=(gain, VMEM))
    left = (shape((3 * depth, seq)), ANY)
    outs = dict(full=(shape((2, *block)), ANY), own=(shape(block), ANY), d_rows=(shape((rows, width), F32), VMEM), gain=(shape((1, width), F32), VMEM), y_rows=(shape((rows, width)), VMEM), left=left, left_other=left)
    scratch = dict(sum=rs_scratch(side, rows, width), sum_p=rs_scratch(side, rows, width), all=ag_scratch(side, rows, width), dy_rows=pltpu.VMEM((rows, width), BF16), dy_sem=dma((K1,)),
                   w=pltpu.VMEM((4 * depth, width), BF16), w_sem=dma((K2, 4)), wd=pltpu.VMEM((2 * depth, width), BF16), wd_sem=dma((K2, K2)),
                   turn=pltpu.VMEM((2, depth, seq), BF16), turn_sem=dma((K3,)), swap_sems=[dma((K3,)), dma((K3,))])
    return call_kernel('sum_mlp', body, ins, outs, scratch, 6e8, 2)


def sum_input(side, dqkv, w_qs, w_k, w_v, hidden, d_rows, gain, gain_mlp_part, normeds):
    seq, depth = dqkv.shape
    width = gain.shape[K1]
    rows = seq // (side * side)
    head = depth // 4
    half_side = side // 2
    tokens = seq // 2
    kv_width = w_k.shape[K1]
    per_kv = 2 * side * side * head // kv_width

    def body(ins, outs, scr):
        torus = Torus(side)
        kv_col = pl.multiple_of(lax.div(torus.chip * 2, per_kv) * head, head)
        weights = Weights([*ins.w_qs, ins.w_k.at[:, pl.ds(kv_col, head)], ins.w_v.at[:, pl.ds(kv_col, head)]], scr.w, scr.w_sem, True)
        weights.start()
        wait = torus.signal_all()
        part = scr.sum.part
        steps = ReduceScatter(torus, scr.sum).steps(fill_partial(torus, part, [ins.dqkv], weights))
        own = (torus.y, torus.x)
        gat = scr.all.gat
        gather = AllGather(torus, scr.all, True)

        def places(where, colour, half):
            chip = where[K0] * side + where[K1]
            tokens_at = pl.ds(pl.multiple_of(lax.rem(chip, 2) * tokens + colour * (tokens // 2), tokens // 2), tokens // 2)
            at = lax.div(chip, 2) * head
            src = gather.piece(gat, where, colour * 2, 2)
            return [(src.at[:, pl.ds(index * head, head)], outs.kv.at[half, tokens_at, pl.ds(pl.multiple_of(at + index * kv_width, head), head)]) for index in PAIR]

        gather.store = Store(torus, scr.all, places)
        rows_at = pl.ds(pl.multiple_of(torus.chip * rows, rows), rows)
        x_load = pltpu.make_async_copy(ins.hidden.at[torus.core, rows_at, :], scr.x_rows, scr.x_sem.at[K0])
        x_load.start()
        turns = Turner(ins.normeds[K0], outs.lefts[K0], scr).steps(8) + Turner(ins.normeds[K1], outs.lefts[K1], scr).steps(8)
        place = lax.rem(torus.x, 2)
        mate = torus.at_chip(torus.y, torus.x + 1 - 2 * place)
        kv_cols = pl.ds(2 * head, 2 * head)

        def mate_add():
            torus.arrive(scr.mate, scr.mate_sems, 0)
            mine = ins.dqkv[pl.ds(place * half_side, half_side), :, :, kv_cols]
            gat[own] = (mine.astype(F32) + scr.mate[...].astype(F32)).astype(BF16).reshape(tokens, 2 * head)

        steps[K0]()
        wait()
        swaps = [(ins.dqkv.at[:, :, :, pl.ds(head, head)], outs.q_other)]
        swap_start(torus, scr.swap_sems, swaps)
        torus.send(ins.dqkv.at[pl.ds((1 - place) * half_side, half_side), :, :, kv_cols], scr.mate, scr.mate_sems, 0, mate)
        for step in steps[1:5]:
            step()
        mate_add()
        run(steps[5:], gather.steps(), turns)
        x_load.wait()
        gain_total = jnp.zeros((1, width), F32)
        for at in row_tiles(rows):
            back, gain_part = rms_back(scr.x_rows[at, :].astype(F32), ins.gain[...], part[(*own, at, slice(None))].astype(F32))
            gain_total = gain_total + gain_part
            outs.rows[at, :] = (ins.d_rows[at, :] + back).astype(BF16)
        row = lax.broadcasted_iota(jnp.int32, (8, width), 0)
        extra = jnp.zeros((8, width), F32)
        for index, value in enumerate((gain_total, ins.gain_mlp[...])):
            for level in range(3):
                rounded = value.astype(BF16).astype(F32)
                extra = jnp.where(row == index * 3 + level, rounded, extra)
                value = value - rounded
        outs.rows[rows:rows + 8, :] = extra.astype(BF16)
        gather.store.drain()
        swap_end(torus, scr.swap_sems, swaps)
        torus.drain()

    dma = pltpu.SemaphoreType.DMA
    ins = dict(dqkv=(dqkv.reshape(side, side, rows, depth), VMEM), w_qs=[(weight, ANY) for weight in w_qs], w_k=(w_k, ANY), w_v=(w_v, ANY), hidden=(hidden, ANY), d_rows=(d_rows, VMEM), normeds=[(normed, ANY) for normed in normeds],
               gain=(gain, VMEM), gain_mlp=(gain_mlp_part, VMEM))
    outs = dict(rows=(shape((rows + 8, width)), VMEM), kv=(shape((2, seq, 2 * kv_width)), ANY), lefts=[(shape((width, seq)), ANY)] * 2, q_other=(shape((side, side, rows, head)), ANY))
    scratch = dict(sum=rs_scratch(side, rows, width), all=ag_scratch(side, tokens, 2 * head, 2), x_rows=pltpu.VMEM((rows, width), BF16), x_sem=dma((K1,)), **turner_scratch(seq, min(256, width // 8)), w=pltpu.VMEM((width, depth), BF16), w_sem=dma((K2, 4)),
                   mate=pltpu.VMEM((half_side, side, rows, 2 * head), BF16), mate_sems=[dma((K1,)), dma((K1,))], swap_sems=[dma((K1,)), dma((K1,))])
    return call_kernel('sum_input', body, ins, outs, scratch, 3e8, 3)


def scores_softmax(qkv, seg_row, seg_col, head_index, tile_index, tile):
    reach = (tile_index + 1) * tile
    queries = qkv[tile_index * tile:reach, head_index * HEAD_DIM:(head_index + 1) * HEAD_DIM]
    scores = dot(qkv[:reach, 2 * HEAD_DIM:3 * HEAD_DIM], queries, NT) * HEAD_DIM ** -0.5
    key_at = lax.broadcasted_iota(jnp.int32, (reach, tile), 0)
    query_at = lax.broadcasted_iota(jnp.int32, (reach, tile), 1) + tile_index * tile
    allowed = (key_at <= query_at) & (seg_col[:reach, :] == seg_row[:, tile_index * tile:reach])
    scores = jnp.where(allowed, scores, -1e30)
    weights = jnp.exp(scores - jnp.max(scores, axis=0, keepdims=True))
    return weights * (1.0 / jnp.sum(weights, axis=0, keepdims=True)), queries


def segments(seg_ref):
    core = lax.rem(lax.axis_index('tp'), 2)
    seg_row = seg_ref[pl.ds(core, 1), :].astype(F32)
    return seg_row, jnp.broadcast_to(seg_row, (8, seg_row.shape[K1])).T[:, :1]


def attention_forward(hidden, seg_ids, gain, w_q, w_k, w_v, w_o, per_kv):
    seq, width = hidden.shape[1:]
    chunk = seq // 4
    tile = min(256, seq)
    depth = 4 * HEAD_DIM

    def body(ins, outs, scr):
        tp_idx = lax.axis_index('tp')
        core = lax.rem(tp_idx, 2)
        kv_col = pl.multiple_of(lax.div(tp_idx, per_kv) * HEAD_DIM, HEAD_DIM)
        partner = dict(tp=tp_idx + 1 - 2 * core)
        barrier = pltpu.get_barrier_semaphore()
        pl.semaphore_signal(barrier, inc=1, device_id=partner, device_id_type=MESH)
        loads = []
        for index in range(4):
            at = pl.ds(index * chunk, chunk)
            loads.append(pltpu.make_async_copy(ins.hidden.at[core, at, :], scr.x.at[at, :], scr.x_sem.at[index]))

        def w_cols(index):
            return scr.w.at[:, pl.ds(index * HEAD_DIM, HEAD_DIM)]

        for index, ref in ((0, ins.w_q), (2, ins.w_k.at[:, pl.ds(kv_col, HEAD_DIM)]), (3, ins.w_v.at[:, pl.ds(kv_col, HEAD_DIM)])):
            loads.append(pltpu.make_async_copy(ref, w_cols(index), scr.w_sem.at[index]))
        for load in loads:
            load.start()
        pl.semaphore_wait(barrier, 1)
        swaps = [(ins.w_q, w_cols(1)), (ins.w_o, outs.w_o), (ins.w_q, outs.w_q)]
        copies = []
        for index, (src, dst) in enumerate(swaps):
            copies.append(pltpu.make_async_remote_copy(src, dst, scr.swap_sems[K0].at[index], scr.swap_sems[K1].at[index], device_id=partner, device_id_type=MESH))
            copies[index].start()
        stores = []
        for index in range(4):
            loads[index].wait()

            def normalize(step, carry, index=index):
                at = pl.ds(pl.multiple_of(index * chunk + step * 16, 16), 16)
                x_float = scr.x[at, :].astype(F32)
                inv = lax.rsqrt(jnp.mean(x_float * x_float, axis=-1, keepdims=True) + EPS)
                scr.normed[at, :] = (x_float * inv * ins.gain[...]).astype(BF16)
                return carry

            lax.fori_loop(0, chunk // 16, normalize, 0)
            at = pl.ds(index * chunk, chunk)
            store = pltpu.make_async_copy(scr.normed.at[at, :], outs.normed.at[at, :], scr.out_sem.at[index])
            store.start()
            stores.append(store)
            if index == 0:
                for load in loads[4:]:
                    load.wait()
                copies[K0].wait_recv()
            outs.qkv[at, :] = dot(scr.normed[at, :], scr.w[...], NN).astype(BF16)
        seg_row, seg_col = segments(ins.seg)
        values_t = outs.qkv[:, 3 * HEAD_DIM:].T
        for head_index in PAIR:
            for tile_index in range(seq // tile):
                probs, _ = scores_softmax(outs.qkv, seg_row, seg_col, head_index, tile_index, tile)
                ctx_t = dot(values_t[:, :(tile_index + 1) * tile], probs.astype(BF16), NN)
                outs.ctx[tile_index * tile:(tile_index + 1) * tile, head_index * HEAD_DIM:(head_index + 1) * HEAD_DIM] = ctx_t.T.astype(BF16)
        for store in stores:
            store.wait()
        copies[K0].wait_send()
        copies[K1].wait()
        copies[K2].wait()

    dma = pltpu.SemaphoreType.DMA
    ins = dict(hidden=(hidden, ANY), seg=(seg_ids, VMEM), gain=(gain, VMEM), w_q=(w_q, ANY), w_o=(w_o, ANY), w_k=(w_k, ANY), w_v=(w_v, ANY))
    outs = dict(normed=(shape((seq, width)), ANY), qkv=(shape((seq, depth)), VMEM), ctx=(shape((seq, 2 * HEAD_DIM)), VMEM), w_q=(shape(w_q.shape), ANY), w_o=(shape(w_o.shape), ANY))
    scratch = dict(swap_sems=[dma((K3,)), dma((K3,))], x=pltpu.VMEM((seq, width), BF16), normed=pltpu.VMEM((seq, width), BF16), w=pltpu.VMEM((width, depth), BF16), x_sem=dma((4,)), w_sem=dma((4,)), out_sem=dma((4,)))
    return call_kernel('attention_forward', body, ins, outs, scratch, 5e9, 4)


def attention_backward(resid, seg_ids, w_outs, qkv, token):
    seq, width = resid.shape
    chunk = seq // 4
    tile = min(256, seq)
    depth = 4 * HEAD_DIM

    def body(ins, outs, scr):
        loads = []
        for index in PAIR:
            at = pl.ds(index * HEAD_DIM, HEAD_DIM)
            loads.append(pltpu.make_async_copy(ins.w_outs[index], scr.w.at[at, :], scr.w_sem.at[index]))
        for index in range(4):
            at = pl.ds(index * chunk, chunk)
            loads.append(pltpu.make_async_copy(ins.resid.at[at, :], scr.resid.at[at, :], scr.in_sem.at[index]))
        for load in loads:
            load.start()
        for load in loads[:2]:
            load.wait()
        for index in range(4):
            loads[2 + index].wait()
            at = pl.ds(index * chunk, chunk)
            scr.grad_ctx[at, :] = dot(scr.resid[at, :], scr.w[...], NT).astype(BF16)
        seg_row, seg_col = segments(ins.seg)
        keys_t = ins.qkv[:, 2 * HEAD_DIM:3 * HEAD_DIM].T
        scr.grad_k[...] = jnp.zeros_like(scr.grad_k)
        scr.grad_v[...] = jnp.zeros_like(scr.grad_v)
        for head_index in PAIR:
            cols = slice(head_index * HEAD_DIM, (head_index + 1) * HEAD_DIM)
            for tile_index in range(seq // tile):
                reach = (tile_index + 1) * tile
                rows = slice(tile_index * tile, reach)
                probs, queries = scores_softmax(ins.qkv, seg_row, seg_col, head_index, tile_index, tile)
                grad_ctx = scr.grad_ctx[rows, cols]
                grad_probs = dot(ins.qkv[:reach, 3 * HEAD_DIM:], grad_ctx, NT)
                centre = jnp.sum(grad_probs * probs, axis=0, keepdims=True)
                grad_scores = (probs * (grad_probs - centre) * HEAD_DIM ** -0.5).astype(BF16)
                scr.grad_v[:reach, :] += dot(probs.astype(BF16), grad_ctx, NN)
                scr.grad_k[:reach, :] += dot(grad_scores, queries, NN)
                outs.dqkv[rows, cols] = dot(keys_t[:, :reach], grad_scores, NN).T.astype(BF16)
        outs.dqkv[:, 2 * HEAD_DIM:3 * HEAD_DIM] = scr.grad_k[...].astype(BF16)
        outs.dqkv[:, 3 * HEAD_DIM:] = scr.grad_v[...].astype(BF16)

    dma = pltpu.SemaphoreType.DMA
    ins = dict(resid=(resid, ANY), seg=(seg_ids, VMEM), w_outs=[(weight, ANY) for weight in w_outs], qkv=(qkv, VMEM), token=(token, ANY))
    outs = dict(dqkv=(shape((seq, depth)), VMEM))
    scratch = dict(resid=pltpu.VMEM((seq, width), BF16), w=pltpu.VMEM((2 * HEAD_DIM, width), BF16), grad_ctx=pltpu.VMEM((seq, 2 * HEAD_DIM), BF16),
                   grad_k=pltpu.VMEM((seq, HEAD_DIM), F32), grad_v=pltpu.VMEM((seq, HEAD_DIM), F32), w_sem=dma((K2,)), in_sem=dma((4,)))
    return call_kernel('attention_backward', body, ins, outs, scratch, 4e9).dqkv


def weight_grads_mlp(mixed_full, grad_out, resid_full, lefts, ctxs):
    seq, width = grad_out.shape[1:]
    depth, head = lefts[K0].shape[K0] // 3, ctxs[K1].shape[K1]
    tile = min(512, width)

    def kernel(m_ref, dy_ref, dh_ref, left_own, left_other, ctx_own, ctx_other, out_gate, out_up, out_down, out_o, token, ctx_t):
        core = lax.rem(lax.axis_index('tp'), 2)

        @pl.when(pl.program_id(0) == 0)
        def _():
            for half, ref in enumerate((ctx_own, ctx_other)):
                ctx_t[half] = ref[:, :head].T

        token[...] = jnp.zeros_like(token)
        halves = (core, 1 - core)
        lefts = (left_own, left_other)

        def product(base, size, ref):
            own, other = (dot(left[base:base + size, :], ref[half], NN) for left, half in zip(lefts, halves))
            return own + other

        both = product(0, 2 * depth, m_ref)
        out_gate[...] = both[:depth]
        out_up[...] = both[depth:]
        out_down[...] = product(2 * depth, depth, dy_ref)
        out_o[...] = dot(ctx_t[K0], dh_ref[core], NN) + dot(ctx_t[K1], dh_ref[1 - core], NN)

    slab = pl.BlockSpec((2, seq, tile), lambda step: (0, 0, step))
    out = lambda size: pl.BlockSpec((size, tile), lambda step: (0, step))
    token = (8, HEAD_DIM)
    return pl.pallas_call(
        kernel,
        name='weight_grads_mlp',
        grid=(width // tile,),
        out_shape=[shape((depth, width), F32)] * 3 + [shape((head, width), F32), shape(token, F32)],
        in_specs=[slab] * 3 + [VMEM] * 4,
        out_specs=[out(depth)] * 3 + [out(head), pl.BlockSpec(token, lambda step: (0, 0))],
        scratch_shapes=[pltpu.VMEM((2, head, seq), BF16)],
        compiler_params=pltpu.CompilerParams(vmem_limit_bytes=LIMIT),
        cost_estimate=pl.CostEstimate(flops=int(18e9), bytes_accessed=int(6e7), transcendentals=0),
    )(mixed_full, grad_out, resid_full, *lefts, *ctxs)


def weight_grads_qkv(lefts, kv_full, grads_q):
    width, seq = lefts[K0].shape
    head = grads_q[K1].shape[K1]
    kv_width = kv_full.shape[K2] // 2
    tile = min(256, width)

    def kernel(a_own, a_other, kv_ref, q_own, q_other, out_q, out_k, out_v):
        core = lax.rem(lax.axis_index('tp'), 2)
        for index, out in enumerate((out_k, out_v)):
            at = pl.ds(index * kv_width, kv_width)
            out[...] = dot(a_own[...], kv_ref[core, :, at], NN) + dot(a_other[...], kv_ref[1 - core, :, at], NN)
        out_q[...] = dot(a_own[...], q_own[:, :head], NN) + dot(a_other[...], q_other[...], NN)

    slab = pl.BlockSpec((tile, seq), lambda step: (step, 0))
    out = lambda size: pl.BlockSpec((tile, size), lambda step: (step, 0))
    return pl.pallas_call(
        kernel,
        name='weight_grads_qkv',
        grid=(width // tile,),
        out_shape=[shape((width, size), F32) for size in (head, kv_width, kv_width)],
        in_specs=[slab] * 2 + [VMEM] * 3,
        out_specs=[out(size) for size in (head, kv_width, kv_width)],
        compiler_params=pltpu.CompilerParams(vmem_limit_bytes=LIMIT),
        cost_estimate=pl.CostEstimate(flops=int(27e9), bytes_accessed=int(6e7), transcendentals=0),
    )(*lefts, kv_full, *grads_q)


def in_place(gathered, rows):
    blocks, _, width = gathered.shape
    slots = 8

    def kernel(src, dst, buf, in_sem, out_sem):
        def load(index):
            return pltpu.make_async_copy(src.at[index, pl.ds(0, rows), :], buf.at[index % slots], in_sem.at[index % slots])

        def store(index):
            return pltpu.make_async_copy(buf.at[index % slots], dst.at[index % 2, index // 2], out_sem.at[index % slots])

        ahead = slots // 2
        for index in range(blocks + ahead):
            if index < blocks:
                if index >= slots:
                    store(index - slots).wait()
                load(index).start()
            if index >= ahead:
                load(index - ahead).wait()
                store(index - ahead).start()
        for index in range(blocks - slots, blocks):
            store(index).wait()

    return pl.pallas_call(
        kernel,
        name='in_place',
        out_shape=shape((2, blocks // 2, rows, width)),
        in_specs=[ANY],
        out_specs=ANY,
        scratch_shapes=[pltpu.VMEM((slots, rows, width), BF16), pltpu.SemaphoreType.DMA((slots,)), pltpu.SemaphoreType.DMA((slots,))],
        compiler_params=pltpu.CompilerParams(vmem_limit_bytes=LIMIT),
        cost_estimate=pl.CostEstimate(flops=int(2e7), bytes_accessed=int(2e7), transcendentals=0),
    )(gathered)


def solution(mesh):
    tp_size = mesh.shape['tp']
    chips = tp_size // 2
    side = math.isqrt(chips)

    def device_step(hidden, seg_ids, grad_out, gain_attn, gain_mlp, w_q, w_k, w_v, w_o, w_gate, w_up, w_down):
        seq_len, width = hidden.shape[1:]
        kv_heads = w_k.shape[K1] // HEAD_DIM
        per_kv = tp_size // kv_heads
        rows = seq_len // chips

        def flat(value):
            return value.reshape(seq_len, value.shape[-1])

        gain_attn_row = gain_attn[None, :]
        gain_mlp_row = gain_mlp[None, :]

        attn = attention_forward(hidden, seg_ids, gain_attn_row, w_q, w_k, w_v, w_o, per_kv)
        w_qs, w_outs = (w_q, attn.w_q), (w_o, attn.w_o)
        mlp = sum_attention(side, attn, w_outs, hidden, grad_out, gain_mlp_row, w_gate.T, w_up.T, w_down)
        mixed_full = mlp.full.reshape(2, seq_len, width)
        second = sum_mlp(side, mlp, (w_gate.T, mlp.w_gate), (w_up.T, mlp.w_up), (w_down, mlp.w_down), grad_out, gain_mlp_row)
        resid_full = second.full.reshape(2, seq_len, width)

        y_out = in_place(lax.all_gather(second.y_rows, 'tp'), rows).reshape(2, seq_len, width)
        grad_gate_t, grad_up_t, grad_w_down, grad_w_o, token = weight_grads_mlp(mixed_full, grad_out, resid_full, (second.left, second.left_other), (attn.ctx, flat(mlp.ctx_other)))
        dqkv = attention_backward(flat(second.own), seg_ids, w_outs, attn.qkv, token)
        third = sum_input(side, dqkv, w_qs, w_k, w_v, hidden, second.d_rows, gain_attn_row, second.gain, (attn.normed, mlp.normed_other))

        gathered = lax.all_gather(third.rows, 'tp')
        grad_in = in_place(gathered, rows).reshape(2, seq_len, width)
        gain_grads = jnp.sum(gathered[:, rows:].astype(F32), axis=0)
        grad_gain_attn = gain_grads[K0] + gain_grads[K1] + gain_grads[K2]
        grad_gain_mlp = gain_grads[K3] + gain_grads[4] + gain_grads[5]
        grad_w_q, grad_w_k, grad_w_v = weight_grads_qkv(third.lefts, third.kv, (dqkv, flat(third.q_other)))
        return (y_out, grad_in, grad_gain_attn, grad_gain_mlp, grad_w_q, grad_w_k, grad_w_v, grad_w_o, grad_gate_t.T, grad_up_t.T, grad_w_down)

    spec_act = P('data', None, None)
    spec_rows = P('data', None)
    spec_gain = P(None)
    spec_cols = P(None, 'tp')
    spec_tprows = P('tp', None)
    spec_whole = P(None, None)
    spec_stack = P(('data', 'tp'), None)
    in_specs = (spec_act, spec_rows, spec_act, spec_gain, spec_gain, spec_cols, spec_whole, spec_whole, spec_tprows, spec_cols, spec_cols, spec_tprows)
    out_specs = (spec_act, spec_act, P('data'), P('data'), P('data', 'tp'), spec_rows, spec_rows, spec_stack, P('data', 'tp'), P('data', 'tp'), spec_stack)
    return jax.shard_map(device_step, mesh=mesh, in_specs=in_specs, out_specs=out_specs, check_vma=False)
```

time: 493 us -> 454 us (0.921)
  Pallas kernels: 430 us -> 413 us
  waiting for transfers between devices: 27.8 us -> 16.1 us
  local copies, waits for them, and re-layouts: 5.47 us -> 0 us
    pallas_call x6 -> x5, Pallas kernels: 341 us -> 327 us  [call_kernel(): pl.pallas_call(kernel, name=name, out_shape=[leaf[K0] for leaf in out_lea...]
    ppermute x5 -> x0, waiting for transfers between devices: 13.5 us -> none  [swap(): return lax.ppermute(value, 'tp', swap_pairs)]
  transfers between devices with their start and end apart: 7 -> 2, of which waited for: 2 -> 1; matrix products, arithmetic and copies ran while one was open for 1% -> 0% of each run, Pallas kernels for 54% -> 36%
where the time goes in v4:
time: 454 us; the launch traced here: 446 us
  Pallas kernels  413 us (91%)
  waiting for transfers between devices  16.1 us (4%)
  between operations  14.6 us (3%)
    pallas_call x5, Pallas kernels, call_kernel(): pl.pallas_call(kernel, name=name, out_shape=[leaf[K0] for leaf in out_lea...  327 us
    pallas_call x1, Pallas kernels, weight_grads_qkv(): pl.pallas_call(kernel, name='weight_grads_qkv', grid=(width // tile,), ou...  37.2 us
    pallas_call x1, Pallas kernels, weight_grads_mlp(): pl.pallas_call(kernel, name='weight_grads_mlp', grid=(width // tile,), ou...  27.8 us
    pallas_call x2, Pallas kernels, in_place(): pl.pallas_call(kernel, name='in_place', out_shape=shape((2, blocks // 2,...  21.3 us
    all_gather x1, waiting for transfers between devices, device_step(): gathered = lax.all_gather(third.rows, 'tp')  15.9 us
  transfers between devices with their start and end apart: 2, of which 1 were waited for; matrix products, arithmetic and copies ran while one was open for 0% of the time, Pallas kernels for 36%

profile of v4, /device:TPU:97, one launch (start us, length us, event | category | flops | bytes accessed | tf_op | source)
XLA Modules:
  0.0 446.2 jit_solution(8034457405439845552)
XLA Ops:
  7.2 0.1 all-gather.5.cloned.1.call-start
  7.3 18.1 %attention_forward.1 = (bf16[768,256]{1,0:T(8,128)(2,1)}, bf16[768,4096]{1,0:T(8,128)(2,1)}, bf16[768,512]{1,0:T(8,128)(2,1)}, bf16[128,4096]{1,0:T(8,128)(2,1)}, bf16[4096,128]{1,0:T(8,128)(2,1)}) custom-call(f32[1,4096]{1,0:T(1,128)} %bitcast.32, bf16[2,768,4096]{2,1,0:T(8,128)(2,1)} %refs_4_.5, s32[2,768]{1,0:T(2,128)} %refs_2_.5, ...), custom_call_target="tpu_custom_call" | custom-call | flops 5000000000 | bytes 40000000 | tf_op jit(solution)/shard_map/attention_forward/pallas_call | solution.py:494
  25.4 98.7 %sum_attention.1 = (bf16[4,4,48,448]{3,2,1,0:T(8,128)(2,1)}, bf16[4,4,48,448]{3,2,1,0:T(8,128)(2,1)}, bf16[4,4,48,128]{3,2,1,0:T(8,128)(2,1)}, bf16[2,4,4,48,409...) custom-call(bf16[4,4,48,256]{3,2,1,0:T(8,128)(2,1)} %bitcast.29, ...), custom_call_target="tpu_custom_call" | custom-call | flops 400000000 | bytes 40000000 | tf_op jit(solution)/shard_map/sum_attention/pallas_call | solution.py:494
  124.1 126.2 %sum_mlp.1 = (f32[48,4096]{1,0:T(8,128)}, bf16[2,4,4,48,4096]{4,3,2,1,0:T(8,128)(2,1)}, f32[1,4096]{1,0:T(1,128)}, bf16[1344,768]{1,0:T(8,128)(2,1)}, bf16[1344,...) custom-call(bf16[4,4,48,448]{3,2,1,0:T(8,128)(2,1)} %get-tuple-element.52.refs_0_, ...), custom_call_target="tpu_custom_call" | custom-call | flops 600000000 | bytes 40000000 | tf_op jit(solution)/shard_map/sum_mlp/pallas_call | solution.py:494
  250.3 0.1 all-gather.5.cloned.1.call-update
  250.3 0.1 all-gather.7.cloned.1.call-start
  250.4 27.8 %weight_grads_mlp.1 = (f32[448,4096]{1,0:T(8,128)}, f32[448,4096]{1,0:T(8,128)}, f32[448,4096]{1,0:T(8,128)}, f32[128,4096]{1,0:T(8,128)}, f32[8,128]{1,0:T(8,128)}) custom-call(bf16[2,768,4096]{2,1,0:T(8,128)(2,1)} %bitcast.36, bf16[2,768,4096]{2,1,0:T(8,128)(2,1)} %dy_ref.1, bf16[2,768,4096]{2,1,0:T(8,128)(2,1)} %bitcast.37, ...), custom_call_target="tpu_custom_call" | custom-call | flops 17999998976 | bytes 60000000 | tf_op jit(solution)/shard_map/weight_grads_mlp/pallas_call | solution.py:966
  278.2 14.2 %attention_backward.1.q_own = bf16[768,512]{1,0:T(8,128)(2,1)} custom-call(bf16[768,512]{1,0:T(8,128)(2,1)} %get-tuple-element.64.refs_0_, bf16[768,4096]{1,0:T(8,128)(2,1)} %bitcast.38, s32[2,768]{1,0:T(2,128)} %refs_2_.5, f32[8,128]{1,0:T(8,128)} %get-tuple-element.71.refs_3_, bf16[128,4096]{1,0:T(8,128)(2,1)} %refs_4_.4, ...), custom_call_target="tpu_custom_call" | custom-call | flops 4000000000 | bytes 40000000 | tf_op jit(solution)/shard_map/attention_backward/pallas_call | solution.py:494
  292.4 69.3 %sum_input.1 = (bf16[2,768,2048]{2,1,0:T(8,128)(2,1)}, bf16[4096,768]{1,0:T(8,128)(2,1)}, bf16[4096,768]{1,0:T(8,128)(2,1)}, bf16[4,4,48,128]{3,2,1,0:T(8,128)(2,1)}, bf16[56,4096]{1,0:T(8,128)(2,1)}) custom-call(f32[48,4096]{1,0:T(8,128)} %get-tuple-element.63.refs_0_, bf16[4,4,48,512]{3,2,1,0:T(8,128)(2,1)} %bitcast.28, f32[1,4096]{1,0:T(1,128)} %bitcast.33, ...), custom_call_target="tpu_custom_call" | custom-call | flops 300000000 | bytes 40000000 | tf_op jit(solution)/shard_map/sum_input/pallas_call | solution.py:494
  361.7 0.1 all-gather.7.cloned.1.call-update
  361.8 37.2 %weight_grads_qkv.1 = (f32[4096,128]{1,0:T(8,128)}, f32[4096,1024]{1,0:T(8,128)}, f32[4096,1024]{1,0:T(8,128)}) custom-call(bf16[4096,768]{1,0:T(8,128)(2,1)} %get-tuple-element.76.a_own, bf16[4096,768]{1,0:T(8,128)(2,1)} %get-tuple-element.77.a_other, bf16[2,768,2048]{2,1,0:T(8,128)(2,1)} %get-tuple-element.78.kv_ref, ...), custom_call_target="tpu_custom_call" | custom-call | flops 27000000512 | bytes 60000000 | tf_op jit(solution)/shard_map/weight_grads_qkv/pallas_call | solution.py:994
  399.0 0.0 all-gather.5.cloned.1.call-done
  399.0 10.7 %in_place.2 = bf16[2,16,48,4096]{3,2,1,0:T(8,128)(2,1)} custom-call(bf16[32,48,4096]{2,1,0:T(8,128)(2,1)} %bitcast.25), custom_call_target="tpu_custom_call" | custom-call | flops 20000000 | bytes 20000000 | tf_op jit(solution)/shard_map/in_place/pallas_call | solution.py:1029
  409.7 15.9 %all-gather.7.cloned.1.call-done = bf16[1792,4096]{1,0:T(8,128)(2,1)} async-done(((bf16[56,4096]{1,0:T(8,128)(2,1)}), bf16[1792,4096]{1,0:T(8,128)(2,1)}) %all-gather.7.cloned.1.call-update) | async-done | bytes 14680080 | tf_op jit(solution)/shard_map/all_gather | solution.py:1070
  425.6 10.7 %in_place.3 = bf16[2,16,48,4096]{3,2,1,0:T(8,128)(2,1)} custom-call(bf16[32,56,4096]{2,1,0:T(8,128)(2,1)} %bitcast.19), custom_call_target="tpu_custom_call" | custom-call | flops 20000000 | bytes 20000000 | tf_op jit(solution)/shard_map/in_place/pallas_call | solution.py:1029
  436.3 1.9 convert_reduce_fusion
  438.2 0.7 slice_add_fusion
Async XLA Ops:
  7.2 391.8 %all-gather.5.cloned.1.call-start = ((), (), s32[]{:S(2)}) async-start(), calls=%async_computation | async-start | bytes 12976128 | tf_op jit(solution)/shard_map/all_gather | solution.py:1065
  250.3 175.3 %all-gather.7.cloned.1.call-start = ((), (), s32[]{:S(2)}) async-start(), calls=%async_computation.1 | async-start | bytes 15138816 | tf_op jit(solution)/shard_map/all_gather | solution.py:1070
Sparse Core Ops, SparseCore 0:
  250.5 58.9 all-gather.4
  361.9 63.6 all-gather.6

commit v5 on v4

--- a/solution.py
+++ b/solution.py
@@ -714,7 +714,7 @@
     return call_kernel('sum_mlp', body, ins, outs, scratch, 6e8, 2)
 
 
-def sum_input(side, dqkv, w_qs, w_k, w_v, hidden, d_rows, gain, gain_mlp_part, normeds):
+def sum_input(side, dqkv, w_qs, w_k, w_v, hidden, second, gain, normeds):
     seq, depth = dqkv.shape
     width = gain.shape[K1]
     rows = seq // (side * side)
@@ -772,6 +772,7 @@
             back, gain_part = rms_back(scr.x_rows[at, :].astype(F32), ins.gain[...], part[(*own, at, slice(None))].astype(F32))
             gain_total = gain_total + gain_part
             outs.rows[at, :] = (ins.d_rows[at, :] + back).astype(BF16)
+            outs.rows[pl.ds(rows + at.start, at.size), :] = ins.y_rows[at, :]
         row = lax.broadcasted_iota(jnp.int32, (8, width), 0)
         extra = jnp.zeros((8, width), F32)
         for index, value in enumerate((gain_total, ins.gain_mlp[...])):
@@ -779,15 +780,15 @@
                 rounded = value.astype(BF16).astype(F32)
                 extra = jnp.where(row == index * 3 + level, rounded, extra)
                 value = value - rounded
-        outs.rows[rows:rows + 8, :] = extra.astype(BF16)
+        outs.rows[2 * rows:2 * rows + 8, :] = extra.astype(BF16)
         gather.store.drain()
         swap_end(torus, scr.swap_sems, swaps)
         torus.drain()
 
     dma = pltpu.SemaphoreType.DMA
-    ins = dict(dqkv=(dqkv.reshape(side, side, rows, depth), VMEM), w_qs=[(weight, ANY) for weight in w_qs], w_k=(w_k, ANY), w_v=(w_v, ANY), hidden=(hidden, ANY), d_rows=(d_rows, VMEM), normeds=[(normed, ANY) for normed in normeds],
-               gain=(gain, VMEM), gain_mlp=(gain_mlp_part, VMEM))
-    outs = dict(rows=(shape((rows + 8, width)), VMEM), kv=(shape((2, seq, 2 * kv_width)), ANY), lefts=[(shape((width, seq)), ANY)] * 2, q_other=(shape((side, side, rows, head)), ANY))
+    ins = dict(dqkv=(dqkv.reshape(side, side, rows, depth), VMEM), w_qs=[(weight, ANY) for weight in w_qs], w_k=(w_k, ANY), w_v=(w_v, ANY), hidden=(hidden, ANY), d_rows=(second.d_rows, VMEM), y_rows=(second.y_rows, VMEM), normeds=[(normed, ANY) for normed in normeds],
+               gain=(gain, VMEM), gain_mlp=(second.gain, VMEM))
+    outs = dict(rows=(shape((2 * rows + 8, width)), VMEM), kv=(shape((2, seq, 2 * kv_width)), ANY), lefts=[(shape((width, seq)), ANY)] * 2, q_other=(shape((side, side, rows, head)), ANY))
     scratch = dict(sum=rs_scratch(side, rows, width), all=ag_scratch(side, tokens, 2 * head, 2), x_rows=pltpu.VMEM((rows, width), BF16), x_sem=dma((K1,)), **turner_scratch(seq, min(256, width // 8)), w=pltpu.VMEM((width, depth), BF16), w_sem=dma((K2, 4)),
                    mate=pltpu.VMEM((half_side, side, rows, 2 * head), BF16), mate_sems=[dma((K1,)), dma((K1,))], swap_sems=[dma((K1,)), dma((K1,))])
     return call_kernel('sum_input', body, ins, outs, scratch, 3e8, 3)
@@ -883,7 +884,7 @@
     return call_kernel('attention_forward', body, ins, outs, scratch, 5e9, 4)
 
 
-def attention_backward(resid, seg_ids, w_outs, qkv, token):
+def attention_backward(resid, seg_ids, w_outs, qkv):
     seq, width = resid.shape
     chunk = seq // 4
     tile = min(256, seq)
@@ -926,19 +927,19 @@
         outs.dqkv[:, 3 * HEAD_DIM:] = scr.grad_v[...].astype(BF16)
 
     dma = pltpu.SemaphoreType.DMA
-    ins = dict(resid=(resid, ANY), seg=(seg_ids, VMEM), w_outs=[(weight, ANY) for weight in w_outs], qkv=(qkv, VMEM), token=(token, ANY))
+    ins = dict(resid=(resid, ANY), seg=(seg_ids, VMEM), w_outs=[(weight, ANY) for weight in w_outs], qkv=(qkv, VMEM))
     outs = dict(dqkv=(shape((seq, depth)), VMEM))
     scratch = dict(resid=pltpu.VMEM((seq, width), BF16), w=pltpu.VMEM((2 * HEAD_DIM, width), BF16), grad_ctx=pltpu.VMEM((seq, 2 * HEAD_DIM), BF16),
                    grad_k=pltpu.VMEM((seq, HEAD_DIM), F32), grad_v=pltpu.VMEM((seq, HEAD_DIM), F32), w_sem=dma((K2,)), in_sem=dma((4,)))
     return call_kernel('attention_backward', body, ins, outs, scratch, 4e9).dqkv
 
 
-def weight_grads_mlp(mixed_full, grad_out, resid_full, lefts, ctxs):
+def weight_grads_mlp(mixed_full, grad_out, resid_full, lefts, ctxs, token):
     seq, width = grad_out.shape[1:]
     depth, head = lefts[K0].shape[K0] // 3, ctxs[K1].shape[K1]
     tile = min(512, width)
 
-    def kernel(m_ref, dy_ref, dh_ref, left_own, left_other, ctx_own, ctx_other, out_gate, out_up, out_down, out_o, token, ctx_t):
+    def kernel(m_ref, dy_ref, dh_ref, left_own, left_other, ctx_own, ctx_other, _, out_gate, out_up, out_down, out_o, ctx_t):
         core = lax.rem(lax.axis_index('tp'), 2)
 
         @pl.when(pl.program_id(0) == 0)
@@ -946,7 +947,6 @@
             for half, ref in enumerate((ctx_own, ctx_other)):
                 ctx_t[half] = ref[:, :head].T
 
-        token[...] = jnp.zeros_like(token)
         halves = (core, 1 - core)
         lefts = (left_own, left_other)
 
@@ -962,25 +962,24 @@
 
     slab = pl.BlockSpec((2, seq, tile), lambda step: (0, 0, step))
     out = lambda size: pl.BlockSpec((size, tile), lambda step: (0, step))
-    token = (8, HEAD_DIM)
     return pl.pallas_call(
         kernel,
         name='weight_grads_mlp',
         grid=(width // tile,),
-        out_shape=[shape((depth, width), F32)] * 3 + [shape((head, width), F32), shape(token, F32)],
-        in_specs=[slab] * 3 + [VMEM] * 4,
-        out_specs=[out(depth)] * 3 + [out(head), pl.BlockSpec(token, lambda step: (0, 0))],
+        out_shape=[shape((depth, width), F32)] * 3 + [shape((head, width), F32)],
+        in_specs=[slab] * 3 + [VMEM] * 4 + [ANY],
+        out_specs=[out(depth)] * 3 + [out(head)],
         scratch_shapes=[pltpu.VMEM((2, head, seq), BF16)],
         compiler_params=pltpu.CompilerParams(vmem_limit_bytes=LIMIT),
         cost_estimate=pl.CostEstimate(flops=int(18e9), bytes_accessed=int(6e7), transcendentals=0),
-    )(mixed_full, grad_out, resid_full, *lefts, *ctxs)
+    )(mixed_full, grad_out, resid_full, *lefts, *ctxs, token)
 
 
 def weight_grads_qkv(lefts, kv_full, grads_q):
     width, seq = lefts[K0].shape
     head = grads_q[K1].shape[K1]
     kv_width = kv_full.shape[K2] // 2
-    tile = min(256, width)
+    tile = min(512, width)
 
     def kernel(a_own, a_other, kv_ref, q_own, q_other, out_q, out_k, out_v):
         core = lax.rem(lax.axis_index('tp'), 2)
@@ -1005,34 +1004,47 @@
 
 def in_place(gathered, rows):
     blocks, _, width = gathered.shape
-    slots = 8
-
-    def kernel(src, dst, buf, in_sem, out_sem):
+    slots = 24
+    pieces = 2 * blocks
+
+    def kernel(src, dx_ref, y_ref, gain_attn, gain_mlp, buf, extra, in_sem, out_sem, extra_sem):
+        gains = pltpu.make_async_copy(src.at[:, pl.ds(2 * rows, 8), :], extra, extra_sem.at[K0])
+
         def load(index):
-            return pltpu.make_async_copy(src.at[index, pl.ds(0, rows), :], buf.at[index % slots], in_sem.at[index % slots])
+            at = pl.ds(index // blocks * rows, rows)
+            return pltpu.make_async_copy(src.at[index % blocks, at, :], buf.at[index % slots], in_sem.at[index % slots])
 
         def store(index):
-            return pltpu.make_async_copy(buf.at[index % slots], dst.at[index % 2, index // 2], out_sem.at[index % slots])
+            dst, block = (dx_ref, y_ref)[index // blocks], index % blocks
+            return pltpu.make_async_copy(buf.at[index % slots], dst.at[block % 2, block // 2], out_sem.at[index % slots])
 
         ahead = slots // 2
-        for index in range(blocks + ahead):
-            if index < blocks:
+        for index in range(pieces + ahead):
+            if index < pieces:
                 if index >= slots:
                     store(index - slots).wait()
                 load(index).start()
+            if index == ahead:
+                gains.start()
             if index >= ahead:
                 load(index - ahead).wait()
                 store(index - ahead).start()
-        for index in range(blocks - slots, blocks):
+        gains.wait()
+        total = jnp.sum(extra[...].astype(F32), axis=0)
+        for first, ref in ((0, gain_attn), (3, gain_mlp)):
+            ref[...] = total[first:first + 1] + total[first + 1:first + 2] + total[first + 2:first + 3]
+        for index in range(pieces - slots, pieces):
             store(index).wait()
 
+    dma = pltpu.SemaphoreType.DMA
+    whole = shape((2, blocks // 2, rows, width))
     return pl.pallas_call(
         kernel,
         name='in_place',
-        out_shape=shape((2, blocks // 2, rows, width)),
+        out_shape=[whole, whole, shape((1, width), F32), shape((1, width), F32)],
         in_specs=[ANY],
-        out_specs=ANY,
-        scratch_shapes=[pltpu.VMEM((slots, rows, width), BF16), pltpu.SemaphoreType.DMA((slots,)), pltpu.SemaphoreType.DMA((slots,))],
+        out_specs=[ANY, ANY, VMEM, VMEM],
+        scratch_shapes=[pltpu.VMEM((slots, rows, width), BF16), pltpu.VMEM((blocks, 8, width), BF16), dma((slots,)), dma((slots,)), dma((K1,))],
         compiler_params=pltpu.CompilerParams(vmem_limit_bytes=LIMIT),
         cost_estimate=pl.CostEstimate(flops=int(2e7), bytes_accessed=int(2e7), transcendentals=0),
     )(gathered)
@@ -1062,18 +1074,14 @@
         second = sum_mlp(side, mlp, (w_gate.T, mlp.w_gate), (w_up.T, mlp.w_up), (w_down, mlp.w_down), grad_out, gain_mlp_row)
         resid_full = second.full.reshape(2, seq_len, width)
 
-        y_out = in_place(lax.all_gather(second.y_rows, 'tp'), rows).reshape(2, seq_len, width)
-        grad_gate_t, grad_up_t, grad_w_down, grad_w_o, token = weight_grads_mlp(mixed_full, grad_out, resid_full, (second.left, second.left_other), (attn.ctx, flat(mlp.ctx_other)))
-        dqkv = attention_backward(flat(second.own), seg_ids, w_outs, attn.qkv, token)
-        third = sum_input(side, dqkv, w_qs, w_k, w_v, hidden, second.d_rows, gain_attn_row, second.gain, (attn.normed, mlp.normed_other))
-
-        gathered = lax.all_gather(third.rows, 'tp')
-        grad_in = in_place(gathered, rows).reshape(2, seq_len, width)
-        gain_grads = jnp.sum(gathered[:, rows:].astype(F32), axis=0)
-        grad_gain_attn = gain_grads[K0] + gain_grads[K1] + gain_grads[K2]
-        grad_gain_mlp = gain_grads[K3] + gain_grads[4] + gain_grads[5]
+        dqkv = attention_backward(flat(second.own), seg_ids, w_outs, attn.qkv)
+        third = sum_input(side, dqkv, w_qs, w_k, w_v, hidden, second, gain_attn_row, (attn.normed, mlp.normed_other))
+
+        grad_in, y_out, grad_gain_attn, grad_gain_mlp = in_place(lax.all_gather(third.rows, 'tp'), rows)
+        grad_gate_t, grad_up_t, grad_w_down, grad_w_o = weight_grads_mlp(
+            mixed_full, grad_out, resid_full, (second.left, second.left_other), (attn.ctx, flat(mlp.ctx_other)), third.q_other)
         grad_w_q, grad_w_k, grad_w_v = weight_grads_qkv(third.lefts, third.kv, (dqkv, flat(third.q_other)))
-        return (y_out, grad_in, grad_gain_attn, grad_gain_mlp, grad_w_q, grad_w_k, grad_w_v, grad_w_o, grad_gate_t.T, grad_up_t.T, grad_w_down)
+        return (y_out.reshape(hidden.shape), grad_in.reshape(hidden.shape), grad_gain_attn[K0], grad_gain_mlp[K0], grad_w_q, grad_w_k, grad_w_v, grad_w_o, grad_gate_t.T, grad_up_t.T, grad_w_down)
 
     spec_act = P('data', None, None)
     spec_rows = P('data', None)

time: 454 us -> 456 us (level)
  waiting for transfers between devices: 16.1 us -> 28.4 us
  Pallas kernels: 413 us -> 406 us
    all_gather x2 -> x1, waiting for transfers between devices: 15.9 us -> 28.4 us  [device_step(): lax.all_gather(third.rows, 'tp')]
    pallas_call x2 -> x1, Pallas kernels: 21.3 us -> 18.7 us  [in_place(): pl.pallas_call(kernel, name='in_place', out_shape=[whole, whole, shape((1...]
  transfers between devices with their start and end apart: 2 -> 1, of which waited for: 1 -> 1; matrix products, arithmetic and copies ran while one was open for 0% -> 0% of each run, Pallas kernels for 36% -> 14%
where the time goes in v5:
time: 456 us; the launch traced here: 449 us
  Pallas kernels  406 us (89%)
  waiting for transfers between devices  28.4 us (6%)
  between operations  14.6 us (3%)
    pallas_call x5, Pallas kernels, call_kernel(): pl.pallas_call(kernel, name=name, out_shape=[leaf[K0] for leaf in out_lea...  323 us
    pallas_call x1, Pallas kernels, weight_grads_qkv(): pl.pallas_call(kernel, name='weight_grads_qkv', grid=(width // tile,), ou...  36.5 us
    all_gather x1, waiting for transfers between devices, device_step(): lax.all_gather(third.rows, 'tp')  28.4 us
    pallas_call x1, Pallas kernels, weight_grads_mlp(): pl.pallas_call(kernel, name='weight_grads_mlp', grid=(width // tile,), ou...  27.8 us
    pallas_call x1, Pallas kernels, in_place(): pl.pallas_call(kernel, name='in_place', out_shape=[whole, whole, shape((1...  18.7 us
  transfers between devices with their start and end apart: 1, of which 1 were waited for; matrix products, arithmetic and copies ran while one was open for 0% of the time, Pallas kernels for 14%

profile of v5, /device:TPU:97, one launch (start us, length us, event | category | flops | bytes accessed | tf_op | source)
XLA Modules:
  0.0 449.3 jit_solution(2175420193664827863)
XLA Ops:
  7.2 0.1 all-gather.3.cloned.1.call-start
  7.3 18.1 %attention_forward.1 = (bf16[768,256]{1,0:T(8,128)(2,1)}, bf16[768,4096]{1,0:T(8,128)(2,1)}, bf16[768,512]{1,0:T(8,128)(2,1)}, bf16[128,4096]{1,0:T(8,128)(2,1)}, bf16[4096,128]{1,0:T(8,128)(2,1)}) custom-call(f32[1,4096]{1,0:T(1,128)} %bitcast.27, bf16[2,768,4096]{2,1,0:T(8,128)(2,1)} %refs_4_.3, s32[2,768]{1,0:T(2,128)} %refs_2_.5, ...), custom_call_target="tpu_custom_call" | custom-call | flops 5000000000 | bytes 40000000 | tf_op jit(solution)/shard_map/attention_forward/pallas_call | solution.py:494
  25.3 98.7 %sum_attention.1 = (bf16[4,4,48,448]{3,2,1,0:T(8,128)(2,1)}, bf16[4,4,48,448]{3,2,1,0:T(8,128)(2,1)}, bf16[4,4,48,128]{3,2,1,0:T(8,128)(2,1)}, bf16[2,4,4,48,409...) custom-call(bf16[4,4,48,256]{3,2,1,0:T(8,128)(2,1)} %bitcast.24, ...), custom_call_target="tpu_custom_call" | custom-call | flops 400000000 | bytes 40000000 | tf_op jit(solution)/shard_map/sum_attention/pallas_call | solution.py:494
  124.0 126.1 %sum_mlp.1 = (f32[48,4096]{1,0:T(8,128)}, bf16[2,4,4,48,4096]{4,3,2,1,0:T(8,128)(2,1)}, f32[1,4096]{1,0:T(1,128)}, bf16[1344,768]{1,0:T(8,128)(2,1)}, bf16[1344,...) custom-call(bf16[4,4,48,448]{3,2,1,0:T(8,128)(2,1)} %get-tuple-element.55.refs_0_, ...), custom_call_target="tpu_custom_call" | custom-call | flops 600000000 | bytes 40000000 | tf_op jit(solution)/shard_map/sum_mlp/pallas_call | solution.py:494
  250.2 14.4 %attention_backward.1.q_own = bf16[768,512]{1,0:T(8,128)(2,1)} custom-call(bf16[768,512]{1,0:T(8,128)(2,1)} %get-tuple-element.66.refs_0_, bf16[768,4096]{1,0:T(8,128)(2,1)} %bitcast.33, s32[2,768]{1,0:T(2,128)} %refs_2_.5, bf16[128,4096]{1,0:T(8,128)(2,1)} %refs_3_.7, bf16[128,4096]{1,0:T(8,128)(2,1)} %get-tuple-element.54.refs_8_.refs_4_), custom_call_target="tpu_custom_call" | custom-call | flops 4000000000 | bytes 40000000 | tf_op jit(solution)/shard_map/attention_backward/pallas_call | solution.py:494
  264.6 65.8 %sum_input.1 = (bf16[2,768,2048]{2,1,0:T(8,128)(2,1)}, bf16[4096,768]{1,0:T(8,128)(2,1)}, bf16[4096,768]{1,0:T(8,128)(2,1)}, bf16[4,4,48,128]{3,2,1,0:T(8,128)(2,1)}, bf16[104,4096]{1,0:T(8,128)(2,1)}) custom-call(f32[48,4096]{1,0:T(8,128)} %get-tuple-element.65.refs_0_, bf16[4,4,48,512]{3,2,1,0:T(8,128)(2,1)} %bitcast.23, f32[1,4096]{1,0:T(1,128)} %bitcast.28, ...), custom_call_target="tpu_custom_call" | custom-call | flops 300000000 | bytes 40000000 | tf_op jit(solution)/shard_map/sum_input/pallas_call | solution.py:494
  330.4 0.1 all-gather.3.cloned.1.call-update
  330.5 27.8 %weight_grads_mlp.1 = (f32[448,4096]{1,0:T(8,128)}, f32[448,4096]{1,0:T(8,128)}, f32[448,4096]{1,0:T(8,128)}, f32[128,4096]{1,0:T(8,128)}) custom-call(bf16[2,768,4096]{2,1,0:T(8,128)(2,1)} %bitcast.29, bf16[2,768,4096]{2,1,0:T(8,128)(2,1)} %dy_ref.1, bf16[2,768,4096]{2,1,0:T(8,128)(2,1)} %bitcast.30, bf16[1344,768]{1,0:T(8,128)(2,1)} %get-tuple-element.86.left_own, ...), custom_call_target="tpu_custom_call" | custom-call | flops 17999998976 | bytes 60000000 | tf_op jit(solution)/shard_map/weight_grads_mlp/pallas_call | solution.py:965
  358.3 36.5 %weight_grads_qkv.1 = (f32[4096,128]{1,0:T(8,128)}, f32[4096,1024]{1,0:T(8,128)}, f32[4096,1024]{1,0:T(8,128)}) custom-call(bf16[4096,768]{1,0:T(8,128)(2,1)} %get-tuple-element.77.a_own, bf16[4096,768]{1,0:T(8,128)(2,1)} %get-tuple-element.78.a_other, bf16[2,768,2048]{2,1,0:T(8,128)(2,1)} %get-tuple-element.79.kv_ref, ...), custom_call_target="tpu_custom_call" | custom-call | flops 27000000512 | bytes 60000000 | tf_op jit(solution)/shard_map/weight_grads_qkv/pallas_call | solution.py:993
  394.8 28.4 %all-gather.3.cloned.1.call-done = bf16[3328,4096]{1,0:T(8,128)(2,1)} async-done(((bf16[104,4096]{1,0:T(8,128)(2,1)}), bf16[3328,4096]{1,0:T(8,128)(2,1)}) %all-gather.3.cloned.1.call-update) | async-done | bytes 27262992 | tf_op jit(solution)/shard_map/all_gather | solution.py:1080
  423.2 18.7 %in_place.1 = (bf16[2,16,48,4096]{3,2,1,0:T(8,128)(2,1)}, bf16[2,16,48,4096]{3,2,1,0:T(8,128)(2,1)}, f32[1,4096]{1,0:T(1,128)}, f32[1,4096]{1,0:T(1,128)}) custom-call(bf16[32,104,4096]{2,1,0:T(8,128)(2,1)} %bitcast.18), custom_call_target="tpu_custom_call" | custom-call | flops 20000000 | bytes 20000000 | tf_op jit(solution)/shard_map/in_place/pallas_call | solution.py:1041
Async XLA Ops:
  7.2 416.0 %all-gather.3.cloned.1.call-start = ((), (), s32[]{:S(2)}) async-start(), calls=%async_computation | async-start | bytes 28114944 | tf_op jit(solution)/shard_map/all_gather | solution.py:1080
Sparse Core Ops, SparseCore 0:
  330.6 92.5 all-gather.2

commit v6 on v5

--- a/solution.py
+++ b/solution.py
@@ -412,57 +412,6 @@
             torus.arrive(dst, sems, index)
 
 
-class Turner:
-    def __init__(self, src, dst, scr):
-        self.src, self.dst, self.scr = src, dst, scr
-        self.unit = scr.turn_in.shape[K2]
-        self.count = src.shape[K1] // self.unit
-
-    def load(self, index):
-        at = pl.ds(pl.multiple_of(index * self.unit, self.unit), self.unit)
-        slot = lax.rem(index, 2)
-        return pltpu.make_async_copy(self.src.at[:, at], self.scr.turn_in.at[slot], self.scr.turn_in_sem.at[slot])
-
-    def save(self, index):
-        at = pl.ds(pl.multiple_of(index * self.unit, self.unit), self.unit)
-        slot = lax.rem(index, 2)
-        return pltpu.make_async_copy(self.scr.turn_out.at[slot], self.dst.at[at, :], self.scr.turn_out_sem.at[slot])
-
-    def steps(self, parts):
-        each = self.count // parts
-
-        def step(part):
-            if part == 0:
-                self.load(0).start()
-
-            def body(index, carry):
-                @pl.when(index + 1 < self.count)
-                def _():
-                    self.load(index + 1).start()
-
-                self.load(index).wait()
-
-                @pl.when(index >= 2)
-                def _():
-                    self.save(index - 2).wait()
-
-                self.scr.turn_out[lax.rem(index, 2)] = self.scr.turn_in[lax.rem(index, 2)].T
-                self.save(index).start()
-                return carry
-
-            lax.fori_loop(part * each, (part + 1) * each, body, 0)
-            if part == parts - 1:
-                self.save(self.count - 2).wait()
-                self.save(self.count - 1).wait()
-
-        return [functools.partial(step, part) for part in range(parts)]
-
-
-def turner_scratch(rows, unit):
-    dma = pltpu.SemaphoreType.DMA
-    return dict(turn_in=pltpu.VMEM((2, rows, unit), BF16), turn_out=pltpu.VMEM((2, unit, rows), BF16), turn_in_sem=dma((K2,)), turn_out_sem=dma((K2,)))
-
-
 def row_tiles(rows):
     return [pl.ds(start, 16) for start in range(0, rows, 16)]
 
@@ -654,6 +603,9 @@
 
         turned = []
 
+        def half_at(half):
+            return pl.ds(pl.multiple_of(half * seq, seq), seq)
+
         def turn(index):
             kind, core = index // 2, index % 2
             src = (ins.grads[2 * core], ins.grads[2 * core + 1], ins.acts[core])[kind]
@@ -661,13 +613,13 @@
             if index >= 2:
                 turned[index - 2]()
             scr.turn[slot] = src[...].reshape(seq, depth).T
-            at = pl.ds(kind * depth, depth)
+            at = pl.ds(kind * depth, depth), half_at(torus.core)
             if core == 0:
-                save = pltpu.make_async_copy(scr.turn.at[slot], outs.left.at[at, :], scr.turn_sem.at[kind])
+                save = pltpu.make_async_copy(scr.turn.at[slot], outs.left.at[at], scr.turn_sem.at[kind])
                 save.start()
                 turned.append(save.wait)
             else:
-                torus.send(scr.turn.at[slot], outs.left_other.at[at, :], scr.swap_sems, kind, torus.partner)
+                torus.send(scr.turn.at[slot], outs.left.at[at], scr.swap_sems, kind, torus.partner)
                 turned.append(torus.pending.pop().wait_send)
 
         turns = [functools.partial(turn, index) for index in range(6)]
@@ -698,7 +650,7 @@
         turned[4]()
         turned[5]()
         for kind in range(3):
-            torus.arrive(outs.left_other.at[pl.ds(kind * depth, depth), :], scr.swap_sems, kind)
+            torus.arrive(outs.left.at[pl.ds(kind * depth, depth), half_at(1 - torus.core)], scr.swap_sems, kind)
         gather.store.drain()
         torus.drain()
 
@@ -706,15 +658,14 @@
     ins = dict(grads=[(grad, VMEM) for grad in (mlp.gates[K0], mlp.ups[K0], mlp.gates[K1], mlp.ups[K1])], acts=[(act, VMEM) for act in mlp.acts],
                w_in=[(weight, ANY) for weight in (w_gates[K0], w_ups[K0], w_gates[K1], w_ups[K1])], w_downs=[(weight, ANY) for weight in w_downs],
                h_rows=(mlp.h_rows, VMEM), grad_out=(grad_out, ANY), gain=(gain, VMEM))
-    left = (shape((3 * depth, seq)), ANY)
-    outs = dict(full=(shape((2, *block)), ANY), own=(shape(block), ANY), d_rows=(shape((rows, width), F32), VMEM), gain=(shape((1, width), F32), VMEM), y_rows=(shape((rows, width)), VMEM), left=left, left_other=left)
+    outs = dict(full=(shape((2, *block)), ANY), own=(shape(block), ANY), d_rows=(shape((rows, width), F32), VMEM), gain=(shape((1, width), F32), VMEM), y_rows=(shape((rows, width)), VMEM), left=(shape((3 * depth, 2 * seq)), ANY))
     scratch = dict(sum=rs_scratch(side, rows, width), sum_p=rs_scratch(side, rows, width), all=ag_scratch(side, rows, width), dy_rows=pltpu.VMEM((rows, width), BF16), dy_sem=dma((K1,)),
                    w=pltpu.VMEM((4 * depth, width), BF16), w_sem=dma((K2, 4)), wd=pltpu.VMEM((2 * depth, width), BF16), wd_sem=dma((K2, K2)),
                    turn=pltpu.VMEM((2, depth, seq), BF16), turn_sem=dma((K3,)), swap_sems=[dma((K3,)), dma((K3,))])
     return call_kernel('sum_mlp', body, ins, outs, scratch, 6e8, 2)
 
 
-def sum_input(side, dqkv, w_qs, w_k, w_v, hidden, second, gain, normeds):
+def sum_input(side, dqkv, w_qs, w_k, w_v, hidden, second, gain):
     seq, depth = dqkv.shape
     width = gain.shape[K1]
     rows = seq // (side * side)
@@ -747,7 +698,6 @@
         rows_at = pl.ds(pl.multiple_of(torus.chip * rows, rows), rows)
         x_load = pltpu.make_async_copy(ins.hidden.at[torus.core, rows_at, :], scr.x_rows, scr.x_sem.at[K0])
         x_load.start()
-        turns = Turner(ins.normeds[K0], outs.lefts[K0], scr).steps(8) + Turner(ins.normeds[K1], outs.lefts[K1], scr).steps(8)
         place = lax.rem(torus.x, 2)
         mate = torus.at_chip(torus.y, torus.x + 1 - 2 * place)
         kv_cols = pl.ds(2 * head, 2 * head)
@@ -765,14 +715,13 @@
         for step in steps[1:5]:
             step()
         mate_add()
-        run(steps[5:], gather.steps(), turns)
+        run(steps[5:], gather.steps())
         x_load.wait()
         gain_total = jnp.zeros((1, width), F32)
         for at in row_tiles(rows):
             back, gain_part = rms_back(scr.x_rows[at, :].astype(F32), ins.gain[...], part[(*own, at, slice(None))].astype(F32))
             gain_total = gain_total + gain_part
             outs.rows[at, :] = (ins.d_rows[at, :] + back).astype(BF16)
-            outs.rows[pl.ds(rows + at.start, at.size), :] = ins.y_rows[at, :]
         row = lax.broadcasted_iota(jnp.int32, (8, width), 0)
         extra = jnp.zeros((8, width), F32)
         for index, value in enumerate((gain_total, ins.gain_mlp[...])):
@@ -780,16 +729,16 @@
                 rounded = value.astype(BF16).astype(F32)
                 extra = jnp.where(row == index * 3 + level, rounded, extra)
                 value = value - rounded
-        outs.rows[2 * rows:2 * rows + 8, :] = extra.astype(BF16)
+        outs.rows[rows:rows + 8, :] = extra.astype(BF16)
         gather.store.drain()
         swap_end(torus, scr.swap_sems, swaps)
         torus.drain()
 
     dma = pltpu.SemaphoreType.DMA
-    ins = dict(dqkv=(dqkv.reshape(side, side, rows, depth), VMEM), w_qs=[(weight, ANY) for weight in w_qs], w_k=(w_k, ANY), w_v=(w_v, ANY), hidden=(hidden, ANY), d_rows=(second.d_rows, VMEM), y_rows=(second.y_rows, VMEM), normeds=[(normed, ANY) for normed in normeds],
+    ins = dict(dqkv=(dqkv.reshape(side, side, rows, depth), VMEM), w_qs=[(weight, ANY) for weight in w_qs], w_k=(w_k, ANY), w_v=(w_v, ANY), hidden=(hidden, ANY), d_rows=(second.d_rows, VMEM),
                gain=(gain, VMEM), gain_mlp=(second.gain, VMEM))
-    outs = dict(rows=(shape((2 * rows + 8, width)), VMEM), kv=(shape((2, seq, 2 * kv_width)), ANY), lefts=[(shape((width, seq)), ANY)] * 2, q_other=(shape((side, side, rows, head)), ANY))
-    scratch = dict(sum=rs_scratch(side, rows, width), all=ag_scratch(side, tokens, 2 * head, 2), x_rows=pltpu.VMEM((rows, width), BF16), x_sem=dma((K1,)), **turner_scratch(seq, min(256, width // 8)), w=pltpu.VMEM((width, depth), BF16), w_sem=dma((K2, 4)),
+    outs = dict(rows=(shape((rows + 8, width)), VMEM), kv=(shape((2, seq, 2 * kv_width)), ANY), q_other=(shape((side, side, rows, head)), ANY))
+    scratch = dict(sum=rs_scratch(side, rows, width), all=ag_scratch(side, tokens, 2 * head, 2), x_rows=pltpu.VMEM((rows, width), BF16), x_sem=dma((K1,)), w=pltpu.VMEM((width, depth), BF16), w_sem=dma((K2, 4)),
                    mate=pltpu.VMEM((half_side, side, rows, 2 * head), BF16), mate_sems=[dma((K1,)), dma((K1,))], swap_sems=[dma((K1,)), dma((K1,))])
     return call_kernel('sum_input', body, ins, outs, scratch, 3e8, 3)
 
@@ -934,31 +883,26 @@
     return call_kernel('attention_backward', body, ins, outs, scratch, 4e9).dqkv
 
 
-def weight_grads_mlp(mixed_full, grad_out, resid_full, lefts, ctxs, token):
+def weight_grads_mlp(mixed_full, grad_out, resid_full, left, ctxs, token):
     seq, width = grad_out.shape[1:]
-    depth, head = lefts[K0].shape[K0] // 3, ctxs[K1].shape[K1]
+    depth, head = left.shape[K0] // 3, ctxs[K1].shape[K1]
     tile = min(512, width)
 
-    def kernel(m_ref, dy_ref, dh_ref, left_own, left_other, ctx_own, ctx_other, _, out_gate, out_up, out_down, out_o, ctx_t):
+    def kernel(m_ref, dy_ref, dh_ref, left_ref, ctx_own, ctx_other, _, out_gate, out_up, out_down, out_o, ctx_t):
         core = lax.rem(lax.axis_index('tp'), 2)
 
         @pl.when(pl.program_id(0) == 0)
         def _():
-            for half, ref in enumerate((ctx_own, ctx_other)):
-                ctx_t[half] = ref[:, :head].T
-
-        halves = (core, 1 - core)
-        lefts = (left_own, left_other)
-
-        def product(base, size, ref):
-            own, other = (dot(left[base:base + size, :], ref[half], NN) for left, half in zip(lefts, halves))
-            return own + other
-
-        both = product(0, 2 * depth, m_ref)
-        out_gate[...] = both[:depth]
-        out_up[...] = both[depth:]
-        out_down[...] = product(2 * depth, depth, dy_ref)
-        out_o[...] = dot(ctx_t[K0], dh_ref[core], NN) + dot(ctx_t[K1], dh_ref[1 - core], NN)
+            for half, ref in ((core, ctx_own), (1 - core, ctx_other)):
+                ctx_t[:, pl.ds(pl.multiple_of(half * seq, seq), seq)] = ref[:, :head].T
+
+        def both(ref):
+            return ref[...].reshape(2 * seq, tile)
+
+        out_gate[...] = dot(left_ref[:depth, :], both(m_ref), NN)
+        out_up[...] = dot(left_ref[depth:2 * depth, :], both(m_ref), NN)
+        out_down[...] = dot(left_ref[2 * depth:, :], both(dy_ref), NN)
+        out_o[...] = dot(ctx_t[...], both(dh_ref), NN)
 
     slab = pl.BlockSpec((2, seq, tile), lambda step: (0, 0, step))
     out = lambda size: pl.BlockSpec((size, tile), lambda step: (0, step))
@@ -967,28 +911,37 @@
         name='weight_grads_mlp',
         grid=(width // tile,),
         out_shape=[shape((depth, width), F32)] * 3 + [shape((head, width), F32)],
-        in_specs=[slab] * 3 + [VMEM] * 4 + [ANY],
+        in_specs=[slab] * 3 + [VMEM] * 3 + [ANY],
         out_specs=[out(depth)] * 3 + [out(head)],
-        scratch_shapes=[pltpu.VMEM((2, head, seq), BF16)],
+        scratch_shapes=[pltpu.VMEM((head, 2 * seq), BF16)],
         compiler_params=pltpu.CompilerParams(vmem_limit_bytes=LIMIT),
         cost_estimate=pl.CostEstimate(flops=int(18e9), bytes_accessed=int(6e7), transcendentals=0),
-    )(mixed_full, grad_out, resid_full, *lefts, *ctxs, token)
-
-
-def weight_grads_qkv(lefts, kv_full, grads_q):
-    width, seq = lefts[K0].shape
+    )(mixed_full, grad_out, resid_full, left, *ctxs, token)
+
+
+def weight_grads_qkv(normeds, kv_full, grads_q):
+    seq, width = normeds[K0].shape
     head = grads_q[K1].shape[K1]
     kv_width = kv_full.shape[K2] // 2
     tile = min(512, width)
 
-    def kernel(a_own, a_other, kv_ref, q_own, q_other, out_q, out_k, out_v):
+    def kernel(a_own, a_other, kv_ref, q_own, q_other, out_q, out_k, out_v, left, q_both):
         core = lax.rem(lax.axis_index('tp'), 2)
+        halves = [pl.ds(pl.multiple_of(half * seq, seq), seq) for half in (core, 1 - core)]
+
+        @pl.when(pl.program_id(0) == 0)
+        def _():
+            q_both[halves[K0], :] = q_own[:, :head]
+            q_both[halves[K1], :] = q_other[...]
+
+        left[:, halves[K0]] = a_own[...].T
+        left[:, halves[K1]] = a_other[...].T
+        out_q[...] = dot(left[...], q_both[...], NN)
         for index, out in enumerate((out_k, out_v)):
-            at = pl.ds(index * kv_width, kv_width)
-            out[...] = dot(a_own[...], kv_ref[core, :, at], NN) + dot(a_other[...], kv_ref[1 - core, :, at], NN)
-        out_q[...] = dot(a_own[...], q_own[:, :head], NN) + dot(a_other[...], q_other[...], NN)
-
-    slab = pl.BlockSpec((tile, seq), lambda step: (step, 0))
+            right = kv_ref[:, :, pl.ds(index * kv_width, kv_width)].reshape(2 * seq, kv_width)
+            out[...] = dot(left[...], right, NN)
+
+    slab = pl.BlockSpec((seq, tile), lambda step: (0, step))
     out = lambda size: pl.BlockSpec((tile, size), lambda step: (step, 0))
     return pl.pallas_call(
         kernel,
@@ -997,53 +950,53 @@
         out_shape=[shape((width, size), F32) for size in (head, kv_width, kv_width)],
         in_specs=[slab] * 2 + [VMEM] * 3,
         out_specs=[out(size) for size in (head, kv_width, kv_width)],
+        scratch_shapes=[pltpu.VMEM((tile, 2 * seq), BF16), pltpu.VMEM((2 * seq, head), BF16)],
         compiler_params=pltpu.CompilerParams(vmem_limit_bytes=LIMIT),
         cost_estimate=pl.CostEstimate(flops=int(27e9), bytes_accessed=int(6e7), transcendentals=0),
-    )(*lefts, kv_full, *grads_q)
+    )(*normeds, kv_full, *grads_q)
 
 
 def in_place(gathered, rows):
-    blocks, _, width = gathered.shape
+    blocks, held, width = gathered.shape
     slots = 24
-    pieces = 2 * blocks
-
-    def kernel(src, dx_ref, y_ref, gain_attn, gain_mlp, buf, extra, in_sem, out_sem, extra_sem):
-        gains = pltpu.make_async_copy(src.at[:, pl.ds(2 * rows, 8), :], extra, extra_sem.at[K0])
+    gains = 2 if held > rows else 0
+
+    def kernel(src, dst, *refs):
+        buf, extra, in_sem, out_sem, extra_sem = refs[gains:]
 
         def load(index):
-            at = pl.ds(index // blocks * rows, rows)
-            return pltpu.make_async_copy(src.at[index % blocks, at, :], buf.at[index % slots], in_sem.at[index % slots])
+            return pltpu.make_async_copy(src.at[index, pl.ds(0, rows), :], buf.at[index % slots], in_sem.at[index % slots])
 
         def store(index):
-            dst, block = (dx_ref, y_ref)[index // blocks], index % blocks
-            return pltpu.make_async_copy(buf.at[index % slots], dst.at[block % 2, block // 2], out_sem.at[index % slots])
+            return pltpu.make_async_copy(buf.at[index % slots], dst.at[index % 2, index // 2], out_sem.at[index % slots])
 
         ahead = slots // 2
-        for index in range(pieces + ahead):
-            if index < pieces:
+        for index in range(blocks + ahead):
+            if index < blocks:
                 if index >= slots:
                     store(index - slots).wait()
                 load(index).start()
-            if index == ahead:
-                gains.start()
+            if index == ahead and gains:
+                last = pltpu.make_async_copy(src.at[:, pl.ds(held - 8, 8), :], extra, extra_sem.at[K0])
+                last.start()
             if index >= ahead:
                 load(index - ahead).wait()
                 store(index - ahead).start()
-        gains.wait()
-        total = jnp.sum(extra[...].astype(F32), axis=0)
-        for first, ref in ((0, gain_attn), (3, gain_mlp)):
-            ref[...] = total[first:first + 1] + total[first + 1:first + 2] + total[first + 2:first + 3]
-        for index in range(pieces - slots, pieces):
+        if gains:
+            last.wait()
+            total = jnp.sum(extra[...].astype(F32), axis=0)
+            for first, ref in zip((0, 3), refs):
+                ref[...] = total[first:first + 1] + total[first + 1:first + 2] + total[first + 2:first + 3]
+        for index in range(blocks - slots, blocks):
             store(index).wait()
 
     dma = pltpu.SemaphoreType.DMA
-    whole = shape((2, blocks // 2, rows, width))
     return pl.pallas_call(
         kernel,
         name='in_place',
-        out_shape=[whole, whole, shape((1, width), F32), shape((1, width), F32)],
+        out_shape=[shape((2, blocks // 2, rows, width))] + [shape((1, width), F32)] * gains,
         in_specs=[ANY],
-        out_specs=[ANY, ANY, VMEM, VMEM],
+        out_specs=[ANY] + [VMEM] * gains,
         scratch_shapes=[pltpu.VMEM((slots, rows, width), BF16), pltpu.VMEM((blocks, 8, width), BF16), dma((slots,)), dma((slots,)), dma((K1,))],
         compiler_params=pltpu.CompilerParams(vmem_limit_bytes=LIMIT),
         cost_estimate=pl.CostEstimate(flops=int(2e7), bytes_accessed=int(2e7), transcendentals=0),
@@ -1074,13 +1027,12 @@
         second = sum_mlp(side, mlp, (w_gate.T, mlp.w_gate), (w_up.T, mlp.w_up), (w_down, mlp.w_down), grad_out, gain_mlp_row)
         resid_full = second.full.reshape(2, seq_len, width)
 
+        (y_out,) = in_place(lax.all_gather(second.y_rows, 'tp'), rows)
         dqkv = attention_backward(flat(second.own), seg_ids, w_outs, attn.qkv)
-        third = sum_input(side, dqkv, w_qs, w_k, w_v, hidden, second, gain_attn_row, (attn.normed, mlp.normed_other))
-
-        grad_in, y_out, grad_gain_attn, grad_gain_mlp = in_place(lax.all_gather(third.rows, 'tp'), rows)
-        grad_gate_t, grad_up_t, grad_w_down, grad_w_o = weight_grads_mlp(
-            mixed_full, grad_out, resid_full, (second.left, second.left_other), (attn.ctx, flat(mlp.ctx_other)), third.q_other)
-        grad_w_q, grad_w_k, grad_w_v = weight_grads_qkv(third.lefts, third.kv, (dqkv, flat(third.q_other)))
+        third = sum_input(side, dqkv, w_qs, w_k, w_v, hidden, second, gain_attn_row)
+        grad_in, grad_gain_attn, grad_gain_mlp = in_place(lax.all_gather(third.rows, 'tp'), rows)
+        grad_gate_t, grad_up_t, grad_w_down, grad_w_o = weight_grads_mlp(mixed_full, grad_out, resid_full, second.left, (attn.ctx, flat(mlp.ctx_other)), third.q_other)
+        grad_w_q, grad_w_k, grad_w_v = weight_grads_qkv((attn.normed, mlp.normed_other), third.kv, (dqkv, flat(third.q_other)))
         return (y_out.reshape(hidden.shape), grad_in.reshape(hidden.shape), grad_gain_attn[K0], grad_gain_mlp[K0], grad_w_q, grad_w_k, grad_w_v, grad_w_o, grad_gate_t.T, grad_up_t.T, grad_w_down)
 
     spec_act = P('data', None, None)

time: 456 us -> 457 us (level)
  Pallas kernels: 406 us -> 435 us
  waiting for transfers between devices: 28.4 us -> 0.13 us
    all_gather x1, waiting for transfers between devices: 28.4 us -> 0.02 us  [device_step(): lax.all_gather(third.rows, 'tp')]
    pallas_call x5, Pallas kernels: 323 us -> 348 us  [call_kernel(): pl.pallas_call(kernel, name=name, out_shape=[leaf[K0] for leaf in out_lea...]
    pallas_call x1 -> x2, Pallas kernels: 18.7 us -> 20.3 us  [in_place(): pl.pallas_call(kernel, name='in_place', out_shape=[shape((2, blocks // 2,...]
  transfers between devices with their start and end apart: 1 -> 2, of which waited for: 1 -> 0; matrix products, arithmetic and copies ran while one was open for 0% -> 0% of each run, Pallas kernels for 14% -> 40%
where the time goes in v6:
time: 457 us; the launch traced here: 450 us
  Pallas kernels  435 us (95%)
  between operations  14.7 us (3%)
    pallas_call x5, Pallas kernels, call_kernel(): pl.pallas_call(kernel, name=name, out_shape=[leaf[K0] for leaf in out_lea...  348 us
    pallas_call x1, Pallas kernels, weight_grads_qkv(): pl.pallas_call(kernel, name='weight_grads_qkv', grid=(width // tile,), ou...  39.7 us
    pallas_call x1, Pallas kernels, weight_grads_mlp(): pl.pallas_call(kernel, name='weight_grads_mlp', grid=(width // tile,), ou...  27.3 us
    pallas_call x2, Pallas kernels, in_place(): pl.pallas_call(kernel, name='in_place', out_shape=[shape((2, blocks // 2,...  20.3 us
  transfers between devices with their start and end apart: 2, of which 0 were waited for; matrix products, arithmetic and copies ran while one was open for 0% of the time, Pallas kernels for 40%

profile of v6, /device:TPU:97, one launch (start us, length us, event | category | flops | bytes accessed | tf_op | source)
XLA Modules:
  0.0 450.1 jit_solution(10894967351106732223)
XLA Ops:
  7.2 0.1 all-gather.5.cloned.1.call-start
  7.3 18.1 %attention_forward.1 = (bf16[768,256]{1,0:T(8,128)(2,1)}, bf16[768,4096]{1,0:T(8,128)(2,1)}, bf16[768,512]{1,0:T(8,128)(2,1)}, bf16[128,4096]{1,0:T(8,128)(2,1)}, bf16[4096,128]{1,0:T(8,128)(2,1)}) custom-call(f32[1,4096]{1,0:T(1,128)} %bitcast.30, bf16[2,768,4096]{2,1,0:T(8,128)(2,1)} %refs_4_.3, s32[2,768]{1,0:T(2,128)} %refs_2_.5, ...), custom_call_target="tpu_custom_call" | custom-call | flops 5000000000 | bytes 40000000 | tf_op jit(solution)/shard_map/attention_forward/pallas_call | solution.py:443
  25.4 98.8 %sum_attention.1 = (bf16[4,4,48,448]{3,2,1,0:T(8,128)(2,1)}, bf16[4,4,48,448]{3,2,1,0:T(8,128)(2,1)}, bf16[4,4,48,128]{3,2,1,0:T(8,128)(2,1)}, bf16[2,4,4,48,409...) custom-call(bf16[4,4,48,256]{3,2,1,0:T(8,128)(2,1)} %bitcast.27, ...), custom_call_target="tpu_custom_call" | custom-call | flops 400000000 | bytes 40000000 | tf_op jit(solution)/shard_map/sum_attention/pallas_call | solution.py:443
  124.2 126.2 %sum_mlp.1 = (f32[48,4096]{1,0:T(8,128)}, bf16[2,4,4,48,4096]{4,3,2,1,0:T(8,128)(2,1)}, f32[1,4096]{1,0:T(1,128)}, bf16[1344,1536]{1,0:T(8,128)(2,1)}, bf16[4,4,...) custom-call(bf16[4,4,48,448]{3,2,1,0:T(8,128)(2,1)} %get-tuple-element.51.refs_0_, ...), custom_call_target="tpu_custom_call" | custom-call | flops 600000000 | bytes 40000000 | tf_op jit(solution)/shard_map/sum_mlp/pallas_call | solution.py:443
  250.4 0.1 all-gather.5.cloned.1.call-update
  250.4 0.3 all-gather.7.cloned.1.call-start
  250.7 14.2 %attention_backward.1.q_own = bf16[768,512]{1,0:T(8,128)(2,1)} custom-call(bf16[768,512]{1,0:T(8,128)(2,1)} %get-tuple-element.63.refs_0_, bf16[768,4096]{1,0:T(8,128)(2,1)} %bitcast.35, s32[2,768]{1,0:T(2,128)} %refs_2_.5, bf16[128,4096]{1,0:T(8,128)(2,1)} %refs_3_.7, bf16[128,4096]{1,0:T(8,128)(2,1)} %get-tuple-element.50.refs_8_.refs_4_), custom_call_target="tpu_custom_call" | custom-call | flops 4000000000 | bytes 40000000 | tf_op jit(solution)/shard_map/attention_backward/pallas_call | solution.py:443
  264.9 90.4 %sum_input.1 = (bf16[2,768,2048]{2,1,0:T(8,128)(2,1)}, bf16[4,4,48,128]{3,2,1,0:T(8,128)(2,1)}, bf16[56,4096]{1,0:T(8,128)(2,1)}) custom-call(f32[48,4096]{1,0:T(8,128)} %get-tuple-element.62.refs_0_, bf16[4,4,48,512]{3,2,1,0:T(8,128)(2,1)} %bitcast.26, f32[1,4096]{1,0:T(1,128)} %bitcast.31, f32[1,4096]{1,0:T(1,128)} %get-tuple-element.65.refs_3_, ...), custom_call_target="tpu_custom_call" | custom-call | flops 300000000 | bytes 40000000 | tf_op jit(solution)/shard_map/sum_input/pallas_call | solution.py:443
  355.3 0.1 all-gather.7.cloned.1.call-update
  355.4 27.3 %weight_grads_mlp.1 = (f32[448,4096]{1,0:T(8,128)}, f32[448,4096]{1,0:T(8,128)}, f32[448,4096]{1,0:T(8,128)}, f32[128,4096]{1,0:T(8,128)}) custom-call(bf16[2,768,4096]{2,1,0:T(8,128)(2,1)} %bitcast.32, bf16[2,768,4096]{2,1,0:T(8,128)(2,1)} %dy_ref.1, bf16[2,768,4096]{2,1,0:T(8,128)(2,1)} %bitcast.33, bf16[1344,1536]{1,0:T(8,128)(2,1)} %get-tuple-element.79.left_ref, ...), custom_call_target="tpu_custom_call" | custom-call | flops 17999998976 | bytes 60000000 | tf_op jit(solution)/shard_map/weight_grads_mlp/pallas_call | solution.py:909
  382.7 39.7 %weight_grads_qkv.1 = (f32[4096,128]{1,0:T(8,128)}, f32[4096,1024]{1,0:T(8,128)}, f32[4096,1024]{1,0:T(8,128)}) custom-call(bf16[768,4096]{1,0:T(8,128)(2,1)} %get-tuple-element.49.refs_4_.a_own, bf16[768,4096]{1,0:T(8,128)(2,1)} %get-tuple-element.71.a_other, bf16[2,768,2048]{2,1,0:T(8,128)(2,1)} %get-tuple-element.72.kv_ref, ...), custom_call_target="tpu_custom_call" | custom-call | flops 27000000512 | bytes 60000000 | tf_op jit(solution)/shard_map/weight_grads_qkv/pallas_call | solution.py:946
  422.3 0.0 all-gather.5.cloned.1.call-done
  422.3 9.3 %in_place.2 = bf16[2,16,48,4096]{3,2,1,0:T(8,128)(2,1)} custom-call(bf16[32,48,4096]{2,1,0:T(8,128)(2,1)} %bitcast.24), custom_call_target="tpu_custom_call" | custom-call | flops 20000000 | bytes 20000000 | tf_op jit(solution)/shard_map/in_place/pallas_call | solution.py:994
  431.7 0.0 all-gather.7.cloned.1.call-done
  431.7 11.0 %in_place.3 = (bf16[2,16,48,4096]{3,2,1,0:T(8,128)(2,1)}, f32[1,4096]{1,0:T(1,128)}, f32[1,4096]{1,0:T(1,128)}) custom-call(bf16[32,56,4096]{2,1,0:T(8,128)(2,1)} %bitcast.23), custom_call_target="tpu_custom_call" | custom-call | flops 20000000 | bytes 20000000 | tf_op jit(solution)/shard_map/in_place/pallas_call | solution.py:994
Async XLA Ops:
  7.2 415.1 %all-gather.5.cloned.1.call-start = ((), (), s32[]{:S(2)}) async-start(), calls=%async_computation | async-start | bytes 12976128 | tf_op jit(solution)/shard_map/all_gather | solution.py:1030
  250.4 181.3 %all-gather.7.cloned.1.call-start = ((), (), s32[]{:S(2)}) async-start(), calls=%async_computation.1 | async-start | bytes 15138816 | tf_op jit(solution)/shard_map/all_gather | solution.py:1033
Sparse Core Ops, SparseCore 0:
  250.5 79.6 all-gather.4
  355.5 61.6 all-gather.6

commit v7 on v6

--- a/solution.py
+++ b/solution.py
@@ -430,23 +430,65 @@
     return [bag(value) for value in tree] if isinstance(tree, list) else tree
 
 
+class Staging:
+    def __init__(self, loads, saves):
+        self.loads, self.saves, self.left = loads, saves, {}
+
+    def start(self):
+        for load in self.loads:
+            load.start()
+
+    def wait(self):
+        for load in self.loads:
+            load.wait()
+
+    def save(self, *refs):
+        for ref, save in self.saves:
+            if any(ref is one for one in refs):
+                save.start()
+                self.left[id(ref)] = save
+
+    def finish(self):
+        self.save(*[ref for ref, _ in self.saves if id(ref) not in self.left])
+        for save in self.left.values():
+            save.wait()
+
+
 def call_kernel(name, body, ins, outs, scratch, flops, collective_id=None):
     is_leaf = lambda value: isinstance(value, tuple)
     in_leaves, in_tree = jax.tree.flatten(ins, is_leaf=is_leaf)
     out_leaves, out_tree = jax.tree.flatten(outs, is_leaf=is_leaf)
     scr_leaves, scr_tree = jax.tree.flatten(scratch)
     first_scr = len(in_leaves) + len(out_leaves)
+    staged = [index for index, leaf in enumerate(in_leaves + out_leaves) if leaf[K1] is VMEM]
+    stages = []
+    for index in staged:
+        leaf = (in_leaves + out_leaves)[index][K0]
+        stages.append(pltpu.VMEM(leaf.shape, leaf.dtype))
 
     def kernel(*refs):
-        body(bag(in_tree.unflatten(refs[:len(in_leaves)])), bag(out_tree.unflatten(refs[len(in_leaves):first_scr])), bag(scr_tree.unflatten(refs[first_scr:])))
+        refs = list(refs)
+        own = refs[first_scr + len(scr_leaves):]
+        sem = own.pop()
+        loads, saves = [], []
+        for slot, (index, ref) in enumerate(zip(staged, own)):
+            if index < len(in_leaves):
+                loads.append(pltpu.make_async_copy(refs[index], ref, sem.at[slot]))
+            else:
+                saves.append((ref, pltpu.make_async_copy(ref, refs[index], sem.at[slot])))
+            refs[index] = ref
+        staging = Staging(loads, saves)
+        staging.start()
+        body(bag(in_tree.unflatten(refs[:len(in_leaves)])), bag(out_tree.unflatten(refs[len(in_leaves):first_scr])), bag(scr_tree.unflatten(refs[first_scr:first_scr + len(scr_leaves)])), staging)
+        staging.finish()
 
     results = pl.pallas_call(
         kernel,
         name=name,
         out_shape=[leaf[K0] for leaf in out_leaves],
-        in_specs=[leaf[K1] for leaf in in_leaves],
-        out_specs=[leaf[K1] for leaf in out_leaves],
-        scratch_shapes=scr_leaves,
+        in_specs=[ANY] * len(in_leaves),
+        out_specs=[ANY] * len(out_leaves),
+        scratch_shapes=scr_leaves + stages + [pltpu.SemaphoreType.DMA((len(staged),))],
         compiler_params=pltpu.CompilerParams(collective_id=collective_id, has_side_effects=collective_id is not None, vmem_limit_bytes=LIMIT),
         cost_estimate=pl.CostEstimate(flops=int(flops), bytes_accessed=int(4e7), transcendentals=0),
     )(*[leaf[K0] for leaf in in_leaves])
@@ -463,7 +505,7 @@
     hidden_loc = w_gate.shape[K0]
     rows = seq // (side * side)
 
-    def body(ins, outs, scr):
+    def body(ins, outs, scr, staging):
         torus = Torus(side)
         weights = Weights(ins.w_outs, scr.w, scr.w_sem, False)
         weights.start()
@@ -480,6 +522,7 @@
         wait = torus.signal_all()
         part = scr.sum.part
         steps = ReduceScatter(torus, scr.sum).steps(fill_partial(torus, part, [ins.ctx], weights))
+        staging.wait()
         steps[K0]()
         wait()
         other_ctx = ins.ctx.at[:, :, :, pl.ds(depth // 2, depth // 2)]
@@ -521,6 +564,7 @@
             z_in = resid.astype(F32)
             inv = lax.rsqrt(jnp.mean(z_in * z_in, axis=-1, keepdims=True) + EPS)
             gat[(*own, at, slice(None))] = (z_in * inv * ins.gain[...]).astype(BF16)
+        staging.save(outs.h_rows)
         gather = AllGather(torus, scr.all, False)
         gather.store = Store(torus, scr.all, plain_places(gather, outs.full))
 
@@ -554,14 +598,18 @@
                         grad = scr.grad_act[core, y_at, x_at]
                         sigmoid_g = 1.0 / (1.0 + jnp.exp(-gate))
                         silu_g = gate * sigmoid_g
-                        outs.acts[core][y_at, x_at] = (silu_g * upper).astype(BF16)
-                        outs.gates[core][y_at, x_at] = (grad * upper * sigmoid_g * (1.0 + gate * (1.0 - sigmoid_g))).astype(BF16)
-                        outs.ups[core][y_at, x_at] = (grad * silu_g).astype(BF16)
+                        scr.results[core, y_at, x_at] = (silu_g * upper).astype(BF16)
+                        scr.results[2 + core, y_at, x_at] = (grad * upper * sigmoid_g * (1.0 + gate * (1.0 - sigmoid_g))).astype(BF16)
+                        scr.results[4 + core, y_at, x_at] = (grad * silu_g).astype(BF16)
+                    for kind, out in enumerate(outs.acts + outs.gates + outs.ups):
+                        pltpu.make_async_copy(scr.results.at[kind, y_at, x_at], out.at[y_at, x_at], scr.result_sem.at[kind]).start()
                     return carry
 
                 lax.fori_loop(0, count, block, 0)
 
         run(gather.steps(products))
+        for kind, out in enumerate(outs.acts + outs.gates + outs.ups):
+            pltpu.make_async_copy(scr.results.at[kind], out, scr.result_sem.at[kind]).wait()
         gather.store.drain()
         swap_end(torus, scr.swap_sems, swaps, 3)
         torus.drain()
@@ -570,12 +618,12 @@
     block = (side, side, rows, hidden_loc)
     ins = dict(ctx=(attn.ctx.reshape(side, side, rows, depth), VMEM), w_outs=[(weight, ANY) for weight in w_outs], hidden=(hidden, ANY), grad_out=(grad_out, ANY), gain=(gain, VMEM),
                normed=(attn.normed, ANY), w_gate=(w_gate, ANY), w_up=(w_up, ANY), w_down=(w_down, ANY))
-    out, weight = (shape(block), VMEM), (shape((hidden_loc, width)), ANY)
+    out, weight = (shape(block), ANY), (shape((hidden_loc, width)), ANY)
     outs = dict(full=(shape((2, side, side, rows, width)), ANY), h_rows=(shape((rows, width)), VMEM), ctx_other=(shape((side, side, rows, depth // 2)), ANY), normed_other=(shape((seq, width)), ANY),
                 w_gate=weight, w_up=weight, w_down=weight, acts=[out, out], gates=[out, out], ups=[out, out])
     scratch = dict(sum=rs_scratch(side, rows, width), all=ag_scratch(side, rows, width), w=pltpu.VMEM((depth, width), BF16), w_sem=dma((K2, K2)), swap_sems=[dma((5,)), dma((5,))],
                    x_rows=pltpu.VMEM((rows, width), BF16), x_sem=dma((K1,)), w_mlp=pltpu.VMEM((4, hidden_loc, width), BF16), w_mlp_sem=dma((4,)),
-                   dy=pltpu.VMEM((2, side * rows, width), BF16), dy_sem=dma((K2,)), pre=pltpu.VMEM((4, *block), F32), grad_act=pltpu.VMEM((2, *block), F32))
+                   dy=pltpu.VMEM((2, side * rows, width), BF16), dy_sem=dma((K2,)), pre=pltpu.VMEM((4, *block), F32), grad_act=pltpu.VMEM((2, *block), F32), results=pltpu.VMEM((6, *block), BF16), result_sem=dma((6,)))
     return call_kernel('sum_attention', body, ins, outs, scratch, 4e8, 1)
 
 
@@ -586,7 +634,7 @@
     seq = rows * side * side
     block = (side, side, rows, width)
 
-    def body(ins, outs, scr):
+    def body(ins, outs, scr, staging):
         torus = Torus(side)
         weights = Weights(ins.w_in, scr.w, scr.w_sem, False)
         weights.start()
@@ -598,6 +646,7 @@
         wait = torus.signal_all()
         steps = ReduceScatter(torus, scr.sum).steps(fill_partial(torus, scr.sum.part, ins.grads, weights))
         steps_p = ReduceScatter(torus, scr.sum_p).steps(fill_partial(torus, scr.sum_p.part, ins.acts, weights_p))
+        staging.wait()
         steps[K0]()
         wait()
 
@@ -613,13 +662,13 @@
             if index >= 2:
                 turned[index - 2]()
             scr.turn[slot] = src[...].reshape(seq, depth).T
-            at = pl.ds(kind * depth, depth), half_at(torus.core)
+            at = slice(None), half_at(torus.core)
             if core == 0:
-                save = pltpu.make_async_copy(scr.turn.at[slot], outs.left.at[at], scr.turn_sem.at[kind])
+                save = pltpu.make_async_copy(scr.turn.at[slot], outs.lefts[kind].at[at], scr.turn_sem.at[kind])
                 save.start()
                 turned.append(save.wait)
             else:
-                torus.send(scr.turn.at[slot], outs.left.at[at], scr.swap_sems, kind, torus.partner)
+                torus.send(scr.turn.at[slot], outs.lefts[kind].at[at], scr.swap_sems, kind, torus.partner)
                 turned.append(torus.pending.pop().wait_send)
 
         turns = [functools.partial(turn, index) for index in range(6)]
@@ -642,15 +691,17 @@
             outs.d_rows[at, :] = total
             gat[(*own, at, slice(None))] = total.astype(BF16)
         outs.gain[...] = gain_total
+        staging.save(outs.d_rows, outs.gain)
         gather = AllGather(torus, scr.all, False)
         gather.store = Store(torus, scr.all, plain_places(gather, outs.full), outs.own)
         run(gather.steps(), rest_p[3:], turns)
         for at in row_tiles(rows):
             outs.y_rows[at, :] = (ins.h_rows[at, :].astype(F32) + scr.sum_p.part[(*own, at, slice(None))].astype(F32)).astype(BF16)
+        staging.save(outs.y_rows)
         turned[4]()
         turned[5]()
         for kind in range(3):
-            torus.arrive(outs.left.at[pl.ds(kind * depth, depth), half_at(1 - torus.core)], scr.swap_sems, kind)
+            torus.arrive(outs.lefts[kind].at[:, half_at(1 - torus.core)], scr.swap_sems, kind)
         gather.store.drain()
         torus.drain()
 
@@ -658,7 +709,7 @@
     ins = dict(grads=[(grad, VMEM) for grad in (mlp.gates[K0], mlp.ups[K0], mlp.gates[K1], mlp.ups[K1])], acts=[(act, VMEM) for act in mlp.acts],
                w_in=[(weight, ANY) for weight in (w_gates[K0], w_ups[K0], w_gates[K1], w_ups[K1])], w_downs=[(weight, ANY) for weight in w_downs],
                h_rows=(mlp.h_rows, VMEM), grad_out=(grad_out, ANY), gain=(gain, VMEM))
-    outs = dict(full=(shape((2, *block)), ANY), own=(shape(block), ANY), d_rows=(shape((rows, width), F32), VMEM), gain=(shape((1, width), F32), VMEM), y_rows=(shape((rows, width)), VMEM), left=(shape((3 * depth, 2 * seq)), ANY))
+    outs = dict(full=(shape((2, *block)), ANY), own=(shape(block), ANY), d_rows=(shape((rows, width), F32), VMEM), gain=(shape((1, width), F32), VMEM), y_rows=(shape((rows, width)), VMEM), lefts=[(shape((depth, 2 * seq)), ANY)] * 3)
     scratch = dict(sum=rs_scratch(side, rows, width), sum_p=rs_scratch(side, rows, width), all=ag_scratch(side, rows, width), dy_rows=pltpu.VMEM((rows, width), BF16), dy_sem=dma((K1,)),
                    w=pltpu.VMEM((4 * depth, width), BF16), w_sem=dma((K2, 4)), wd=pltpu.VMEM((2 * depth, width), BF16), wd_sem=dma((K2, K2)),
                    turn=pltpu.VMEM((2, depth, seq), BF16), turn_sem=dma((K3,)), swap_sems=[dma((K3,)), dma((K3,))])
@@ -675,7 +726,7 @@
     kv_width = w_k.shape[K1]
     per_kv = 2 * side * side * head // kv_width
 
-    def body(ins, outs, scr):
+    def body(ins, outs, scr, staging):
         torus = Torus(side)
         kv_col = pl.multiple_of(lax.div(torus.chip * 2, per_kv) * head, head)
         weights = Weights([*ins.w_qs, ins.w_k.at[:, pl.ds(kv_col, head)], ins.w_v.at[:, pl.ds(kv_col, head)]], scr.w, scr.w_sem, True)
@@ -707,6 +758,7 @@
             mine = ins.dqkv[pl.ds(place * half_side, half_side), :, :, kv_cols]
             gat[own] = (mine.astype(F32) + scr.mate[...].astype(F32)).astype(BF16).reshape(tokens, 2 * head)
 
+        staging.wait()
         steps[K0]()
         wait()
         swaps = [(ins.dqkv.at[:, :, :, pl.ds(head, head)], outs.q_other)]
@@ -730,6 +782,7 @@
                 extra = jnp.where(row == index * 3 + level, rounded, extra)
                 value = value - rounded
         outs.rows[rows:rows + 8, :] = extra.astype(BF16)
+        staging.save(outs.rows)
         gather.store.drain()
         swap_end(torus, scr.swap_sems, swaps)
         torus.drain()
@@ -767,7 +820,7 @@
     tile = min(256, seq)
     depth = 4 * HEAD_DIM
 
-    def body(ins, outs, scr):
+    def body(ins, outs, scr, staging):
         tp_idx = lax.axis_index('tp')
         core = lax.rem(tp_idx, 2)
         kv_col = pl.multiple_of(lax.div(tp_idx, per_kv) * HEAD_DIM, HEAD_DIM)
@@ -796,11 +849,28 @@
         for index in range(4):
             loads[index].wait()
 
+            if index == 0:
+                staging.wait()
+
+            def square(step, carry, index=index):
+                at = pl.ds(pl.multiple_of(index * chunk + step * 16, 16), 16)
+                total = jnp.zeros((16, HEAD_DIM), F32)
+                for lane in range(0, width, HEAD_DIM):
+                    value = scr.x[at, lane:lane + HEAD_DIM].astype(F32)
+                    total = total + value * value
+                scr.squares[pl.ds(pl.multiple_of(step * 16, 16), 16), :] = total
+                return carry
+
+            lax.fori_loop(0, chunk // 16, square, 0)
+            inv = lax.rsqrt(jnp.sum(scr.squares[...], axis=-1, keepdims=True) / width + EPS)
+            scr.squares[...] = jnp.broadcast_to(inv, scr.squares.shape)
+
             def normalize(step, carry, index=index):
                 at = pl.ds(pl.multiple_of(index * chunk + step * 16, 16), 16)
-                x_float = scr.x[at, :].astype(F32)
-                inv = lax.rsqrt(jnp.mean(x_float * x_float, axis=-1, keepdims=True) + EPS)
-                scr.normed[at, :] = (x_float * inv * ins.gain[...]).astype(BF16)
+                scale = scr.squares[pl.ds(pl.multiple_of(step * 16, 16), 16), :]
+                for lane in range(0, width, HEAD_DIM):
+                    cols = slice(lane, lane + HEAD_DIM)
+                    scr.normed[at, cols] = (scr.x[at, cols].astype(F32) * scale * ins.gain[:, cols]).astype(BF16)
                 return carry
 
             lax.fori_loop(0, chunk // 16, normalize, 0)
@@ -813,6 +883,7 @@
                     load.wait()
                 copies[K0].wait_recv()
             outs.qkv[at, :] = dot(scr.normed[at, :], scr.w[...], NN).astype(BF16)
+        staging.save(outs.qkv)
         seg_row, seg_col = segments(ins.seg)
         values_t = outs.qkv[:, 3 * HEAD_DIM:].T
         for head_index in PAIR:
@@ -829,17 +900,17 @@
     dma = pltpu.SemaphoreType.DMA
     ins = dict(hidden=(hidden, ANY), seg=(seg_ids, VMEM), gain=(gain, VMEM), w_q=(w_q, ANY), w_o=(w_o, ANY), w_k=(w_k, ANY), w_v=(w_v, ANY))
     outs = dict(normed=(shape((seq, width)), ANY), qkv=(shape((seq, depth)), VMEM), ctx=(shape((seq, 2 * HEAD_DIM)), VMEM), w_q=(shape(w_q.shape), ANY), w_o=(shape(w_o.shape), ANY))
-    scratch = dict(swap_sems=[dma((K3,)), dma((K3,))], x=pltpu.VMEM((seq, width), BF16), normed=pltpu.VMEM((seq, width), BF16), w=pltpu.VMEM((width, depth), BF16), x_sem=dma((4,)), w_sem=dma((4,)), out_sem=dma((4,)))
+    scratch = dict(squares=pltpu.VMEM((chunk, HEAD_DIM), F32), swap_sems=[dma((K3,)), dma((K3,))], x=pltpu.VMEM((seq, width), BF16), normed=pltpu.VMEM((seq, width), BF16), w=pltpu.VMEM((width, depth), BF16), x_sem=dma((4,)), w_sem=dma((4,)), out_sem=dma((4,)))
     return call_kernel('attention_forward', body, ins, outs, scratch, 5e9, 4)
 
 
-def attention_backward(resid, seg_ids, w_outs, qkv):
+def attention_backward(resid, seg_ids, w_outs, qkv, token):
     seq, width = resid.shape
     chunk = seq // 4
     tile = min(256, seq)
     depth = 4 * HEAD_DIM
 
-    def body(ins, outs, scr):
+    def body(ins, outs, scr, staging):
         loads = []
         for index in PAIR:
             at = pl.ds(index * HEAD_DIM, HEAD_DIM)
@@ -851,6 +922,7 @@
             load.start()
         for load in loads[:2]:
             load.wait()
+        staging.wait()
         for index in range(4):
             loads[2 + index].wait()
             at = pl.ds(index * chunk, chunk)
@@ -876,47 +948,72 @@
         outs.dqkv[:, 3 * HEAD_DIM:] = scr.grad_v[...].astype(BF16)
 
     dma = pltpu.SemaphoreType.DMA
-    ins = dict(resid=(resid, ANY), seg=(seg_ids, VMEM), w_outs=[(weight, ANY) for weight in w_outs], qkv=(qkv, VMEM))
+    ins = dict(resid=(resid, ANY), seg=(seg_ids, VMEM), w_outs=[(weight, ANY) for weight in w_outs], qkv=(qkv, VMEM), token=(token, ANY))
     outs = dict(dqkv=(shape((seq, depth)), VMEM))
     scratch = dict(resid=pltpu.VMEM((seq, width), BF16), w=pltpu.VMEM((2 * HEAD_DIM, width), BF16), grad_ctx=pltpu.VMEM((seq, 2 * HEAD_DIM), BF16),
                    grad_k=pltpu.VMEM((seq, HEAD_DIM), F32), grad_v=pltpu.VMEM((seq, HEAD_DIM), F32), w_sem=dma((K2,)), in_sem=dma((4,)))
     return call_kernel('attention_backward', body, ins, outs, scratch, 4e9).dqkv
 
 
-def weight_grads_mlp(mixed_full, grad_out, resid_full, left, ctxs, token):
-    seq, width = grad_out.shape[1:]
-    depth, head = left.shape[K0] // 3, ctxs[K1].shape[K1]
+def weight_grads(name, groups, ctxs, tokens=()):
+    seq, width = groups[K0][K1].shape[1:]
+    head = ctxs[K1].shape[K1] if ctxs else 0
     tile = min(512, width)
-
-    def kernel(m_ref, dy_ref, dh_ref, left_ref, ctx_own, ctx_other, _, out_gate, out_up, out_down, out_o, ctx_t):
-        core = lax.rem(lax.axis_index('tp'), 2)
-
-        @pl.when(pl.program_id(0) == 0)
-        def _():
-            for half, ref in ((core, ctx_own), (1 - core, ctx_other)):
-                ctx_t[:, pl.ds(pl.multiple_of(half * seq, seq), seq)] = ref[:, :head].T
-
-        def both(ref):
-            return ref[...].reshape(2 * seq, tile)
-
-        out_gate[...] = dot(left_ref[:depth, :], both(m_ref), NN)
-        out_up[...] = dot(left_ref[depth:2 * depth, :], both(m_ref), NN)
-        out_down[...] = dot(left_ref[2 * depth:, :], both(dy_ref), NN)
-        out_o[...] = dot(ctx_t[...], both(dh_ref), NN)
+    lefts = [left for left, _ in groups if left is not None]
+    sizes = [head if left is None else left.shape[K0] for left, _ in groups]
+    given = len(groups) + len(lefts) + len(ctxs)
+
+    def kernel(*refs):
+        rights, left_refs = refs[:len(groups)], list(refs[len(groups):len(groups) + len(lefts)])
+        outs = refs[given + len(tokens):given + len(tokens) + len(groups)]
+        if ctxs:
+            core = lax.rem(lax.axis_index('tp'), 2)
+            ctx_t = refs[-1]
+
+            @pl.when(pl.program_id(0) == 0)
+            def _():
+                for half, ref in zip((core, 1 - core), refs[given - 2:given]):
+                    ctx_t[:, pl.ds(pl.multiple_of(half * seq, seq), seq)] = ref[:, :head].T
+
+        for (left, _), right, out in zip(groups, rights, outs):
+            ref = ctx_t if left is None else left_refs.pop(0)
+            out[...] = dot(ref[...], right[...].reshape(2 * seq, tile), NN)
 
     slab = pl.BlockSpec((2, seq, tile), lambda step: (0, 0, step))
-    out = lambda size: pl.BlockSpec((size, tile), lambda step: (0, step))
     return pl.pallas_call(
         kernel,
-        name='weight_grads_mlp',
+        name=name,
         grid=(width // tile,),
-        out_shape=[shape((depth, width), F32)] * 3 + [shape((head, width), F32)],
-        in_specs=[slab] * 3 + [VMEM] * 3 + [ANY],
-        out_specs=[out(depth)] * 3 + [out(head)],
-        scratch_shapes=[pltpu.VMEM((head, 2 * seq), BF16)],
+        out_shape=[shape((size, width), F32) for size in sizes],
+        in_specs=[slab] * len(groups) + [VMEM] * (len(lefts) + len(ctxs)) + [ANY] * len(tokens),
+        out_specs=[pl.BlockSpec((size, tile), lambda step: (0, step)) for size in sizes],
+        scratch_shapes=[pltpu.VMEM((head, 2 * seq), BF16)] if ctxs else [],
         compiler_params=pltpu.CompilerParams(vmem_limit_bytes=LIMIT),
-        cost_estimate=pl.CostEstimate(flops=int(18e9), bytes_accessed=int(6e7), transcendentals=0),
-    )(mixed_full, grad_out, resid_full, left, *ctxs, token)
+        cost_estimate=pl.CostEstimate(flops=int(1e10), bytes_accessed=int(4e7), transcendentals=0),
+    )(*[right for _, right in groups], *lefts, *ctxs, *tokens)
+
+
+def weight_grads_pair(left_gate, left_up, mixed_full):
+    seq, width = mixed_full.shape[1:]
+    depth = left_gate.shape[K0]
+    tile = min(512, width)
+
+    def kernel(m_ref, gate_ref, up_ref, out_gate, out_up):
+        mixed = m_ref[...].reshape(2 * seq, tile)
+        out_gate[...] = dot(gate_ref[...], mixed, NN)
+        out_up[...] = dot(up_ref[...], mixed, NN)
+
+    out = pl.BlockSpec((depth, tile), lambda step: (0, step))
+    return pl.pallas_call(
+        kernel,
+        name='weight_grads_pair',
+        grid=(width // tile,),
+        out_shape=[shape((depth, width), F32)] * 2,
+        in_specs=[pl.BlockSpec((2, seq, tile), lambda step: (0, 0, step)), VMEM, VMEM],
+        out_specs=[out, out],
+        compiler_params=pltpu.CompilerParams(vmem_limit_bytes=LIMIT),
+        cost_estimate=pl.CostEstimate(flops=int(1e10), bytes_accessed=int(4e7), transcendentals=0),
+    )(mixed_full, left_gate, left_up)
 
 
 def weight_grads_qkv(normeds, kv_full, grads_q):
@@ -1028,10 +1125,12 @@
         resid_full = second.full.reshape(2, seq_len, width)
 
         (y_out,) = in_place(lax.all_gather(second.y_rows, 'tp'), rows)
-        dqkv = attention_backward(flat(second.own), seg_ids, w_outs, attn.qkv)
+        left_gate, left_up, left_act = second.lefts
+        grad_gate_t, grad_up_t = weight_grads_pair(left_gate, left_up, mixed_full)
+        dqkv = attention_backward(flat(second.own), seg_ids, w_outs, attn.qkv, grad_up_t)
         third = sum_input(side, dqkv, w_qs, w_k, w_v, hidden, second, gain_attn_row)
         grad_in, grad_gain_attn, grad_gain_mlp = in_place(lax.all_gather(third.rows, 'tp'), rows)
-        grad_gate_t, grad_up_t, grad_w_down, grad_w_o = weight_grads_mlp(mixed_full, grad_out, resid_full, second.left, (attn.ctx, flat(mlp.ctx_other)), third.q_other)
+        grad_w_down, grad_w_o = weight_grads('weight_grads_down', [(left_act, grad_out), (None, resid_full)], (attn.ctx, flat(mlp.ctx_other)), (third.q_other,))
         grad_w_q, grad_w_k, grad_w_v = weight_grads_qkv((attn.normed, mlp.normed_other), third.kv, (dqkv, flat(third.q_other)))
         return (y_out.reshape(hidden.shape), grad_in.reshape(hidden.shape), grad_gain_attn[K0], grad_gain_mlp[K0], grad_w_q, grad_w_k, grad_w_v, grad_w_o, grad_gate_t.T, grad_up_t.T, grad_w_down)
 

time: 457 us -> 447 us (0.978)
  Pallas kernels: 435 us -> 425 us
    pallas_call x5, Pallas kernels: 348 us -> 332 us  [call_kernel(): pl.pallas_call(kernel, name=name, out_shape=[leaf[K0] for leaf in out_lea...]
    pallas_call x1 -> x2, Pallas kernels: 27.3 us -> 33.4 us  [the longest x1 16.7 us: weight_grads_pair(): pl.pallas_call(kernel, name='weight_grads_pair', grid=(width // tile,), o...]
where the time goes in v7:
time: 447 us; the launch traced here: 440 us
  Pallas kernels  425 us (95%)
  between operations  14.6 us (3%)
    pallas_call x5, Pallas kernels, call_kernel(): pl.pallas_call(kernel, name=name, out_shape=[leaf[K0] for leaf in out_lea...  332 us
    pallas_call x1, Pallas kernels, weight_grads_qkv(): pl.pallas_call(kernel, name='weight_grads_qkv', grid=(width // tile,), ou...  39.4 us
    pallas_call x2, Pallas kernels, in_place(): pl.pallas_call(kernel, name='in_place', out_shape=[shape((2, blocks // 2,...  20.3 us
    pallas_call x1, Pallas kernels, weight_grads_pair(): pl.pallas_call(kernel, name='weight_grads_pair', grid=(width // tile,), o...  16.7 us
    pallas_call x1, Pallas kernels, weight_grads(): pl.pallas_call(kernel, name=name, grid=(width // tile,), out_shape=[shape...  16.7 us
  transfers between devices with their start and end apart: 2, of which 0 were waited for; matrix products, arithmetic and copies ran while one was open for 0% of the time, Pallas kernels for 40%

profile of v7, /device:TPU:97, one launch (start us, length us, event | category | flops | bytes accessed | tf_op | source)
XLA Modules:
  0.0 439.5 jit_solution(4313509797307100076)
XLA Ops:
  7.2 0.1 all-gather.5.cloned.1.call-start
  7.3 15.1 %attention_forward.1 = (bf16[768,256]{1,0:T(8,128)(2,1)}, bf16[768,4096]{1,0:T(8,128)(2,1)}, bf16[768,512]{1,0:T(8,128)(2,1)}, bf16[128,4096]{1,0:T(8,128)(2,1)}, bf16[4096,128]{1,0:T(8,128)(2,1)}) custom-call(f32[1,4096]{1,0:T(1,128)} %bitcast.32, bf16[2,768,4096]{2,1,0:T(8,128)(2,1)} %refs_4_.5, s32[2,768]{1,0:T(2,128)} %refs_2_.5, ...), custom_call_target="tpu_custom_call" | custom-call | flops 5000000000 | bytes 40000000 | tf_op jit(solution)/shard_map/attention_forward/pallas_call | solution.py:485
  22.4 97.8 %sum_attention.1 = (bf16[4,4,48,448]{3,2,1,0:T(8,128)(2,1)}, bf16[4,4,48,448]{3,2,1,0:T(8,128)(2,1)}, bf16[4,4,48,128]{3,2,1,0:T(8,128)(2,1)}, bf16[2,4,4,48,409...) custom-call(bf16[4,4,48,256]{3,2,1,0:T(8,128)(2,1)} %bitcast.29, ...), custom_call_target="tpu_custom_call" | custom-call | flops 400000000 | bytes 40000000 | tf_op jit(solution)/shard_map/sum_attention/pallas_call | solution.py:485
  120.2 125.9 %sum_mlp.1 = (f32[48,4096]{1,0:T(8,128)}, bf16[2,4,4,48,4096]{4,3,2,1,0:T(8,128)(2,1)}, f32[1,4096]{1,0:T(1,128)}, bf16[448,1536]{1,0:T(8,128)(2,1)}, bf16[448,1...) custom-call(bf16[4,4,48,448]{3,2,1,0:T(8,128)(2,1)} %get-tuple-element, ...), custom_call_target="tpu_custom_call" | custom-call | flops 600000000 | bytes 40000000 | tf_op jit(solution)/shard_map/sum_mlp/pallas_call | solution.py:485
  246.1 0.1 all-gather.5.cloned.1.call-update
  246.2 0.1 all-gather.7.cloned.1.call-start
  246.2 16.7 %weight_grads_pair.1 = (f32[448,4096]{1,0:T(8,128)}, f32[448,4096]{1,0:T(8,128)}) custom-call(bf16[2,768,4096]{2,1,0:T(8,128)(2,1)} %bitcast.35, bf16[448,1536]{1,0:T(8,128)(2,1)} %get-tuple-element.68.gate_ref, bf16[448,1536]{1,0:T(8,128)(2,1)} %get-tuple-element.69.up_ref), custom_call_target="tpu_custom_call" | custom-call | flops 10000000000 | bytes 40000000 | tf_op jit(solution)/shard_map/weight_grads_pair/pallas_call | solution.py:1007
  262.9 13.3 %attention_backward.1.q_own = bf16[768,512]{1,0:T(8,128)(2,1)} custom-call(bf16[768,512]{1,0:T(8,128)(2,1)} %get-tuple-element.65.refs_0_, bf16[768,4096]{1,0:T(8,128)(2,1)} %bitcast.27, s32[2,768]{1,0:T(2,128)} %refs_2_.5, f32[448,4096]{1,0:T(8,128)} %get-tuple-element.70.refs_3_, bf16[128,4096]{1,0:T(8,128)(2,1)} %refs_4_.4, ...), custom_call_target="tpu_custom_call" | custom-call | flops 4000000000 | bytes 40000000 | tf_op jit(solution)/shard_map/attention_backward/pallas_call | solution.py:485
  276.2 79.5 %sum_input.1 = (bf16[2,768,2048]{2,1,0:T(8,128)(2,1)}, bf16[4,4,48,128]{3,2,1,0:T(8,128)(2,1)}, bf16[56,4096]{1,0:T(8,128)(2,1)}) custom-call(f32[48,4096]{1,0:T(8,128)} %get-tuple-element.64.refs_0_, bf16[4,4,48,512]{3,2,1,0:T(8,128)(2,1)} %bitcast.28, f32[1,4096]{1,0:T(1,128)} %bitcast.33, f32[1,4096]{1,0:T(1,128)} %get-tuple-element.71.refs_3_, ...), custom_call_target="tpu_custom_call" | custom-call | flops 300000000 | bytes 40000000 | tf_op jit(solution)/shard_map/sum_input/pallas_call | solution.py:485
  355.7 0.1 all-gather.7.cloned.1.call-update
  355.8 16.7 %weight_grads_down.1 = (f32[448,4096]{1,0:T(8,128)}, f32[128,4096]{1,0:T(8,128)}) custom-call(bf16[2,768,4096]{2,1,0:T(8,128)(2,1)} %refs_0_.1, bf16[2,768,4096]{2,1,0:T(8,128)(2,1)} %bitcast.34, bf16[448,1536]{1,0:T(8,128)(2,1)} %get-tuple-element.84.refs_2_, bf16[768,256]{1,0:T(8,128)(2,1)} %get-tuple-element.50.refs_3_, bf16[768,128]{1,0:T(8,128)(2,1)} %bitcast.37, ...), custom_call_target="tpu_custom_call" | custom-call | flops 10000000000 | bytes 40000000 | tf_op jit(solution)/shard_map/weight_grads_down/pallas_call | solution.py:983
  372.5 39.4 %weight_grads_qkv.1 = (f32[4096,128]{1,0:T(8,128)}, f32[4096,1024]{1,0:T(8,128)}, f32[4096,1024]{1,0:T(8,128)}) custom-call(bf16[768,4096]{1,0:T(8,128)(2,1)} %get-tuple-element.51.refs_4_.a_own, bf16[768,4096]{1,0:T(8,128)(2,1)} %get-tuple-element.77.a_other, bf16[2,768,2048]{2,1,0:T(8,128)(2,1)} %get-tuple-element.78.kv_ref, ...), custom_call_target="tpu_custom_call" | custom-call | flops 27000000512 | bytes 60000000 | tf_op jit(solution)/shard_map/weight_grads_qkv/pallas_call | solution.py:1043
  411.8 0.0 all-gather.5.cloned.1.call-done
  411.8 9.3 %in_place.2 = bf16[2,16,48,4096]{3,2,1,0:T(8,128)(2,1)} custom-call(bf16[32,48,4096]{2,1,0:T(8,128)(2,1)} %bitcast.24), custom_call_target="tpu_custom_call" | custom-call | flops 20000000 | bytes 20000000 | tf_op jit(solution)/shard_map/in_place/pallas_call | solution.py:1091
  421.2 0.0 all-gather.7.cloned.1.call-done
  421.2 11.0 %in_place.3 = (bf16[2,16,48,4096]{3,2,1,0:T(8,128)(2,1)}, f32[1,4096]{1,0:T(1,128)}, f32[1,4096]{1,0:T(1,128)}) custom-call(bf16[32,56,4096]{2,1,0:T(8,128)(2,1)} %bitcast.23), custom_call_target="tpu_custom_call" | custom-call | flops 20000000 | bytes 20000000 | tf_op jit(solution)/shard_map/in_place/pallas_call | solution.py:1091
Async XLA Ops:
  7.2 404.6 %all-gather.5.cloned.1.call-start = ((), (), s32[]{:S(2)}) async-start(), calls=%async_computation | async-start | bytes 12976128 | tf_op jit(solution)/shard_map/all_gather | solution.py:1127
  246.2 175.0 %all-gather.7.cloned.1.call-start = ((), (), s32[]{:S(2)}) async-start(), calls=%async_computation.1 | async-start | bytes 15138816 | tf_op jit(solution)/shard_map/all_gather | solution.py:1132
Sparse Core Ops, SparseCore 0:
  246.3 69.1 all-gather.4
  355.9 63.3 all-gather.6

commit v8 on v7

--- a/solution.py
+++ b/solution.py
@@ -182,6 +182,15 @@
                 call(self.relay, K3), call(self.end, K2), call(self.near2, K1), call(self.relay2, K1), call(self.end, K3),
                 self.end2]
 
+    def slow_steps(self, fill):
+        call = functools.partial
+        steps = range(self.torus.side)
+        result = [call(fill, K2)] + [call(self.far, step) for step in steps] + [call(fill, K1), call(fill, K3)]
+        for step in steps:
+            result += [call(self.near, step), call(self.relay, step)]
+        return result + [call(fill, K0), call(self.end, K0), self.far2, call(self.end, K1), call(self.near2, K0), call(self.relay2, K0),
+                         call(self.end, K2), call(self.near2, K1), call(self.relay2, K1), call(self.end, K3), self.end2]
+
 
 class AllGather:
     def __init__(self, torus, scr, by_rows):
@@ -255,22 +264,19 @@
         call = functools.partial
         whole = whole or (lambda step: None)
         here, beside, across = (K0,), (K1, self.torus.side - 1), (K2,)
+
+        def rest(step):
+            return [call(self.arrive1, step, K1), call(self.keep, step, beside), call(self.relayed1, step), call(self.keep, step, across), call(whole, step)]
+
         result = []
         for turn in PAIR:
             result += [call(self.own2, turn), call(self.send1, K0, turn)]
-        result += [call(self.keep, K0, here), call(self.arrive2, K0, K0), call(self.arrive2, K1, K0)]
-        for way in PAIR:
-            step = way + K1
-            result += [call(self.arrive2, way, K1), call(self.send1, step, K0), call(self.send1, step, K1), call(self.keep, step, here)]
-        result += [call(self.arrive1, K0, K0), self.relayed2, call(self.send1, K3, K0), call(self.send1, K3, K1), call(self.keep, K3, here),
-                   call(self.arrive1, K0, K1), call(self.keep, K0, beside), call(self.arrive1, K1, K0), call(self.arrive1, K2, K0),
-                   call(self.relayed1, K0), call(self.keep, K0, across), call(whole, K0)]
-        for step in (K1, K2):
-            result += [call(self.arrive1, step, K1), call(self.keep, step, beside)]
-        result += [call(self.arrive1, K3, K0)]
-        for step in (K1, K2):
-            result += [call(self.relayed1, step), call(self.keep, step, across), call(whole, step)]
-        return result + [call(self.arrive1, K3, K1), call(self.keep, K3, beside), call(self.relayed1, K3), call(self.keep, K3, across), call(whole, K3)]
+        result += [call(self.keep, K0, here), call(self.arrive2, K0, K0), call(self.arrive2, K1, K0), call(self.arrive1, K0, K0),
+                   call(self.arrive2, K0, K1), call(self.send1, K1, K0), call(self.send1, K1, K1), call(self.keep, K1, here),
+                   call(self.arrive2, K1, K1), call(self.send1, K2, K0), call(self.keep, K2, here),
+                   call(self.arrive1, K1, K0), call(self.send1, K2, K1), self.relayed2, call(self.send1, K3, K0), call(self.keep, K3, here)]
+        result += rest(K0) + [call(self.arrive1, K2, K0), call(self.send1, K3, K1)]
+        return result + rest(K1) + [call(self.arrive1, K3, K0)] + rest(K2) + rest(K3)
 
 
 class Store:
@@ -644,8 +650,8 @@
         dy_load = pltpu.make_async_copy(ins.grad_out.at[torus.core, rows_at, :], scr.dy_rows, scr.dy_sem.at[K0])
         dy_load.start()
         wait = torus.signal_all()
-        steps = ReduceScatter(torus, scr.sum).steps(fill_partial(torus, scr.sum.part, ins.grads, weights))
-        steps_p = ReduceScatter(torus, scr.sum_p).steps(fill_partial(torus, scr.sum_p.part, ins.acts, weights_p))
+        steps = ReduceScatter(torus, scr.sum).slow_steps(fill_partial(torus, scr.sum.part, ins.grads, weights))
+        steps_p = ReduceScatter(torus, scr.sum_p).slow_steps(fill_partial(torus, scr.sum_p.part, ins.acts, weights_p))
         staging.wait()
         steps[K0]()
         wait()
@@ -672,13 +678,9 @@
                 turned.append(torus.pending.pop().wait_send)
 
         turns = [functools.partial(turn, index) for index in range(6)]
-        fills = (K0, K3, 4, 10)
-        early = [steps_p[index] for index in fills]
-        rest_p = [step for index, step in enumerate(steps_p) if index not in fills]
-        late = 22
-        run(steps[1:late], early)
-        for step in rest_p[:3]:
-            step()
+        late, begun = 18, 3
+        run(steps[1:late])
+        run(steps_p[:begun])
         run(steps[late:])
         own = (torus.y, torus.x)
         gain_total = jnp.zeros((1, width), F32)
@@ -694,7 +696,7 @@
         staging.save(outs.d_rows, outs.gain)
         gather = AllGather(torus, scr.all, False)
         gather.store = Store(torus, scr.all, plain_places(gather, outs.full), outs.own)
-        run(gather.steps(), rest_p[3:], turns)
+        run(gather.steps(), steps_p[begun:], turns)
         for at in row_tiles(rows):
             outs.y_rows[at, :] = (ins.h_rows[at, :].astype(F32) + scr.sum_p.part[(*own, at, slice(None))].astype(F32)).astype(BF16)
         staging.save(outs.y_rows)
@@ -716,8 +718,53 @@
     return call_kernel('sum_mlp', body, ins, outs, scratch, 6e8, 2)
 
 
-def sum_input(side, dqkv, w_qs, w_k, w_v, hidden, second, gain):
-    seq, depth = dqkv.shape
+def attention_backward(side, ins, outs, scr, staging):
+    resid = scr.sum.part
+    rows, width = resid.shape[2:]
+    band = side * rows
+    tile = min(256, side * band)
+    loads = []
+    for index in PAIR:
+        at = pl.ds(index * HEAD_DIM, HEAD_DIM)
+        loads.append(pltpu.make_async_copy(ins.w_outs[index], scr.w_out.at[at, :], scr.w_out_sem.at[index]))
+    for index in range(side):
+        loads.append(pltpu.make_async_copy(ins.resid.at[index], resid.at[index], scr.resid_sem.at[index]))
+    for load in loads:
+        load.start()
+    for load in loads[:2]:
+        load.wait()
+    for index in range(side):
+        loads[2 + index].wait()
+        scr.grad_ctx[index * band:(index + 1) * band, :] = dot(resid[index].reshape(band, width), scr.w_out[...], NT).astype(BF16)
+    staging.wait()
+    seg_row, seg_col = segments(ins.seg)
+    keys_t = ins.qkv[:, 2 * HEAD_DIM:3 * HEAD_DIM].T
+    scr.grad_k[...] = jnp.zeros_like(scr.grad_k)
+    scr.grad_v[...] = jnp.zeros_like(scr.grad_v)
+
+    def put(first, count, cols, value):
+        for start in range(first, first + count, 16):
+            where = (start // band, start // rows % side, slice(start % rows, start % rows + 16), cols)
+            outs.dqkv[where] = value[start - first:start - first + 16].astype(BF16)
+
+    for head_index in PAIR:
+        cols = slice(head_index * HEAD_DIM, (head_index + 1) * HEAD_DIM)
+        for tile_index in range(side * band // tile):
+            reach = (tile_index + 1) * tile
+            probs, queries = scores_softmax(ins.qkv, seg_row, seg_col, head_index, tile_index, tile)
+            grad_ctx = scr.grad_ctx[tile_index * tile:reach, cols]
+            grad_probs = dot(ins.qkv[:reach, 3 * HEAD_DIM:], grad_ctx, NT)
+            centre = jnp.sum(grad_probs * probs, axis=0, keepdims=True)
+            grad_scores = (probs * (grad_probs - centre) * HEAD_DIM ** -0.5).astype(BF16)
+            scr.grad_v[:reach, :] += dot(probs.astype(BF16), grad_ctx, NN)
+            scr.grad_k[:reach, :] += dot(grad_scores, queries, NN)
+            put(tile_index * tile, tile, cols, dot(keys_t[:, :reach], grad_scores, NN).T)
+    for index, ref in ((2, scr.grad_k), (3, scr.grad_v)):
+        put(0, side * band, slice(index * HEAD_DIM, (index + 1) * HEAD_DIM), ref[...])
+
+
+def sum_input(side, qkv, seg_ids, w_outs, w_qs, w_k, w_v, hidden, second, gain, token):
+    seq, depth = qkv.shape
     width = gain.shape[K1]
     rows = seq // (side * side)
     head = depth // 4
@@ -733,7 +780,7 @@
         weights.start()
         wait = torus.signal_all()
         part = scr.sum.part
-        steps = ReduceScatter(torus, scr.sum).steps(fill_partial(torus, part, [ins.dqkv], weights))
+        steps = ReduceScatter(torus, scr.sum).steps(fill_partial(torus, part, [outs.dqkv], weights))
         own = (torus.y, torus.x)
         gat = scr.all.gat
         gather = AllGather(torus, scr.all, True)
@@ -755,15 +802,16 @@
 
         def mate_add():
             torus.arrive(scr.mate, scr.mate_sems, 0)
-            mine = ins.dqkv[pl.ds(place * half_side, half_side), :, :, kv_cols]
+            mine = outs.dqkv[pl.ds(place * half_side, half_side), :, :, kv_cols]
             gat[own] = (mine.astype(F32) + scr.mate[...].astype(F32)).astype(BF16).reshape(tokens, 2 * head)
 
-        staging.wait()
+        attention_backward(side, ins, outs, scr, staging)
+        staging.save(outs.dqkv)
         steps[K0]()
         wait()
-        swaps = [(ins.dqkv.at[:, :, :, pl.ds(head, head)], outs.q_other)]
+        swaps = [(outs.dqkv.at[:, :, :, pl.ds(head, head)], outs.q_other)]
         swap_start(torus, scr.swap_sems, swaps)
-        torus.send(ins.dqkv.at[pl.ds((1 - place) * half_side, half_side), :, :, kv_cols], scr.mate, scr.mate_sems, 0, mate)
+        torus.send(outs.dqkv.at[pl.ds((1 - place) * half_side, half_side), :, :, kv_cols], scr.mate, scr.mate_sems, 0, mate)
         for step in steps[1:5]:
             step()
         mate_add()
@@ -788,10 +836,11 @@
         torus.drain()
 
     dma = pltpu.SemaphoreType.DMA
-    ins = dict(dqkv=(dqkv.reshape(side, side, rows, depth), VMEM), w_qs=[(weight, ANY) for weight in w_qs], w_k=(w_k, ANY), w_v=(w_v, ANY), hidden=(hidden, ANY), d_rows=(second.d_rows, VMEM),
+    ins = dict(qkv=(qkv, VMEM), seg=(seg_ids, VMEM), resid=(second.own, ANY), w_outs=[(weight, ANY) for weight in w_outs], token=(token, ANY), w_qs=[(weight, ANY) for weight in w_qs], w_k=(w_k, ANY), w_v=(w_v, ANY), hidden=(hidden, ANY), d_rows=(second.d_rows, VMEM),
                gain=(gain, VMEM), gain_mlp=(second.gain, VMEM))
-    outs = dict(rows=(shape((rows + 8, width)), VMEM), kv=(shape((2, seq, 2 * kv_width)), ANY), q_other=(shape((side, side, rows, head)), ANY))
-    scratch = dict(sum=rs_scratch(side, rows, width), all=ag_scratch(side, tokens, 2 * head, 2), x_rows=pltpu.VMEM((rows, width), BF16), x_sem=dma((K1,)), w=pltpu.VMEM((width, depth), BF16), w_sem=dma((K2, 4)),
+    outs = dict(rows=(shape((rows + 8, width)), VMEM), kv=(shape((2, seq, 2 * kv_width)), ANY), q_other=(shape((side, side, rows, head)), ANY), dqkv=(shape((side, side, rows, depth)), VMEM))
+    scratch = dict(w_out=pltpu.VMEM((2 * head, width), BF16), grad_ctx=pltpu.VMEM((seq, 2 * head), BF16), grad_k=pltpu.VMEM((seq, head), F32), grad_v=pltpu.VMEM((seq, head), F32), w_out_sem=dma((K2,)), resid_sem=dma((side,)),
+                   sum=rs_scratch(side, rows, width), all=ag_scratch(side, tokens, 2 * head, 2), x_rows=pltpu.VMEM((rows, width), BF16), x_sem=dma((K1,)), w=pltpu.VMEM((width, depth), BF16), w_sem=dma((K2, 4)),
                    mate=pltpu.VMEM((half_side, side, rows, 2 * head), BF16), mate_sems=[dma((K1,)), dma((K1,))], swap_sems=[dma((K1,)), dma((K1,))])
     return call_kernel('sum_input', body, ins, outs, scratch, 3e8, 3)
 
@@ -904,57 +953,6 @@
     return call_kernel('attention_forward', body, ins, outs, scratch, 5e9, 4)
 
 
-def attention_backward(resid, seg_ids, w_outs, qkv, token):
-    seq, width = resid.shape
-    chunk = seq // 4
-    tile = min(256, seq)
-    depth = 4 * HEAD_DIM
-
-    def body(ins, outs, scr, staging):
-        loads = []
-        for index in PAIR:
-            at = pl.ds(index * HEAD_DIM, HEAD_DIM)
-            loads.append(pltpu.make_async_copy(ins.w_outs[index], scr.w.at[at, :], scr.w_sem.at[index]))
-        for index in range(4):
-            at = pl.ds(index * chunk, chunk)
-            loads.append(pltpu.make_async_copy(ins.resid.at[at, :], scr.resid.at[at, :], scr.in_sem.at[index]))
-        for load in loads:
-            load.start()
-        for load in loads[:2]:
-            load.wait()
-        staging.wait()
-        for index in range(4):
-            loads[2 + index].wait()
-            at = pl.ds(index * chunk, chunk)
-            scr.grad_ctx[at, :] = dot(scr.resid[at, :], scr.w[...], NT).astype(BF16)
-        seg_row, seg_col = segments(ins.seg)
-        keys_t = ins.qkv[:, 2 * HEAD_DIM:3 * HEAD_DIM].T
-        scr.grad_k[...] = jnp.zeros_like(scr.grad_k)
-        scr.grad_v[...] = jnp.zeros_like(scr.grad_v)
-        for head_index in PAIR:
-            cols = slice(head_index * HEAD_DIM, (head_index + 1) * HEAD_DIM)
-            for tile_index in range(seq // tile):
-                reach = (tile_index + 1) * tile
-                rows = slice(tile_index * tile, reach)
-                probs, queries = scores_softmax(ins.qkv, seg_row, seg_col, head_index, tile_index, tile)
-                grad_ctx = scr.grad_ctx[rows, cols]
-                grad_probs = dot(ins.qkv[:reach, 3 * HEAD_DIM:], grad_ctx, NT)
-                centre = jnp.sum(grad_probs * probs, axis=0, keepdims=True)
-                grad_scores = (probs * (grad_probs - centre) * HEAD_DIM ** -0.5).astype(BF16)
-                scr.grad_v[:reach, :] += dot(probs.astype(BF16), grad_ctx, NN)
-                scr.grad_k[:reach, :] += dot(grad_scores, queries, NN)
-                outs.dqkv[rows, cols] = dot(keys_t[:, :reach], grad_scores, NN).T.astype(BF16)
-        outs.dqkv[:, 2 * HEAD_DIM:3 * HEAD_DIM] = scr.grad_k[...].astype(BF16)
-        outs.dqkv[:, 3 * HEAD_DIM:] = scr.grad_v[...].astype(BF16)
-
-    dma = pltpu.SemaphoreType.DMA
-    ins = dict(resid=(resid, ANY), seg=(seg_ids, VMEM), w_outs=[(weight, ANY) for weight in w_outs], qkv=(qkv, VMEM), token=(token, ANY))
-    outs = dict(dqkv=(shape((seq, depth)), VMEM))
-    scratch = dict(resid=pltpu.VMEM((seq, width), BF16), w=pltpu.VMEM((2 * HEAD_DIM, width), BF16), grad_ctx=pltpu.VMEM((seq, 2 * HEAD_DIM), BF16),
-                   grad_k=pltpu.VMEM((seq, HEAD_DIM), F32), grad_v=pltpu.VMEM((seq, HEAD_DIM), F32), w_sem=dma((K2,)), in_sem=dma((4,)))
-    return call_kernel('attention_backward', body, ins, outs, scratch, 4e9).dqkv
-
-
 def weight_grads(name, groups, ctxs, tokens=()):
     seq, width = groups[K0][K1].shape[1:]
     head = ctxs[K1].shape[K1] if ctxs else 0
@@ -1127,11 +1125,10 @@
         (y_out,) = in_place(lax.all_gather(second.y_rows, 'tp'), rows)
         left_gate, left_up, left_act = second.lefts
         grad_gate_t, grad_up_t = weight_grads_pair(left_gate, left_up, mixed_full)
-        dqkv = attention_backward(flat(second.own), seg_ids, w_outs, attn.qkv, grad_up_t)
-        third = sum_input(side, dqkv, w_qs, w_k, w_v, hidden, second, gain_attn_row)
+        third = sum_input(side, attn.qkv, seg_ids, w_outs, w_qs, w_k, w_v, hidden, second, gain_attn_row, grad_up_t)
         grad_in, grad_gain_attn, grad_gain_mlp = in_place(lax.all_gather(third.rows, 'tp'), rows)
         grad_w_down, grad_w_o = weight_grads('weight_grads_down', [(left_act, grad_out), (None, resid_full)], (attn.ctx, flat(mlp.ctx_other)), (third.q_other,))
-        grad_w_q, grad_w_k, grad_w_v = weight_grads_qkv((attn.normed, mlp.normed_other), third.kv, (dqkv, flat(third.q_other)))
+        grad_w_q, grad_w_k, grad_w_v = weight_grads_qkv((attn.normed, mlp.normed_other), third.kv, (flat(third.dqkv), flat(third.q_other)))
         return (y_out.reshape(hidden.shape), grad_in.reshape(hidden.shape), grad_gain_attn[K0], grad_gain_mlp[K0], grad_w_q, grad_w_k, grad_w_v, grad_w_o, grad_gate_t.T, grad_up_t.T, grad_w_down)
 
     spec_act = P('data', None, None)

time: 447 us -> 435 us (0.973)
  Pallas kernels: 425 us -> 413 us
    pallas_call x5 -> x4, Pallas kernels: 332 us -> 320 us  [call_kernel(): pl.pallas_call(kernel, name=name, out_shape=[leaf[K0] for leaf in out_lea...]
  transfers between devices with their start and end apart: 2 -> 2, of which waited for: 0 -> 0; matrix products, arithmetic and copies ran while one was open for 0% -> 0% of each run, Pallas kernels for 40% -> 41%
where the time goes in v8:
time: 435 us; the launch traced here: 428 us
  Pallas kernels  413 us (95%)
  between operations  14.4 us (3%)
    pallas_call x4, Pallas kernels, call_kernel(): pl.pallas_call(kernel, name=name, out_shape=[leaf[K0] for leaf in out_lea...  320 us
    pallas_call x1, Pallas kernels, weight_grads_qkv(): pl.pallas_call(kernel, name='weight_grads_qkv', grid=(width // tile,), ou...  39.4 us
    pallas_call x2, Pallas kernels, in_place(): pl.pallas_call(kernel, name='in_place', out_shape=[shape((2, blocks // 2,...  20.3 us
    pallas_call x1, Pallas kernels, weight_grads(): pl.pallas_call(kernel, name=name, grid=(width // tile,), out_shape=[shape...  16.7 us
    pallas_call x1, Pallas kernels, weight_grads_pair(): pl.pallas_call(kernel, name='weight_grads_pair', grid=(width // tile,), o...  16.5 us
  transfers between devices with their start and end apart: 2, of which 0 were waited for; matrix products, arithmetic and copies ran while one was open for 0% of the time, Pallas kernels for 41%

profile of v8, /device:TPU:97, one launch (start us, length us, event | category | flops | bytes accessed | tf_op | source)
XLA Modules:
  0.0 427.6 jit_solution(12151952239820494100)
XLA Ops:
  7.2 0.1 all-gather.5.cloned.1.call-start
  7.3 15.1 %attention_forward.1 = (bf16[768,256]{1,0:T(8,128)(2,1)}, bf16[768,4096]{1,0:T(8,128)(2,1)}, bf16[768,512]{1,0:T(8,128)(2,1)}, bf16[128,4096]{1,0:T(8,128)(2,1)}, bf16[4096,128]{1,0:T(8,128)(2,1)}) custom-call(f32[1,4096]{1,0:T(1,128)} %bitcast.29, bf16[2,768,4096]{2,1,0:T(8,128)(2,1)} %refs_3_.7, s32[2,768]{1,0:T(2,128)} %refs_6_.3, ...), custom_call_target="tpu_custom_call" | custom-call | flops 5000000000 | bytes 40000000 | tf_op jit(solution)/shard_map/attention_forward/pallas_call | solution.py:491
  22.3 91.8 %sum_attention.1 = (bf16[4,4,48,448]{3,2,1,0:T(8,128)(2,1)}, bf16[4,4,48,448]{3,2,1,0:T(8,128)(2,1)}, bf16[4,4,48,128]{3,2,1,0:T(8,128)(2,1)}, bf16[2,4,4,48,409...) custom-call(bf16[4,4,48,256]{3,2,1,0:T(8,128)(2,1)} %bitcast.26, ...), custom_call_target="tpu_custom_call" | custom-call | flops 400000000 | bytes 40000000 | tf_op jit(solution)/shard_map/sum_attention/pallas_call | solution.py:491
  114.1 118.8 %sum_mlp.1 = (f32[48,4096]{1,0:T(8,128)}, bf16[2,4,4,48,4096]{4,3,2,1,0:T(8,128)(2,1)}, f32[1,4096]{1,0:T(1,128)}, bf16[448,1536]{1,0:T(8,128)(2,1)}, bf16[448,1...) custom-call(bf16[4,4,48,448]{3,2,1,0:T(8,128)(2,1)} %get-tuple-element, ...), custom_call_target="tpu_custom_call" | custom-call | flops 600000000 | bytes 40000000 | tf_op jit(solution)/shard_map/sum_mlp/pallas_call | solution.py:491
  232.9 0.1 all-gather.5.cloned.1.call-update
  233.0 0.1 all-gather.7.cloned.1.call-start
  233.1 16.5 %weight_grads_pair.1 = (f32[448,4096]{1,0:T(8,128)}, f32[448,4096]{1,0:T(8,128)}) custom-call(bf16[2,768,4096]{2,1,0:T(8,128)(2,1)} %bitcast.32, bf16[448,1536]{1,0:T(8,128)(2,1)} %get-tuple-element.70.gate_ref, bf16[448,1536]{1,0:T(8,128)(2,1)} %get-tuple-element.71.up_ref), custom_call_target="tpu_custom_call" | custom-call | flops 10000000000 | bytes 40000000 | tf_op jit(solution)/shard_map/weight_grads_pair/pallas_call | solution.py:1005
  249.5 94.5 %sum_input.1 = (bf16[4,4,48,512]{3,2,1,0:T(8,128)(2,1)}, bf16[2,768,2048]{2,1,0:T(8,128)(2,1)}, bf16[4,4,48,128]{3,2,1,0:T(8,128)(2,1)}, bf16[56,4096]{1,0:T(8,128)(2,1)}) custom-call(f32[48,4096]{1,0:T(8,128)} %get-tuple-element.65.refs_0_, f32[1,4096]{1,0:T(1,128)} %bitcast.30, f32[1,4096]{1,0:T(1,128)} %get-tuple-element.66.refs_2_, ...), custom_call_target="tpu_custom_call" | custom-call | flops 300000000 | bytes 40000000 | tf_op jit(solution)/shard_map/sum_input/pallas_call | solution.py:491
  344.0 0.1 all-gather.7.cloned.1.call-update
  344.1 16.7 %weight_grads_down.1 = (f32[448,4096]{1,0:T(8,128)}, f32[128,4096]{1,0:T(8,128)}) custom-call(bf16[2,768,4096]{2,1,0:T(8,128)(2,1)} %refs_0_.1, bf16[2,768,4096]{2,1,0:T(8,128)(2,1)} %bitcast.31, bf16[448,1536]{1,0:T(8,128)(2,1)} %get-tuple-element.86.refs_2_, bf16[768,256]{1,0:T(8,128)(2,1)} %get-tuple-element.51.refs_3_, bf16[768,128]{1,0:T(8,128)(2,1)} %bitcast.35, ...), custom_call_target="tpu_custom_call" | custom-call | flops 10000000000 | bytes 40000000 | tf_op jit(solution)/shard_map/weight_grads_down/pallas_call | solution.py:981
  360.8 39.4 %weight_grads_qkv.1 = (f32[4096,128]{1,0:T(8,128)}, f32[4096,1024]{1,0:T(8,128)}, f32[4096,1024]{1,0:T(8,128)}) custom-call(bf16[768,4096]{1,0:T(8,128)(2,1)} %get-tuple-element.52.refs_4_.a_own, bf16[768,4096]{1,0:T(8,128)(2,1)} %get-tuple-element.78.a_other, bf16[2,768,2048]{2,1,0:T(8,128)(2,1)} %get-tuple-element.79.kv_ref, bf16[768,512]{1,0:T(8,128)(2,1)} %bitcast.34, ...), custom_call_target="tpu_custom_call" | custom-call | flops 27000000512 | bytes 60000000 | tf_op jit(solution)/shard_map/weight_grads_qkv/pallas_call | solution.py:1041
  400.1 0.0 all-gather.5.cloned.1.call-done
  400.1 9.3 %in_place.2 = bf16[2,16,48,4096]{3,2,1,0:T(8,128)(2,1)} custom-call(bf16[32,48,4096]{2,1,0:T(8,128)(2,1)} %bitcast.23), custom_call_target="tpu_custom_call" | custom-call | flops 20000000 | bytes 20000000 | tf_op jit(solution)/shard_map/in_place/pallas_call | solution.py:1089
  409.5 0.0 all-gather.7.cloned.1.call-done
  409.5 11.0 %in_place.3 = (bf16[2,16,48,4096]{3,2,1,0:T(8,128)(2,1)}, f32[1,4096]{1,0:T(1,128)}, f32[1,4096]{1,0:T(1,128)}) custom-call(bf16[32,56,4096]{2,1,0:T(8,128)(2,1)} %bitcast.22), custom_call_target="tpu_custom_call" | custom-call | flops 20000000 | bytes 20000000 | tf_op jit(solution)/shard_map/in_place/pallas_call | solution.py:1089
Async XLA Ops:
  7.2 393.0 %all-gather.5.cloned.1.call-start = ((), (), s32[]{:S(2)}) async-start(), calls=%async_computation | async-start | bytes 12976128 | tf_op jit(solution)/shard_map/all_gather | solution.py:1125
  233.0 176.5 %all-gather.7.cloned.1.call-start = ((), (), s32[]{:S(2)}) async-start(), calls=%async_computation.1 | async-start | bytes 15138816 | tf_op jit(solution)/shard_map/all_gather | solution.py:1129
Sparse Core Ops, SparseCore 0:
  233.1 73.6 all-gather.4
  344.2 63.6 all-gather.6

commit v9 on v8

--- a/solution.py
+++ b/solution.py
@@ -633,7 +633,7 @@
     return call_kernel('sum_attention', body, ins, outs, scratch, 4e8, 1)
 
 
-def sum_mlp(side, mlp, w_gates, w_ups, w_downs, grad_out, gain):
+def sum_mlp(side, mlp, w_gates, w_ups, grad_out, gain):
     depth = w_gates[K0].shape[K0]
     width = gain.shape[K1]
     rows = mlp.h_rows.shape[K0]
@@ -644,14 +644,11 @@
         torus = Torus(side)
         weights = Weights(ins.w_in, scr.w, scr.w_sem, False)
         weights.start()
-        weights_p = Weights(ins.w_downs, scr.wd, scr.wd_sem, False)
-        weights_p.start()
         rows_at = pl.ds(pl.multiple_of(torus.chip * rows, rows), rows)
         dy_load = pltpu.make_async_copy(ins.grad_out.at[torus.core, rows_at, :], scr.dy_rows, scr.dy_sem.at[K0])
         dy_load.start()
         wait = torus.signal_all()
         steps = ReduceScatter(torus, scr.sum).slow_steps(fill_partial(torus, scr.sum.part, ins.grads, weights))
-        steps_p = ReduceScatter(torus, scr.sum_p).slow_steps(fill_partial(torus, scr.sum_p.part, ins.acts, weights_p))
         staging.wait()
         steps[K0]()
         wait()
@@ -678,10 +675,7 @@
                 turned.append(torus.pending.pop().wait_send)
 
         turns = [functools.partial(turn, index) for index in range(6)]
-        late, begun = 18, 3
-        run(steps[1:late])
-        run(steps_p[:begun])
-        run(steps[late:])
+        run(steps[1:])
         own = (torus.y, torus.x)
         gain_total = jnp.zeros((1, width), F32)
         gat = scr.all.gat
@@ -696,10 +690,7 @@
         staging.save(outs.d_rows, outs.gain)
         gather = AllGather(torus, scr.all, False)
         gather.store = Store(torus, scr.all, plain_places(gather, outs.full), outs.own)
-        run(gather.steps(), steps_p[begun:], turns)
-        for at in row_tiles(rows):
-            outs.y_rows[at, :] = (ins.h_rows[at, :].astype(F32) + scr.sum_p.part[(*own, at, slice(None))].astype(F32)).astype(BF16)
-        staging.save(outs.y_rows)
+        run(gather.steps(), turns)
         turned[4]()
         turned[5]()
         for kind in range(3):
@@ -709,21 +700,21 @@
 
     dma = pltpu.SemaphoreType.DMA
     ins = dict(grads=[(grad, VMEM) for grad in (mlp.gates[K0], mlp.ups[K0], mlp.gates[K1], mlp.ups[K1])], acts=[(act, VMEM) for act in mlp.acts],
-               w_in=[(weight, ANY) for weight in (w_gates[K0], w_ups[K0], w_gates[K1], w_ups[K1])], w_downs=[(weight, ANY) for weight in w_downs],
+               w_in=[(weight, ANY) for weight in (w_gates[K0], w_ups[K0], w_gates[K1], w_ups[K1])],
                h_rows=(mlp.h_rows, VMEM), grad_out=(grad_out, ANY), gain=(gain, VMEM))
-    outs = dict(full=(shape((2, *block)), ANY), own=(shape(block), ANY), d_rows=(shape((rows, width), F32), VMEM), gain=(shape((1, width), F32), VMEM), y_rows=(shape((rows, width)), VMEM), lefts=[(shape((depth, 2 * seq)), ANY)] * 3)
-    scratch = dict(sum=rs_scratch(side, rows, width), sum_p=rs_scratch(side, rows, width), all=ag_scratch(side, rows, width), dy_rows=pltpu.VMEM((rows, width), BF16), dy_sem=dma((K1,)),
-                   w=pltpu.VMEM((4 * depth, width), BF16), w_sem=dma((K2, 4)), wd=pltpu.VMEM((2 * depth, width), BF16), wd_sem=dma((K2, K2)),
+    outs = dict(full=(shape((2, *block)), ANY), own=(shape(block), ANY), d_rows=(shape((rows, width), F32), VMEM), gain=(shape((1, width), F32), VMEM), lefts=[(shape((depth, 2 * seq)), ANY)] * 3)
+    scratch = dict(sum=rs_scratch(side, rows, width), all=ag_scratch(side, rows, width), dy_rows=pltpu.VMEM((rows, width), BF16), dy_sem=dma((K1,)),
+                   w=pltpu.VMEM((4 * depth, width), BF16), w_sem=dma((K2, 4)),
                    turn=pltpu.VMEM((2, depth, seq), BF16), turn_sem=dma((K3,)), swap_sems=[dma((K3,)), dma((K3,))])
     return call_kernel('sum_mlp', body, ins, outs, scratch, 6e8, 2)
 
 
-def attention_backward(side, ins, outs, scr, staging):
+def attention_backward(side, ins, outs, scr):
     resid = scr.sum.part
     rows, width = resid.shape[2:]
     band = side * rows
     tile = min(256, side * band)
-    loads = []
+    loads, shared = [], []
     for index in PAIR:
         at = pl.ds(index * HEAD_DIM, HEAD_DIM)
         loads.append(pltpu.make_async_copy(ins.w_outs[index], scr.w_out.at[at, :], scr.w_out_sem.at[index]))
@@ -731,39 +722,46 @@
         loads.append(pltpu.make_async_copy(ins.resid.at[index], resid.at[index], scr.resid_sem.at[index]))
     for load in loads:
         load.start()
-    for load in loads[:2]:
-        load.wait()
-    for index in range(side):
+
+    def context(index):
+        if index == 0:
+            for load in loads[:2]:
+                load.wait()
         loads[2 + index].wait()
         scr.grad_ctx[index * band:(index + 1) * band, :] = dot(resid[index].reshape(band, width), scr.w_out[...], NT).astype(BF16)
-    staging.wait()
-    seg_row, seg_col = segments(ins.seg)
-    keys_t = ins.qkv[:, 2 * HEAD_DIM:3 * HEAD_DIM].T
-    scr.grad_k[...] = jnp.zeros_like(scr.grad_k)
-    scr.grad_v[...] = jnp.zeros_like(scr.grad_v)
+
+    def begin():
+        shared.extend([*segments(ins.seg), ins.qkv[:, 2 * HEAD_DIM:3 * HEAD_DIM].T])
+        scr.grad_k[...] = jnp.zeros_like(scr.grad_k)
+        scr.grad_v[...] = jnp.zeros_like(scr.grad_v)
 
     def put(first, count, cols, value):
         for start in range(first, first + count, 16):
             where = (start // band, start // rows % side, slice(start % rows, start % rows + 16), cols)
             outs.dqkv[where] = value[start - first:start - first + 16].astype(BF16)
 
-    for head_index in PAIR:
+    def head_tile(head_index, tile_index):
         cols = slice(head_index * HEAD_DIM, (head_index + 1) * HEAD_DIM)
-        for tile_index in range(side * band // tile):
-            reach = (tile_index + 1) * tile
-            probs, queries = scores_softmax(ins.qkv, seg_row, seg_col, head_index, tile_index, tile)
-            grad_ctx = scr.grad_ctx[tile_index * tile:reach, cols]
-            grad_probs = dot(ins.qkv[:reach, 3 * HEAD_DIM:], grad_ctx, NT)
-            centre = jnp.sum(grad_probs * probs, axis=0, keepdims=True)
-            grad_scores = (probs * (grad_probs - centre) * HEAD_DIM ** -0.5).astype(BF16)
-            scr.grad_v[:reach, :] += dot(probs.astype(BF16), grad_ctx, NN)
-            scr.grad_k[:reach, :] += dot(grad_scores, queries, NN)
-            put(tile_index * tile, tile, cols, dot(keys_t[:, :reach], grad_scores, NN).T)
-    for index, ref in ((2, scr.grad_k), (3, scr.grad_v)):
-        put(0, side * band, slice(index * HEAD_DIM, (index + 1) * HEAD_DIM), ref[...])
-
-
-def sum_input(side, qkv, seg_ids, w_outs, w_qs, w_k, w_v, hidden, second, gain, token):
+        reach = (tile_index + 1) * tile
+        probs, queries = scores_softmax(ins.qkv, *shared[:2], head_index, tile_index, tile)
+        grad_ctx = scr.grad_ctx[tile_index * tile:reach, cols]
+        grad_probs = dot(ins.qkv[:reach, 3 * HEAD_DIM:], grad_ctx, NT)
+        centre = jnp.sum(grad_probs * probs, axis=0, keepdims=True)
+        grad_scores = (probs * (grad_probs - centre) * HEAD_DIM ** -0.5).astype(BF16)
+        scr.grad_v[:reach, :] += dot(probs.astype(BF16), grad_ctx, NN)
+        scr.grad_k[:reach, :] += dot(grad_scores, queries, NN)
+        put(tile_index * tile, tile, cols, dot(shared[K2][:, :reach], grad_scores, NN).T)
+
+    def end():
+        for index, ref in ((2, scr.grad_k), (3, scr.grad_v)):
+            put(0, side * band, slice(index * HEAD_DIM, (index + 1) * HEAD_DIM), ref[...])
+
+    call = functools.partial
+    tiles = [call(head_tile, head_index, tile_index) for head_index in PAIR for tile_index in range(side * band // tile)]
+    return [call(context, index) for index in range(side)] + [begin] + tiles + [end]
+
+
+def sum_input(side, qkv, seg_ids, w_outs, w_qs, w_k, w_v, hidden, second, gain, mlp, w_downs):
     seq, depth = qkv.shape
     width = gain.shape[K1]
     rows = seq // (side * side)
@@ -778,8 +776,12 @@
         kv_col = pl.multiple_of(lax.div(torus.chip * 2, per_kv) * head, head)
         weights = Weights([*ins.w_qs, ins.w_k.at[:, pl.ds(kv_col, head)], ins.w_v.at[:, pl.ds(kv_col, head)]], scr.w, scr.w_sem, True)
         weights.start()
+        weights_p = Weights(ins.w_downs, scr.wd, scr.wd_sem, False)
+        weights_p.start()
         wait = torus.signal_all()
         part = scr.sum.part
+        attention = attention_backward(side, ins, outs, scr)
+        steps_p = ReduceScatter(torus, scr.sum_p).slow_steps(fill_partial(torus, scr.sum_p.part, ins.acts, weights_p))
         steps = ReduceScatter(torus, scr.sum).steps(fill_partial(torus, part, [outs.dqkv], weights))
         own = (torus.y, torus.x)
         gat = scr.all.gat
@@ -805,23 +807,29 @@
             mine = outs.dqkv[pl.ds(place * half_side, half_side), :, :, kv_cols]
             gat[own] = (mine.astype(F32) + scr.mate[...].astype(F32)).astype(BF16).reshape(tokens, 2 * head)
 
-        attention_backward(side, ins, outs, scr, staging)
+        staging.wait()
+        steps_p[K0]()
+        wait()
+        sent, ringed = 5, 15
+        run(steps_p[1:sent])
+        run(attention, steps_p[sent:ringed])
         staging.save(outs.dqkv)
         steps[K0]()
-        wait()
         swaps = [(outs.dqkv.at[:, :, :, pl.ds(head, head)], outs.q_other)]
         swap_start(torus, scr.swap_sems, swaps)
         torus.send(outs.dqkv.at[pl.ds((1 - place) * half_side, half_side), :, :, kv_cols], scr.mate, scr.mate_sems, 0, mate)
         for step in steps[1:5]:
             step()
         mate_add()
-        run(steps[5:], gather.steps())
+        run(steps[5:], gather.steps(), steps_p[ringed:])
         x_load.wait()
         gain_total = jnp.zeros((1, width), F32)
         for at in row_tiles(rows):
             back, gain_part = rms_back(scr.x_rows[at, :].astype(F32), ins.gain[...], part[(*own, at, slice(None))].astype(F32))
             gain_total = gain_total + gain_part
             outs.rows[at, :] = (ins.d_rows[at, :] + back).astype(BF16)
+            y_at = pl.ds(rows + at.start, at.size)
+            outs.rows[y_at, :] = (ins.h_rows[at, :].astype(F32) + scr.sum_p.part[(*own, at, slice(None))].astype(F32)).astype(BF16)
         row = lax.broadcasted_iota(jnp.int32, (8, width), 0)
         extra = jnp.zeros((8, width), F32)
         for index, value in enumerate((gain_total, ins.gain_mlp[...])):
@@ -829,17 +837,17 @@
                 rounded = value.astype(BF16).astype(F32)
                 extra = jnp.where(row == index * 3 + level, rounded, extra)
                 value = value - rounded
-        outs.rows[rows:rows + 8, :] = extra.astype(BF16)
+        outs.rows[2 * rows:2 * rows + 8, :] = extra.astype(BF16)
         staging.save(outs.rows)
         gather.store.drain()
         swap_end(torus, scr.swap_sems, swaps)
         torus.drain()
 
     dma = pltpu.SemaphoreType.DMA
-    ins = dict(qkv=(qkv, VMEM), seg=(seg_ids, VMEM), resid=(second.own, ANY), w_outs=[(weight, ANY) for weight in w_outs], token=(token, ANY), w_qs=[(weight, ANY) for weight in w_qs], w_k=(w_k, ANY), w_v=(w_v, ANY), hidden=(hidden, ANY), d_rows=(second.d_rows, VMEM),
+    ins = dict(qkv=(qkv, VMEM), seg=(seg_ids, VMEM), resid=(second.own, ANY), w_outs=[(weight, ANY) for weight in w_outs], acts=[(act, VMEM) for act in mlp.acts], w_downs=[(weight, ANY) for weight in w_downs], h_rows=(mlp.h_rows, VMEM), w_qs=[(weight, ANY) for weight in w_qs], w_k=(w_k, ANY), w_v=(w_v, ANY), hidden=(hidden, ANY), d_rows=(second.d_rows, VMEM),
                gain=(gain, VMEM), gain_mlp=(second.gain, VMEM))
-    outs = dict(rows=(shape((rows + 8, width)), VMEM), kv=(shape((2, seq, 2 * kv_width)), ANY), q_other=(shape((side, side, rows, head)), ANY), dqkv=(shape((side, side, rows, depth)), VMEM))
-    scratch = dict(w_out=pltpu.VMEM((2 * head, width), BF16), grad_ctx=pltpu.VMEM((seq, 2 * head), BF16), grad_k=pltpu.VMEM((seq, head), F32), grad_v=pltpu.VMEM((seq, head), F32), w_out_sem=dma((K2,)), resid_sem=dma((side,)),
+    outs = dict(rows=(shape((2 * rows + 8, width)), VMEM), kv=(shape((2, seq, 2 * kv_width)), ANY), q_other=(shape((side, side, rows, head)), ANY), dqkv=(shape((side, side, rows, depth)), VMEM))
+    scratch = dict(w_out=pltpu.VMEM((2 * head, width), BF16), grad_ctx=pltpu.VMEM((seq, 2 * head), BF16), grad_k=pltpu.VMEM((seq, head), F32), grad_v=pltpu.VMEM((seq, head), F32), w_out_sem=dma((K2,)), resid_sem=dma((side,)), sum_p=rs_scratch(side, rows, width), wd=pltpu.VMEM((2 * mlp.acts[K0].shape[K3], width), BF16), wd_sem=dma((K2, K2)),
                    sum=rs_scratch(side, rows, width), all=ag_scratch(side, tokens, 2 * head, 2), x_rows=pltpu.VMEM((rows, width), BF16), x_sem=dma((K1,)), w=pltpu.VMEM((width, depth), BF16), w_sem=dma((K2, 4)),
                    mate=pltpu.VMEM((half_side, side, rows, 2 * head), BF16), mate_sems=[dma((K1,)), dma((K1,))], swap_sems=[dma((K1,)), dma((K1,))])
     return call_kernel('sum_input', body, ins, outs, scratch, 3e8, 3)
@@ -991,12 +999,12 @@
     )(*[right for _, right in groups], *lefts, *ctxs, *tokens)
 
 
-def weight_grads_pair(left_gate, left_up, mixed_full):
+def weight_grads_pair(left_gate, left_up, mixed_full, token):
     seq, width = mixed_full.shape[1:]
     depth = left_gate.shape[K0]
     tile = min(512, width)
 
-    def kernel(m_ref, gate_ref, up_ref, out_gate, out_up):
+    def kernel(m_ref, gate_ref, up_ref, _, out_gate, out_up):
         mixed = m_ref[...].reshape(2 * seq, tile)
         out_gate[...] = dot(gate_ref[...], mixed, NN)
         out_up[...] = dot(up_ref[...], mixed, NN)
@@ -1007,11 +1015,11 @@
         name='weight_grads_pair',
         grid=(width // tile,),
         out_shape=[shape((depth, width), F32)] * 2,
-        in_specs=[pl.BlockSpec((2, seq, tile), lambda step: (0, 0, step)), VMEM, VMEM],
+        in_specs=[pl.BlockSpec((2, seq, tile), lambda step: (0, 0, step)), VMEM, VMEM, ANY],
         out_specs=[out, out],
         compiler_params=pltpu.CompilerParams(vmem_limit_bytes=LIMIT),
         cost_estimate=pl.CostEstimate(flops=int(1e10), bytes_accessed=int(4e7), transcendentals=0),
-    )(mixed_full, left_gate, left_up)
+    )(mixed_full, left_gate, left_up, token)
 
 
 def weight_grads_qkv(normeds, kv_full, grads_q):
@@ -1052,46 +1060,47 @@
 
 
 def in_place(gathered, rows):
-    blocks, held, width = gathered.shape
+    blocks, _, width = gathered.shape
     slots = 24
-    gains = 2 if held > rows else 0
-
-    def kernel(src, dst, *refs):
-        buf, extra, in_sem, out_sem, extra_sem = refs[gains:]
+    pieces = 2 * blocks
+
+    def kernel(src, dx_ref, y_ref, gain_attn, gain_mlp, buf, extra, in_sem, out_sem, extra_sem):
+        gains = pltpu.make_async_copy(src.at[:, pl.ds(2 * rows, 8), :], extra, extra_sem.at[K0])
 
         def load(index):
-            return pltpu.make_async_copy(src.at[index, pl.ds(0, rows), :], buf.at[index % slots], in_sem.at[index % slots])
+            at = pl.ds(index // blocks * rows, rows)
+            return pltpu.make_async_copy(src.at[index % blocks, at, :], buf.at[index % slots], in_sem.at[index % slots])
 
         def store(index):
-            return pltpu.make_async_copy(buf.at[index % slots], dst.at[index % 2, index // 2], out_sem.at[index % slots])
+            dst, block = (dx_ref, y_ref)[index // blocks], index % blocks
+            return pltpu.make_async_copy(buf.at[index % slots], dst.at[block % 2, block // 2], out_sem.at[index % slots])
 
         ahead = slots // 2
-        for index in range(blocks + ahead):
-            if index < blocks:
+        for index in range(pieces + ahead):
+            if index < pieces:
                 if index >= slots:
                     store(index - slots).wait()
                 load(index).start()
-            if index == ahead and gains:
-                last = pltpu.make_async_copy(src.at[:, pl.ds(held - 8, 8), :], extra, extra_sem.at[K0])
-                last.start()
+            if index == ahead:
+                gains.start()
             if index >= ahead:
                 load(index - ahead).wait()
                 store(index - ahead).start()
-        if gains:
-            last.wait()
-            total = jnp.sum(extra[...].astype(F32), axis=0)
-            for first, ref in zip((0, 3), refs):
-                ref[...] = total[first:first + 1] + total[first + 1:first + 2] + total[first + 2:first + 3]
-        for index in range(blocks - slots, blocks):
+        gains.wait()
+        total = jnp.sum(extra[...].astype(F32), axis=0)
+        for first, ref in ((0, gain_attn), (3, gain_mlp)):
+            ref[...] = total[first:first + 1] + total[first + 1:first + 2] + total[first + 2:first + 3]
+        for index in range(pieces - slots, pieces):
             store(index).wait()
 
     dma = pltpu.SemaphoreType.DMA
+    whole = shape((2, blocks // 2, rows, width))
     return pl.pallas_call(
         kernel,
         name='in_place',
-        out_shape=[shape((2, blocks // 2, rows, width))] + [shape((1, width), F32)] * gains,
+        out_shape=[whole, whole, shape((1, width), F32), shape((1, width), F32)],
         in_specs=[ANY],
-        out_specs=[ANY] + [VMEM] * gains,
+        out_specs=[ANY, ANY, VMEM, VMEM],
         scratch_shapes=[pltpu.VMEM((slots, rows, width), BF16), pltpu.VMEM((blocks, 8, width), BF16), dma((slots,)), dma((slots,)), dma((K1,))],
         compiler_params=pltpu.CompilerParams(vmem_limit_bytes=LIMIT),
         cost_estimate=pl.CostEstimate(flops=int(2e7), bytes_accessed=int(2e7), transcendentals=0),
@@ -1119,14 +1128,14 @@
         w_qs, w_outs = (w_q, attn.w_q), (w_o, attn.w_o)
         mlp = sum_attention(side, attn, w_outs, hidden, grad_out, gain_mlp_row, w_gate.T, w_up.T, w_down)
         mixed_full = mlp.full.reshape(2, seq_len, width)
-        second = sum_mlp(side, mlp, (w_gate.T, mlp.w_gate), (w_up.T, mlp.w_up), (w_down, mlp.w_down), grad_out, gain_mlp_row)
+        second = sum_mlp(side, mlp, (w_gate.T, mlp.w_gate), (w_up.T, mlp.w_up), grad_out, gain_mlp_row)
         resid_full = second.full.reshape(2, seq_len, width)
 
-        (y_out,) = in_place(lax.all_gather(second.y_rows, 'tp'), rows)
+        third = sum_input(side, attn.qkv, seg_ids, w_outs, w_qs, w_k, w_v, hidden, second, gain_attn_row, mlp, (w_down, mlp.w_down))
+
+        grad_in, y_out, grad_gain_attn, grad_gain_mlp = in_place(lax.all_gather(third.rows, 'tp'), rows)
         left_gate, left_up, left_act = second.lefts
-        grad_gate_t, grad_up_t = weight_grads_pair(left_gate, left_up, mixed_full)
-        third = sum_input(side, attn.qkv, seg_ids, w_outs, w_qs, w_k, w_v, hidden, second, gain_attn_row, grad_up_t)
-        grad_in, grad_gain_attn, grad_gain_mlp = in_place(lax.all_gather(third.rows, 'tp'), rows)
+        grad_gate_t, grad_up_t = weight_grads_pair(left_gate, left_up, mixed_full, third.q_other)
         grad_w_down, grad_w_o = weight_grads('weight_grads_down', [(left_act, grad_out), (None, resid_full)], (attn.ctx, flat(mlp.ctx_other)), (third.q_other,))
         grad_w_q, grad_w_k, grad_w_v = weight_grads_qkv((attn.normed, mlp.normed_other), third.kv, (flat(third.dqkv), flat(third.q_other)))
         return (y_out.reshape(hidden.shape), grad_in.reshape(hidden.shape), grad_gain_attn[K0], grad_gain_mlp[K0], grad_w_q, grad_w_k, grad_w_v, grad_w_o, grad_gate_t.T, grad_up_t.T, grad_w_down)

time: 435 us -> 428 us (0.984)
  Pallas kernels: 413 us -> 386 us
  waiting for transfers between devices: 0.13 us -> 20.2 us
    pallas_call x4, Pallas kernels: 320 us -> 295 us  [call_kernel(): pl.pallas_call(kernel, name=name, out_shape=[leaf[K0] for leaf in out_lea...]
    all_gather x1, waiting for transfers between devices: 0.02 us -> 20.1 us  [device_step(): lax.all_gather(third.rows, 'tp')]
    pallas_call x2 -> x1, Pallas kernels: 20.3 us -> 18.7 us  [in_place(): pl.pallas_call(kernel, name='in_place', out_shape=[whole, whole, shape((1...]
  transfers between devices with their start and end apart: 2 -> 1, of which waited for: 0 -> 1; matrix products, arithmetic and copies ran while one was open for 0% -> 0% of each run, Pallas kernels for 41% -> 17%
where the time goes in v9:
time: 428 us; the launch traced here: 421 us
  Pallas kernels  386 us (90%)
  waiting for transfers between devices  20.2 us (5%)
  between operations  14.3 us (3%)
    pallas_call x4, Pallas kernels, call_kernel(): pl.pallas_call(kernel, name=name, out_shape=[leaf[K0] for leaf in out_lea...  295 us
    pallas_call x1, Pallas kernels, weight_grads_qkv(): pl.pallas_call(kernel, name='weight_grads_qkv', grid=(width // tile,), ou...  39.4 us
    all_gather x1, waiting for transfers between devices, device_step(): lax.all_gather(third.rows, 'tp')  20.1 us
    pallas_call x1, Pallas kernels, in_place(): pl.pallas_call(kernel, name='in_place', out_shape=[whole, whole, shape((1...  18.7 us
    pallas_call x1, Pallas kernels, weight_grads(): pl.pallas_call(kernel, name=name, grid=(width // tile,), out_shape=[shape...  16.7 us
    pallas_call x1, Pallas kernels, weight_grads_pair(): pl.pallas_call(kernel, name='weight_grads_pair', grid=(width // tile,), o...  16.5 us
  transfers between devices with their start and end apart: 1, of which 1 were waited for; matrix products, arithmetic and copies ran while one was open for 0% of the time, Pallas kernels for 17%

profile of v9, /device:TPU:97, one launch (start us, length us, event | category | flops | bytes accessed | tf_op | source)
XLA Modules:
  0.0 421.0 jit_solution(11196692225264896921)
XLA Ops:
  7.2 0.1 all-gather.3.cloned.1.call-start
  7.3 15.1 %attention_forward.1 = (bf16[768,256]{1,0:T(8,128)(2,1)}, bf16[768,4096]{1,0:T(8,128)(2,1)}, bf16[768,512]{1,0:T(8,128)(2,1)}, bf16[128,4096]{1,0:T(8,128)(2,1)}, bf16[4096,128]{1,0:T(8,128)(2,1)}) custom-call(f32[1,4096]{1,0:T(1,128)} %bitcast.25, bf16[2,768,4096]{2,1,0:T(8,128)(2,1)} %refs_6_.3, s32[2,768]{1,0:T(2,128)} %refs_9_.1, ...), custom_call_target="tpu_custom_call" | custom-call | flops 5000000000 | bytes 40000000 | tf_op jit(solution)/shard_map/attention_forward/pallas_call | solution.py:491
  22.3 91.5 %sum_attention.1 = (bf16[4,4,48,448]{3,2,1,0:T(8,128)(2,1)}, bf16[4,4,48,448]{3,2,1,0:T(8,128)(2,1)}, bf16[4,4,48,128]{3,2,1,0:T(8,128)(2,1)}, bf16[2,4,4,48,409...) custom-call(bf16[4,4,48,256]{3,2,1,0:T(8,128)(2,1)} %bitcast.22, ...), custom_call_target="tpu_custom_call" | custom-call | flops 400000000 | bytes 40000000 | tf_op jit(solution)/shard_map/sum_attention/pallas_call | solution.py:491
  113.8 86.9 %sum_mlp.1 = (f32[48,4096]{1,0:T(8,128)}, bf16[2,4,4,48,4096]{4,3,2,1,0:T(8,128)(2,1)}, f32[1,4096]{1,0:T(1,128)}, bf16[448,1536]{1,0:T(8,128)(2,1)}, bf16[448,1...) custom-call(bf16[4,4,48,448]{3,2,1,0:T(8,128)(2,1)} %get-tuple-element.54.refs_0_, ...), custom_call_target="tpu_custom_call" | custom-call | flops 600000000 | bytes 40000000 | tf_op jit(solution)/shard_map/sum_mlp/pallas_call | solution.py:491
  200.7 101.8 %sum_input.1 = (bf16[4,4,48,512]{3,2,1,0:T(8,128)(2,1)}, bf16[2,768,2048]{2,1,0:T(8,128)(2,1)}, bf16[4,4,48,128]{3,2,1,0:T(8,128)(2,1)}, bf16[104,4096]{1,0:T(8,128)(2,1)}) custom-call(bf16[4,4,48,448]{3,2,1,0:T(8,128)(2,1)} %get-tuple-element.54.refs_0_, bf16[4,4,48,448]{3,2,1,0:T(8,128)(2,1)} %get-tuple-element.55.refs_1_, ...), custom_call_target="tpu_custom_call" | custom-call | flops 300000000 | bytes 40000000 | tf_op jit(solution)/shard_map/sum_input/pallas_call | solution.py:491
  302.5 0.1 all-gather.3.cloned.1.call-update
  302.6 16.7 %weight_grads_down.1 = (f32[448,4096]{1,0:T(8,128)}, f32[128,4096]{1,0:T(8,128)}) custom-call(bf16[2,768,4096]{2,1,0:T(8,128)(2,1)} %refs_0_.1, bf16[2,768,4096]{2,1,0:T(8,128)(2,1)} %bitcast.28, bf16[448,1536]{1,0:T(8,128)(2,1)} %get-tuple-element.82.refs_2_, bf16[768,256]{1,0:T(8,128)(2,1)} %get-tuple-element.51.refs_3_, bf16[768,128]{1,0:T(8,128)(2,1)} %bitcast.32, ...), custom_call_target="tpu_custom_call" | custom-call | flops 10000000000 | bytes 40000000 | tf_op jit(solution)/shard_map/weight_grads_down/pallas_call | solution.py:989
  319.3 16.5 %weight_grads_pair.1 = (f32[448,4096]{1,0:T(8,128)}, f32[448,4096]{1,0:T(8,128)}) custom-call(bf16[2,768,4096]{2,1,0:T(8,128)(2,1)} %bitcast.27, bf16[448,1536]{1,0:T(8,128)(2,1)} %get-tuple-element.86.gate_ref, bf16[448,1536]{1,0:T(8,128)(2,1)} %get-tuple-element.87.up_ref, bf16[4,4,48,128]{3,2,1,0:T(8,128)(2,1)} %get-tuple-element.77.refs_5_._), custom_call_target="tpu_custom_call" | custom-call | flops 10000000000 | bytes 40000000 | tf_op jit(solution)/shard_map/weight_grads_pair/pallas_call | solution.py:1013
  335.7 39.4 %weight_grads_qkv.1 = (f32[4096,128]{1,0:T(8,128)}, f32[4096,1024]{1,0:T(8,128)}, f32[4096,1024]{1,0:T(8,128)}) custom-call(bf16[768,4096]{1,0:T(8,128)(2,1)} %get-tuple-element.52.refs_4_.a_own, bf16[768,4096]{1,0:T(8,128)(2,1)} %get-tuple-element.74.a_other, bf16[2,768,2048]{2,1,0:T(8,128)(2,1)} %get-tuple-element.75.kv_ref, bf16[768,512]{1,0:T(8,128)(2,1)} %bitcast.31, ...), custom_call_target="tpu_custom_call" | custom-call | flops 27000000512 | bytes 60000000 | tf_op jit(solution)/shard_map/weight_grads_qkv/pallas_call | solution.py:1049
  375.1 20.1 %all-gather.3.cloned.1.call-done = bf16[3328,4096]{1,0:T(8,128)(2,1)} async-done(((bf16[104,4096]{1,0:T(8,128)(2,1)}), bf16[3328,4096]{1,0:T(8,128)(2,1)}) %all-gather.3.cloned.1.call-update) | async-done | bytes 27262992 | tf_op jit(solution)/shard_map/all_gather | solution.py:1136
  395.2 18.7 %in_place.1 = (bf16[2,16,48,4096]{3,2,1,0:T(8,128)(2,1)}, bf16[2,16,48,4096]{3,2,1,0:T(8,128)(2,1)}, f32[1,4096]{1,0:T(1,128)}, f32[1,4096]{1,0:T(1,128)}) custom-call(bf16[32,104,4096]{2,1,0:T(8,128)(2,1)} %bitcast.17), custom_call_target="tpu_custom_call" | custom-call | flops 20000000 | bytes 20000000 | tf_op jit(solution)/shard_map/in_place/pallas_call | solution.py:1098
Async XLA Ops:
  7.2 388.0 %all-gather.3.cloned.1.call-start = ((), (), s32[]{:S(2)}) async-start(), calls=%async_computation | async-start | bytes 28114944 | tf_op jit(solution)/shard_map/all_gather | solution.py:1136
Sparse Core Ops, SparseCore 0:
  302.7 92.4 all-gather.2

commit v10 on v9

--- a/solution.py
+++ b/solution.py
@@ -364,7 +364,7 @@
 
 def fill_partial(torus, part, lhs, weights):
     rows, width = part.shape[2:]
-    tile = min(512, width // 2)
+    tile = min(1024, width // 2)
 
     def fill(shift):
         for col in torus.colours:
@@ -874,6 +874,7 @@
 def attention_forward(hidden, seg_ids, gain, w_q, w_k, w_v, w_o, per_kv):
     seq, width = hidden.shape[1:]
     chunk = seq // 4
+    group = 64
     tile = min(256, seq)
     depth = 4 * HEAD_DIM
 
@@ -910,27 +911,27 @@
                 staging.wait()
 
             def square(step, carry, index=index):
-                at = pl.ds(pl.multiple_of(index * chunk + step * 16, 16), 16)
-                total = jnp.zeros((16, HEAD_DIM), F32)
+                at = pl.ds(pl.multiple_of(index * chunk + step * group, group), group)
+                total = jnp.zeros((group, HEAD_DIM), F32)
                 for lane in range(0, width, HEAD_DIM):
                     value = scr.x[at, lane:lane + HEAD_DIM].astype(F32)
                     total = total + value * value
-                scr.squares[pl.ds(pl.multiple_of(step * 16, 16), 16), :] = total
+                scr.squares[pl.ds(pl.multiple_of(step * group, group), group), :] = total
                 return carry
 
-            lax.fori_loop(0, chunk // 16, square, 0)
+            lax.fori_loop(0, chunk // group, square, 0)
             inv = lax.rsqrt(jnp.sum(scr.squares[...], axis=-1, keepdims=True) / width + EPS)
             scr.squares[...] = jnp.broadcast_to(inv, scr.squares.shape)
 
             def normalize(step, carry, index=index):
-                at = pl.ds(pl.multiple_of(index * chunk + step * 16, 16), 16)
-                scale = scr.squares[pl.ds(pl.multiple_of(step * 16, 16), 16), :]
+                at = pl.ds(pl.multiple_of(index * chunk + step * group, group), group)
+                scale = scr.squares[pl.ds(pl.multiple_of(step * group, group), group), :]
                 for lane in range(0, width, HEAD_DIM):
                     cols = slice(lane, lane + HEAD_DIM)
                     scr.normed[at, cols] = (scr.x[at, cols].astype(F32) * scale * ins.gain[:, cols]).astype(BF16)
                 return carry
 
-            lax.fori_loop(0, chunk // 16, normalize, 0)
+            lax.fori_loop(0, chunk // group, normalize, 0)
             at = pl.ds(index * chunk, chunk)
             store = pltpu.make_async_copy(scr.normed.at[at, :], outs.normed.at[at, :], scr.out_sem.at[index])
             store.start()
@@ -1061,8 +1062,7 @@
 
 def in_place(gathered, rows):
     blocks, _, width = gathered.shape
-    slots = 24
-    pieces = 2 * blocks
+    slots = pieces = 2 * blocks
 
     def kernel(src, dx_ref, y_ref, gain_attn, gain_mlp, buf, extra, in_sem, out_sem, extra_sem):
         gains = pltpu.make_async_copy(src.at[:, pl.ds(2 * rows, 8), :], extra, extra_sem.at[K0])

time: 428 us -> 425 us (level)
    pallas_call x4, Pallas kernels: 295 us -> 291 us  [call_kernel(): pl.pallas_call(kernel, name=name, out_shape=[leaf[K0] for leaf in out_lea...]
where the time goes in v10:
time: 425 us; the launch traced here: 417 us
  Pallas kernels  382 us (90%)
  waiting for transfers between devices  20.1 us (5%)
  between operations  14.6 us (3%)
    pallas_call x4, Pallas kernels, call_kernel(): pl.pallas_call(kernel, name=name, out_shape=[leaf[K0] for leaf in out_lea...  291 us
    pallas_call x1, Pallas kernels, weight_grads_qkv(): pl.pallas_call(kernel, name='weight_grads_qkv', grid=(width // tile,), ou...  39.4 us
    all_gather x1, waiting for transfers between devices, device_step(): lax.all_gather(third.rows, 'tp')  20.1 us
    pallas_call x1, Pallas kernels, in_place(): pl.pallas_call(kernel, name='in_place', out_shape=[whole, whole, shape((1...  19.2 us
    pallas_call x1, Pallas kernels, weight_grads(): pl.pallas_call(kernel, name=name, grid=(width // tile,), out_shape=[shape...  16.7 us
    pallas_call x1, Pallas kernels, weight_grads_pair(): pl.pallas_call(kernel, name='weight_grads_pair', grid=(width // tile,), o...  16.5 us
  transfers between devices with their start and end apart: 1, of which 1 were waited for; matrix products, arithmetic and copies ran while one was open for 0% of the time, Pallas kernels for 17%

profile of v10, /device:TPU:97, one launch (start us, length us, event | category | flops | bytes accessed | tf_op | source)
XLA Modules:
  0.0 417.1 jit_solution(11012666214588716815)
XLA Ops:
  7.2 0.1 all-gather.3.cloned.1.call-start
  7.3 14.5 %attention_forward.1 = (bf16[768,256]{1,0:T(8,128)(2,1)}, bf16[768,4096]{1,0:T(8,128)(2,1)}, bf16[768,512]{1,0:T(8,128)(2,1)}, bf16[128,4096]{1,0:T(8,128)(2,1)}, bf16[4096,128]{1,0:T(8,128)(2,1)}) custom-call(f32[1,4096]{1,0:T(1,128)} %bitcast.25, bf16[2,768,4096]{2,1,0:T(8,128)(2,1)} %refs_6_.3, s32[2,768]{1,0:T(2,128)} %refs_9_.1, ...), custom_call_target="tpu_custom_call" | custom-call | flops 5000000000 | bytes 40000000 | tf_op jit(solution)/shard_map/attention_forward/pallas_call | solution.py:491
  21.7 90.8 %sum_attention.1 = (bf16[4,4,48,448]{3,2,1,0:T(8,128)(2,1)}, bf16[4,4,48,448]{3,2,1,0:T(8,128)(2,1)}, bf16[4,4,48,128]{3,2,1,0:T(8,128)(2,1)}, bf16[2,4,4,48,409...) custom-call(bf16[4,4,48,256]{3,2,1,0:T(8,128)(2,1)} %bitcast.22, ...), custom_call_target="tpu_custom_call" | custom-call | flops 400000000 | bytes 40000000 | tf_op jit(solution)/shard_map/sum_attention/pallas_call | solution.py:491
  112.6 85.0 %sum_mlp.1 = (f32[48,4096]{1,0:T(8,128)}, bf16[2,4,4,48,4096]{4,3,2,1,0:T(8,128)(2,1)}, f32[1,4096]{1,0:T(1,128)}, bf16[448,1536]{1,0:T(8,128)(2,1)}, bf16[448,1...) custom-call(bf16[4,4,48,448]{3,2,1,0:T(8,128)(2,1)} %get-tuple-element.54.refs_0_, ...), custom_call_target="tpu_custom_call" | custom-call | flops 600000000 | bytes 40000000 | tf_op jit(solution)/shard_map/sum_mlp/pallas_call | solution.py:491
  197.6 100.2 %sum_input.1 = (bf16[4,4,48,512]{3,2,1,0:T(8,128)(2,1)}, bf16[2,768,2048]{2,1,0:T(8,128)(2,1)}, bf16[4,4,48,128]{3,2,1,0:T(8,128)(2,1)}, bf16[104,4096]{1,0:T(8,128)(2,1)}) custom-call(bf16[4,4,48,448]{3,2,1,0:T(8,128)(2,1)} %get-tuple-element.54.refs_0_, bf16[4,4,48,448]{3,2,1,0:T(8,128)(2,1)} %get-tuple-element.55.refs_1_, ...), custom_call_target="tpu_custom_call" | custom-call | flops 300000000 | bytes 40000000 | tf_op jit(solution)/shard_map/sum_input/pallas_call | solution.py:491
  297.9 0.1 all-gather.3.cloned.1.call-update
  298.0 16.7 %weight_grads_down.1 = (f32[448,4096]{1,0:T(8,128)}, f32[128,4096]{1,0:T(8,128)}) custom-call(bf16[2,768,4096]{2,1,0:T(8,128)(2,1)} %refs_0_.1, bf16[2,768,4096]{2,1,0:T(8,128)(2,1)} %bitcast.28, bf16[448,1536]{1,0:T(8,128)(2,1)} %get-tuple-element.82.refs_2_, bf16[768,256]{1,0:T(8,128)(2,1)} %get-tuple-element.51.refs_3_, bf16[768,128]{1,0:T(8,128)(2,1)} %bitcast.32, ...), custom_call_target="tpu_custom_call" | custom-call | flops 10000000000 | bytes 40000000 | tf_op jit(solution)/shard_map/weight_grads_down/pallas_call | solution.py:990
  314.6 16.5 %weight_grads_pair.1 = (f32[448,4096]{1,0:T(8,128)}, f32[448,4096]{1,0:T(8,128)}) custom-call(bf16[2,768,4096]{2,1,0:T(8,128)(2,1)} %bitcast.27, bf16[448,1536]{1,0:T(8,128)(2,1)} %get-tuple-element.86.gate_ref, bf16[448,1536]{1,0:T(8,128)(2,1)} %get-tuple-element.87.up_ref, bf16[4,4,48,128]{3,2,1,0:T(8,128)(2,1)} %get-tuple-element.77.refs_5_._), custom_call_target="tpu_custom_call" | custom-call | flops 10000000000 | bytes 40000000 | tf_op jit(solution)/shard_map/weight_grads_pair/pallas_call | solution.py:1014
  331.1 39.4 %weight_grads_qkv.1 = (f32[4096,128]{1,0:T(8,128)}, f32[4096,1024]{1,0:T(8,128)}, f32[4096,1024]{1,0:T(8,128)}) custom-call(bf16[768,4096]{1,0:T(8,128)(2,1)} %get-tuple-element.52.refs_4_.a_own, bf16[768,4096]{1,0:T(8,128)(2,1)} %get-tuple-element.74.a_other, bf16[2,768,2048]{2,1,0:T(8,128)(2,1)} %get-tuple-element.75.kv_ref, bf16[768,512]{1,0:T(8,128)(2,1)} %bitcast.31, ...), custom_call_target="tpu_custom_call" | custom-call | flops 27000000512 | bytes 60000000 | tf_op jit(solution)/shard_map/weight_grads_qkv/pallas_call | solution.py:1050
  370.5 20.1 %all-gather.3.cloned.1.call-done = bf16[3328,4096]{1,0:T(8,128)(2,1)} async-done(((bf16[104,4096]{1,0:T(8,128)(2,1)}), bf16[3328,4096]{1,0:T(8,128)(2,1)}) %all-gather.3.cloned.1.call-update) | async-done | bytes 27262992 | tf_op jit(solution)/shard_map/all_gather | solution.py:1136
  390.5 19.2 %in_place.1 = (bf16[2,16,48,4096]{3,2,1,0:T(8,128)(2,1)}, bf16[2,16,48,4096]{3,2,1,0:T(8,128)(2,1)}, f32[1,4096]{1,0:T(1,128)}, f32[1,4096]{1,0:T(1,128)}) custom-call(bf16[32,104,4096]{2,1,0:T(8,128)(2,1)} %bitcast.17), custom_call_target="tpu_custom_call" | custom-call | flops 20000000 | bytes 20000000 | tf_op jit(solution)/shard_map/in_place/pallas_call | solution.py:1098
Async XLA Ops:
  7.2 383.4 %all-gather.3.cloned.1.call-start = ((), (), s32[]{:S(2)}) async-start(), calls=%async_computation | async-start | bytes 28114944 | tf_op jit(solution)/shard_map/all_gather | solution.py:1136
Sparse Core Ops, SparseCore 0:
  298.1 92.4 all-gather.2

commit v11 on v10

--- a/solution.py
+++ b/solution.py
@@ -810,7 +810,7 @@
         staging.wait()
         steps_p[K0]()
         wait()
-        sent, ringed = 5, 15
+        sent, ringed = 5, 18
         run(steps_p[1:sent])
         run(attention, steps_p[sent:ringed])
         staging.save(outs.dqkv)
@@ -895,7 +895,7 @@
 
         for index, ref in ((0, ins.w_q), (2, ins.w_k.at[:, pl.ds(kv_col, HEAD_DIM)]), (3, ins.w_v.at[:, pl.ds(kv_col, HEAD_DIM)])):
             loads.append(pltpu.make_async_copy(ref, w_cols(index), scr.w_sem.at[index]))
-        for load in loads:
+        for load in loads[4:] + loads[:4]:
             load.start()
         pl.semaphore_wait(barrier, 1)
         swaps = [(ins.w_q, w_cols(1)), (ins.w_o, outs.w_o), (ins.w_q, outs.w_q)]
@@ -1062,7 +1062,8 @@
 
 def in_place(gathered, rows):
     blocks, _, width = gathered.shape
-    slots = pieces = 2 * blocks
+    slots = 24
+    pieces = 2 * blocks
 
     def kernel(src, dx_ref, y_ref, gain_attn, gain_mlp, buf, extra, in_sem, out_sem, extra_sem):
         gains = pltpu.make_async_copy(src.at[:, pl.ds(2 * rows, 8), :], extra, extra_sem.at[K0])

time: 425 us -> 424 us (level)
  no operation moved by 1% of the time
where the time goes in v11:
time: 424 us; the launch traced here: 416 us
  Pallas kernels  381 us (90%)
  waiting for transfers between devices  20.1 us (5%)
  between operations  14.6 us (3%)
    pallas_call x4, Pallas kernels, call_kernel(): pl.pallas_call(kernel, name=name, out_shape=[leaf[K0] for leaf in out_lea...  290 us
    pallas_call x1, Pallas kernels, weight_grads_qkv(): pl.pallas_call(kernel, name='weight_grads_qkv', grid=(width // tile,), ou...  39.4 us
    all_gather x1, waiting for transfers between devices, device_step(): lax.all_gather(third.rows, 'tp')  20.1 us
    pallas_call x1, Pallas kernels, in_place(): pl.pallas_call(kernel, name='in_place', out_shape=[whole, whole, shape((1...  18.7 us
    pallas_call x1, Pallas kernels, weight_grads(): pl.pallas_call(kernel, name=name, grid=(width // tile,), out_shape=[shape...  16.7 us
    pallas_call x1, Pallas kernels, weight_grads_pair(): pl.pallas_call(kernel, name='weight_grads_pair', grid=(width // tile,), o...  16.5 us
  transfers between devices with their start and end apart: 1, of which 1 were waited for; matrix products, arithmetic and copies ran while one was open for 0% of the time, Pallas kernels for 17%

profile of v11, /device:TPU:97, one launch (start us, length us, event | category | flops | bytes accessed | tf_op | source)
XLA Modules:
  0.0 415.7 jit_solution(9145340876690321405)
XLA Ops:
  7.2 0.1 all-gather.3.cloned.1.call-start
  7.3 14.5 %attention_forward.1 = (bf16[768,256]{1,0:T(8,128)(2,1)}, bf16[768,4096]{1,0:T(8,128)(2,1)}, bf16[768,512]{1,0:T(8,128)(2,1)}, bf16[128,4096]{1,0:T(8,128)(2,1)}, bf16[4096,128]{1,0:T(8,128)(2,1)}) custom-call(f32[1,4096]{1,0:T(1,128)} %bitcast.25, bf16[2,768,4096]{2,1,0:T(8,128)(2,1)} %refs_6_.3, s32[2,768]{1,0:T(2,128)} %refs_9_.1, ...), custom_call_target="tpu_custom_call" | custom-call | flops 5000000000 | bytes 40000000 | tf_op jit(solution)/shard_map/attention_forward/pallas_call | solution.py:491
  21.7 89.9 %sum_attention.1 = (bf16[4,4,48,448]{3,2,1,0:T(8,128)(2,1)}, bf16[4,4,48,448]{3,2,1,0:T(8,128)(2,1)}, bf16[4,4,48,128]{3,2,1,0:T(8,128)(2,1)}, bf16[2,4,4,48,409...) custom-call(bf16[4,4,48,256]{3,2,1,0:T(8,128)(2,1)} %bitcast.22, ...), custom_call_target="tpu_custom_call" | custom-call | flops 400000000 | bytes 40000000 | tf_op jit(solution)/shard_map/sum_attention/pallas_call | solution.py:491
  111.6 85.0 %sum_mlp.1 = (f32[48,4096]{1,0:T(8,128)}, bf16[2,4,4,48,4096]{4,3,2,1,0:T(8,128)(2,1)}, f32[1,4096]{1,0:T(1,128)}, bf16[448,1536]{1,0:T(8,128)(2,1)}, bf16[448,1...) custom-call(bf16[4,4,48,448]{3,2,1,0:T(8,128)(2,1)} %get-tuple-element.54.refs_0_, ...), custom_call_target="tpu_custom_call" | custom-call | flops 600000000 | bytes 40000000 | tf_op jit(solution)/shard_map/sum_mlp/pallas_call | solution.py:491
  196.7 100.3 %sum_input.1 = (bf16[4,4,48,512]{3,2,1,0:T(8,128)(2,1)}, bf16[2,768,2048]{2,1,0:T(8,128)(2,1)}, bf16[4,4,48,128]{3,2,1,0:T(8,128)(2,1)}, bf16[104,4096]{1,0:T(8,128)(2,1)}) custom-call(bf16[4,4,48,448]{3,2,1,0:T(8,128)(2,1)} %get-tuple-element.54.refs_0_, bf16[4,4,48,448]{3,2,1,0:T(8,128)(2,1)} %get-tuple-element.55.refs_1_, ...), custom_call_target="tpu_custom_call" | custom-call | flops 300000000 | bytes 40000000 | tf_op jit(solution)/shard_map/sum_input/pallas_call | solution.py:491
  296.9 0.1 all-gather.3.cloned.1.call-update
  297.0 16.7 %weight_grads_down.1 = (f32[448,4096]{1,0:T(8,128)}, f32[128,4096]{1,0:T(8,128)}) custom-call(bf16[2,768,4096]{2,1,0:T(8,128)(2,1)} %refs_0_.1, bf16[2,768,4096]{2,1,0:T(8,128)(2,1)} %bitcast.28, bf16[448,1536]{1,0:T(8,128)(2,1)} %get-tuple-element.82.refs_2_, bf16[768,256]{1,0:T(8,128)(2,1)} %get-tuple-element.51.refs_3_, bf16[768,128]{1,0:T(8,128)(2,1)} %bitcast.32, ...), custom_call_target="tpu_custom_call" | custom-call | flops 10000000000 | bytes 40000000 | tf_op jit(solution)/shard_map/weight_grads_down/pallas_call | solution.py:990
  313.7 16.5 %weight_grads_pair.1 = (f32[448,4096]{1,0:T(8,128)}, f32[448,4096]{1,0:T(8,128)}) custom-call(bf16[2,768,4096]{2,1,0:T(8,128)(2,1)} %bitcast.27, bf16[448,1536]{1,0:T(8,128)(2,1)} %get-tuple-element.86.gate_ref, bf16[448,1536]{1,0:T(8,128)(2,1)} %get-tuple-element.87.up_ref, bf16[4,4,48,128]{3,2,1,0:T(8,128)(2,1)} %get-tuple-element.77.refs_5_._), custom_call_target="tpu_custom_call" | custom-call | flops 10000000000 | bytes 40000000 | tf_op jit(solution)/shard_map/weight_grads_pair/pallas_call | solution.py:1014
  330.1 39.4 %weight_grads_qkv.1 = (f32[4096,128]{1,0:T(8,128)}, f32[4096,1024]{1,0:T(8,128)}, f32[4096,1024]{1,0:T(8,128)}) custom-call(bf16[768,4096]{1,0:T(8,128)(2,1)} %get-tuple-element.52.refs_4_.a_own, bf16[768,4096]{1,0:T(8,128)(2,1)} %get-tuple-element.74.a_other, bf16[2,768,2048]{2,1,0:T(8,128)(2,1)} %get-tuple-element.75.kv_ref, bf16[768,512]{1,0:T(8,128)(2,1)} %bitcast.31, ...), custom_call_target="tpu_custom_call" | custom-call | flops 27000000512 | bytes 60000000 | tf_op jit(solution)/shard_map/weight_grads_qkv/pallas_call | solution.py:1050
  369.5 20.1 %all-gather.3.cloned.1.call-done = bf16[3328,4096]{1,0:T(8,128)(2,1)} async-done(((bf16[104,4096]{1,0:T(8,128)(2,1)}), bf16[3328,4096]{1,0:T(8,128)(2,1)}) %all-gather.3.cloned.1.call-update) | async-done | bytes 27262992 | tf_op jit(solution)/shard_map/all_gather | solution.py:1137
  389.6 18.7 %in_place.1 = (bf16[2,16,48,4096]{3,2,1,0:T(8,128)(2,1)}, bf16[2,16,48,4096]{3,2,1,0:T(8,128)(2,1)}, f32[1,4096]{1,0:T(1,128)}, f32[1,4096]{1,0:T(1,128)}) custom-call(bf16[32,104,4096]{2,1,0:T(8,128)(2,1)} %bitcast.17), custom_call_target="tpu_custom_call" | custom-call | flops 20000000 | bytes 20000000 | tf_op jit(solution)/shard_map/in_place/pallas_call | solution.py:1099
Async XLA Ops:
  7.2 382.4 %all-gather.3.cloned.1.call-start = ((), (), s32[]{:S(2)}) async-start(), calls=%async_computation | async-start | bytes 28114944 | tf_op jit(solution)/shard_map/all_gather | solution.py:1137
Sparse Core Ops, SparseCore 0:
  297.1 92.4 all-gather.2
